TPU v7x, 256 devices: a whole 4x4x8 slice. The times are simulated.
256 devices in a mesh: tm: 4 (over y), users: 64 (over z, x, core).
Axes of the slice: x: 4, y: 4, z: 8, core: 2. Of those that a mesh axis runs over, the one named last changes fastest.
Arguments:
- features: float32 [1048576, 128], P(('tm', 'users')), may hold values from -6 to 6
- home: int32 [1048576, 1], P(('tm', 'users')), may hold values from 0 to 63; in each aligned block of 4096 rows (0 to 4095, 4096 to 8191, ...) at most 128 rows name the same one
- account: int32 [1048576], P(('tm', 'users')), may hold values from 0 to 127
- flags: int32 [1048576], P(('tm', 'users')), may hold values 0 or 1
Outputs:
- session_mean: float32 [1048576, 128], P(('tm', 'users'))
Inputs may be any that keep to these rules, and one draw needn't show every extreme that they name: `home`: the 4096 events of one device name one owner at most 128 times, a bound that some block reaches.
All inputs are finite; a program needn't handle non-finite values. No bound on the sum of `flags` on one device may be relied on, other than what follows from the above.
Results may differ from a plain program's by a relative error of at most 0.00007.
Values sent between devices are 32-bit elements; how exact they have to be, the bound alone decides.
No kernel may reach another device: no remote copies, remote signals or barrier semaphores. Data moves between devices by JAX's collectives and lax.ppermute only.
A program may use at most 64 MiB of HBM per device.

v0:
```python
import math

import jax
import jax.numpy as jnp
from jax import lax
from jax.sharding import PartitionSpec as P

ACCOUNTS = 128


EXACT_MATMUL = lax.Precision.HIGHEST


def sent_to_all(x, axis):
    copies = jnp.broadcast_to(x, (lax.axis_size(axis), *x.shape))
    return lax.all_to_all(copies, axis, split_axis=0, concat_axis=0, tiled=True)


def laid_out(parts, dim):
    lengths = list(parts.shape[1:])
    lengths[dim] *= parts.shape[0]
    return jnp.moveaxis(parts, 0, dim).reshape(lengths)


def gather_directly(x, axis, dim):
    parts = sent_to_all(x, axis)
    return laid_out(parts, dim)


def side_by_side(arrays, axis, dim, along):
    widths = [math.prod(a.shape[along:]) for a in arrays]
    both = jnp.concatenate(
        [a.reshape(*a.shape[:along], w) for a, w in zip(arrays, widths)], axis=along
    )
    result = gather_directly(both, axis, dim)
    parts = jnp.split(result, [sum(widths[:k]) for k in range(1, len(widths))], axis=along)
    return tuple(
        (b.reshape(*result.shape[:along], *a.shape[along:]) for a, b in zip(arrays, parts))
    )


def destination_rank(owner_of, owners):
    count_per_row = owner_of.shape[0]
    block_rows = math.gcd(count_per_row, 512)
    blocks = count_per_row // block_rows
    strict_lower = (
        lax.broadcasted_iota(jnp.int32, (block_rows, block_rows), 0)
        > lax.broadcasted_iota(jnp.int32, (block_rows, block_rows), 1)
    ).astype(jnp.float32)
    columns = jnp.arange(owners, dtype=jnp.int32)

    def destination_advance(before, block_data):
        choose_mask = (block_data[:, None] == columns[None, :]).astype(jnp.float32)
        earlier = jnp.dot(strict_lower, choose_mask, precision=EXACT_MATMUL) + before[None, :]
        return (before + jnp.sum(choose_mask, axis=0), jnp.sum(earlier * choose_mask, axis=1))

    ignored, rank_rows = lax.scan(
        destination_advance, jnp.zeros((owners,), jnp.float32), owner_of.reshape(blocks, block_rows)
    )
    return rank_rows.reshape(count_per_row).astype(jnp.int32)


def decode_rows(code_rows):
    code_ints = code_rows.astype(jnp.int32)
    is_valid = code_ints >= 0
    account_rows = jnp.where(is_valid, code_ints // 2, -1)
    flag_rows = jnp.where(is_valid, code_ints % 2, 0).astype(jnp.float32)
    return (account_rows, flag_rows)


def session_sweep(values, account_rows, flag_rows, accounts):
    count_per_row, feature_count = values.shape
    block_rows = math.gcd(count_per_row, 512)
    blocks = count_per_row // block_rows
    row_ids = lax.broadcasted_iota(jnp.int32, (block_rows, block_rows), 0)
    col_ids = lax.broadcasted_iota(jnp.int32, (block_rows, block_rows), 1)
    up_to = col_ids <= row_ids
    later_rows = col_ids > row_ids
    up_to_float = up_to.astype(jnp.float32)
    columns = jnp.arange(accounts, dtype=jnp.int32)

    def session_advance(carried, block_data):
        open_sum, open_count, already_seen = carried
        rows_values, rows_account, rows_flag = block_data
        is_live = rows_account >= 0
        indicator_matrix = (rows_account[:, None] == columns[None, :]).astype(jnp.float32)
        flag_counts = jnp.dot(
            up_to_float, indicator_matrix * rows_flag[:, None], precision=EXACT_MATMUL
        )
        own_flags = jnp.sum(flag_counts * indicator_matrix, axis=1)
        same_user = (
            (rows_account[:, None] == rows_account[None, :]) & is_live[None, :] & is_live[:, None]
        )
        same_session = (same_user & up_to & (own_flags[:, None] == own_flags[None, :])).astype(
            jnp.float32
        )
        inside_sum = jnp.dot(same_session, rows_values, precision=EXACT_MATMUL)
        inside_count = jnp.sum(same_session, axis=1)
        session_continues = jnp.where(is_live & (own_flags == 0.0), 1.0, 0.0)
        running_sum = inside_sum + session_continues[:, None] * jnp.dot(
            indicator_matrix, open_sum, precision=EXACT_MATMUL
        )
        running_count = inside_count + session_continues * jnp.dot(
            indicator_matrix, open_count, precision=EXACT_MATMUL
        )
        without_flag = session_continues * (
            1.0 - jnp.dot(indicator_matrix, already_seen, precision=EXACT_MATMUL)
        )
        followers = jnp.sum((same_user & later_rows).astype(jnp.float32), axis=1)
        last_weight = jnp.where(is_live & (followers == 0.0), 1.0, 0.0)
        present = jnp.minimum(jnp.sum(indicator_matrix, axis=0), 1.0)
        updated_sum = (
            jnp.einsum(
                "ra,rf->af",
                indicator_matrix,
                last_weight[:, None] * running_sum,
                precision=EXACT_MATMUL,
            )
            + (1.0 - present)[:, None] * open_sum
        )
        updated_count = (
            jnp.dot(last_weight * running_count, indicator_matrix, precision=EXACT_MATMUL)
            + (1.0 - present) * open_count
        )
        any_flag = jnp.minimum(jnp.sum(indicator_matrix * rows_flag[:, None], axis=0), 1.0)
        updated_seen = jnp.maximum(already_seen, any_flag)
        return (
            (updated_sum, updated_count, updated_seen),
            (running_sum, running_count, without_flag),
        )

    start_state = (
        jnp.zeros((accounts, feature_count), jnp.float32),
        jnp.zeros((accounts,), jnp.float32),
        jnp.zeros((accounts,), jnp.float32),
    )
    block_data = (
        values.reshape(blocks, block_rows, feature_count),
        account_rows.reshape(blocks, block_rows),
        flag_rows.reshape(blocks, block_rows),
    )
    closing_state, row_pieces = lax.scan(session_advance, start_state, block_data)
    running_sum = row_pieces[0].reshape(count_per_row, feature_count)
    running_count = row_pieces[1].reshape(count_per_row)
    without_flag = row_pieces[2].reshape(count_per_row)
    return (closing_state, running_sum, running_count, without_flag)


def combine_states(earlier, later):
    carry_on = 1.0 - later[2]
    return (
        later[0] + carry_on[:, None] * earlier[0],
        later[1] + carry_on * earlier[1],
        jnp.maximum(earlier[2], later[2]),
    )


def body(features, home, account, flags):
    owners = lax.axis_size("users")
    event_rows, feature_count = features.shape
    slot_cap = 2 * event_rows // owners
    accounts = ACCOUNTS
    owner_of = home[:, 0]
    rank_rows = destination_rank(owner_of, owners)
    slot_index = owner_of * slot_cap + rank_rows
    code_values = (account * 2 + flags).astype(jnp.float32)
    send_values = (
        jnp.zeros((owners * slot_cap, feature_count), jnp.float32).at[slot_index].set(features)
    )
    send_codes = jnp.full((owners * slot_cap,), -1.0, jnp.float32).at[slot_index].set(code_values)
    got_values, got_codes = (
        lax.all_to_all(
            send_values.reshape(owners, slot_cap, feature_count),
            "users",
            split_axis=0,
            concat_axis=0,
            tiled=True,
        ),
        lax.all_to_all(
            send_codes.reshape(owners, slot_cap), "users", split_axis=0, concat_axis=0, tiled=True
        ),
    )
    account_rows, flag_rows = decode_rows(got_codes.reshape(owners * slot_cap))
    closing_state, running_sum, running_count, without_flag = session_sweep(
        got_values.reshape(owners * slot_cap, feature_count), account_rows, flag_rows, accounts
    )
    identity = (
        jnp.zeros((accounts, feature_count), jnp.float32),
        jnp.zeros((accounts,), jnp.float32),
        jnp.zeros((accounts,), jnp.float32),
    )
    gathered = side_by_side((closing_state[0], closing_state[1], closing_state[2]), "tm", 0, 1)
    my_group = lax.axis_index("tm")
    incoming = identity
    for position in range(lax.axis_size("tm")):
        group_state = (
            gathered[0][position * accounts : (position + 1) * accounts],
            gathered[1][position * accounts : (position + 1) * accounts],
            gathered[2][position * accounts : (position + 1) * accounts],
        )
        merged = combine_states(incoming, group_state)
        incoming = (
            jnp.where(position < my_group, merged[0], incoming[0]),
            jnp.where(position < my_group, merged[1], incoming[1]),
            jnp.where(position < my_group, merged[2], incoming[2]),
        )
    columns = jnp.arange(accounts, dtype=jnp.int32)
    onehot_rows = (account_rows[:, None] == columns[None, :]).astype(jnp.float32)
    overall_sum = running_sum + without_flag[:, None] * jnp.dot(
        onehot_rows, incoming[0], precision=EXACT_MATMUL
    )
    overall_count = running_count + without_flag * jnp.dot(
        onehot_rows, incoming[1], precision=EXACT_MATMUL
    )
    session_means = overall_sum / jnp.where(overall_count > 0.0, overall_count, 1.0)[:, None]
    returned_means = lax.all_to_all(
        session_means.reshape(owners, slot_cap, feature_count),
        "users",
        split_axis=0,
        concat_axis=0,
        tiled=True,
    )
    result = returned_means.reshape(owners * slot_cap, feature_count)[slot_index]
    return result


def solution(mesh):
    return jax.shard_map(
        body,
        mesh=mesh,
        in_specs=(
            P(("tm", "users"), None),
            P(("tm", "users"), None),
            P(("tm", "users")),
            P(("tm", "users")),
        ),
        out_specs=P(("tm", "users"), None),
        check_vma=False,
    )
```

profile of v0, /device:TPU:1, one launch (start us, length us, event | category | flops | bytes accessed | tf_op | source)
XLA Modules:
  0.0 389.0 jit_solution(14913307435275098245)
XLA Ops:
  0.6 1.4 reduce.9
  2.1 5.6 %while.34 = (s32[]{:T(128)}, f32[64]{0:T(128)S(1)}, f32[8,512]{1,0:T(8,128)S(1)}, s32[8,512]{1,0:T(8,128)S(1)}, s32[]{:T(128)}, /*index=5*/s32[]{:T(128)}) while((s32[]{:T(128)}, f32[64]{0:T(128)S(1)}, f32[8,512]{1,0:T(8,128)S(1)}, s32[8,512]{1,0:T(8,128)S(1)}, s32[]{:T(128)}, /*index=5*/s32[]{:T(128)}) %tuple.69), condition=%wide.region_3.4_spmd.clone, body=%wide.region_0.3_spmd.clone.sunk | while | flops 202112576 | bytes 15967 | solution.py:57
  9.2 16.1 %scatter_custom_fusion = f32[8192]{0:T(1024)} fusion(s32[4096]{0:T(1024)S(1)} %bitcast.178, f32[4096]{0:T(1024)S(1)} %add_convert_fusion, f32[]{:T(128)} %constant.54.clone.1), kind=kCustom, calls=%fused_computation.136 | custom fusion | bytes 32772 | tf_op jit(solution)/shard_map/scatter | solution.py:170
  25.3 13.0 %all-to-all-start = ((f32[64,1,128]{2,1,0:T(1,128)}), f32[64,1,128]{2,1,0:T(1,128)S(1)}, u32[]{:S(2)}, u32[]{:S(2)}) async-start(f32[64,1,128]{2,1,0:T(1,128)} %bitcast.1), calls=%async_computation | async-start | bytes 65536 | tf_op jit(solution)/shard_map/all_to_all | solution.py:179
  38.2 13.1 %scatter_custom_fusion.1 = f32[8192,128]{1,0:T(8,128)} fusion(s32[4096]{0:T(1024)S(1)} %bitcast.179, f32[4096,128]{1,0:T(8,128)} %param.8, f32[]{:T(128)} %constant.49.clone.1), kind=kCustom, calls=%fused_computation.88 | custom fusion | bytes 4194816 | tf_op jit(solution)/shard_map/scatter | solution.py:168
  51.4 10.5 %all-to-all-start.1 = ((f32[64,128,128]{2,1,0:T(8,128)}), f32[64,128,128]{2,1,0:T(8,128)}, u32[]{:S(2)}, u32[]{:S(2)}) async-start(f32[64,128,128]{2,1,0:T(8,128)} %bitcast.151), calls=%async_computation.1 | async-start | bytes 8388608 | tf_op jit(solution)/shard_map/all_to_all | solution.py:172
  62.1 94.4 %all-to-all-done.1 = f32[64,128,128]{2,1,0:T(8,128)} async-done(((f32[64,128,128]{2,1,0:T(8,128)}), f32[64,128,128]{2,1,0:T(8,128)}, u32[]{:S(2)}, u32[]{:S(2)}) %all-to-all-start.1) | async-done | bytes 4194336 | tf_op jit(solution)/shard_map/all_to_all | solution.py:172
  156.6 90.4 %while.35 = (s32[]{:T(128)}, f32[128,128]{1,0:T(8,128)S(1)}, f32[128]{0:T(128)S(1)}, f32[128]{0:T(128)S(1)}, f32[16,512,128]{2,1,0:T(8,128)}, /*index=5*/f32[16,...) while((s32[]{:T(128)}, f32[128,128]{1,0:T(8,128)S(1)}, ...), condition=%wide.region_12.13_spmd.clone, body=%wide.region_6.12_spmd.clone.sunk | while | flops 1016011008 | bytes 1867940 | solution.py:142
  158.9 1.7 fusion.151
  160.7 1.1 bitcast_dynamic-update-slice_fusion.2
  164.6 1.7 fusion.151
  166.3 1.1 bitcast_dynamic-update-slice_fusion.2
  170.2 1.7 fusion.151
  171.9 1.1 bitcast_dynamic-update-slice_fusion.2
  175.9 1.7 fusion.151
  177.6 1.1 bitcast_dynamic-update-slice_fusion.2
  181.5 1.7 fusion.151
  183.2 1.1 bitcast_dynamic-update-slice_fusion.2
  187.2 1.7 fusion.151
  188.9 1.1 bitcast_dynamic-update-slice_fusion.2
  192.9 1.7 fusion.151
  194.6 1.1 bitcast_dynamic-update-slice_fusion.2
  198.5 1.7 fusion.151
  200.2 1.1 bitcast_dynamic-update-slice_fusion.2
  204.2 1.7 fusion.151
  205.9 1.1 bitcast_dynamic-update-slice_fusion.2
  209.8 1.7 fusion.151
  211.5 1.1 bitcast_dynamic-update-slice_fusion.2
  215.5 1.7 fusion.151
  217.2 1.1 bitcast_dynamic-update-slice_fusion.2
  221.1 1.7 fusion.151
  222.8 1.1 bitcast_dynamic-update-slice_fusion.2
  224.5 0.9 fusion.149
  226.8 1.7 fusion.151
  228.5 1.1 bitcast_dynamic-update-slice_fusion.2
  232.4 1.7 fusion.151
  234.1 1.1 bitcast_dynamic-update-slice_fusion.2
  238.1 1.7 fusion.151
  239.8 1.1 bitcast_dynamic-update-slice_fusion.2
  243.7 1.7 fusion.151
  245.4 1.1 bitcast_dynamic-update-slice_fusion.2
  248.1 4.2 %all-to-all-start.2 = ((f32[4,128,130]{1,2,0:T(8,128)}), f32[4,128,130]{1,2,0:T(8,128)S(1)}, u32[]{:S(2)}, u32[]{:S(2)}) async-start(f32[4,128,130]{1,2,0:T(8,128)} %broadcast_in_dim.79), calls=%async_computation.2 | async-start | bytes 557056 | tf_op jit(solution)/shard_map/all_to_all | solution.py:16
  252.3 5.6 %all-to-all-done.2 = f32[4,128,130]{1,2,0:T(8,128)S(1)} async-done(((f32[4,128,130]{1,2,0:T(8,128)}), f32[4,128,130]{1,2,0:T(8,128)S(1)}, u32[]{:S(2)}, u32[]{:S(2)}) %all-to-all-start.2) | async-done | bytes 266272 | tf_op jit(solution)/shard_map/all_to_all | solution.py:16
  258.1 2.9 fusion.58
  261.0 8.2 %fusion.57 = f32[8192,128]{1,0:T(8,128)} fusion(f32[8192,128]{1,0:T(8,128)} %bitcast.191, f32[8192]{0:T(1024)S(1)} %compare_select_fusion.1, s32[8192]{0:T(1024)S(1)} %fusion.78, f32[8192]{0:T(1024)S(1)} %bitcast.176, f32[512,130]{0,1:T(8,128)S(1)} %bitcast.167, f32[128]{0:T(128)S(1)} %get-tuple-element.229, f32[128]{0:T(128)S(1)} %get-tuple-element.228, ...), kind=kOutput, calls=%fused_computation.83 | convolution fusion | flops 1614987264 | bytes 8751108 | tf_op jit(solution)/shard_map/dot_general | solution.py:209
  269.2 8.6 %all-to-all-start.3 = ((f32[64,128,128]{2,1,0:T(8,128)}), f32[64,128,128]{2,1,0:T(8,128)}, u32[]{:S(2)}, u32[]{:S(2)}) async-start(f32[64,128,128]{2,1,0:T(8,128)} %bitcast.152), calls=%async_computation.3 | async-start | bytes 8388608 | tf_op jit(solution)/shard_map/all_to_all | solution.py:216
  277.9 94.8 %all-to-all-done.3 = f32[64,128,128]{2,1,0:T(8,128)} async-done(((f32[64,128,128]{2,1,0:T(8,128)}), f32[64,128,128]{2,1,0:T(8,128)}, u32[]{:S(2)}, u32[]{:S(2)}) %all-to-all-start.3) | async-done | bytes 4194336 | tf_op jit(solution)/shard_map/all_to_all | solution.py:216
  372.7 16.4 %gather_fusion = f32[4096,128]{1,0:T(8,128)} fusion(f32[8192,128]{1,0:T(8,128)} %bitcast.19, s32[4096]{0:T(1024)S(1)} %broadcast_clamp_fusion), kind=kCustom, calls=%fused_computation | custom fusion | bytes 4210688 | tf_op jit(solution)/shard_map/gather | solution.py:223
  (296 shorter events, 52.1 us)
Async XLA Ops:
  25.3 26.1 %all-to-all-start = ((f32[64,1,128]{2,1,0:T(1,128)}), f32[64,1,128]{2,1,0:T(1,128)S(1)}, u32[]{:S(2)}, u32[]{:S(2)}) async-start(f32[64,1,128]{2,1,0:T(1,128)} %bitcast.1), calls=%async_computation | async-start | bytes 65536 | tf_op jit(solution)/shard_map/all_to_all | solution.py:179
  51.4 105.2 %all-to-all-start.1 = ((f32[64,128,128]{2,1,0:T(8,128)}), f32[64,128,128]{2,1,0:T(8,128)}, u32[]{:S(2)}, u32[]{:S(2)}) async-start(f32[64,128,128]{2,1,0:T(8,128)} %bitcast.151), calls=%async_computation.1 | async-start | bytes 8388608 | tf_op jit(solution)/shard_map/all_to_all | solution.py:172
  248.1 9.8 %all-to-all-start.2 = ((f32[4,128,130]{1,2,0:T(8,128)}), f32[4,128,130]{1,2,0:T(8,128)S(1)}, u32[]{:S(2)}, u32[]{:S(2)}) async-start(f32[4,128,130]{1,2,0:T(8,128)} %broadcast_in_dim.79), calls=%async_computation.2 | async-start | bytes 557056 | tf_op jit(solution)/shard_map/all_to_all | solution.py:16
  269.2 103.4 %all-to-all-start.3 = ((f32[64,128,128]{2,1,0:T(8,128)}), f32[64,128,128]{2,1,0:T(8,128)}, u32[]{:S(2)}, u32[]{:S(2)}) async-start(f32[64,128,128]{2,1,0:T(8,128)} %bitcast.152), calls=%async_computation.3 | async-start | bytes 8388608 | tf_op jit(solution)/shard_map/all_to_all | solution.py:216
where the time goes:
time: 391 us; the launch traced here: 389 us
  waiting for transfers between devices  195 us (50%)
  matrix products  89.2 us (23%)
  local copies, waits for them, and re-layouts  50.9 us (13%)
  starting transfers between devices  36.2 us (9%)
  other arithmetic  16.2 us (4%)
    all_to_all x1, waiting for transfers between devices, body(): lax.all_to_all(session_means.reshape(owners, slot_cap, feature_count), 'u...  94.8 us
    all_to_all x1, waiting for transfers between devices, body(): lax.all_to_all(send_values.reshape(owners, slot_cap, feature_count), 'use...  94.4 us
    dot_general x16, matrix products, session_advance(): inside_sum = jnp.dot(same_session, rows_values, precision=EXACT_MATMUL)  27.3 us
    dot_general x16, matrix products, session_advance(): jnp.dot(indicator_matrix, open_sum, precision=EXACT_MATMUL)  17.8 us
    gather x1, local copies, waits for them, and re-layouts, body(): returned_means.reshape(owners * slot_cap, feature_count)[slot_index]  16.4 us
    scatter x1, local copies, waits for them, and re-layouts, body(): jnp.full((owners * slot_cap,), -1.0, jnp.float32).at[slot_index]  16.1 us
    dot_general x16, matrix products, session_advance(): jnp.dot(up_to_float, indicator_matrix * rows_flag[:, None], precision=EXA...  14.1 us
    scatter x1, local copies, waits for them, and re-layouts, body(): jnp.zeros((owners * slot_cap, feature_count), jnp.float32).at[slot_index]  13.1 us
  transfers between devices with their start and end apart: 4, of which 3 were waited for; matrix products, arithmetic and copies ran while one was open for 3% of the time, Pallas kernels for 0%

commit v1 on v0

v1 whole, which is shorter than its diff:
```python
import functools

import jax
import jax.numpy as jnp
from jax import lax
from jax.experimental import pallas as pl
from jax.experimental.pallas import tpu as pltpu
from jax.sharding import Mesh, PartitionSpec as P

LANES = 128
ROWS = 136
NZ, NX, NC = 8, 4, 2
OWNERS = NZ * NX * NC
HALF = OWNERS // NC
CHUNK = HALF // NX
BF16, F32, I32 = jnp.bfloat16, jnp.float32, jnp.int32
VMEM = pl.BlockSpec(memory_space=pltpu.VMEM)
SMEM = pl.BlockSpec(memory_space=pltpu.SMEM)


def dot(a, b):
    return lax.dot_general(a, b, (((1,), (0,)), ((), ())), preferred_element_type=F32)


def dot_nt(a, b):
    return lax.dot_general(a, b, (((1,), (1,)), ((), ())), preferred_element_type=F32)


def iota(shape, dim):
    return lax.broadcasted_iota(I32, shape, dim)


def as_bf16(mask):
    return jnp.where(mask, 1.0, 0.0).astype(BF16)


def two_parts(v):
    high = v.astype(BF16)
    low = (v - high.astype(F32)).astype(BF16)
    return jnp.concatenate([high, low], axis=1)


def masked_sum(mask, parts):
    both = dot(mask, parts)
    return both[:, :LANES] + both[:, LANES:]


def column(row):
    return jnp.broadcast_to(row, (LANES, LANES)).T


def call(kernel, out, args, specs, out_specs=None, scratch=(), cost=1_000_000, limit=24):
    return pl.pallas_call(
        kernel,
        out_shape=out,
        in_specs=specs,
        out_specs=out_specs or jax.tree.map(lambda _: VMEM, out),
        scratch_shapes=list(scratch),
        cost_estimate=pl.CostEstimate(flops=cost, bytes_accessed=1_000_000, transcendentals=0),
        compiler_params=pltpu.CompilerParams(vmem_limit_bytes=limit << 20),
    )(*args)


def block(n=None):
    shape = (ROWS, LANES) if n is None else (n, ROWS, LANES)
    return jax.ShapeDtypeStruct(shape, F32)


def regroup_kernel(
    place, home, account, flags, features, slot_out, acc_out, flag_out, grouped, other, mine,
    slots, sem,
):
    lines = home.shape[0]
    below = as_bf16(iota((LANES, LANES), 0) < iota((LANES, LANES), 1))
    with_total = jnp.concatenate([below, jnp.ones((LANES, LANES), BF16)], axis=1)
    owner_ids = iota((OWNERS, LANES), 0)
    before = jnp.zeros((OWNERS, LANES), F32)
    codes = jnp.zeros((OWNERS, LANES), F32)
    for b in range(lines):
        home_row = home[b : b + 1, :]
        chosen = owner_ids == home_row
        counted = dot(as_bf16(chosen), with_total)
        rank = jnp.sum(
            jnp.where(chosen, counted[:, :LANES] + before, 0.0), axis=0, keepdims=True
        )
        before = before + counted[:, LANES:]
        slot_out[b : b + 1, :] = home_row * LANES + rank.astype(I32)
        code = (account[b : b + 1, :] * 2 + flags[b : b + 1, :] + 1).astype(F32)
        rank_of = as_bf16(iota((LANES, LANES), 0) == rank.astype(I32))
        codes = codes + dot_nt(jnp.where(chosen, code, 0.0).astype(BF16), rank_of)
    copy = pltpu.make_async_copy(slot_out, slots, sem)
    copy.start()
    code_ids = codes.astype(I32) - 1
    acc_out[...] = jnp.right_shift(code_ids, 1)
    flag_out[...] = jnp.where(code_ids >= 0, jnp.bitwise_and(code_ids, 1), 0).astype(F32)
    zero = jnp.zeros((LANES, LANES), F32)

    def clear(o, _):
        grouped[pl.ds(o * LANES, LANES), :] = zero
        return 0

    lax.fori_loop(0, OWNERS, clear, 0)
    copy.wait()

    def spread(b, _):
        for j in range(LANES):
            grouped[pl.ds(slots[b, j], 1), :] = features[pl.ds(b * LANES + j, 1), :]
        return 0

    lax.fori_loop(0, lines, spread, 0)

    after = as_bf16(iota((LANES, LANES), 0) > iota((LANES, LANES), 1))
    ones = jnp.ones((8, LANES), BF16)
    sub = iota((8, LANES), 0)
    half_of = place[0]

    def closing(o, out, at):
        acc_row = acc_out[pl.ds(o, 1), :]
        flag_row = flag_out[pl.ds(o, 1), :]
        member = iota((LANES, LANES), 0) == acc_row
        member_flags = jnp.where(member, flag_row, 0.0).astype(BF16)
        later_flags = dot(member_flags, after)
        counted = as_bf16(member & (later_flags < 0.5))
        values = two_parts(grouped[pl.ds(pl.multiple_of(o * LANES, LANES), LANES), :])
        out[at, :LANES, :] = masked_sum(counted, values)
        count = dot_nt(ones, counted)
        mark = jnp.minimum(dot_nt(ones, member_flags), 1.0)
        out[at, LANES:, :] = jnp.where(sub == 0, count, jnp.where(sub == 1, mark, 0.0))

    for out, base in ((other, (1 - half_of) * HALF), (mine, half_of * HALF)):

        def some(g, _, out=out, base=base):
            for i in range(4):
                closing(base + g * 4 + i, out, g * 4 + i)
            return 0

        lax.fori_loop(0, HALF // 4, some, 0)


def running_kernel(
    slots, slot_rows, home, account, acc_rows, flag_rows, grouped,
    run_out, count_out, open_out, user_out, run, counts, opens,
):
    lines = home.shape[0]
    after = as_bf16(iota((LANES, LANES), 0) > iota((LANES, LANES), 1))
    up_to = iota((LANES, LANES), 1) <= iota((LANES, LANES), 0)
    ones = jnp.ones((8, LANES), BF16)

    def some(g, _):
        rows = pl.ds(pl.multiple_of(g * 8, 8), 8)
        acc8 = acc_rows[rows, :]
        flag8 = flag_rows[rows, :]
        acc_cols = acc8.astype(F32).T
        count8, open8 = [], []
        for i in range(8):
            acc_row = acc8[i : i + 1, :].astype(F32)
            acc_col = jnp.broadcast_to(acc_cols[:, i : i + 1], (LANES, LANES))
            same = (acc_col == acc_row) & (acc_row >= 0.0) & up_to
            same_flags = jnp.where(same, flag8[i : i + 1, :], 0.0).astype(BF16)
            between = dot(same_flags, after)
            session = as_bf16(same & (between < 0.5))
            at = pl.ds(pl.multiple_of((g * 8 + i) * LANES, LANES), LANES)
            run[at, :] = masked_sum(session, two_parts(grouped[at, :]))
            count8.append(dot_nt(ones, session)[:1, :])
            open8.append(dot_nt(ones, same_flags)[:1, :])
        counts[rows, :] = jnp.concatenate(count8, axis=0)
        opens[rows, :] = jnp.where(jnp.concatenate(open8, axis=0) < 0.5, 1.0, 0.0)
        return 0

    lax.fori_loop(0, OWNERS // 8, some, 0)

    def scalars(t, _):
        rows = pl.ds(pl.multiple_of(t * 8, 8), 8)
        home8 = home[rows, :]
        rank = slot_rows[rows, :] - home8 * LANES
        count = jnp.zeros((8, LANES), F32)
        is_open = jnp.zeros((8, LANES), F32)
        for o in range(OWNERS):
            here = home8 == o
            for_count = jnp.broadcast_to(counts[o : o + 1, :], (8, LANES))
            for_open = jnp.broadcast_to(opens[o : o + 1, :], (8, LANES))
            count = jnp.where(here, jnp.take_along_axis(for_count, rank, axis=1), count)
            is_open = jnp.where(here, jnp.take_along_axis(for_open, rank, axis=1), is_open)
        count_out[rows, :] = count
        open_out[rows, :] = is_open
        user_out[rows, :] = home8 * ROWS + jnp.where(is_open > 0.5, account[rows, :], ROWS - 1)
        return 0

    lax.fori_loop(0, lines // 8, scalars, 0)

    def collect(b, _):
        for j in range(LANES):
            run_out[pl.ds(b * LANES + j, 1), :] = run[pl.ds(slots[b, j], 1), :]
        return 0

    lax.fori_loop(0, lines, collect, 0)


def joined(earlier, later):
    mark = later[LANES + 1 : LANES + 2, :]
    sums = later[:LANES, :] + column(1.0 - mark) * earlier[:LANES, :]
    sub = iota((8, LANES), 0)
    tail, first = later[LANES:, :], earlier[LANES:, :]
    tail = jnp.where(
        sub == 0, tail + (1.0 - mark) * first, jnp.where(sub == 1, jnp.maximum(tail, first), 0.0)
    )
    return jnp.concatenate([sums, tail], axis=0)


def core_kernel(place, mine, got, *outs):
    first, x = place[0] == 0, place[1]
    for k in range(NX):
        base = lax.rem(x + k, NX) * CHUNK

        def one(i, _, k=k, base=base):
            a, b = mine[base + i], got[base + i]
            outs[k][i] = joined(jnp.where(first, a, b), jnp.where(first, b, a))
            return 0

        lax.fori_loop(0, CHUNK, one, 0)


def row_kernel(place, t0, t1, t2, t3, out):
    tables = (t0, t1, t2, t3)
    for x in range(NX):

        @pl.when(place[1] == x)
        def _(x=x):
            def one(i, _):
                total = tables[x % NX][i]
                for j in range(1, NX):
                    total = joined(total, tables[(x - j) % NX][i])
                out[i] = total
                return 0

            lax.fori_loop(0, CHUNK, one, 0)


def plane_kernel(rows, out):
    total = rows[0]
    for z in range(1, NZ):
        total = joined(total, rows[z])
    out[...] = total


def rows_back_kernel(place, rows, planes, out):
    state = jnp.zeros((ROWS, LANES), F32)
    for y in range(planes.shape[0] - 1):
        state = jnp.where(y < place[2], joined(state, planes[y]), state)
    for z in range(NZ):
        out[z] = state
        if z < NZ - 1:
            state = joined(state, rows[z])


def chips_back_kernel(place, came, t0, t1, t2, t3, *outs):
    tables = (t0, t1, t2, t3)
    for x in range(NX):

        @pl.when(place[1] == x)
        def _(x=x):
            def one(i, _):
                state = came[i]
                for j in range(NX):
                    k = (x - j) % NX
                    outs[k][i] = state
                    if j < NX - 1:
                        state = joined(state, tables[k][i])
                return 0

            lax.fori_loop(0, CHUNK, one, 0)


def cores_back_kernel(place, p0, p1, p2, p3, mine, got, keep, send):
    parts = (p0, p1, p2, p3)
    first, x = place[0] == 0, place[1]
    for k in range(NX):
        base = lax.rem(x + k, NX) * CHUNK

        def one(i, _, k=k, base=base):
            state = parts[k][i]
            second = joined(state, jnp.where(first, mine[base + i], got[base + i]))
            keep[base + i] = jnp.where(first, state, second)
            send[base + i] = jnp.where(first, second, state)
            return 0

        lax.fori_loop(0, CHUNK, one, 0)


def finish_kernel(
    place, users, run, count, is_open, home, account, mine, got, out, table, picked, sems
):
    half_of = place[0]
    copies = [
        pltpu.make_async_copy(mine, table.at[pl.ds(half_of * HALF, HALF)], sems.at[0]),
        pltpu.make_async_copy(got, table.at[pl.ds((1 - half_of) * HALF, HALF)], sems.at[1]),
    ]
    for copy in copies:
        copy.start()
    for copy in copies:
        copy.wait()
    lines = home.shape[0]
    flat = table.reshape(OWNERS * ROWS, LANES)
    scale = []
    for t in range(lines // 8):
        rows = slice(8 * t, 8 * t + 8)
        home8, account8 = home[rows, :], account[rows, :]

        def owner(o, came):
            row = jnp.broadcast_to(table[o, LANES : LANES + 1, :], (8, LANES))
            return jnp.where(home8 == o, jnp.take_along_axis(row, account8, axis=1), came)

        came = jnp.zeros((8, LANES), F32)
        for o in range(OWNERS):
            came = owner(o, came)
        scale.append(1.0 / (count[rows, :] + is_open[rows, :] * came))
    scale = jnp.concatenate(scale, axis=0)
    if lines < LANES:
        scale = jnp.concatenate([scale, jnp.zeros((LANES - lines, LANES), F32)], axis=0)
    scale = scale.T

    def pick(b, _):
        for j in range(LANES):
            picked[pl.ds(b * LANES + j, 1), :] = flat[pl.ds(users[b, j], 1), :]
        return 0

    lax.fori_loop(0, lines, pick, 0)
    for b in range(lines):
        at = pl.ds(b * LANES, LANES)
        factor = jnp.broadcast_to(scale[:, b : b + 1], (LANES, LANES))
        out[at, :] = (run[at, :] + picked[at, :]) * factor


def ring(n, k):
    return [(i, (i + k) % n) for i in range(n)]


def body(features, home, account, flags):
    rows = features.shape[0]
    lines = rows // LANES
    home = home.reshape(lines, LANES)
    account = account.reshape(lines, LANES)
    flags = flags.reshape(lines, LANES)
    place = jnp.stack([lax.axis_index(a).astype(I32) for a in ("c", "x", "y", "z")])
    small = jax.ShapeDtypeStruct((lines, LANES), I32)
    small_f = jax.ShapeDtypeStruct((lines, LANES), F32)
    by_owner = functools.partial(jax.ShapeDtypeStruct, (OWNERS, LANES))
    slot, acc_rows, flag_rows, grouped, other, mine = call(
        regroup_kernel,
        [small, by_owner(I32), by_owner(F32),
         jax.ShapeDtypeStruct((OWNERS * LANES, LANES), F32), block(HALF), block(HALF)],
        (place, home, account, flags, features),
        [SMEM, VMEM, VMEM, VMEM, VMEM],
        scratch=[pltpu.SMEM((lines, LANES), I32), pltpu.SemaphoreType.DMA],
        cost=10_000_000_000,
    )
    swap = ring(NC, 1)
    got = lax.ppermute(other, "c", swap)
    run, count, is_open, users = call(
        running_kernel,
        [jax.ShapeDtypeStruct((rows, LANES), F32), small_f, small_f, small],
        (slot, slot, home, account, acc_rows, flag_rows, grouped),
        [SMEM] + [VMEM] * 6,
        scratch=[pltpu.VMEM((OWNERS * LANES, LANES), F32), pltpu.VMEM((OWNERS, LANES), F32),
                 pltpu.VMEM((OWNERS, LANES), F32)],
        cost=20_000_000_000,
    )
    chunks = call(core_kernel, [block(CHUNK)] * NX, (place, mine, got), [SMEM, VMEM, VMEM])
    tables = [chunks[0]] + [lax.ppermute(chunks[k], "x", ring(NX, k)) for k in range(1, NX)]
    row_total = call(row_kernel, block(CHUNK), (place, *tables), [SMEM] + [VMEM] * NX)
    row_totals = lax.all_to_all(row_total, "z", 0, 0, tiled=True)
    plane_total = call(plane_kernel, block(), (row_totals,), [VMEM])
    planes = lax.all_gather(plane_total, "y", axis=0)
    came = call(
        rows_back_kernel, block(NZ), (place, row_totals, planes), [SMEM, VMEM, VMEM]
    )
    came = lax.all_to_all(came, "z", 0, 0, tiled=True)
    parts = call(
        chips_back_kernel, [block(CHUNK)] * NX, (place, came, *tables), [SMEM] + [VMEM] * (NX + 1)
    )
    parts = [parts[0]] + [lax.ppermute(parts[k], "x", ring(NX, -k)) for k in range(1, NX)]
    keep, send = call(
        cores_back_kernel, [block(HALF)] * 2, (place, *parts, mine, got), [SMEM] + [VMEM] * (NX + 2)
    )
    last = lax.ppermute(send, "c", swap)
    anywhere = pl.BlockSpec(memory_space=pl.ANY)
    return call(
        finish_kernel,
        jax.ShapeDtypeStruct((rows, LANES), F32),
        (place, users, run, count, is_open, home, account, keep, last),
        [SMEM, SMEM] + [VMEM] * 5 + [anywhere] * 2,
        scratch=[pltpu.VMEM((OWNERS, ROWS, LANES), F32), pltpu.VMEM((rows, LANES), F32),
                 pltpu.SemaphoreType.DMA((2,))],
    )


def solution(mesh):
    split = Mesh(mesh.devices.reshape(-1, NZ, NX, NC), ("y", "z", "x", "c"))
    axes = ("y", "z", "x", "c")
    return jax.shard_map(
        body,
        mesh=split,
        in_specs=(P(axes, None), P(axes, None), P(axes), P(axes)),
        out_specs=P(axes, None),
        check_vma=False,
    )
```

time: 391 us -> 178 us (0.46)
  waiting for transfers between devices: 195 us -> 54.8 us
  matrix products: 89.2 us -> 0 us
  Pallas kernels: 0 us -> 56.7 us
  blocking collectives: 0 us -> 48.5 us
  local copies, waits for them, and re-layouts: 50.9 us -> 3.75 us
  starting transfers between devices: 36.2 us -> 13.2 us
  other arithmetic: 16.2 us -> 0.08 us
    all_to_all x4 -> x0, waiting for transfers between devices: 195 us -> none  [the longest x1 94.8 us: body(): lax.all_to_all(session_means.reshape(owners, slot_cap, feature_count), 'u...]
    dot_general x122 -> x0, matrix products: 89.2 us -> none  [the longest x16 27.3 us: session_advance(): inside_sum = jnp.dot(same_session, rows_values, precision=EXACT_MATMUL)]
    pallas_call x0 -> x9, Pallas kernels: none -> 56.7 us  [call(): pl.pallas_call(kernel, out_shape=out, in_specs=specs, out_specs=out_specs...]
    ppermute x0 -> x8, waiting for transfers between devices: none -> 54.8 us  [the longest x3 26.6 us: body(): lax.ppermute(parts[k], 'x', ring(NX, -k))]
    all_to_all x0 -> x2, blocking collectives: none -> 38.5 us  [the longest x1 23 us: body(): row_totals = lax.all_to_all(row_total, 'z', 0, 0, tiled=True)]
    all_to_all x4 -> x0, starting transfers between devices: 36.2 us -> none  [the longest x1 13 us: body(): lax.all_to_all(send_codes.reshape(owners, slot_cap), 'users', split_axis=...]
    scatter x2 -> x0, local copies, waits for them, and re-layouts: 29.2 us -> none  [the longest x1 16.1 us: body(): jnp.full((owners * slot_cap,), -1.0, jnp.float32).at[slot_index]]
    gather x1 -> x0, local copies, waits for them, and re-layouts: 16.4 us -> none  [body(): returned_means.reshape(owners * slot_cap, feature_count)[slot_index]]
  transfers between devices with their start and end apart: 4 -> 8, of which waited for: 3 -> 6; matrix products, arithmetic and copies ran while one was open for 3% -> 0% of each run, Pallas kernels for 0% -> 10%
where the time goes in v1:
time: 178 us; the launch traced here: 177 us
  Pallas kernels  56.7 us (32%)
  waiting for transfers between devices  54.8 us (31%)
  blocking collectives  48.5 us (27%)
  starting transfers between devices  13.2 us (7%)
  local copies, waits for them, and re-layouts  3.75 us (2%)
    pallas_call x9, Pallas kernels, call(): pl.pallas_call(kernel, out_shape=out, in_specs=specs, out_specs=out_specs...  56.7 us
    ppermute x3, waiting for transfers between devices, body(): lax.ppermute(parts[k], 'x', ring(NX, -k))  26.6 us
    ppermute x3, waiting for transfers between devices, body(): lax.ppermute(chunks[k], 'x', ring(NX, k))  24.2 us
    all_to_all x1, blocking collectives, body(): row_totals = lax.all_to_all(row_total, 'z', 0, 0, tiled=True)  23 us
    all_to_all x1, blocking collectives, body(): came = lax.all_to_all(came, 'z', 0, 0, tiled=True)  15.5 us
    all_gather x1, blocking collectives, body(): planes = lax.all_gather(plane_total, 'y', axis=0)  9.92 us
    ppermute x3, starting transfers between devices, body(): lax.ppermute(parts[k], 'x', ring(NX, -k))  5.75 us
    ppermute x1, waiting for transfers between devices, body(): got = lax.ppermute(other, 'c', swap)  3.97 us
  transfers between devices with their start and end apart: 8, of which 6 were waited for; matrix products, arithmetic and copies ran while one was open for 0% of the time, Pallas kernels for 10%

profile of v1, /device:TPU:1, one launch (start us, length us, event | category | flops | bytes accessed | tf_op | source)
XLA Modules:
  0.0 177.1 jit_solution(4349370402982986372)
XLA Ops:
  0.0 0.1 pad_add_fusion.place
  0.1 0.0 copy-start
  0.1 0.7 copy-done
  0.8 0.0 copy-start.2
  0.8 0.7 copy-done.2
  1.5 0.0 copy-start.4
  1.5 1.6 copy-done.4
  3.1 0.0 copy-start.5
  3.1 0.7 copy-done.5
  3.8 19.5 %shard_map.46 = (s32[32,128]{1,0:T(8,128)S(1)}, s32[64,128]{1,0:T(8,128)S(1)}, f32[64,128]{1,0:T(8,128)S(1)}, f32[8192,128]{1,0:T(8,128)S(1)}, f32[32,136,128]{2,1,0:T(8,128)S(1)}, /*index=5*/f32[32,136,128]{2,1,0:T(8,128)S(1)}) custom-call(s32[4]{0:T(128)S(1)} %pad_add_fusion.place, s32[32,128]{1,0:T(8,128)S(1)} %bitcast.9, s32[32,128]{1,0:T(8,128)S(1)} %bitcast.12, ...), custom_call_target="tpu_custom_call" | custom-call | flops 10000000000 | bytes 1000000 | tf_op jit(solution)/shard_map/pallas_call | solution.py:53
  23.3 3.3 %collective-permute-start = (f32[32,136,128]{2,1,0:T(8,128)S(1)}, f32[32,136,128]{2,1,0:T(8,128)S(1)}, u32[]{:S(2)}, u32[]{:S(2)}) collective-permute-start(f32[32,136,128]{2,1,0:T(8,128)S(1)} %get-tuple-element.34), channel_id=1, source_target_pairs={{0,1},{1,0},{2,3},{3,2},{4,5},{5,4},{6,7},{7,6},{8,9},{9,8},{10,11... | collective-permute-start | bytes 6684680 | tf_op jit(solution)/shard_map/ppermute | solution.py:358
  26.6 4.0 %collective-permute-done.got = f32[32,136,128]{2,1,0:T(8,128)S(1)} collective-permute-done((f32[32,136,128]{2,1,0:T(8,128)S(1)}, f32[32,136,128]{2,1,0:T(8,128)S(1)}, u32[]{:S(2)}, u32[]{:S(2)}) %collective-permute-start) | collective-permute-done | bytes 2228256 | tf_op jit(solution)/shard_map/ppermute | solution.py:358
  30.6 3.9 %shard_map.48 = (f32[8,136,128]{2,1,0:T(8,128)S(1)}, f32[8,136,128]{2,1,0:T(8,128)S(1)}, f32[8,136,128]{2,1,0:T(8,128)S(1)}, f32[8,136,128]{2,1,0:T(8,128)S(1)}) custom-call(s32[4]{0:T(128)S(1)} %pad_add_fusion.place, f32[32,136,128]{2,1,0:T(8,128)S(1)} %get-tuple-element.33.mine, f32[32,136,128]{2,1,0:T(8,128)S(1)} %collective-permute-done.got), custom_call_target="tpu_custom_call" | custom-call | flops 1000000 | bytes 1000000 | tf_op jit(solution)/shard_map/pallas_call | solution.py:53
  34.5 0.1 collective-permute-start.1
  34.6 1.9 %collective-permute-start.2 = (f32[8,136,128]{2,1,0:T(8,128)S(1)}, f32[8,136,128]{2,1,0:T(8,128)S(1)}, u32[]{:S(2)}, u32[]{:S(2)}) collective-permute-start(f32[8,136,128]{2,1,0:T(8,128)S(1)} %get-tuple-element.37), channel_id=1, source_target_pairs={{0,4},{2,6},{4,0},{6,2},{1,5},{3,7},{5,1},{7,3},{8,12},{10,14},{12... | collective-permute-start | bytes 1671176 | tf_op jit(solution)/shard_map/ppermute | solution.py:369
  36.5 1.2 collective-permute-start.3
  37.7 12.6 %collective-permute-done.1.t1 = f32[8,136,128]{2,1,0:T(8,128)S(1)} collective-permute-done((f32[8,136,128]{2,1,0:T(8,128)S(1)}, f32[8,136,128]{2,1,0:T(8,128)S(1)}, u32[]{:S(2)}, u32[]{:S(2)}) %collective-permute-start.1) | collective-permute-done | bytes 557088 | tf_op jit(solution)/shard_map/ppermute | solution.py:369
  50.3 10.5 %collective-permute-done.2.t2 = f32[8,136,128]{2,1,0:T(8,128)S(1)} collective-permute-done((f32[8,136,128]{2,1,0:T(8,128)S(1)}, f32[8,136,128]{2,1,0:T(8,128)S(1)}, u32[]{:S(2)}, u32[]{:S(2)}) %collective-permute-start.2) | collective-permute-done | bytes 557088 | tf_op jit(solution)/shard_map/ppermute | solution.py:369
  60.9 1.0 collective-permute-done.3.t3
  61.9 1.7 shard_map.49
  63.6 23.0 %all_to_all.10.rows = f32[8,136,128]{2,1,0:T(8,128)S(1)} all-to-all(f32[8,136,128]{2,1,0:T(8,128)S(1)} %shard_map.49), channel_id=1, replica_groups=mesh['y'=4,'z'=8,'x'=4,'c'=2] {'z'}, dimensions={0} | all-to-all | bytes 1114112 | tf_op jit(solution)/shard_map/all_to_all | solution.py:371
  86.6 0.2 shard_map.50
  86.8 9.9 %all-gather = f32[544,128]{1,0:T(8,128)S(1)} all-gather(f32[136,128]{1,0:T(8,128)S(1)} %shard_map.50), channel_id=2, replica_groups=mesh['y'=4,'z'=8,'x'=4,'c'=2] {'y'}, dimensions={0}, use_global_device_ids=true | all-gather | bytes 348160 | tf_op jit(solution)/shard_map/all_gather | solution.py:373
  96.7 0.8 shard_map.51
  97.5 15.5 %all_to_all.11.came = f32[8,136,128]{2,1,0:T(8,128)S(1)} all-to-all(f32[8,136,128]{2,1,0:T(8,128)S(1)} %shard_map.51), channel_id=1, replica_groups=mesh['y'=4,'z'=8,'x'=4,'c'=2] {'z'}, dimensions={0} | all-to-all | bytes 1114112 | tf_op jit(solution)/shard_map/all_to_all | solution.py:377
  113.0 1.7 shard_map.52
  114.7 5.1 %collective-permute-start.4 = (f32[8,136,128]{2,1,0:T(8,128)S(1)}, f32[8,136,128]{2,1,0:T(8,128)S(1)}, u32[]{:S(2)}, u32[]{:S(2)}) collective-permute-start(f32[8,136,128]{2,1,0:T(8,128)S(1)} %get-tuple-element.40), channel_id=1, source_target_pairs={{0,6},{2,0},{4,2},{6,4},{1,7},{3,1},{5,3},{7,5},{8,14},{10,8},{12,... | collective-permute-start | bytes 1671176 | tf_op jit(solution)/shard_map/ppermute | solution.py:381
  119.8 0.0 collective-permute-start.5
  119.8 0.7 collective-permute-start.6
  120.5 10.9 %collective-permute-done.4.p1 = f32[8,136,128]{2,1,0:T(8,128)S(1)} collective-permute-done((f32[8,136,128]{2,1,0:T(8,128)S(1)}, f32[8,136,128]{2,1,0:T(8,128)S(1)}, u32[]{:S(2)}, u32[]{:S(2)}) %collective-permute-start.4) | collective-permute-done | bytes 557088 | tf_op jit(solution)/shard_map/ppermute | solution.py:381
  131.4 0.0 collective-permute-done.5.p2
  131.4 15.7 %collective-permute-done.6.p3 = f32[8,136,128]{2,1,0:T(8,128)S(1)} collective-permute-done((f32[8,136,128]{2,1,0:T(8,128)S(1)}, f32[8,136,128]{2,1,0:T(8,128)S(1)}, u32[]{:S(2)}, u32[]{:S(2)}) %collective-permute-start.6) | collective-permute-done | bytes 557088 | tf_op jit(solution)/shard_map/ppermute | solution.py:381
  147.1 0.0 copy-start.1
  147.1 0.0 copy-start.3
  147.1 4.0 %shard_map.53 = (f32[32,136,128]{2,1,0:T(8,128)S(1)}, f32[32,136,128]{2,1,0:T(8,128)S(1)}) custom-call(s32[4]{0:T(128)S(1)} %pad_add_fusion.place, f32[8,136,128]{2,1,0:T(8,128)S(1)} %get-tuple-element.39.p0, f32[8,136,128]{2,1,0:T(8,128)S(1)} %collective-permute-done.4.p1, f32[8,136,128]{2,1,0:T(8,128)S(1)} %collective-permute-done.5.p2, ...), custom_call_target="tpu_custom_call" | custom-call | flops 1000000 | bytes 1000000 | tf_op jit(solution)/shard_map/pallas_call | solution.py:53
  151.0 1.0 collective-permute-start.7
  152.0 0.0 copy-done.1
  152.0 0.0 copy-done.3
  152.0 17.8 %shard_map.47 = (f32[4096,128]{1,0:T(8,128)S(1)}, f32[32,128]{1,0:T(8,128)S(1)}, f32[32,128]{1,0:T(8,128)S(1)}, s32[32,128]{1,0:T(8,128)S(1)}) custom-call(s32[32,128]{1,0:T(8,128)S(1)} %get-tuple-element.25.slots.slot_rows, s32[32,128]{1,0:T(8,128)S(1)} %get-tuple-element.25.slots.slot_rows, s32[32,128]{1,0:T(8,128)S(1)} %bitcast.10, ...), custom_call_target="tpu_custom_call" | custom-call | flops 20000000000 | bytes 1000000 | tf_op jit(solution)/shard_map/pallas_call | solution.py:53
  169.8 0.0 collective-permute-done.7.got
  169.9 7.2 %shard_map.54 = f32[4096,128]{1,0:T(8,128)} custom-call(s32[4]{0:T(128)S(1)} %pad_add_fusion.place, s32[32,128]{1,0:T(8,128)S(1)} %get-tuple-element.29.users, f32[4096,128]{1,0:T(8,128)S(1)} %get-tuple-element.30.run, f32[32,128]{1,0:T(8,128)S(1)} %get-tuple-element.31.count, f32[32,128]{1,0:T(8,128)S(1)} %get-tuple-element.32.is_open, ...), custom_call_target="tpu_custom_call" | custom-call | flops 1000000 | bytes 1000000 | tf_op jit(solution)/shard_map/pallas_call | solution.py:53
Async XLA Ops:
  0.1 0.7 copy-start
  0.8 0.7 copy-start.2
  1.5 1.6 copy-start.4
  3.1 0.7 copy-start.5
  23.3 7.3 %collective-permute-start = (f32[32,136,128]{2,1,0:T(8,128)S(1)}, f32[32,136,128]{2,1,0:T(8,128)S(1)}, u32[]{:S(2)}, u32[]{:S(2)}) collective-permute-start(f32[32,136,128]{2,1,0:T(8,128)S(1)} %get-tuple-element.34), channel_id=1, source_target_pairs={{0,1},{1,0},{2,3},{3,2},{4,5},{5,4},{6,7},{7,6},{8,9},{9,8},{10,11... | collective-permute-start | bytes 6684680 | tf_op jit(solution)/shard_map/ppermute | solution.py:358
  34.5 15.8 %collective-permute-start.1 = (f32[8,136,128]{2,1,0:T(8,128)S(1)}, f32[8,136,128]{2,1,0:T(8,128)S(1)}, u32[]{:S(2)}, u32[]{:S(2)}) collective-permute-start(f32[8,136,128]{2,1,0:T(8,128)S(1)} %get-tuple-element.36), channel_id=1, source_target_pairs={{0,2},{2,4},{4,6},{6,0},{1,3},{3,5},{5,7},{7,1},{8,10},{10,12},{12... | collective-permute-start | bytes 1671176 | tf_op jit(solution)/shard_map/ppermute | solution.py:369
  34.6 26.3 %collective-permute-start.2 = (f32[8,136,128]{2,1,0:T(8,128)S(1)}, f32[8,136,128]{2,1,0:T(8,128)S(1)}, u32[]{:S(2)}, u32[]{:S(2)}) collective-permute-start(f32[8,136,128]{2,1,0:T(8,128)S(1)} %get-tuple-element.37), channel_id=1, source_target_pairs={{0,4},{2,6},{4,0},{6,2},{1,5},{3,7},{5,1},{7,3},{8,12},{10,14},{12... | collective-permute-start | bytes 1671176 | tf_op jit(solution)/shard_map/ppermute | solution.py:369
  36.5 25.3 %collective-permute-start.3 = (f32[8,136,128]{2,1,0:T(8,128)S(1)}, f32[8,136,128]{2,1,0:T(8,128)S(1)}, u32[]{:S(2)}, u32[]{:S(2)}) collective-permute-start(f32[8,136,128]{2,1,0:T(8,128)S(1)} %get-tuple-element.38), channel_id=1, source_target_pairs={{0,6},{2,0},{4,2},{6,4},{1,7},{3,1},{5,3},{7,5},{8,14},{10,8},{12,... | collective-permute-start | bytes 1671176 | tf_op jit(solution)/shard_map/ppermute | solution.py:369
  114.7 16.7 %collective-permute-start.4 = (f32[8,136,128]{2,1,0:T(8,128)S(1)}, f32[8,136,128]{2,1,0:T(8,128)S(1)}, u32[]{:S(2)}, u32[]{:S(2)}) collective-permute-start(f32[8,136,128]{2,1,0:T(8,128)S(1)} %get-tuple-element.40), channel_id=1, source_target_pairs={{0,6},{2,0},{4,2},{6,4},{1,7},{3,1},{5,3},{7,5},{8,14},{10,8},{12,... | collective-permute-start | bytes 1671176 | tf_op jit(solution)/shard_map/ppermute | solution.py:381
  119.8 11.6 %collective-permute-start.5 = (f32[8,136,128]{2,1,0:T(8,128)S(1)}, f32[8,136,128]{2,1,0:T(8,128)S(1)}, u32[]{:S(2)}, u32[]{:S(2)}) collective-permute-start(f32[8,136,128]{2,1,0:T(8,128)S(1)} %get-tuple-element.41), channel_id=1, source_target_pairs={{0,4},{2,6},{4,0},{6,2},{1,5},{3,7},{5,1},{7,3},{8,12},{10,14},{12... | collective-permute-start | bytes 1671176 | tf_op jit(solution)/shard_map/ppermute | solution.py:381
  119.8 27.3 %collective-permute-start.6 = (f32[8,136,128]{2,1,0:T(8,128)S(1)}, f32[8,136,128]{2,1,0:T(8,128)S(1)}, u32[]{:S(2)}, u32[]{:S(2)}) collective-permute-start(f32[8,136,128]{2,1,0:T(8,128)S(1)} %get-tuple-element.42), channel_id=1, source_target_pairs={{0,2},{2,4},{4,6},{6,0},{1,3},{3,5},{5,7},{7,1},{8,10},{10,12},{12... | collective-permute-start | bytes 1671176 | tf_op jit(solution)/shard_map/ppermute | solution.py:381
  147.1 5.0 %copy-start.1 = (s32[4096,1]{0,1:T(1,128)S(1)}, s32[4096,1]{0,1:T(1,128)}, u32[]{:S(2)}) copy-start(s32[4096,1]{0,1:T(1,128)} %param.5) | copy-start | bytes 49156
  147.1 5.0 %copy-start.3 = (s32[4096]{0:T(1024)S(1)}, s32[4096]{0:T(1024)}, u32[]{:S(2)}) copy-start(s32[4096]{0:T(1024)} %param.6) | copy-start | bytes 49156
  151.0 18.8 %collective-permute-start.7 = (f32[32,136,128]{2,1,0:T(8,128)S(1)}, f32[32,136,128]{2,1,0:T(8,128)S(1)}, u32[]{:S(2)}, u32[]{:S(2)}) collective-permute-start(f32[32,136,128]{2,1,0:T(8,128)S(1)} %get-tuple-element.44), channel_id=1, source_target_pairs={{0,1},{1,0},{2,3},{3,2},{4,5},{5,4},{6,7},{7,6},{8,9},{9,8},{10,11... | collective-permute-start | bytes 6684680 | tf_op jit(solution)/shard_map/ppermute | solution.py:385

commit v2 on v1

v2 whole, which is shorter than its diff:
```python
import functools

import jax
import jax.numpy as jnp
from jax import lax
from jax.experimental import pallas as pl
from jax.experimental.pallas import tpu as pltpu
from jax.sharding import Mesh, PartitionSpec as P

LANES = 128
GROUPS = 1
PART = LANES // GROUPS
ROWS = PART + 8
NZ, NX, NC = 8, 4, 2
OWNERS = NZ * NX * NC
HALF = OWNERS // NC
CHUNK = HALF // NX
BF16, F32, I32 = jnp.bfloat16, jnp.float32, jnp.int32
VMEM = pl.BlockSpec(memory_space=pltpu.VMEM)
SMEM = pl.BlockSpec(memory_space=pltpu.SMEM)
HBM = pl.BlockSpec(memory_space=pltpu.HBM)
ANY = pl.BlockSpec(memory_space=pl.ANY)


def dot(a, b):
    return lax.dot_general(a, b, (((1,), (0,)), ((), ())), preferred_element_type=F32)


def dot_nt(a, b):
    return lax.dot_general(a, b, (((1,), (1,)), ((), ())), preferred_element_type=F32)


def iota(shape, dim):
    return lax.broadcasted_iota(I32, shape, dim)


def as_bf16(mask):
    return jnp.where(mask, 1.0, 0.0).astype(BF16)


def two_parts(v):
    high = v.astype(BF16)
    low = (v - high.astype(F32)).astype(BF16)
    return jnp.concatenate([high, low], axis=1)


def masked_sum(mask, parts):
    both = dot(mask, parts)
    return both[:, :LANES] + both[:, LANES:]


def call(kernel, out, args, specs, out_specs=None, scratch=(), cost=1_000_000, limit=24):
    return pl.pallas_call(
        kernel,
        out_shape=out,
        in_specs=specs,
        out_specs=out_specs or jax.tree.map(lambda _: VMEM, out),
        scratch_shapes=list(scratch),
        cost_estimate=pl.CostEstimate(flops=cost, bytes_accessed=1_000_000, transcendentals=0),
        compiler_params=pltpu.CompilerParams(vmem_limit_bytes=limit << 20),
    )(*args)


def block(*lead):
    return jax.ShapeDtypeStruct((*lead, ROWS, LANES), F32)


def regroup_kernel(
    events, features_in, slot_out, acc_out, flag_out, grouped, features, slots, sems,
):
    arrival = pltpu.make_async_copy(features_in, features, sems.at[0])
    arrival.start()
    lines = slot_out.shape[0]
    zero = jnp.zeros((LANES, LANES), F32)
    below = as_bf16(iota((LANES, LANES), 0) < iota((LANES, LANES), 1))
    with_total = jnp.concatenate([below, jnp.ones((LANES, LANES), BF16)], axis=1)
    owner_ids = iota((OWNERS, LANES), 0)
    before = jnp.zeros((OWNERS, LANES), F32)
    codes = jnp.zeros((OWNERS, LANES), F32)
    each = grouped.shape[0] // LANES // lines
    for b in range(lines):
        home_row = events[b : b + 1, :]
        account_row = events[lines + b : lines + b + 1, :]
        flag_row = events[2 * lines + b : 2 * lines + b + 1, :]
        chosen = owner_ids == home_row
        counted = dot(as_bf16(chosen), with_total)
        rank = jnp.sum(
            jnp.where(chosen, counted[:, :LANES] + before, 0.0), axis=0, keepdims=True
        )
        before = before + counted[:, LANES:]
        slot_out[b : b + 1, :] = home_row * LANES + rank.astype(I32)
        code = (account_row * 2 + flag_row + 1).astype(F32)
        rank_of = as_bf16(iota((LANES, LANES), 0) == rank.astype(I32))
        codes = codes + dot_nt(jnp.where(chosen, code, 0.0).astype(BF16), rank_of)
        for i in range(each):
            grouped[(b * each + i) * LANES : (b * each + i + 1) * LANES, :] = zero
    copy = pltpu.make_async_copy(slot_out, slots, sems.at[1])
    copy.start()
    code_ids = codes.astype(I32) - 1
    acc_out[...] = jnp.right_shift(code_ids, 1)
    flag_out[...] = jnp.where(code_ids >= 0, jnp.bitwise_and(code_ids, 1), 0).astype(F32)
    arrival.wait()
    copy.wait()

    def spread(b, _):
        for j in range(LANES):
            grouped[pl.ds(slots[b, j], 1), :] = features[pl.ds(b * LANES + j, 1), :]
        return 0

    lax.fori_loop(0, lines, spread, 0)


def closing_kernel(k, place, acc_rows, flag_rows, grouped, ready, other, mine):
    after = as_bf16(iota((LANES, LANES), 0) > iota((LANES, LANES), 1))
    ones = jnp.ones((8, LANES), BF16)
    sub = iota((8, LANES), 0)
    chunk = lax.rem(place[1] + k, NX) * CHUNK
    for out, half_of in ((other, 1 - place[0]), (mine, place[0])):
        base = pl.multiple_of(half_of * HALF + chunk, CHUNK)
        acc8 = acc_rows[pl.ds(base, CHUNK), :]
        flag8 = flag_rows[pl.ds(base, CHUNK), :]
        for i in range(CHUNK):
            member = iota((LANES, LANES), 0) == acc8[i : i + 1, :]
            member_flags = jnp.where(member, flag8[i : i + 1, :], 0.0).astype(BF16)
            later_flags = dot(member_flags, after)
            counted = as_bf16(member & (later_flags < 0.5))
            at = pl.multiple_of((base + i) * LANES, LANES)
            sums = masked_sum(counted, two_parts(grouped[pl.ds(at, LANES), :]))
            count = dot_nt(ones, counted)
            mark = jnp.minimum(dot_nt(ones, member_flags), 1.0)
            tail = jnp.where(sub == 0, count, jnp.where(sub == 1, mark, 0.0))
            for g in range(GROUPS):
                out[g, i, :PART, :] = sums[g * PART : (g + 1) * PART, :]
                out[g, i, PART:, :] = tail


def running_kernel(
    slots, slot_rows, home, account, acc_rows, flag_rows, grouped,
    ready, run_out, count_out, open_out, user_out, run, counts, opens,
):
    lines = home.shape[0]
    after = as_bf16(iota((LANES, LANES), 0) > iota((LANES, LANES), 1))
    up_to = iota((LANES, LANES), 1) <= iota((LANES, LANES), 0)
    ones = jnp.ones((8, LANES), BF16)

    def some(g, _):
        rows = pl.ds(pl.multiple_of(g * 8, 8), 8)
        acc8 = acc_rows[rows, :]
        flag8 = flag_rows[rows, :]
        acc_cols = acc8.astype(F32).T
        count8, open8 = [], []
        for i in range(8):
            acc_row = acc8[i : i + 1, :].astype(F32)
            acc_col = jnp.broadcast_to(acc_cols[:, i : i + 1], (LANES, LANES))
            same = (acc_col == acc_row) & (acc_row >= 0.0) & up_to
            same_flags = jnp.where(same, flag8[i : i + 1, :], 0.0).astype(BF16)
            between = dot(same_flags, after)
            session = as_bf16(same & (between < 0.5))
            at = pl.ds(pl.multiple_of((g * 8 + i) * LANES, LANES), LANES)
            run[at, :] = masked_sum(session, two_parts(grouped[at, :]))
            count8.append(dot_nt(ones, session)[:1, :])
            open8.append(dot_nt(ones, same_flags)[:1, :])
        counts[rows, :] = jnp.concatenate(count8, axis=0)
        opens[rows, :] = jnp.where(jnp.concatenate(open8, axis=0) < 0.5, 1.0, 0.0)
        return 0

    lax.fori_loop(0, OWNERS // 8, some, 0)

    def scalars(t, _):
        rows = pl.ds(pl.multiple_of(t * 8, 8), 8)
        home8 = home[rows, :]
        rank = slot_rows[rows, :] - home8 * LANES
        count = jnp.zeros((8, LANES), F32)
        is_open = jnp.zeros((8, LANES), F32)
        for o in range(OWNERS):
            here = home8 == o
            for_count = jnp.broadcast_to(counts[o : o + 1, :], (8, LANES))
            for_open = jnp.broadcast_to(opens[o : o + 1, :], (8, LANES))
            count = jnp.where(here, jnp.take_along_axis(for_count, rank, axis=1), count)
            is_open = jnp.where(here, jnp.take_along_axis(for_open, rank, axis=1), is_open)
        count_out[rows, :] = count
        open_out[rows, :] = is_open
        account8 = account[rows, :]
        group = account8 // PART
        row = jnp.where(is_open > 0.5, account8 - group * PART, ROWS - 1)
        user_out[rows, :] = (group * OWNERS + home8) * ROWS + row
        return 0

    lax.fori_loop(0, lines // 8, scalars, 0)

    def collect(b, _):
        for j in range(LANES):
            run_out[pl.ds(b * LANES + j, 1), :] = run[pl.ds(slots[b, j], 1), :]
        return 0

    lax.fori_loop(0, lines, collect, 0)


def keeps(blocks):
    marks = jnp.concatenate([b[PART + 1 : PART + 2, :] for b in blocks], axis=0)
    return (1.0 - marks).T


def joined(group, earlier, later, keep):
    keep = keep[group * PART : (group + 1) * PART, :]
    sums = later[:PART, :] + jnp.broadcast_to(keep, (PART, LANES)) * earlier[:PART, :]
    tail, first = later[PART:, :], earlier[PART:, :]
    mark = tail[1:2, :]
    sub = iota((8, LANES), 0)
    tail = jnp.where(
        sub == 0, tail + (1.0 - mark) * first, jnp.where(sub == 1, jnp.maximum(tail, first), 0.0)
    )
    return jnp.concatenate([sums, tail], axis=0)


def core_kernel(place, mine, got, *outs):
    first = place[0] == 0
    for g in range(GROUPS):
        pairs = [(mine[g, i], got[g, i]) for i in range(CHUNK)]
        early = [jnp.where(first, a, b) for a, b in pairs]
        late = [jnp.where(first, b, a) for a, b in pairs]
        keep = keeps(late)
        for i in range(CHUNK):
            outs[g][i] = joined(g, early[i], late[i], keep[:, i : i + 1])


def row_kernel(group, place, t0, t1, t2, t3, out):
    tables = (t0, t1, t2, t3)
    for x in range(NX):

        @pl.when(place[1] == x)
        def _(x=x):
            order = [tables[(x - j) % NX] for j in range(NX)]
            keep = [None] + [keeps([t[i] for i in range(CHUNK)]) for t in order[1:]]
            for i in range(CHUNK):
                total = order[0][i]
                for j in range(1, NX):
                    total = joined(group, total, order[j][i], keep[j][:, i : i + 1])
                out[i] = total


def plane_kernel(*refs):
    out = refs[-1]
    for g in range(GROUPS):
        rows = refs[g]
        keep = keeps([rows[z] for z in range(NZ)])
        total = rows[0]
        for z in range(1, NZ):
            total = joined(g, total, rows[z], keep[:, z : z + 1])
        out[g] = total


def rows_back_kernel(place, *refs):
    planes = refs[:3]
    for g in range(GROUPS):
        rows, out = refs[3 + g], refs[3 + GROUPS + g]
        keep = keeps([planes[r][g] for r in range(3)] + [rows[z] for z in range(5)])
        keep_rest = keeps([rows[z] for z in range(8)])
        state = jnp.zeros((ROWS, LANES), F32)
        for r in range(2, -1, -1):
            more = joined(g, state, planes[r][g], keep[:, r : r + 1])
            state = jnp.where(place[2] > r, more, state)
        for z in range(NZ):
            out[z] = state
            if z < NZ - 1:
                state = joined(g, state, rows[z], keep_rest[:, z : z + 1])


def chips_back_kernel(group, place, came, t0, t1, t2, t3, *outs):
    tables = (t0, t1, t2, t3)
    for x in range(NX):

        @pl.when(place[1] == x)
        def _(x=x):
            order = [(x - j) % NX for j in range(NX)]
            keep = [keeps([tables[k][i] for i in range(CHUNK)]) for k in order[:-1]]
            for i in range(CHUNK):
                state = came[i]
                for j, k in enumerate(order):
                    outs[k][i] = state
                    if j < NX - 1:
                        state = joined(group, state, tables[k][i], keep[j][:, i : i + 1])


def cores_back_kernel(group, place, ready, *refs):
    parts, mine, got = refs[:NX], refs[NX : 2 * NX], refs[2 * NX : 3 * NX]
    keep_out, send = refs[3 * NX :]
    first = place[0] == 0
    for k in range(NX):
        base = lax.rem(place[1] + k, NX) * CHUNK
        early = [jnp.where(first, mine[k][group, i], got[k][group, i]) for i in range(CHUNK)]
        keep = keeps(early)
        for i in range(CHUNK):
            state = parts[k][i]
            second = joined(group, state, early[i], keep[:, i : i + 1])
            keep_out[base + i] = jnp.where(first, state, second)
            send[base + i] = jnp.where(first, second, state)


def finish_kernel(place, users, run, count, is_open, home, account, *refs):
    keep, got = refs[:GROUPS], refs[GROUPS : 2 * GROUPS]
    out, table, picked, sems = refs[2 * GROUPS :]
    bases = (place[0] * HALF, (1 - place[0]) * HALF)
    copies = [
        pltpu.make_async_copy(
            side[g], table.at[pl.ds(g * OWNERS + bases[s], HALF)], sems.at[2 * g + s]
        )
        for g in range(GROUPS)
        for s, side in enumerate((keep, got))
    ]
    for copy in copies:
        copy.start()
    lines = home.shape[0]
    flat = table.reshape(GROUPS * OWNERS * ROWS, LANES)
    scale = []
    for t in range(lines // 8):
        rows = slice(8 * t, 8 * t + 8)
        home8, account8 = home[rows, :], account[rows, :]
        came = jnp.zeros((8, LANES), F32)
        for s, side in enumerate((keep[0], got[0])):
            for i in range(HALF):
                row = jnp.broadcast_to(side[i, PART : PART + 1, :], (8, LANES))
                found = jnp.take_along_axis(row, account8, axis=1)
                came = jnp.where(home8 == bases[s] + i, found, came)
        scale.append(1.0 / (count[rows, :] + is_open[rows, :] * came))
    scale = jnp.concatenate(scale, axis=0)
    if lines < LANES:
        scale = jnp.concatenate([scale, jnp.zeros((LANES - lines, LANES), F32)], axis=0)
    scale = scale.T
    for copy in copies:
        copy.wait()

    def pick(b, _):
        for j in range(LANES):
            picked[pl.ds(b * LANES + j, 1), :] = flat[pl.ds(users[b, j], 1), :]
        return 0

    lax.fori_loop(0, lines, pick, 0)
    for b in range(lines):
        at = pl.ds(b * LANES, LANES)
        factor = jnp.broadcast_to(scale[:, b : b + 1], (LANES, LANES))
        out[at, :] = (run[at, :] + picked[at, :]) * factor


def ring(n, k):
    return [(i, (i + k) % n) for i in range(n)]


def body(features, home, account, flags):
    rows = features.shape[0]
    lines = rows // LANES
    home = home.reshape(lines, LANES)
    account = account.reshape(lines, LANES)
    flags = flags.reshape(lines, LANES)
    place = jnp.stack([lax.axis_index(a).astype(I32) for a in ("c", "x", "y")])
    small = jax.ShapeDtypeStruct((lines, LANES), I32)
    small_f = jax.ShapeDtypeStruct((lines, LANES), F32)
    by_owner = functools.partial(jax.ShapeDtypeStruct, (OWNERS, LANES))
    slot, acc_rows, flag_rows, grouped = call(
        regroup_kernel,
        [small, by_owner(I32), by_owner(F32),
         jax.ShapeDtypeStruct((OWNERS * LANES, LANES), F32)],
        (jnp.concatenate([home, account, flags]), features),
        [VMEM, HBM],
        scratch=[pltpu.VMEM((rows, LANES), F32), pltpu.SMEM((lines, LANES), I32),
                 pltpu.SemaphoreType.DMA((2,))],
        cost=5_000_000_000,
    )
    swap = ring(NC, 1)
    mine, got, tables = [None] * NX, [None] * NX, [[None] * NX for _ in range(GROUPS)]
    order = (2, 1, 3, 0)
    chunks = [None] * NX

    def meet(k):
        chunks[k] = call(core_kernel, [block(CHUNK)] * GROUPS, (place, mine[k], got[k]),
                         [SMEM] + [VMEM] * 2, cost=300_000_000)
        for g in range(GROUPS):
            part = chunks[k][g]
            tables[g][k] = lax.ppermute(part, "x", ring(NX, k)) if k else part

    for at, k in enumerate(order):
        ready = chunks[order[at - 2]][0] if at >= 2 else acc_rows
        other, mine[k] = call(
            functools.partial(closing_kernel, k),
            [block(GROUPS, CHUNK)] * 2,
            (place, acc_rows, flag_rows, grouped, ready),
            [SMEM] + [VMEM] * 3 + [ANY],
            cost=1_500_000_000,
        )
        got[k] = lax.ppermute(other, "c", swap)
        if at:
            meet(order[at - 1])
    meet(order[-1])
    row_totals = []
    for g in range(GROUPS):
        total = call(functools.partial(row_kernel, g), block(CHUNK), (place, *tables[g]),
                     [SMEM] + [VMEM] * NX)
        row_totals.append(lax.all_to_all(total, "z", 0, 0, tiled=True))
    plane = call(plane_kernel, block(GROUPS), tuple(row_totals), [VMEM] * GROUPS)
    ny = lax.axis_size("y")
    planes = [
        lax.ppermute(plane, "y", [(i, i + r) for i in range(ny - r)]) for r in range(1, ny)
    ]
    came = call(rows_back_kernel, [block(NZ)] * GROUPS, (place, *planes, *row_totals),
                [SMEM] + [VMEM] * (3 + GROUPS))
    parts = []
    for g in range(GROUPS):
        mid = lax.all_to_all(came[g], "z", 0, 0, tiled=True)
        part = call(functools.partial(chips_back_kernel, g), [block(CHUNK)] * NX,
                    (place, mid, *tables[g]), [SMEM] + [VMEM] * (NX + 1))
        parts.append(
            [lax.ppermute(part[k], "x", ring(NX, -k)) if k else part[k] for k in range(NX)]
        )
    run, count, is_open, users = call(
        running_kernel,
        [jax.ShapeDtypeStruct((rows, LANES), F32), small_f, small_f, small],
        (slot, slot, home, account, acc_rows, flag_rows, grouped, parts[-1][0]),
        [SMEM] + [VMEM] * 6 + [ANY],
        scratch=[pltpu.VMEM((OWNERS * LANES, LANES), F32), pltpu.VMEM((OWNERS, LANES), F32),
                 pltpu.VMEM((OWNERS, LANES), F32)],
        cost=20_000_000_000,
    )
    keep, last = [], []
    for g in range(GROUPS):
        stay, send = call(
            functools.partial(cores_back_kernel, g), [block(HALF)] * 2,
            (place, count, *parts[g], *mine, *got), [SMEM, ANY] + [VMEM] * (3 * NX)
        )
        keep.append(stay)
        last.append(lax.ppermute(send, "c", swap))
    return call(
        finish_kernel,
        jax.ShapeDtypeStruct((rows, LANES), F32),
        (place, users, run, count, is_open, home, account, *keep, *last),
        [SMEM, SMEM] + [VMEM] * (5 + 2 * GROUPS),
        scratch=[pltpu.VMEM((GROUPS * OWNERS, ROWS, LANES), F32), pltpu.VMEM((rows, LANES), F32),
                 pltpu.SemaphoreType.DMA((2 * GROUPS,))],
    )


def solution(mesh):
    split = Mesh(mesh.devices.reshape(-1, NZ, NX, NC), ("y", "z", "x", "c"))
    axes = ("y", "z", "x", "c")
    return jax.shard_map(
        body,
        mesh=split,
        in_specs=(P(axes, None), P(axes, None), P(axes), P(axes)),
        out_specs=P(axes, None),
        check_vma=False,
    )
```

time: 178 us -> 151 us (0.85)
  waiting for transfers between devices: 54.8 us -> 32.3 us
  starting transfers between devices: 13.2 us -> 22.3 us
  blocking collectives: 48.5 us -> 40.2 us
  Pallas kernels: 56.7 us -> 53.5 us
  local copies, waits for them, and re-layouts: 3.75 us -> 1.6 us
    ppermute x8 -> x14, waiting for transfers between devices: 54.8 us -> 32.3 us  [the longest x3 17.6 us: meet(): tables[g][k] = lax.ppermute(part, 'x', ring(NX, k)) if k else part]
    all_gather x1 -> x0, blocking collectives: 9.92 us -> none  [body(): planes = lax.all_gather(plane_total, 'y', axis=0)]
    ppermute x8 -> x14, starting transfers between devices: 13.2 us -> 22.3 us  [the longest x3 8.42 us: body(): lax.ppermute(plane, 'y', [(i, i + r) for i in range(ny - r)])]
    pallas_call x9 -> x16, Pallas kernels: 56.7 us -> 53.5 us  [call(): pl.pallas_call(kernel, out_shape=out, in_specs=specs, out_specs=out_specs...]
    unnamed x12 -> x6, local copies, waits for them, and re-layouts: 3.75 us -> 1.6 us
  transfers between devices with their start and end apart: 8 -> 14, of which waited for: 6 -> 5; matrix products, arithmetic and copies ran while one was open for 0% -> 0% of each run, Pallas kernels for 10% -> 21%
where the time goes in v2:
time: 151 us
  Pallas kernels  53.5 us (35%)
  blocking collectives  40.2 us (27%)
  waiting for transfers between devices  32.3 us (21%)
  starting transfers between devices  22.3 us (15%)
  local copies, waits for them, and re-layouts  1.6 us (1%)
    pallas_call x16, Pallas kernels, call(): pl.pallas_call(kernel, out_shape=out, in_specs=specs, out_specs=out_specs...  53.5 us
    all_to_all x1, blocking collectives, body(): row_totals.append(lax.all_to_all(total, 'z', 0, 0, tiled=True))  23.2 us
    ppermute x3, waiting for transfers between devices, meet(): tables[g][k] = lax.ppermute(part, 'x', ring(NX, k)) if k else part  17.6 us
    all_to_all x1, blocking collectives, body(): mid = lax.all_to_all(came[g], 'z', 0, 0, tiled=True)  17 us
    ppermute x3, waiting for transfers between devices, body(): lax.ppermute(part[k], 'x', ring(NX, -k))  8.97 us
    ppermute x3, starting transfers between devices, body(): lax.ppermute(plane, 'y', [(i, i + r) for i in range(ny - r)])  8.42 us
    ppermute x3, starting transfers between devices, body(): lax.ppermute(part[k], 'x', ring(NX, -k))  4.92 us
    ppermute x4, starting transfers between devices, body(): got[k] = lax.ppermute(other, 'c', swap)  4.43 us
  transfers between devices with their start and end apart: 14, of which 5 were waited for; matrix products, arithmetic and copies ran while one was open for 0% of the time, Pallas kernels for 21%

profile of v2, /device:TPU:1, one launch (start us, length us, event | category | flops | bytes accessed | tf_op | source)
XLA Modules:
  0.0 151.1 jit_solution(16345596660211968260)
XLA Ops:
  0.0 0.8 pad_add_fusion.events
  0.8 1.6 %copy-done.2 = f32[4096,128]{1,0:T(8,128)S(1)} copy-done((f32[4096,128]{1,0:T(8,128)S(1)}, f32[4096,128]{1,0:T(8,128)}, u32[]{:S(2)}) %copy-start.2) | copy-done | bytes 2097176
  2.3 6.5 %shard_map.46 = (s32[32,128]{1,0:T(8,128)S(1)}, s32[64,128]{1,0:T(8,128)S(1)}, f32[64,128]{1,0:T(8,128)S(1)}, f32[8192,128]{1,0:T(8,128)S(1)}) custom-call(s32[96,128]{1,0:T(8,128)S(1)} %pad_add_fusion.events, f32[4096,128]{1,0:T(8,128)S(1)} %copy-done.2), custom_call_target="tpu_custom_call" | custom-call | flops 5000000000 | bytes 1000000 | tf_op jit(solution)/shard_map/pallas_call | solution.py:53
  8.9 0.1 pad_add_fusion.1.place
  9.0 3.4 %shard_map.51 = (f32[1,8,136,128]{3,2,1,0:T(8,128)S(1)}, f32[1,8,136,128]{3,2,1,0:T(8,128)S(1)}) custom-call(s32[3]{0:T(128)S(1)} %pad_add_fusion.1.place, s32[64,128]{1,0:T(8,128)S(1)} %get-tuple-element.28.acc_rows.ready, f32[64,128]{1,0:T(8,128)S(1)} %get-tuple-element.29.flag_rows, f32[8192,128]{1,0:T(8,128)S(1)} %get-tuple-element.30.grouped, ...), custom_call_target="tpu_custom_call" | custom-call | flops 1500000000 | bytes 1000000 | tf_op jit(solution)/shard_map/pallas_call | solution.py:53
  12.3 3.3 %collective-permute-start.3 = (f32[1,8,136,128]{3,2,1,0:T(8,128)S(1)}, f32[1,8,136,128]{3,2,1,0:T(8,128)S(1)}, u32[]{:S(2)}, u32[]{:S(2)}) collective-permute-start(f32[1,8,136,128]{3,2,1,0:T(8,128)S(1)} %get-tuple-element.36), channel_id=1, source_target_pairs={{0,1},{1,0},{2,3},{3,2},{4,5},{5,4},{6,7},{7,6},{8,9},{9,8},{10,11... | collective-permute-start | bytes 1671176 | tf_op jit(solution)/shard_map/ppermute | solution.py:390
  15.6 3.4 %shard_map.47 = (f32[1,8,136,128]{3,2,1,0:T(8,128)S(1)}, f32[1,8,136,128]{3,2,1,0:T(8,128)S(1)}) custom-call(s32[3]{0:T(128)S(1)} %pad_add_fusion.1.place, s32[64,128]{1,0:T(8,128)S(1)} %get-tuple-element.28.acc_rows.ready, f32[64,128]{1,0:T(8,128)S(1)} %get-tuple-element.29.flag_rows, f32[8192,128]{1,0:T(8,128)S(1)} %get-tuple-element.30.grouped, ...), custom_call_target="tpu_custom_call" | custom-call | flops 1500000000 | bytes 1000000 | tf_op jit(solution)/shard_map/pallas_call | solution.py:53
  19.0 0.1 collective-permute-start
  19.1 0.0 collective-permute-done.3.got.refs_10_
  19.1 0.9 shard_map.52.ready
  20.0 3.4 %shard_map.53 = (f32[1,8,136,128]{3,2,1,0:T(8,128)S(1)}, f32[1,8,136,128]{3,2,1,0:T(8,128)S(1)}) custom-call(s32[3]{0:T(128)S(1)} %pad_add_fusion.1.place, s32[64,128]{1,0:T(8,128)S(1)} %get-tuple-element.28.acc_rows.ready, f32[64,128]{1,0:T(8,128)S(1)} %get-tuple-element.29.flag_rows, f32[8192,128]{1,0:T(8,128)S(1)} %get-tuple-element.30.grouped, ...), custom_call_target="tpu_custom_call" | custom-call | flops 1500000000 | bytes 1000000 | tf_op jit(solution)/shard_map/pallas_call | solution.py:53
  23.4 0.6 collective-permute-start.5
  23.9 1.0 collective-permute-start.4
  25.0 0.0 collective-permute-done.got.refs_9_
  25.0 0.9 shard_map.48.ready
  25.8 3.4 %shard_map.49 = (f32[1,8,136,128]{3,2,1,0:T(8,128)S(1)}, f32[1,8,136,128]{3,2,1,0:T(8,128)S(1)}) custom-call(s32[3]{0:T(128)S(1)} %pad_add_fusion.1.place, s32[64,128]{1,0:T(8,128)S(1)} %get-tuple-element.28.acc_rows.ready, f32[64,128]{1,0:T(8,128)S(1)} %get-tuple-element.29.flag_rows, f32[8192,128]{1,0:T(8,128)S(1)} %get-tuple-element.30.grouped, ...), custom_call_target="tpu_custom_call" | custom-call | flops 1500000000 | bytes 1000000 | tf_op jit(solution)/shard_map/pallas_call | solution.py:53
  29.2 0.5 collective-permute-start.1
  29.7 0.3 collective-permute-start.2
  30.0 0.9 shard_map.54
  30.9 2.6 %collective-permute-start.6 = (f32[8,136,128]{2,1,0:T(8,128)S(1)}, f32[8,136,128]{2,1,0:T(8,128)S(1)}, u32[]{:S(2)}, u32[]{:S(2)}) collective-permute-start(f32[8,136,128]{2,1,0:T(8,128)S(1)} %shard_map.54), channel_id=1, source_target_pairs={{0,6},{2,0},{4,2},{6,4},{1,7},{3,1},{5,3},{7,5},{8,14},{10,8},{12,... | collective-permute-start | bytes 1671176 | tf_op jit(solution)/shard_map/ppermute | solution.py:379
  33.5 0.9 shard_map.50.t0
  34.4 5.2 %collective-permute-done.4.t2 = f32[8,136,128]{2,1,0:T(8,128)S(1)} collective-permute-done((f32[8,136,128]{2,1,0:T(8,128)S(1)}, f32[8,136,128]{2,1,0:T(8,128)S(1)}, u32[]{:S(2)}, u32[]{:S(2)}) %collective-permute-start.4) | collective-permute-done | bytes 557088 | tf_op jit(solution)/shard_map/ppermute | solution.py:379
  39.6 12.4 %collective-permute-done.2.t1 = f32[8,136,128]{2,1,0:T(8,128)S(1)} collective-permute-done((f32[8,136,128]{2,1,0:T(8,128)S(1)}, f32[8,136,128]{2,1,0:T(8,128)S(1)}, u32[]{:S(2)}, u32[]{:S(2)}) %collective-permute-start.2) | collective-permute-done | bytes 557088 | tf_op jit(solution)/shard_map/ppermute | solution.py:379
  52.0 0.0 collective-permute-done.6.t3
  52.0 1.2 shard_map.55
  53.2 23.2 %all_to_all.10.refs_0_.refs_3_ = f32[8,136,128]{2,1,0:T(8,128)S(1)} all-to-all(f32[8,136,128]{2,1,0:T(8,128)S(1)} %shard_map.55), channel_id=1, replica_groups=mesh['y'=4,'z'=8,'x'=4,'c'=2] {'z'}, dimensions={0} | all-to-all | bytes 1114112 | tf_op jit(solution)/shard_map/all_to_all | solution.py:398
  76.4 0.3 shard_map.56
  76.7 4.6 %collective-permute-start.9 = (f32[1,136,128]{2,1,0:T(8,128)S(1)}, f32[1,136,128]{2,1,0:T(8,128)S(1)}, u32[]{:S(2)}, u32[]{:S(2)}) collective-permute-start(f32[1,136,128]{2,1,0:T(8,128)S(1)} %shard_map.56), channel_id=1, source_target_pairs={{0,192},{1,193},{2,194},{3,195},{4,196},{5,197},{6,198},{7,199},{8... | collective-permute-start | bytes 208904 | tf_op jit(solution)/shard_map/ppermute | solution.py:402
  81.3 1.3 collective-permute-start.8
  82.6 2.5 %collective-permute-start.7 = (f32[1,136,128]{2,1,0:T(8,128)S(1)}, f32[1,136,128]{2,1,0:T(8,128)S(1)}, u32[]{:S(2)}, u32[]{:S(2)}) collective-permute-start(f32[1,136,128]{2,1,0:T(8,128)S(1)} %shard_map.56), channel_id=1, source_target_pairs={{0,64},{64,128},{128,192},{1,65},{65,129},{129,193},{2,66},{66,130... | collective-permute-start | bytes 208904 | tf_op jit(solution)/shard_map/ppermute | solution.py:402
  85.1 0.0 collective-permute-done.9.refs_2_
  85.1 0.0 collective-permute-done.8.refs_1_
  85.1 1.7 %collective-permute-done.7.refs_0_ = f32[1,136,128]{2,1,0:T(8,128)S(1)} collective-permute-done((f32[1,136,128]{2,1,0:T(8,128)S(1)}, f32[1,136,128]{2,1,0:T(8,128)S(1)}, u32[]{:S(2)}, u32[]{:S(2)}) %collective-permute-start.7) | collective-permute-done | bytes 69664 | tf_op jit(solution)/shard_map/ppermute | solution.py:402
  86.9 0.9 shard_map.57
  87.8 0.0 copy-start
  87.8 0.0 copy-start.1
  87.8 17.0 %all_to_all.11.came = f32[8,136,128]{2,1,0:T(8,128)S(1)} all-to-all(f32[8,136,128]{2,1,0:T(8,128)S(1)} %shard_map.57), channel_id=1, replica_groups=mesh['y'=4,'z'=8,'x'=4,'c'=2] {'z'}, dimensions={0} | all-to-all | bytes 1114112 | tf_op jit(solution)/shard_map/all_to_all | solution.py:408
  104.8 1.2 shard_map.58
  106.0 3.7 %collective-permute-start.10 = (f32[8,136,128]{2,1,0:T(8,128)S(1)}, f32[8,136,128]{2,1,0:T(8,128)S(1)}, u32[]{:S(2)}, u32[]{:S(2)}) collective-permute-start(f32[8,136,128]{2,1,0:T(8,128)S(1)} %get-tuple-element.44), channel_id=1, source_target_pairs={{0,6},{2,0},{4,2},{6,4},{1,7},{3,1},{5,3},{7,5},{8,14},{10,8},{12,... | collective-permute-start | bytes 1671176 | tf_op jit(solution)/shard_map/ppermute | solution.py:412
  109.8 0.4 collective-permute-start.11
  110.2 0.8 collective-permute-start.12
  111.0 17.8 %shard_map.59 = (f32[4096,128]{1,0:T(8,128)S(1)}, f32[32,128]{1,0:T(8,128)S(1)}, f32[32,128]{1,0:T(8,128)S(1)}, s32[32,128]{1,0:T(8,128)S(1)}) custom-call(s32[32,128]{1,0:T(8,128)S(1)} %get-tuple-element.27.slots.slot_rows, s32[32,128]{1,0:T(8,128)S(1)} %get-tuple-element.27.slots.slot_rows, s32[32,128]{1,0:T(8,128)S(1)} %bitcast.10, ...), custom_call_target="tpu_custom_call" | custom-call | flops 20000000000 | bytes 1000000 | tf_op jit(solution)/shard_map/pallas_call | solution.py:53
  128.8 0.0 collective-permute-done.11.refs_2_
  128.8 9.0 %collective-permute-done.12.refs_3_ = f32[8,136,128]{2,1,0:T(8,128)S(1)} collective-permute-done((f32[8,136,128]{2,1,0:T(8,128)S(1)}, f32[8,136,128]{2,1,0:T(8,128)S(1)}, u32[]{:S(2)}, u32[]{:S(2)}) %collective-permute-start.12) | collective-permute-done | bytes 557088 | tf_op jit(solution)/shard_map/ppermute | solution.py:412
  137.8 1.4 shard_map.60
  139.1 0.6 collective-permute-start.13
  139.7 4.0 %collective-permute-done.13.refs_1_ = f32[32,136,128]{2,1,0:T(8,128)S(1)} collective-permute-done((f32[32,136,128]{2,1,0:T(8,128)S(1)}, f32[32,136,128]{2,1,0:T(8,128)S(1)}, u32[]{:S(2)}, u32[]{:S(2)}) %collective-permute-start.13) | collective-permute-done | bytes 2228256 | tf_op jit(solution)/shard_map/ppermute | solution.py:430
  143.7 7.2 %shard_map.61 = f32[4096,128]{1,0:T(8,128)} custom-call(s32[3]{0:T(128)S(1)} %pad_add_fusion.1.place, s32[32,128]{1,0:T(8,128)S(1)} %get-tuple-element.40.users, f32[4096,128]{1,0:T(8,128)S(1)} %get-tuple-element.41.run, f32[32,128]{1,0:T(8,128)S(1)} %get-tuple-element.42.ready.count, f32[32,128]{1,0:T(8,128)S(1)} %get-tuple-element.43.is_open, ...), custom_call_target="tpu_custom_call" | custom-call | flops 1000000 | bytes 1000000 | tf_op jit(solution)/shard_map/pallas_call | solution.py:53
  (6 shorter events, 0.0 us)
Async XLA Ops:
  0.8 1.6 %copy-start.2 = (f32[4096,128]{1,0:T(8,128)S(1)}, f32[4096,128]{1,0:T(8,128)}, u32[]{:S(2)}) copy-start(f32[4096,128]{1,0:T(8,128)} %features_in.1) | copy-start | bytes 6291460
  12.3 6.8 %collective-permute-start.3 = (f32[1,8,136,128]{3,2,1,0:T(8,128)S(1)}, f32[1,8,136,128]{3,2,1,0:T(8,128)S(1)}, u32[]{:S(2)}, u32[]{:S(2)}) collective-permute-start(f32[1,8,136,128]{3,2,1,0:T(8,128)S(1)} %get-tuple-element.36), channel_id=1, source_target_pairs={{0,1},{1,0},{2,3},{3,2},{4,5},{5,4},{6,7},{7,6},{8,9},{9,8},{10,11... | collective-permute-start | bytes 1671176 | tf_op jit(solution)/shard_map/ppermute | solution.py:390
  19.0 6.0 %collective-permute-start = (f32[1,8,136,128]{3,2,1,0:T(8,128)S(1)}, f32[1,8,136,128]{3,2,1,0:T(8,128)S(1)}, u32[]{:S(2)}, u32[]{:S(2)}) collective-permute-start(f32[1,8,136,128]{3,2,1,0:T(8,128)S(1)} %get-tuple-element.32), channel_id=1, source_target_pairs={{0,1},{1,0},{2,3},{3,2},{4,5},{5,4},{6,7},{7,6},{8,9},{9,8},{10,11... | collective-permute-start | bytes 1671176 | tf_op jit(solution)/shard_map/ppermute | solution.py:390
  23.4 6.7 %collective-permute-start.5 = (f32[1,8,136,128]{3,2,1,0:T(8,128)S(1)}, f32[1,8,136,128]{3,2,1,0:T(8,128)S(1)}, u32[]{:S(2)}, u32[]{:S(2)}) collective-permute-start(f32[1,8,136,128]{3,2,1,0:T(8,128)S(1)} %get-tuple-element.38), channel_id=1, source_target_pairs={{0,1},{1,0},{2,3},{3,2},{4,5},{5,4},{6,7},{7,6},{8,9},{9,8},{10,11... | collective-permute-start | bytes 1671176 | tf_op jit(solution)/shard_map/ppermute | solution.py:390
  23.9 15.6 %collective-permute-start.4 = (f32[8,136,128]{2,1,0:T(8,128)S(1)}, f32[8,136,128]{2,1,0:T(8,128)S(1)}, u32[]{:S(2)}, u32[]{:S(2)}) collective-permute-start(f32[8,136,128]{2,1,0:T(8,128)S(1)} %shard_map.52.ready), channel_id=1, source_target_pairs={{0,4},{2,6},{4,0},{6,2},{1,5},{3,7},{5,1},{7,3},{8,12},{10,14},{12... | collective-permute-start | bytes 1671176 | tf_op jit(solution)/shard_map/ppermute | solution.py:379
  29.2 4.3 %collective-permute-start.1 = (f32[1,8,136,128]{3,2,1,0:T(8,128)S(1)}, f32[1,8,136,128]{3,2,1,0:T(8,128)S(1)}, u32[]{:S(2)}, u32[]{:S(2)}) collective-permute-start(f32[1,8,136,128]{3,2,1,0:T(8,128)S(1)} %get-tuple-element.34), channel_id=1, source_target_pairs={{0,1},{1,0},{2,3},{3,2},{4,5},{5,4},{6,7},{7,6},{8,9},{9,8},{10,11... | collective-permute-start | bytes 1671176 | tf_op jit(solution)/shard_map/ppermute | solution.py:390
  29.7 22.3 %collective-permute-start.2 = (f32[8,136,128]{2,1,0:T(8,128)S(1)}, f32[8,136,128]{2,1,0:T(8,128)S(1)}, u32[]{:S(2)}, u32[]{:S(2)}) collective-permute-start(f32[8,136,128]{2,1,0:T(8,128)S(1)} %shard_map.48.ready), channel_id=1, source_target_pairs={{0,2},{2,4},{4,6},{6,0},{1,3},{3,5},{5,7},{7,1},{8,10},{10,12},{12... | collective-permute-start | bytes 1671176 | tf_op jit(solution)/shard_map/ppermute | solution.py:379
  30.9 21.1 %collective-permute-start.6 = (f32[8,136,128]{2,1,0:T(8,128)S(1)}, f32[8,136,128]{2,1,0:T(8,128)S(1)}, u32[]{:S(2)}, u32[]{:S(2)}) collective-permute-start(f32[8,136,128]{2,1,0:T(8,128)S(1)} %shard_map.54), channel_id=1, source_target_pairs={{0,6},{2,0},{4,2},{6,4},{1,7},{3,1},{5,3},{7,5},{8,14},{10,8},{12,... | collective-permute-start | bytes 1671176 | tf_op jit(solution)/shard_map/ppermute | solution.py:379
  76.7 8.4 %collective-permute-start.9 = (f32[1,136,128]{2,1,0:T(8,128)S(1)}, f32[1,136,128]{2,1,0:T(8,128)S(1)}, u32[]{:S(2)}, u32[]{:S(2)}) collective-permute-start(f32[1,136,128]{2,1,0:T(8,128)S(1)} %shard_map.56), channel_id=1, source_target_pairs={{0,192},{1,193},{2,194},{3,195},{4,196},{5,197},{6,198},{7,199},{8... | collective-permute-start | bytes 208904 | tf_op jit(solution)/shard_map/ppermute | solution.py:402
  81.3 3.8 %collective-permute-start.8 = (f32[1,136,128]{2,1,0:T(8,128)S(1)}, f32[1,136,128]{2,1,0:T(8,128)S(1)}, u32[]{:S(2)}, u32[]{:S(2)}) collective-permute-start(f32[1,136,128]{2,1,0:T(8,128)S(1)} %shard_map.56), channel_id=1, source_target_pairs={{0,128},{64,192},{1,129},{65,193},{2,130},{66,194},{3,131},{67,195... | collective-permute-start | bytes 208904 | tf_op jit(solution)/shard_map/ppermute | solution.py:402
  82.6 4.2 %collective-permute-start.7 = (f32[1,136,128]{2,1,0:T(8,128)S(1)}, f32[1,136,128]{2,1,0:T(8,128)S(1)}, u32[]{:S(2)}, u32[]{:S(2)}) collective-permute-start(f32[1,136,128]{2,1,0:T(8,128)S(1)} %shard_map.56), channel_id=1, source_target_pairs={{0,64},{64,128},{128,192},{1,65},{65,129},{129,193},{2,66},{66,130... | collective-permute-start | bytes 208904 | tf_op jit(solution)/shard_map/ppermute | solution.py:402
  87.8 23.2 %copy-start = (s32[4096]{0:T(1024)S(1)}, s32[4096]{0:T(1024)}, u32[]{:S(2)}) copy-start(s32[4096]{0:T(1024)} %param.6) | copy-start | bytes 49156
  87.8 23.2 %copy-start.1 = (s32[4096,1]{0,1:T(1,128)S(1)}, s32[4096,1]{0,1:T(1,128)}, u32[]{:S(2)}) copy-start(s32[4096,1]{0,1:T(1,128)} %param.5) | copy-start | bytes 49156
  106.0 22.7 %collective-permute-start.10 = (f32[8,136,128]{2,1,0:T(8,128)S(1)}, f32[8,136,128]{2,1,0:T(8,128)S(1)}, u32[]{:S(2)}, u32[]{:S(2)}) collective-permute-start(f32[8,136,128]{2,1,0:T(8,128)S(1)} %get-tuple-element.44), channel_id=1, source_target_pairs={{0,6},{2,0},{4,2},{6,4},{1,7},{3,1},{5,3},{7,5},{8,14},{10,8},{12,... | collective-permute-start | bytes 1671176 | tf_op jit(solution)/shard_map/ppermute | solution.py:412
  109.8 19.0 %collective-permute-start.11 = (f32[8,136,128]{2,1,0:T(8,128)S(1)}, f32[8,136,128]{2,1,0:T(8,128)S(1)}, u32[]{:S(2)}, u32[]{:S(2)}) collective-permute-start(f32[8,136,128]{2,1,0:T(8,128)S(1)} %get-tuple-element.45), channel_id=1, source_target_pairs={{0,4},{2,6},{4,0},{6,2},{1,5},{3,7},{5,1},{7,3},{8,12},{10,14},{12... | collective-permute-start | bytes 1671176 | tf_op jit(solution)/shard_map/ppermute | solution.py:412
  110.2 27.6 %collective-permute-start.12 = (f32[8,136,128]{2,1,0:T(8,128)S(1)}, f32[8,136,128]{2,1,0:T(8,128)S(1)}, u32[]{:S(2)}, u32[]{:S(2)}) collective-permute-start(f32[8,136,128]{2,1,0:T(8,128)S(1)} %get-tuple-element.46), channel_id=1, source_target_pairs={{0,2},{2,4},{4,6},{6,0},{1,3},{3,5},{5,7},{7,1},{8,10},{10,12},{12... | collective-permute-start | bytes 1671176 | tf_op jit(solution)/shard_map/ppermute | solution.py:412
  139.1 4.6 %collective-permute-start.13 = (f32[32,136,128]{2,1,0:T(8,128)S(1)}, f32[32,136,128]{2,1,0:T(8,128)S(1)}, u32[]{:S(2)}, u32[]{:S(2)}) collective-permute-start(f32[32,136,128]{2,1,0:T(8,128)S(1)} %get-tuple-element.48), channel_id=1, source_target_pairs={{0,1},{1,0},{2,3},{3,2},{4,5},{5,4},{6,7},{7,6},{8,9},{9,8},{10,11... | collective-permute-start | bytes 6684680 | tf_op jit(solution)/shard_map/ppermute | solution.py:430

commit v3 on v2

--- a/solution.py
+++ b/solution.py
@@ -7,8 +7,9 @@
 from jax.experimental.pallas import tpu as pltpu
 from jax.sharding import Mesh, PartitionSpec as P
 
+
 LANES = 128
-GROUPS = 1
+GROUPS = 2
 PART = LANES // GROUPS
 ROWS = PART + 8
 NZ, NX, NC = 8, 4, 2
@@ -49,13 +50,14 @@
     return both[:, :LANES] + both[:, LANES:]
 
 
-def call(kernel, out, args, specs, out_specs=None, scratch=(), cost=1_000_000, limit=24):
+def call(kernel, out, args, specs, out_specs=None, scratch=(), cost=1_000_000, limit=24, aliases=None):
     return pl.pallas_call(
         kernel,
         out_shape=out,
         in_specs=specs,
         out_specs=out_specs or jax.tree.map(lambda _: VMEM, out),
         scratch_shapes=list(scratch),
+        input_output_aliases=aliases or {},
         cost_estimate=pl.CostEstimate(flops=cost, bytes_accessed=1_000_000, transcendentals=0),
         compiler_params=pltpu.CompilerParams(vmem_limit_bytes=limit << 20),
     )(*args)
@@ -65,11 +67,7 @@
     return jax.ShapeDtypeStruct((*lead, ROWS, LANES), F32)
 
 
-def regroup_kernel(
-    events, features_in, slot_out, acc_out, flag_out, grouped, features, slots, sems,
-):
-    arrival = pltpu.make_async_copy(features_in, features, sems.at[0])
-    arrival.start()
+def rank_kernel(events, slot_out, acc_out, flag_out, cleared):
     lines = slot_out.shape[0]
     zero = jnp.zeros((LANES, LANES), F32)
     below = as_bf16(iota((LANES, LANES), 0) < iota((LANES, LANES), 1))
@@ -77,7 +75,7 @@
     owner_ids = iota((OWNERS, LANES), 0)
     before = jnp.zeros((OWNERS, LANES), F32)
     codes = jnp.zeros((OWNERS, LANES), F32)
-    each = grouped.shape[0] // LANES // lines
+    each = cleared.shape[0] // LANES // lines
     for b in range(lines):
         home_row = events[b : b + 1, :]
         account_row = events[lines + b : lines + b + 1, :]
@@ -93,13 +91,15 @@
         rank_of = as_bf16(iota((LANES, LANES), 0) == rank.astype(I32))
         codes = codes + dot_nt(jnp.where(chosen, code, 0.0).astype(BF16), rank_of)
         for i in range(each):
-            grouped[(b * each + i) * LANES : (b * each + i + 1) * LANES, :] = zero
-    copy = pltpu.make_async_copy(slot_out, slots, sems.at[1])
-    copy.start()
+            cleared[(b * each + i) * LANES : (b * each + i + 1) * LANES, :] = zero
     code_ids = codes.astype(I32) - 1
     acc_out[...] = jnp.right_shift(code_ids, 1)
     flag_out[...] = jnp.where(code_ids >= 0, jnp.bitwise_and(code_ids, 1), 0).astype(F32)
-    arrival.wait()
+
+
+def spread_kernel(slot_rows, features, cleared, grouped, slots, sem):
+    copy = pltpu.make_async_copy(slot_rows, slots, sem)
+    copy.start()
     copy.wait()
 
     def spread(b, _):
@@ -107,64 +107,89 @@
             grouped[pl.ds(slots[b, j], 1), :] = features[pl.ds(b * LANES + j, 1), :]
         return 0
 
-    lax.fori_loop(0, lines, spread, 0)
+    lax.fori_loop(0, slot_rows.shape[0], spread, 0)
+
+
+def after_and_ones():
+    after = as_bf16(iota((LANES, LANES), 0) > iota((LANES, LANES), 1))
+    return jnp.concatenate([after, jnp.ones((LANES, LANES), BF16)], axis=1)
+
+
+def cut(v, i):
+    return v[i * LANES : (i + 1) * LANES, :]
+
+
+def counted_rows(counted, flagged):
+    count = dot(jnp.concatenate(counted, axis=0), jnp.ones((LANES, LANES), BF16))
+    lane = iota((LANES, LANES), 1)
+    both = jnp.zeros((LANES, LANES), F32)
+    for i in range(8):
+        both = jnp.where(lane == i, cut(count, i), both)
+        both = jnp.where(lane == 8 + i, cut(flagged, i), both)
+    return both.T
 
 
 def closing_kernel(k, place, acc_rows, flag_rows, grouped, ready, other, mine):
-    after = as_bf16(iota((LANES, LANES), 0) > iota((LANES, LANES), 1))
-    ones = jnp.ones((8, LANES), BF16)
     sub = iota((8, LANES), 0)
+    sides = after_and_ones()
     chunk = lax.rem(place[1] + k, NX) * CHUNK
     for out, half_of in ((other, 1 - place[0]), (mine, place[0])):
         base = pl.multiple_of(half_of * HALF + chunk, CHUNK)
         acc8 = acc_rows[pl.ds(base, CHUNK), :]
         flag8 = flag_rows[pl.ds(base, CHUNK), :]
+        member = [iota((LANES, LANES), 0) == acc8[i : i + 1, :] for i in range(CHUNK)]
+        member_flags = [
+            jnp.where(member[i], flag8[i : i + 1, :], 0.0).astype(BF16) for i in range(CHUNK)
+        ]
+        flagged = dot(jnp.concatenate(member_flags, axis=0), sides)
+        counted = [
+            as_bf16(member[i] & (cut(flagged, i)[:, :LANES] < 0.5)) for i in range(CHUNK)
+        ]
+        rows = counted_rows(counted, flagged[:, LANES:])
         for i in range(CHUNK):
-            member = iota((LANES, LANES), 0) == acc8[i : i + 1, :]
-            member_flags = jnp.where(member, flag8[i : i + 1, :], 0.0).astype(BF16)
-            later_flags = dot(member_flags, after)
-            counted = as_bf16(member & (later_flags < 0.5))
             at = pl.multiple_of((base + i) * LANES, LANES)
-            sums = masked_sum(counted, two_parts(grouped[pl.ds(at, LANES), :]))
-            count = dot_nt(ones, counted)
-            mark = jnp.minimum(dot_nt(ones, member_flags), 1.0)
-            tail = jnp.where(sub == 0, count, jnp.where(sub == 1, mark, 0.0))
+            sums = masked_sum(counted[i], two_parts(grouped[pl.ds(at, LANES), :]))
+            mark = jnp.minimum(rows[8 + i : 9 + i, :], 1.0)
+            tail = jnp.where(sub == 0, rows[i : i + 1, :], jnp.where(sub == 1, mark, 0.0))
             for g in range(GROUPS):
                 out[g, i, :PART, :] = sums[g * PART : (g + 1) * PART, :]
                 out[g, i, PART:, :] = tail
 
 
-def running_kernel(
-    slots, slot_rows, home, account, acc_rows, flag_rows, grouped,
-    ready, run_out, count_out, open_out, user_out, run, counts, opens,
+def running_kernel(acc_rows, flag_rows, grouped, ready, run, counts, opens):
+    sides = after_and_ones()
+    up_to = iota((LANES, LANES), 1) <= iota((LANES, LANES), 0)
+
+    def some(g, _):
+        rows = pl.ds(pl.multiple_of(g * 8, 8), 8)
+        acc8 = acc_rows[rows, :].astype(F32)
+        flag8 = flag_rows[rows, :]
+        acc_cols = acc8.T
+        same = []
+        for i in range(8):
+            acc_col = jnp.broadcast_to(acc_cols[:, i : i + 1], (LANES, LANES))
+            same.append((acc_col == acc8[i : i + 1, :]) & (acc_col >= 0.0) & up_to)
+        same_flags = [
+            jnp.where(same[i], flag8[i : i + 1, :], 0.0).astype(BF16) for i in range(8)
+        ]
+        flagged = dot(jnp.concatenate(same_flags, axis=0), sides)
+        session = [as_bf16(same[i] & (cut(flagged, i)[:, :LANES] < 0.5)) for i in range(8)]
+        for i in range(8):
+            at = pl.ds(pl.multiple_of((g * 8 + i) * LANES, LANES), LANES)
+            run[at, :] = masked_sum(session[i], two_parts(grouped[at, :]))
+        found = counted_rows(session, flagged[:, LANES:])
+        counts[rows, :] = found[:8, :]
+        opens[rows, :] = jnp.where(found[8:16, :] < 0.5, 1.0, 0.0)
+        return 0
+
+    lax.fori_loop(0, OWNERS // 8, some, 0)
+
+
+def in_time_kernel(
+    slots, slot_rows, home, account, run, counts, opens, ready,
+    run_out, count_out, open_out, user_out,
 ):
     lines = home.shape[0]
-    after = as_bf16(iota((LANES, LANES), 0) > iota((LANES, LANES), 1))
-    up_to = iota((LANES, LANES), 1) <= iota((LANES, LANES), 0)
-    ones = jnp.ones((8, LANES), BF16)
-
-    def some(g, _):
-        rows = pl.ds(pl.multiple_of(g * 8, 8), 8)
-        acc8 = acc_rows[rows, :]
-        flag8 = flag_rows[rows, :]
-        acc_cols = acc8.astype(F32).T
-        count8, open8 = [], []
-        for i in range(8):
-            acc_row = acc8[i : i + 1, :].astype(F32)
-            acc_col = jnp.broadcast_to(acc_cols[:, i : i + 1], (LANES, LANES))
-            same = (acc_col == acc_row) & (acc_row >= 0.0) & up_to
-            same_flags = jnp.where(same, flag8[i : i + 1, :], 0.0).astype(BF16)
-            between = dot(same_flags, after)
-            session = as_bf16(same & (between < 0.5))
-            at = pl.ds(pl.multiple_of((g * 8 + i) * LANES, LANES), LANES)
-            run[at, :] = masked_sum(session, two_parts(grouped[at, :]))
-            count8.append(dot_nt(ones, session)[:1, :])
-            open8.append(dot_nt(ones, same_flags)[:1, :])
-        counts[rows, :] = jnp.concatenate(count8, axis=0)
-        opens[rows, :] = jnp.where(jnp.concatenate(open8, axis=0) < 0.5, 1.0, 0.0)
-        return 0
-
-    lax.fori_loop(0, OWNERS // 8, some, 0)
 
     def scalars(t, _):
         rows = pl.ds(pl.multiple_of(t * 8, 8), 8)
@@ -213,18 +238,17 @@
     return jnp.concatenate([sums, tail], axis=0)
 
 
-def core_kernel(place, mine, got, *outs):
+def core_kernel(group, place, mine, got, ready, out):
     first = place[0] == 0
-    for g in range(GROUPS):
-        pairs = [(mine[g, i], got[g, i]) for i in range(CHUNK)]
-        early = [jnp.where(first, a, b) for a, b in pairs]
-        late = [jnp.where(first, b, a) for a, b in pairs]
-        keep = keeps(late)
-        for i in range(CHUNK):
-            outs[g][i] = joined(g, early[i], late[i], keep[:, i : i + 1])
-
-
-def row_kernel(group, place, t0, t1, t2, t3, out):
+    pairs = [(mine[group, i], got[group, i]) for i in range(CHUNK)]
+    early = [jnp.where(first, a, b) for a, b in pairs]
+    late = [jnp.where(first, b, a) for a, b in pairs]
+    keep = keeps(late)
+    for i in range(CHUNK):
+        out[i] = joined(group, early[i], late[i], keep[:, i : i + 1])
+
+
+def row_kernel(group, place, t0, t1, t2, t3, ready, out):
     tables = (t0, t1, t2, t3)
     for x in range(NX):
 
@@ -239,6 +263,10 @@
                 out[i] = total
 
 
+def touch_kernel(rows, out):
+    out[...] = rows[0, :8, :]
+
+
 def plane_kernel(*refs):
     out = refs[-1]
     for g in range(GROUPS):
@@ -250,20 +278,18 @@
         out[g] = total
 
 
-def rows_back_kernel(place, *refs):
-    planes = refs[:3]
-    for g in range(GROUPS):
-        rows, out = refs[3 + g], refs[3 + GROUPS + g]
-        keep = keeps([planes[r][g] for r in range(3)] + [rows[z] for z in range(5)])
-        keep_rest = keeps([rows[z] for z in range(8)])
-        state = jnp.zeros((ROWS, LANES), F32)
-        for r in range(2, -1, -1):
-            more = joined(g, state, planes[r][g], keep[:, r : r + 1])
-            state = jnp.where(place[2] > r, more, state)
-        for z in range(NZ):
-            out[z] = state
-            if z < NZ - 1:
-                state = joined(g, state, rows[z], keep_rest[:, z : z + 1])
+def rows_back_kernel(group, place, p1, p2, p3, rows, ready, out):
+    planes = (p1, p2, p3)
+    keep_planes = keeps([p[group] for p in planes] + [rows[z] for z in range(5)])
+    keep = keeps([rows[z] for z in range(NZ)])
+    state = jnp.zeros((ROWS, LANES), F32)
+    for r in range(2, -1, -1):
+        more = joined(group, state, planes[r][group], keep_planes[:, r : r + 1])
+        state = jnp.where(place[2] > r, more, state)
+    for z in range(NZ):
+        out[z] = state
+        if z < NZ - 1:
+            state = joined(group, state, rows[z], keep[:, z : z + 1])
 
 
 def chips_back_kernel(group, place, came, t0, t1, t2, t3, *outs):
@@ -356,69 +382,89 @@
     small = jax.ShapeDtypeStruct((lines, LANES), I32)
     small_f = jax.ShapeDtypeStruct((lines, LANES), F32)
     by_owner = functools.partial(jax.ShapeDtypeStruct, (OWNERS, LANES))
-    slot, acc_rows, flag_rows, grouped = call(
-        regroup_kernel,
-        [small, by_owner(I32), by_owner(F32),
-         jax.ShapeDtypeStruct((OWNERS * LANES, LANES), F32)],
-        (jnp.concatenate([home, account, flags]), features),
-        [VMEM, HBM],
-        scratch=[pltpu.VMEM((rows, LANES), F32), pltpu.SMEM((lines, LANES), I32),
-                 pltpu.SemaphoreType.DMA((2,))],
-        cost=5_000_000_000,
+    by_slot = jax.ShapeDtypeStruct((OWNERS * LANES, LANES), F32)
+    slot, acc_rows, flag_rows, cleared = call(
+        rank_kernel,
+        [small, by_owner(I32), by_owner(F32), by_slot],
+        (jnp.concatenate([home, account, flags]),),
+        [VMEM],
+        cost=2_000_000_000,
+    )
+    grouped = call(
+        spread_kernel,
+        by_slot,
+        (slot, features, cleared),
+        [VMEM] * 3,
+        scratch=[pltpu.SMEM((lines, LANES), I32), pltpu.SemaphoreType.DMA],
+        cost=4_000_000_000,
+        aliases={2: 0},
     )
     swap = ring(NC, 1)
-    mine, got, tables = [None] * NX, [None] * NX, [[None] * NX for _ in range(GROUPS)]
     order = (2, 1, 3, 0)
-    chunks = [None] * NX
-
-    def meet(k):
-        chunks[k] = call(core_kernel, [block(CHUNK)] * GROUPS, (place, mine[k], got[k]),
-                         [SMEM] + [VMEM] * 2, cost=300_000_000)
-        for g in range(GROUPS):
-            part = chunks[k][g]
-            tables[g][k] = lax.ppermute(part, "x", ring(NX, k)) if k else part
-
+    mine, got = [None] * NX, [None] * NX
+    tables = [[None] * NX for _ in range(GROUPS)]
+
+    def meet(g, k, ready):
+        chunk = call(functools.partial(core_kernel, g), block(CHUNK),
+                     (place, mine[k], got[k], ready), [SMEM, VMEM, VMEM, ANY], cost=300_000_000)
+        tables[g][k] = lax.ppermute(chunk, "x", ring(NX, k)) if k else chunk
+        return chunk
+
+    met = []
     for at, k in enumerate(order):
-        ready = chunks[order[at - 2]][0] if at >= 2 else acc_rows
         other, mine[k] = call(
             functools.partial(closing_kernel, k),
             [block(GROUPS, CHUNK)] * 2,
-            (place, acc_rows, flag_rows, grouped, ready),
+            (place, acc_rows, flag_rows, grouped, met[at - 2] if at >= 2 else acc_rows),
             [SMEM] + [VMEM] * 3 + [ANY],
             cost=1_500_000_000,
         )
         got[k] = lax.ppermute(other, "c", swap)
         if at:
-            meet(order[at - 1])
-    meet(order[-1])
+            met.append(meet(0, order[at - 1], acc_rows))
+    for g in range(1, GROUPS):
+        for k in order[:-1]:
+            met.append(meet(g, k, met[-1]))
+    for g in range(GROUPS):
+        met.append(meet(g, 0, met[-1]))
+    run_slots, counts, opens = call(
+        running_kernel,
+        [by_slot, by_owner(F32), by_owner(F32)],
+        (acc_rows, flag_rows, grouped, met[-1]),
+        [VMEM] * 3 + [ANY],
+        cost=8_000_000_000,
+    )
     row_totals = []
     for g in range(GROUPS):
-        total = call(functools.partial(row_kernel, g), block(CHUNK), (place, *tables[g]),
-                     [SMEM] + [VMEM] * NX)
+        ready = counts
+        if g:
+            ready = call(touch_kernel, jax.ShapeDtypeStruct((8, LANES), F32),
+                         (row_totals[-1],), [VMEM])
+        total = call(functools.partial(row_kernel, g), block(CHUNK),
+                     (place, *tables[g], ready), [SMEM] + [VMEM] * NX + [ANY])
         row_totals.append(lax.all_to_all(total, "z", 0, 0, tiled=True))
     plane = call(plane_kernel, block(GROUPS), tuple(row_totals), [VMEM] * GROUPS)
     ny = lax.axis_size("y")
     planes = [
         lax.ppermute(plane, "y", [(i, i + r) for i in range(ny - r)]) for r in range(1, ny)
     ]
-    came = call(rows_back_kernel, [block(NZ)] * GROUPS, (place, *planes, *row_totals),
-                [SMEM] + [VMEM] * (3 + GROUPS))
     parts = []
     for g in range(GROUPS):
-        mid = lax.all_to_all(came[g], "z", 0, 0, tiled=True)
+        ready = parts[-1][0] if g else counts
+        came = call(functools.partial(rows_back_kernel, g), block(NZ),
+                    (place, *planes, row_totals[g], ready), [SMEM] + [VMEM] * 4 + [ANY])
+        mid = lax.all_to_all(came, "z", 0, 0, tiled=True)
         part = call(functools.partial(chips_back_kernel, g), [block(CHUNK)] * NX,
                     (place, mid, *tables[g]), [SMEM] + [VMEM] * (NX + 1))
         parts.append(
             [lax.ppermute(part[k], "x", ring(NX, -k)) if k else part[k] for k in range(NX)]
         )
     run, count, is_open, users = call(
-        running_kernel,
+        in_time_kernel,
         [jax.ShapeDtypeStruct((rows, LANES), F32), small_f, small_f, small],
-        (slot, slot, home, account, acc_rows, flag_rows, grouped, parts[-1][0]),
+        (slot, slot, home, account, run_slots, counts, opens, parts[-1][0]),
         [SMEM] + [VMEM] * 6 + [ANY],
-        scratch=[pltpu.VMEM((OWNERS * LANES, LANES), F32), pltpu.VMEM((OWNERS, LANES), F32),
-                 pltpu.VMEM((OWNERS, LANES), F32)],
-        cost=20_000_000_000,
+        cost=10_000_000_000,
     )
     keep, last = [], []
     for g in range(GROUPS):

time: 151 us -> 170 us (1.13); the launches traced: 151 us -> 168 us
  local copies, waits for them, and re-layouts: 1.6 us -> 19 us
  starting transfers between devices: 22.3 us -> 39.2 us
  blocking collectives: 40.2 us -> 30.2 us
  waiting for transfers between devices: 32.3 us -> 27.7 us
  Pallas kernels: 53.5 us -> 50.6 us
    all_to_all x0 -> x2, waiting for transfers between devices: none -> 17.5 us  [the longest x1 9.26 us: body(): row_totals.append(lax.all_to_all(total, 'z', 0, 0, tiled=True))]
    unnamed x6 -> x78, local copies, waits for them, and re-layouts: 1.6 us -> 19 us
    ppermute x3 -> x6, waiting for transfers between devices: 17.6 us -> 5.25 us  [meet(): tables[g][k] = lax.ppermute(chunk, 'x', ring(NX, k)) if k else chunk]
    all_to_all x0 -> x2, starting transfers between devices: none -> 12.2 us  [the longest x1 8.19 us: body(): row_totals.append(lax.all_to_all(total, 'z', 0, 0, tiled=True))]
    ppermute x3 -> x6, waiting for transfers between devices: 8.97 us -> 0.02 us  [body(): lax.ppermute(part[k], 'x', ring(NX, -k))]
    all_to_all x1, blocking collectives: 23.2 us -> 18 us  [body(): row_totals.append(lax.all_to_all(total, 'z', 0, 0, tiled=True))]
    ppermute x1 -> x2, starting transfers between devices: 0.58 us -> 5.52 us  [body(): last.append(lax.ppermute(send, 'c', swap))]
    all_to_all x1, blocking collectives: 17 us -> 12.2 us  [body(): mid = lax.all_to_all(came, 'z', 0, 0, tiled=True)]
  transfers between devices with their start and end apart: 14 -> 23, of which waited for: 5 -> 7; matrix products, arithmetic and copies ran while one was open for 0% -> 0% of each run, Pallas kernels for 21% -> 16%
where the time goes in v3:
time: 170 us; the launch traced here: 168 us
  Pallas kernels  50.6 us (30%)
  starting transfers between devices  39.2 us (23%)
  blocking collectives  30.2 us (18%)
  waiting for transfers between devices  27.7 us (16%)
  local copies, waits for them, and re-layouts  19 us (11%)
    pallas_call x27, Pallas kernels, call(): pl.pallas_call(kernel, out_shape=out, in_specs=specs, out_specs=out_specs...  50.6 us
    unnamed x78, local copies, waits for them, and re-layouts  19 us
    all_to_all x1, blocking collectives, body(): row_totals.append(lax.all_to_all(total, 'z', 0, 0, tiled=True))  18 us
    all_to_all x1, blocking collectives, body(): mid = lax.all_to_all(came, 'z', 0, 0, tiled=True)  12.2 us
    all_to_all x1, waiting for transfers between devices, body(): row_totals.append(lax.all_to_all(total, 'z', 0, 0, tiled=True))  9.26 us
    ppermute x3, starting transfers between devices, body(): lax.ppermute(plane, 'y', [(i, i + r) for i in range(ny - r)])  8.42 us
    all_to_all x1, waiting for transfers between devices, body(): mid = lax.all_to_all(came, 'z', 0, 0, tiled=True)  8.23 us
    all_to_all x1, starting transfers between devices, body(): row_totals.append(lax.all_to_all(total, 'z', 0, 0, tiled=True))  8.19 us
  transfers between devices with their start and end apart: 23, of which 7 were waited for; matrix products, arithmetic and copies ran while one was open for 0% of the time, Pallas kernels for 16%

profile of v3, /device:TPU:1, one launch (start us, length us, event | category | flops | bytes accessed | tf_op | source)
XLA Modules:
  0.0 168.2 jit_solution(14451915632908565880)
XLA Ops:
  0.8 2.7 %shard_map.46 = (s32[32,128]{1,0:T(8,128)S(1)}, s32[64,128]{1,0:T(8,128)S(1)}, f32[64,128]{1,0:T(8,128)S(1)}, f32[8192,128]{1,0:T(8,128)S(1)}) custom-call(s32[96,128]{1,0:T(8,128)S(1)} %pad_add_fusion.events), custom_call_target="tpu_custom_call" | custom-call | flops 2000000000 | bytes 1000000 | tf_op jit(solution)/shard_map/pallas_call | solution.py:54
  3.6 4.2 %shard_map.47.grouped = f32[8192,128]{1,0:T(8,128)S(1)} custom-call(s32[32,128]{1,0:T(8,128)S(1)} %get-tuple-element.36.slot_rows.slots, f32[4096,128]{1,0:T(8,128)S(1)} %copy-done.29, f32[8192,128]{1,0:T(8,128)S(1)} %get-tuple-element.39.cleared), custom_call_target="tpu_custom_call", output_to_operand_aliasing={{}: (2, {})} | custom-call | flops 4000000000 | bytes 1000000 | tf_op jit(solution)/shard_map/pallas_call | solution.py:54
  7.8 1.6 shard_map.51
  9.4 3.3 %collective-permute-start.2 = (f32[2,8,72,128]{3,2,1,0:T(8,128)S(1)}, f32[2,8,72,128]{3,2,1,0:T(8,128)S(1)}, u32[]{:S(2)}, u32[]{:S(2)}) collective-permute-start(f32[2,8,72,128]{3,2,1,0:T(8,128)S(1)} %get-tuple-element.45), channel_id=1, source_target_pairs={{0,1},{1,0},{2,3},{3,2},{4,5},{5,4},{6,7},{7,6},{8,9},{9,8},{10,11... | collective-permute-start | bytes 1769480 | tf_op jit(solution)/shard_map/ppermute | solution.py:422
  12.7 1.6 shard_map.48
  15.3 1.6 shard_map.53
  18.3 1.6 shard_map.50
  20.0 1.1 collective-permute-start.5
  22.2 2.6 %collective-permute-start.6 = (f32[8,72,128]{2,1,0:T(8,128)S(1)}, f32[8,72,128]{2,1,0:T(8,128)S(1)}, u32[]{:S(2)}, u32[]{:S(2)}) collective-permute-start(f32[8,72,128]{2,1,0:T(8,128)S(1)} %shard_map.54.ready), channel_id=1, source_target_pairs={{0,6},{2,0},{4,2},{6,4},{1,7},{3,1},{5,3},{7,5},{8,14},{10,8},{12,... | collective-permute-start | bytes 884744 | tf_op jit(solution)/shard_map/ppermute | solution.py:410
  24.9 0.8 shard_map.55.ready
  25.7 0.8 shard_map.56.ready
  27.2 0.8 shard_map.57.ready
  29.7 0.8 shard_map.59.ready.t0
  30.5 5.7 %shard_map.60 = (f32[8192,128]{1,0:T(8,128)S(1)}, f32[64,128]{1,0:T(8,128)S(1)}, f32[64,128]{1,0:T(8,128)S(1)}) custom-call(s32[64,128]{1,0:T(8,128)S(1)} %get-tuple-element.37.acc_rows.ready, f32[64,128]{1,0:T(8,128)S(1)} %get-tuple-element.38.flag_rows, f32[8192,128]{1,0:T(8,128)S(1)} %shard_map.47.grouped, f32[8,72,128]{2,1,0:T(8,128)S(1)} %shard_map.59.ready.t0), custom_call_target="tpu_custom_call" | custom-call | flops 8000000000 | bytes 1000000 | tf_op jit(solution)/shard_map/pallas_call | solution.py:54
  36.2 2.0 %copy-done.33 = f32[8192,128]{1,0:T(8,128)} copy-done((f32[8192,128]{1,0:T(8,128)}, f32[8192,128]{1,0:T(8,128)S(1)}, u32[]{:S(2)}) %copy-start.33) | copy-done | bytes 4194328
  38.8 0.9 shard_map.61
  43.3 8.2 %all-to-all-start = ((f32[8,72,128]{2,1,0:T(8,128)}), f32[8,72,128]{2,1,0:T(8,128)}, u32[]{:S(2)}, u32[]{:S(2)}) async-start(f32[8,72,128]{2,1,0:T(8,128)} %copy-done.12), calls=%async_computation | async-start | bytes 589824 | tf_op jit(solution)/shard_map/all_to_all | solution.py:445
  51.5 1.5 collective-permute-start.9
  53.1 9.3 %all-to-all-done.rows.refs_0_ = f32[8,72,128]{2,1,0:T(8,128)} async-done(((f32[8,72,128]{2,1,0:T(8,128)}), f32[8,72,128]{2,1,0:T(8,128)}, u32[]{:S(2)}, u32[]{:S(2)}) %all-to-all-start) | async-done | bytes 294944 | tf_op jit(solution)/shard_map/all_to_all | solution.py:445
  62.4 1.0 shard_map.62.ready
  63.4 1.8 %collective-permute-done.9.t3 = f32[8,72,128]{2,1,0:T(8,128)} collective-permute-done((f32[8,72,128]{2,1,0:T(8,128)}, f32[8,72,128]{2,1,0:T(8,128)}, u32[]{:S(2)}, u32[]{:S(2)}) %collective-permute-start.9) | collective-permute-done | bytes 294944 | tf_op jit(solution)/shard_map/ppermute | solution.py:410
  65.2 3.4 %collective-permute-done.7.t1 = f32[8,72,128]{2,1,0:T(8,128)} collective-permute-done((f32[8,72,128]{2,1,0:T(8,128)}, f32[8,72,128]{2,1,0:T(8,128)}, u32[]{:S(2)}, u32[]{:S(2)}) %collective-permute-start.7) | collective-permute-done | bytes 294944 | tf_op jit(solution)/shard_map/ppermute | solution.py:410
  68.6 1.0 copy-done.7
  69.6 1.7 %shard_map.63 = f32[8,72,128]{2,1,0:T(8,128)S(1)} custom-call(s32[3]{0:T(128)S(1)} %pad_add_fusion.1.place, f32[8,72,128]{2,1,0:T(8,128)S(1)} %copy-done.7, f32[8,72,128]{2,1,0:T(8,128)} %collective-permute-done.7.t1, f32[8,72,128]{2,1,0:T(8,128)} %collective-permute-done.8.t2, f32[8,72,128]{2,1,0:T(8,128)} %collective-permute-done.9.t3, ...), custom_call_target="tpu_custom_call" | custom-call | flops 1000000 | bytes 1000000 | tf_op jit(solution)/shard_map/pallas_call | solution.py:54
  71.3 18.0 %all_to_all.20.refs_1_.rows = f32[8,72,128]{2,1,0:T(8,128)S(1)} all-to-all(f32[8,72,128]{2,1,0:T(8,128)S(1)} %shard_map.63), channel_id=1, replica_groups=mesh['y'=4,'z'=8,'x'=4,'c'=2] {'z'}, dimensions={0} | all-to-all | bytes 589824 | tf_op jit(solution)/shard_map/all_to_all | solution.py:445
  89.3 1.2 shard_map.64
  90.5 4.6 %collective-permute-start.12 = (f32[2,72,128]{2,1,0:T(8,128)S(1)}, f32[2,72,128]{2,1,0:T(8,128)S(1)}, u32[]{:S(2)}, u32[]{:S(2)}) collective-permute-start(f32[2,72,128]{2,1,0:T(8,128)S(1)} %shard_map.64), channel_id=1, source_target_pairs={{0,192},{1,193},{2,194},{3,195},{4,196},{5,197},{6,198},{7,199},{8... | collective-permute-start | bytes 221192 | tf_op jit(solution)/shard_map/ppermute | solution.py:449
  95.2 1.3 collective-permute-start.11
  96.5 2.5 %collective-permute-start.10 = (f32[2,72,128]{2,1,0:T(8,128)S(1)}, f32[2,72,128]{2,1,0:T(8,128)S(1)}, u32[]{:S(2)}, u32[]{:S(2)}) collective-permute-start(f32[2,72,128]{2,1,0:T(8,128)S(1)} %shard_map.64), channel_id=1, source_target_pairs={{0,64},{64,128},{128,192},{1,65},{65,129},{129,193},{2,66},{66,130... | collective-permute-start | bytes 221192 | tf_op jit(solution)/shard_map/ppermute | solution.py:449
  99.0 2.0 %collective-permute-done.10.p1 = f32[2,72,128]{2,1,0:T(8,128)S(1)} collective-permute-done((f32[2,72,128]{2,1,0:T(8,128)S(1)}, f32[2,72,128]{2,1,0:T(8,128)S(1)}, u32[]{:S(2)}, u32[]{:S(2)}) %collective-permute-start.10) | collective-permute-done | bytes 73760 | tf_op jit(solution)/shard_map/ppermute | solution.py:449
  101.0 1.2 shard_map.65
  102.3 12.2 %all_to_all.21.came = f32[8,72,128]{2,1,0:T(8,128)S(1)} all-to-all(f32[8,72,128]{2,1,0:T(8,128)S(1)} %shard_map.65), channel_id=1, replica_groups=mesh['y'=4,'z'=8,'x'=4,'c'=2] {'z'}, dimensions={0} | all-to-all | bytes 589824 | tf_op jit(solution)/shard_map/all_to_all | solution.py:456
  114.5 0.9 shard_map.66
  117.6 0.9 shard_map.67
  119.9 4.1 %all-to-all-start.3 = ((f32[8,72,128]{2,1,0:T(8,128)}), f32[8,72,128]{2,1,0:T(8,128)}, u32[]{:S(2)}, u32[]{:S(2)}) async-start(f32[8,72,128]{2,1,0:T(8,128)} %copy-done.11), calls=%async_computation.3 | async-start | bytes 589824 | tf_op jit(solution)/shard_map/all_to_all | solution.py:456
  124.1 0.9 collective-permute-start.14
  125.5 8.2 %all-to-all-done.3.came = f32[8,72,128]{2,1,0:T(8,128)} async-done(((f32[8,72,128]{2,1,0:T(8,128)}), f32[8,72,128]{2,1,0:T(8,128)}, u32[]{:S(2)}, u32[]{:S(2)}) %all-to-all-start.3) | async-done | bytes 294944 | tf_op jit(solution)/shard_map/all_to_all | solution.py:456
  133.8 1.0 copy-done.8
  134.7 1.7 %shard_map.68 = (f32[8,72,128]{2,1,0:T(8,128)S(1)}, f32[8,72,128]{2,1,0:T(8,128)S(1)}, f32[8,72,128]{2,1,0:T(8,128)S(1)}, f32[8,72,128]{2,1,0:T(8,128)S(1)}) custom-call(s32[3]{0:T(128)S(1)} %pad_add_fusion.1.place, f32[8,72,128]{2,1,0:T(8,128)} %all-to-all-done.3.came, f32[8,72,128]{2,1,0:T(8,128)S(1)} %copy-done.8, ...), custom_call_target="tpu_custom_call" | custom-call | flops 1000000 | bytes 1000000 | tf_op jit(solution)/shard_map/pallas_call | solution.py:54
  136.8 0.9 collective-permute-start.17
  140.4 2.2 %copy-done.34 = f32[8192,128]{1,0:T(8,128)S(1)} copy-done((f32[8192,128]{1,0:T(8,128)S(1)}, f32[8192,128]{1,0:T(8,128)}, u32[]{:S(2)}) %copy-start.34) | copy-done | bytes 4194328
  144.1 5.0 %shard_map.69 = (f32[4096,128]{1,0:T(8,128)S(1)}, f32[32,128]{1,0:T(8,128)S(1)}, f32[32,128]{1,0:T(8,128)S(1)}, s32[32,128]{1,0:T(8,128)S(1)}) custom-call(s32[32,128]{1,0:T(8,128)S(1)} %copy-done.36, s32[32,128]{1,0:T(8,128)S(1)} %copy-done.36, s32[32,128]{1,0:T(8,128)S(1)} %bitcast.10, s32[32,128]{1,0:T(8,128)S(1)} %bitcast.7, f32[8192,128]{1,0:T(8,128)S(1)} %copy-done.34, ...), custom_call_target="tpu_custom_call" | custom-call | flops 10000000000 | bytes 1000000 | tf_op jit(solution)/shard_map/pallas_call | solution.py:54
  149.1 1.7 shard_map.70
  150.8 5.4 %collective-permute-start.19 = (f32[32,72,128]{2,1,0:T(8,128)S(1)}, f32[32,72,128]{2,1,0:T(8,128)S(1)}, u32[]{:S(2)}, u32[]{:S(2)}) collective-permute-start(f32[32,72,128]{2,1,0:T(8,128)S(1)} %get-tuple-element.65), channel_id=1, source_target_pairs={{0,1},{1,0},{2,3},{3,2},{4,5},{5,4},{6,7},{7,6},{8,9},{9,8},{10,11... | collective-permute-start | bytes 3538952 | tf_op jit(solution)/shard_map/ppermute | solution.py:476
  156.2 1.1 shard_map.71
  157.5 1.2 collective-permute-done.19.refs_2_
  158.7 1.7 %collective-permute-done.20.refs_3_ = f32[32,72,128]{2,1,0:T(8,128)S(1)} collective-permute-done((f32[32,72,128]{2,1,0:T(8,128)S(1)}, f32[32,72,128]{2,1,0:T(8,128)S(1)}, u32[]{:S(2)}, u32[]{:S(2)}) %collective-permute-start.20) | collective-permute-done | bytes 1179680 | tf_op jit(solution)/shard_map/ppermute | solution.py:476
  160.4 7.6 %shard_map.72 = f32[4096,128]{1,0:T(8,128)} custom-call(s32[3]{0:T(128)S(1)} %pad_add_fusion.1.place, s32[32,128]{1,0:T(8,128)S(1)} %get-tuple-element.53.users, f32[4096,128]{1,0:T(8,128)S(1)} %get-tuple-element.54.run, f32[32,128]{1,0:T(8,128)S(1)} %get-tuple-element.55.ready.count, f32[32,128]{1,0:T(8,128)S(1)} %get-tuple-element.56.is_open, ...), custom_call_target="tpu_custom_call" | custom-call | flops 1000000 | bytes 1000000 | tf_op jit(solution)/shard_map/pallas_call | solution.py:54
  (107 shorter events, 19.8 us)
Async XLA Ops:
  0.8 2.8 %copy-start.29 = (f32[4096,128]{1,0:T(8,128)S(1)}, f32[4096,128]{1,0:T(8,128)}, u32[]{:S(2)}) copy-start(f32[4096,128]{1,0:T(8,128)} %features.1) | copy-start | bytes 6291460
  3.5 4.3 %copy-start.35 = (s32[32,128]{1,0:T(8,128)}, s32[32,128]{1,0:T(8,128)S(1)}, u32[]{:S(2)}) copy-start(s32[32,128]{1,0:T(8,128)S(1)} %get-tuple-element.36.slot_rows.slots) | copy-start | bytes 49156
  9.4 5.0 %collective-permute-start.2 = (f32[2,8,72,128]{3,2,1,0:T(8,128)S(1)}, f32[2,8,72,128]{3,2,1,0:T(8,128)S(1)}, u32[]{:S(2)}, u32[]{:S(2)}) collective-permute-start(f32[2,8,72,128]{3,2,1,0:T(8,128)S(1)} %get-tuple-element.45), channel_id=1, source_target_pairs={{0,1},{1,0},{2,3},{3,2},{4,5},{5,4},{6,7},{7,6},{8,9},{9,8},{10,11... | collective-permute-start | bytes 1769480 | tf_op jit(solution)/shard_map/ppermute | solution.py:422
  14.3 3.1 %collective-permute-start = (f32[2,8,72,128]{3,2,1,0:T(8,128)S(1)}, f32[2,8,72,128]{3,2,1,0:T(8,128)S(1)}, u32[]{:S(2)}, u32[]{:S(2)}) collective-permute-start(f32[2,8,72,128]{3,2,1,0:T(8,128)S(1)} %get-tuple-element.41), channel_id=1, source_target_pairs={{0,1},{1,0},{2,3},{3,2},{4,5},{5,4},{6,7},{7,6},{8,9},{9,8},{10,11... | collective-permute-start | bytes 1769480 | tf_op jit(solution)/shard_map/ppermute | solution.py:422
  16.9 4.6 %collective-permute-start.3 = (f32[2,8,72,128]{3,2,1,0:T(8,128)S(1)}, f32[2,8,72,128]{3,2,1,0:T(8,128)S(1)}, u32[]{:S(2)}, u32[]{:S(2)}) collective-permute-start(f32[2,8,72,128]{3,2,1,0:T(8,128)S(1)} %get-tuple-element.47), channel_id=1, source_target_pairs={{0,1},{1,0},{2,3},{3,2},{4,5},{5,4},{6,7},{7,6},{8,9},{9,8},{10,11... | collective-permute-start | bytes 1769480 | tf_op jit(solution)/shard_map/ppermute | solution.py:422
  19.9 9.0 %copy-start = (f32[2,8,72,128]{3,2,1,0:T(8,128)}, f32[2,8,72,128]{3,2,1,0:T(8,128)S(1)}, u32[]{:S(2)}) copy-start(f32[2,8,72,128]{3,2,1,0:T(8,128)S(1)} %get-tuple-element.42.mine.refs_4_) | copy-start | bytes 1769476
  19.9 8.2 %collective-permute-start.1 = (f32[2,8,72,128]{3,2,1,0:T(8,128)S(1)}, f32[2,8,72,128]{3,2,1,0:T(8,128)S(1)}, u32[]{:S(2)}, u32[]{:S(2)}) collective-permute-start(f32[2,8,72,128]{3,2,1,0:T(8,128)S(1)} %get-tuple-element.43), channel_id=1, source_target_pairs={{0,1},{1,0},{2,3},{3,2},{4,5},{5,4},{6,7},{7,6},{8,9},{9,8},{10,11... | collective-permute-start | bytes 1769480 | tf_op jit(solution)/shard_map/ppermute | solution.py:422
  20.0 18.8 %collective-permute-start.5 = (f32[8,72,128]{2,1,0:T(8,128)S(1)}, f32[8,72,128]{2,1,0:T(8,128)S(1)}, u32[]{:S(2)}, u32[]{:S(2)}) collective-permute-start(f32[8,72,128]{2,1,0:T(8,128)S(1)} %shard_map.52.ready), channel_id=1, source_target_pairs={{0,4},{2,6},{4,0},{6,2},{1,5},{3,7},{5,1},{7,3},{8,12},{10,14},{12... | collective-permute-start | bytes 884744 | tf_op jit(solution)/shard_map/ppermute | solution.py:410
  21.1 17.7 %collective-permute-start.4 = (f32[8,72,128]{2,1,0:T(8,128)S(1)}, f32[8,72,128]{2,1,0:T(8,128)S(1)}, u32[]{:S(2)}, u32[]{:S(2)}) collective-permute-start(f32[8,72,128]{2,1,0:T(8,128)S(1)} %shard_map.49.ready), channel_id=1, source_target_pairs={{0,2},{2,4},{4,6},{6,0},{1,3},{3,5},{5,7},{7,1},{8,10},{10,12},{12... | collective-permute-start | bytes 884744 | tf_op jit(solution)/shard_map/ppermute | solution.py:410
  22.2 16.6 %collective-permute-start.6 = (f32[8,72,128]{2,1,0:T(8,128)S(1)}, f32[8,72,128]{2,1,0:T(8,128)S(1)}, u32[]{:S(2)}, u32[]{:S(2)}) collective-permute-start(f32[8,72,128]{2,1,0:T(8,128)S(1)} %shard_map.54.ready), channel_id=1, source_target_pairs={{0,6},{2,0},{4,2},{6,4},{1,7},{3,1},{5,3},{7,5},{8,14},{10,8},{12,... | collective-permute-start | bytes 884744 | tf_op jit(solution)/shard_map/ppermute | solution.py:410
  27.2 0.8 copy-start.19
  28.1 0.9 copy-start.2
  29.7 9.2 %copy-start.4 = (f32[8,72,128]{2,1,0:T(8,128)}, f32[8,72,128]{2,1,0:T(8,128)S(1)}, u32[]{:S(2)}) copy-start(f32[8,72,128]{2,1,0:T(8,128)S(1)} %shard_map.58.ready.t0) | copy-start | bytes 884740
  30.5 5.7 %copy-start.6 = (f32[8,72,128]{2,1,0:T(8,128)}, f32[8,72,128]{2,1,0:T(8,128)S(1)}, u32[]{:S(2)}) copy-start(f32[8,72,128]{2,1,0:T(8,128)S(1)} %shard_map.59.ready.t0) | copy-start | bytes 884740
  36.2 2.0 %copy-start.33 = (f32[8192,128]{1,0:T(8,128)}, f32[8192,128]{1,0:T(8,128)S(1)}, u32[]{:S(2)}) copy-start(f32[8192,128]{1,0:T(8,128)S(1)} %get-tuple-element.48.run) | copy-start | bytes 12582916
  39.8 0.7 copy-start.12
  41.3 0.7 copy-start.15
  43.3 19.0 %all-to-all-start = ((f32[8,72,128]{2,1,0:T(8,128)}), f32[8,72,128]{2,1,0:T(8,128)}, u32[]{:S(2)}, u32[]{:S(2)}) async-start(f32[8,72,128]{2,1,0:T(8,128)} %copy-done.12), calls=%async_computation | async-start | bytes 589824 | tf_op jit(solution)/shard_map/all_to_all | solution.py:445
  51.5 11.8 %collective-permute-start.8 = (f32[8,72,128]{2,1,0:T(8,128)}, f32[8,72,128]{2,1,0:T(8,128)}, u32[]{:S(2)}, u32[]{:S(2)}) collective-permute-start(f32[8,72,128]{2,1,0:T(8,128)} %copy-done.21), channel_id=1, source_target_pairs={{0,4},{2,6},{4,0},{6,2},{1,5},{3,7},{5,1},{7,3},{8,12},{10,14},{12... | collective-permute-start | bytes 884744 | tf_op jit(solution)/shard_map/ppermute | solution.py:410
  51.5 13.7 %collective-permute-start.9 = (f32[8,72,128]{2,1,0:T(8,128)}, f32[8,72,128]{2,1,0:T(8,128)}, u32[]{:S(2)}, u32[]{:S(2)}) collective-permute-start(f32[8,72,128]{2,1,0:T(8,128)} %copy-done.20), channel_id=1, source_target_pairs={{0,6},{2,0},{4,2},{6,4},{1,7},{3,1},{5,3},{7,5},{8,14},{10,8},{12,... | collective-permute-start | bytes 884744 | tf_op jit(solution)/shard_map/ppermute | solution.py:410
  53.0 15.6 %collective-permute-start.7 = (f32[8,72,128]{2,1,0:T(8,128)}, f32[8,72,128]{2,1,0:T(8,128)}, u32[]{:S(2)}, u32[]{:S(2)}) collective-permute-start(f32[8,72,128]{2,1,0:T(8,128)} %copy-done.19), channel_id=1, source_target_pairs={{0,2},{2,4},{4,6},{6,0},{1,3},{3,5},{5,7},{7,1},{8,10},{10,12},{12... | collective-permute-start | bytes 884744 | tf_op jit(solution)/shard_map/ppermute | solution.py:410
  62.3 52.1 %copy-start.14 = (f32[8,72,128]{2,1,0:T(8,128)S(1)}, f32[8,72,128]{2,1,0:T(8,128)}, u32[]{:S(2)}) copy-start(f32[8,72,128]{2,1,0:T(8,128)} %copy-done.13) | copy-start | bytes 884740
  63.4 51.1 %copy-start.5 = (f32[8,72,128]{2,1,0:T(8,128)S(1)}, f32[8,72,128]{2,1,0:T(8,128)}, u32[]{:S(2)}) copy-start(f32[8,72,128]{2,1,0:T(8,128)} %copy-done.4) | copy-start | bytes 884740
  68.6 1.0 copy-start.7
  69.6 31.4 %copy-start.23 = (f32[64,128]{1,0:T(8,128)S(1)}, f32[64,128]{1,0:T(8,128)}, u32[]{:S(2)}) copy-start(f32[64,128]{1,0:T(8,128)} %copy-done.22) | copy-start | bytes 98308
  69.6 44.9 %copy-start.16 = (f32[8,72,128]{2,1,0:T(8,128)S(1)}, f32[8,72,128]{2,1,0:T(8,128)}, u32[]{:S(2)}) copy-start(f32[8,72,128]{2,1,0:T(8,128)} %copy-done.15) | copy-start | bytes 884740
  69.6 44.9 %copy-start.18 = (f32[8,72,128]{2,1,0:T(8,128)S(1)}, f32[8,72,128]{2,1,0:T(8,128)}, u32[]{:S(2)}) copy-start(f32[8,72,128]{2,1,0:T(8,128)} %copy-done.17) | copy-start | bytes 884740
  90.5 8.4 %collective-permute-start.12 = (f32[2,72,128]{2,1,0:T(8,128)S(1)}, f32[2,72,128]{2,1,0:T(8,128)S(1)}, u32[]{:S(2)}, u32[]{:S(2)}) collective-permute-start(f32[2,72,128]{2,1,0:T(8,128)S(1)} %shard_map.64), channel_id=1, source_target_pairs={{0,192},{1,193},{2,194},{3,195},{4,196},{5,197},{6,198},{7,199},{8... | collective-permute-start | bytes 221192 | tf_op jit(solution)/shard_map/ppermute | solution.py:449
  95.2 3.8 %collective-permute-start.11 = (f32[2,72,128]{2,1,0:T(8,128)S(1)}, f32[2,72,128]{2,1,0:T(8,128)S(1)}, u32[]{:S(2)}, u32[]{:S(2)}) collective-permute-start(f32[2,72,128]{2,1,0:T(8,128)S(1)} %shard_map.64), channel_id=1, source_target_pairs={{0,128},{64,192},{1,129},{65,193},{2,130},{66,194},{3,131},{67,195... | collective-permute-start | bytes 221192 | tf_op jit(solution)/shard_map/ppermute | solution.py:449
  96.5 4.6 %collective-permute-start.10 = (f32[2,72,128]{2,1,0:T(8,128)S(1)}, f32[2,72,128]{2,1,0:T(8,128)S(1)}, u32[]{:S(2)}, u32[]{:S(2)}) collective-permute-start(f32[2,72,128]{2,1,0:T(8,128)S(1)} %shard_map.64), channel_id=1, source_target_pairs={{0,64},{64,128},{128,192},{1,65},{65,129},{129,193},{2,66},{66,130... | collective-permute-start | bytes 221192 | tf_op jit(solution)/shard_map/ppermute | solution.py:449
  119.9 13.8 %all-to-all-start.3 = ((f32[8,72,128]{2,1,0:T(8,128)}), f32[8,72,128]{2,1,0:T(8,128)}, u32[]{:S(2)}, u32[]{:S(2)}) async-start(f32[8,72,128]{2,1,0:T(8,128)} %copy-done.11), calls=%async_computation.3 | async-start | bytes 589824 | tf_op jit(solution)/shard_map/all_to_all | solution.py:456
  124.0 13.7 %collective-permute-start.13 = (f32[8,72,128]{2,1,0:T(8,128)}, f32[8,72,128]{2,1,0:T(8,128)}, u32[]{:S(2)}, u32[]{:S(2)}) collective-permute-start(f32[8,72,128]{2,1,0:T(8,128)} %copy-done.32), channel_id=1, source_target_pairs={{0,6},{2,0},{4,2},{6,4},{1,7},{3,1},{5,3},{7,5},{8,14},{10,8},{12,... | collective-permute-start | bytes 884744 | tf_op jit(solution)/shard_map/ppermute | solution.py:460
  124.1 25.0 %collective-permute-start.14 = (f32[8,72,128]{2,1,0:T(8,128)}, f32[8,72,128]{2,1,0:T(8,128)}, u32[]{:S(2)}, u32[]{:S(2)}) collective-permute-start(f32[8,72,128]{2,1,0:T(8,128)} %copy-done.31), channel_id=1, source_target_pairs={{0,4},{2,6},{4,0},{6,2},{1,5},{3,7},{5,1},{7,3},{8,12},{10,14},{12... | collective-permute-start | bytes 884744 | tf_op jit(solution)/shard_map/ppermute | solution.py:460
  124.9 24.2 %collective-permute-start.15 = (f32[8,72,128]{2,1,0:T(8,128)}, f32[8,72,128]{2,1,0:T(8,128)}, u32[]{:S(2)}, u32[]{:S(2)}) collective-permute-start(f32[8,72,128]{2,1,0:T(8,128)} %copy-done.30), channel_id=1, source_target_pairs={{0,2},{2,4},{4,6},{6,0},{1,3},{3,5},{5,7},{7,1},{8,10},{10,12},{12... | collective-permute-start | bytes 884744 | tf_op jit(solution)/shard_map/ppermute | solution.py:460
  133.8 1.0 copy-start.8
  136.4 19.8 %collective-permute-start.16 = (f32[8,72,128]{2,1,0:T(8,128)S(1)}, f32[8,72,128]{2,1,0:T(8,128)S(1)}, u32[]{:S(2)}, u32[]{:S(2)}) collective-permute-start(f32[8,72,128]{2,1,0:T(8,128)S(1)} %get-tuple-element.61), channel_id=1, source_target_pairs={{0,6},{2,0},{4,2},{6,4},{1,7},{3,1},{5,3},{7,5},{8,14},{10,8},{12,... | collective-permute-start | bytes 884744 | tf_op jit(solution)/shard_map/ppermute | solution.py:460
  136.8 19.5 %collective-permute-start.17 = (f32[8,72,128]{2,1,0:T(8,128)S(1)}, f32[8,72,128]{2,1,0:T(8,128)S(1)}, u32[]{:S(2)}, u32[]{:S(2)}) collective-permute-start(f32[8,72,128]{2,1,0:T(8,128)S(1)} %get-tuple-element.62), channel_id=1, source_target_pairs={{0,4},{2,6},{4,0},{6,2},{1,5},{3,7},{5,1},{7,3},{8,12},{10,14},{12... | collective-permute-start | bytes 884744 | tf_op jit(solution)/shard_map/ppermute | solution.py:460
  137.6 18.6 %collective-permute-start.18 = (f32[8,72,128]{2,1,0:T(8,128)S(1)}, f32[8,72,128]{2,1,0:T(8,128)S(1)}, u32[]{:S(2)}, u32[]{:S(2)}) collective-permute-start(f32[8,72,128]{2,1,0:T(8,128)S(1)} %get-tuple-element.63), channel_id=1, source_target_pairs={{0,2},{2,4},{4,6},{6,0},{1,3},{3,5},{5,7},{7,1},{8,10},{10,12},{12... | collective-permute-start | bytes 884744 | tf_op jit(solution)/shard_map/ppermute | solution.py:460
  138.2 0.8 copy-start.24
  140.4 2.2 %copy-start.34 = (f32[8192,128]{1,0:T(8,128)S(1)}, f32[8192,128]{1,0:T(8,128)}, u32[]{:S(2)}) copy-start(f32[8192,128]{1,0:T(8,128)} %copy-done.33) | copy-start | bytes 12582916
  143.3 0.8 copy-start.38
  144.1 5.0 %copy-start.1 = (f32[2,8,72,128]{3,2,1,0:T(8,128)S(1)}, f32[2,8,72,128]{3,2,1,0:T(8,128)}, u32[]{:S(2)}) copy-start(f32[2,8,72,128]{3,2,1,0:T(8,128)} %copy-done) | copy-start | bytes 1769476
  144.1 5.0 %copy-start.3 = (f32[2,8,72,128]{3,2,1,0:T(8,128)S(1)}, f32[2,8,72,128]{3,2,1,0:T(8,128)}, u32[]{:S(2)}) copy-start(f32[2,8,72,128]{3,2,1,0:T(8,128)} %copy-done.2) | copy-start | bytes 1769476
  144.1 5.1 %copy-start.10 = (f32[8,72,128]{2,1,0:T(8,128)S(1)}, f32[8,72,128]{2,1,0:T(8,128)}, u32[]{:S(2)}) copy-start(f32[8,72,128]{2,1,0:T(8,128)} %copy-done.9) | copy-start | bytes 884740
  150.8 9.6 %copy-start.26 = (s32[4096]{0:T(1024)S(1)}, s32[4096]{0:T(1024)}, u32[]{:S(2)}) copy-start(s32[4096]{0:T(1024)} %param.6) | copy-start | bytes 49156
  150.8 9.6 %copy-start.28 = (s32[4096,1]{0,1:T(1,128)S(1)}, s32[4096,1]{0,1:T(1,128)}, u32[]{:S(2)}) copy-start(s32[4096,1]{0,1:T(1,128)} %param.5) | copy-start | bytes 49156
  150.8 7.9 %collective-permute-start.19 = (f32[32,72,128]{2,1,0:T(8,128)S(1)}, f32[32,72,128]{2,1,0:T(8,128)S(1)}, u32[]{:S(2)}, u32[]{:S(2)}) collective-permute-start(f32[32,72,128]{2,1,0:T(8,128)S(1)} %get-tuple-element.65), channel_id=1, source_target_pairs={{0,1},{1,0},{2,3},{3,2},{4,5},{5,4},{6,7},{7,6},{8,9},{9,8},{10,11... | collective-permute-start | bytes 3538952 | tf_op jit(solution)/shard_map/ppermute | solution.py:476
  157.4 3.0 %collective-permute-start.20 = (f32[32,72,128]{2,1,0:T(8,128)S(1)}, f32[32,72,128]{2,1,0:T(8,128)S(1)}, u32[]{:S(2)}, u32[]{:S(2)}) collective-permute-start(f32[32,72,128]{2,1,0:T(8,128)S(1)} %get-tuple-element.66), channel_id=1, source_target_pairs={{0,1},{1,0},{2,3},{3,2},{4,5},{5,4},{6,7},{7,6},{8,9},{9,8},{10,11... | collective-permute-start | bytes 3538952 | tf_op jit(solution)/shard_map/ppermute | solution.py:476
  (14 other events, 9.9 us)

commit v4 on v3

v4 whole, which is shorter than its diff:
```python
import functools

import jax
import jax.numpy as jnp
from jax import lax
from jax.experimental import pallas as pl
from jax.experimental.pallas import tpu as pltpu
from jax.sharding import Mesh, PartitionSpec as P


LANES = 128
FOUR = 4
TAIL = FOUR * LANES
ROWS = TAIL + 8
ONE = LANES + 8
NH, NL, NX, NC = 4, 2, 4, 2
OWNERS = NH * NL * NX * NC
HALF = OWNERS // NC
CHUNKS = HALF // FOUR
BF16, F32, I32 = jnp.bfloat16, jnp.float32, jnp.int32
VMEM = pl.BlockSpec(memory_space=pltpu.VMEM)
SMEM = pl.BlockSpec(memory_space=pltpu.SMEM)
HBM = pl.BlockSpec(memory_space=pltpu.HBM)
ANY = pl.BlockSpec(memory_space=pl.ANY)


def dot(a, b):
    return lax.dot_general(a, b, (((1,), (0,)), ((), ())), preferred_element_type=F32)


def dot_nt(a, b):
    return lax.dot_general(a, b, (((1,), (1,)), ((), ())), preferred_element_type=F32)


def iota(shape, dim):
    return lax.broadcasted_iota(I32, shape, dim)


def as_bf16(mask):
    return jnp.where(mask, 1.0, 0.0).astype(BF16)


def two_parts(v):
    high = v.astype(BF16)
    low = (v - high.astype(F32)).astype(BF16)
    return jnp.concatenate([high, low], axis=1)


def masked_sum(mask, parts):
    both = dot(mask, parts)
    return both[:, :LANES] + both[:, LANES:]


def call(kernel, out, args, specs, out_specs=None, scratch=(), cost=1_000_000, limit=24, aliases=None):
    return pl.pallas_call(
        kernel,
        out_shape=out,
        in_specs=specs,
        out_specs=out_specs or jax.tree.map(lambda _: VMEM, out),
        scratch_shapes=list(scratch),
        input_output_aliases=aliases or {},
        cost_estimate=pl.CostEstimate(flops=cost, bytes_accessed=1_000_000, transcendentals=0),
        compiler_params=pltpu.CompilerParams(vmem_limit_bytes=limit << 20),
    )(*args)


def block(*lead):
    return jax.ShapeDtypeStruct((*lead, ROWS, LANES), F32)


def one_block(*lead):
    return jax.ShapeDtypeStruct((*lead, ONE, LANES), F32)


def chunk_of(place, dz, dx):
    row = jnp.where(place[2] == 0, dz, 1 - dz)
    return row * NX + lax.rem(place[1] + dx, NX)


def rank_kernel(events, slot_out, acc_out, flag_out, cleared):
    lines = slot_out.shape[0]
    zero = jnp.zeros((LANES, LANES), F32)
    below = as_bf16(iota((LANES, LANES), 0) < iota((LANES, LANES), 1))
    with_total = jnp.concatenate([below, jnp.ones((LANES, LANES), BF16)], axis=1)
    owner_ids = iota((OWNERS, LANES), 0)
    before = jnp.zeros((OWNERS, LANES), F32)
    codes = jnp.zeros((OWNERS, LANES), F32)
    each = cleared.shape[0] // LANES // lines
    for b in range(lines):
        home_row = events[b : b + 1, :]
        account_row = events[lines + b : lines + b + 1, :]
        flag_row = events[2 * lines + b : 2 * lines + b + 1, :]
        chosen = owner_ids == home_row
        counted = dot(as_bf16(chosen), with_total)
        rank = jnp.sum(
            jnp.where(chosen, counted[:, :LANES] + before, 0.0), axis=0, keepdims=True
        )
        before = before + counted[:, LANES:]
        slot_out[b : b + 1, :] = home_row * LANES + rank.astype(I32)
        code = (account_row * 2 + flag_row + 1).astype(F32)
        rank_of = as_bf16(iota((LANES, LANES), 0) == rank.astype(I32))
        codes = codes + dot_nt(jnp.where(chosen, code, 0.0).astype(BF16), rank_of)
        for i in range(each):
            cleared[(b * each + i) * LANES : (b * each + i + 1) * LANES, :] = zero
    code_ids = codes.astype(I32) - 1
    acc_out[...] = jnp.right_shift(code_ids, 1)
    flag_out[...] = jnp.where(code_ids >= 0, jnp.bitwise_and(code_ids, 1), 0).astype(F32)


def spread_kernel(slot_rows, features, cleared, grouped, slots, sem):
    copy = pltpu.make_async_copy(slot_rows, slots, sem)
    copy.start()
    copy.wait()

    def spread(b, _):
        for j in range(LANES):
            grouped[pl.ds(slots[b, j], 1), :] = features[pl.ds(b * LANES + j, 1), :]
        return 0

    lax.fori_loop(0, slot_rows.shape[0], spread, 0)


def after_and_ones():
    after = as_bf16(iota((LANES, LANES), 0) > iota((LANES, LANES), 1))
    return jnp.concatenate([after, jnp.ones((LANES, LANES), BF16)], axis=1)


def cut(v, i):
    return v[i * LANES : (i + 1) * LANES, :]


def counted_rows(counted, flagged):
    count = dot(jnp.concatenate(counted, axis=0), jnp.ones((LANES, LANES), BF16))
    lane = iota((LANES, LANES), 1)
    both = jnp.zeros((LANES, LANES), F32)
    for i in range(8):
        both = jnp.where(lane == i, cut(count, i), both)
        both = jnp.where(lane == 8 + i, cut(flagged, i), both)
    return both.T


def closing_kernel(dx, place, acc_rows, flag_rows, grouped, ready, other, mine):
    sides = after_and_ones()
    for out, half_of in ((other, 1 - place[0]), (mine, place[0])):
        bases = [half_of * HALF + chunk_of(place, dz, dx) * FOUR for dz in range(NL)]
        acc8 = jnp.concatenate([acc_rows[pl.ds(b, FOUR), :] for b in bases], axis=0)
        flag8 = jnp.concatenate([flag_rows[pl.ds(b, FOUR), :] for b in bases], axis=0)
        member = [iota((LANES, LANES), 0) == acc8[i : i + 1, :] for i in range(8)]
        member_flags = [
            jnp.where(member[i], flag8[i : i + 1, :], 0.0).astype(BF16) for i in range(8)
        ]
        flagged = dot(jnp.concatenate(member_flags, axis=0), sides)
        counted = [as_bf16(member[i] & (cut(flagged, i)[:, :LANES] < 0.5)) for i in range(8)]
        rows = counted_rows(counted, flagged[:, LANES:])
        marks = jnp.minimum(rows[8:16, :], 1.0)
        for dz in range(NL):
            for i in range(FOUR):
                at = pl.multiple_of((bases[dz] + i) * LANES, LANES)
                values = two_parts(grouped[pl.ds(at, LANES), :])
                out[dz, i * LANES : (i + 1) * LANES, :] = masked_sum(
                    counted[dz * FOUR + i], values
                )
            own = slice(dz * FOUR, dz * FOUR + FOUR)
            out[dz, TAIL:, :] = jnp.concatenate([rows[own, :], marks[own, :]], axis=0)


def running_kernel(acc_rows, flag_rows, grouped, ready, run, counts, opens):
    sides = after_and_ones()
    up_to = iota((LANES, LANES), 1) <= iota((LANES, LANES), 0)

    def some(g, _):
        rows = pl.ds(pl.multiple_of(g * 8, 8), 8)
        acc8 = acc_rows[rows, :].astype(F32)
        flag8 = flag_rows[rows, :]
        acc_cols = acc8.T
        same = []
        for i in range(8):
            acc_col = jnp.broadcast_to(acc_cols[:, i : i + 1], (LANES, LANES))
            same.append((acc_col == acc8[i : i + 1, :]) & (acc_col >= 0.0) & up_to)
        same_flags = [
            jnp.where(same[i], flag8[i : i + 1, :], 0.0).astype(BF16) for i in range(8)
        ]
        flagged = dot(jnp.concatenate(same_flags, axis=0), sides)
        session = [as_bf16(same[i] & (cut(flagged, i)[:, :LANES] < 0.5)) for i in range(8)]
        for i in range(8):
            at = pl.ds(pl.multiple_of((g * 8 + i) * LANES, LANES), LANES)
            run[at, :] = masked_sum(session[i], two_parts(grouped[at, :]))
        found = counted_rows(session, flagged[:, LANES:])
        counts[rows, :] = found[:8, :]
        opens[rows, :] = jnp.where(found[8:16, :] < 0.5, 1.0, 0.0)
        return 0

    lax.fori_loop(0, OWNERS // 8, some, 0)


def in_time_kernel(
    slots, slot_rows, home, account, run, counts, opens, ready,
    run_out, count_out, open_out, user_out,
):
    lines = home.shape[0]

    def scalars(t, _):
        rows = pl.ds(pl.multiple_of(t * 8, 8), 8)
        home8 = home[rows, :]
        rank = slot_rows[rows, :] - home8 * LANES
        count = jnp.zeros((8, LANES), F32)
        is_open = jnp.zeros((8, LANES), F32)
        for o in range(OWNERS):
            here = home8 == o
            for_count = jnp.broadcast_to(counts[o : o + 1, :], (8, LANES))
            for_open = jnp.broadcast_to(opens[o : o + 1, :], (8, LANES))
            count = jnp.where(here, jnp.take_along_axis(for_count, rank, axis=1), count)
            is_open = jnp.where(here, jnp.take_along_axis(for_open, rank, axis=1), is_open)
        count_out[rows, :] = count
        open_out[rows, :] = is_open
        chunk = jnp.right_shift(home8, 2)
        row = (home8 - chunk * FOUR) * LANES + account[rows, :]
        user_out[rows, :] = chunk * ROWS + jnp.where(is_open > 0.5, row, TAIL + FOUR)
        return 0

    lax.fori_loop(0, lines // 8, scalars, 0)

    def collect(b, _):
        for j in range(LANES):
            run_out[pl.ds(b * LANES + j, 1), :] = run[pl.ds(slots[b, j], 1), :]
        return 0

    lax.fori_loop(0, lines, collect, 0)


def sums_of(chunk, i):
    return chunk[i * LANES : (i + 1) * LANES, :]


def keep_of(tail):
    return (1.0 - tail).T


def joined_sums(keep, i, earlier, later):
    return later + jnp.broadcast_to(keep[:, i : i + 1], (LANES, LANES)) * earlier


def joined_tail(earlier, later):
    marks = jnp.concatenate([later[FOUR:, :], later[:FOUR, :]], axis=0)
    return jnp.where(
        iota((8, LANES), 0) < FOUR, later + (1.0 - marks) * earlier, jnp.maximum(later, earlier)
    )


def joined_one(earlier, later):
    tail, first = later[LANES:, :], earlier[LANES:, :]
    mark = tail[1:2, :]
    sub = iota((8, LANES), 0)
    sums = joined_sums(keep_of(tail), 1, earlier[:LANES, :], later[:LANES, :])
    tail = jnp.where(
        sub == 0, tail + (1.0 - mark) * first, jnp.where(sub == 1, jnp.maximum(tail, first), 0.0)
    )
    return jnp.concatenate([sums, tail], axis=0)


def core_kernel(place, mine, got, *outs):
    first = place[0] == 0
    for dz in range(NL):
        a, b = mine[dz, TAIL:, :], got[dz, TAIL:, :]
        early, late = jnp.where(first, a, b), jnp.where(first, b, a)
        keep = keep_of(late)
        for i in range(FOUR):
            at = slice(i * LANES, (i + 1) * LANES)
            a, b = mine[dz, at, :], got[dz, at, :]
            outs[dz][at, :] = joined_sums(
                keep, FOUR + i, jnp.where(first, a, b), jnp.where(first, b, a)
            )
        outs[dz][TAIL:, :] = joined_tail(early, late)


def row_kernel(place, *refs):
    tables = (refs[:NX], refs[NX : 2 * NX])
    totals = refs[2 * NX + 1 : 2 * NX + 3]
    outs, pair = refs[2 * NX + 3 : 2 * NX + 3 + NH], refs[-1]
    for x in range(NX):

        @pl.when(place[1] == x)
        def _(x=x):
            for dz in range(NL):
                order = [tables[dz][(x - j) % NX] for j in range(NX)]
                tails = [t[TAIL:, :] for t in order]
                keep = [keep_of(t) for t in tails]
                for i in range(FOUR):
                    total = sums_of(order[0], i)
                    for j in range(1, NX):
                        total = joined_sums(keep[j], FOUR + i, total, sums_of(order[j], i))
                    totals[dz][i * LANES : (i + 1) * LANES, :] = total
                tail = tails[0]
                for j in range(1, NX):
                    tail = joined_tail(tail, tails[j])
                totals[dz][TAIL:, :] = tail

    own, near = totals
    first = place[2] == 0
    a, b = own[TAIL:, :], near[TAIL:, :]
    early, late = jnp.where(first, a, b), jnp.where(first, b, a)
    keep = keep_of(late)
    tail = joined_tail(early, late)
    sub = iota((8, LANES), 0)
    for i in range(FOUR):
        a, b = sums_of(own, i), sums_of(near, i)
        pair[i, :LANES, :] = joined_sums(
            keep, FOUR + i, jnp.where(first, a, b), jnp.where(first, b, a)
        )
        pair[i, LANES:, :] = jnp.where(
            sub == 0, tail[i : i + 1, :],
            jnp.where(sub == 1, tail[FOUR + i : FOUR + i + 1, :], 0.0),
        )
    for r in range(NH):
        outs[r][...] = pair[lax.rem(place[3] + r, NH)]


def plane_kernel(place, r0, r1, r2, r3, out):
    rows = (r0, r1, r2, r3)
    for h in range(NH):

        @pl.when(place[3] == h)
        def _(h=h):
            total = rows[h][...]
            for j in range(1, NH):
                total = joined_one(total, rows[(h - j) % NH][...])
            out[...] = total


def rows_back_kernel(place, p1, p2, p3, r0, r1, r2, r3, *outs):
    rows = (r0, r1, r2, r3)
    start = jnp.zeros((ONE, LANES), F32)
    for r, plane in ((2, p3), (1, p2), (0, p1)):
        start = jnp.where(place[4] > r, joined_one(start, plane[...]), start)
    for h in range(NH):

        @pl.when(place[3] == h)
        def _(h=h):
            state = start
            for j in range(NH):
                k = (h - j) % NH
                outs[k][...] = state
                if j < NH - 1:
                    state = joined_one(state, rows[k][...])


def chips_back_kernel(place, e0, e1, e2, e3, own, near, *refs):
    tables, outs = (refs[:NX], refs[NX : 2 * NX]), (refs[2 * NX : 3 * NX], refs[3 * NX : 4 * NX])
    came = refs[-1]
    for r, e in enumerate((e0, e1, e2, e3)):
        came[lax.rem(place[3] + r, NH)] = e[...]
    first = place[2] == 0
    sub = iota((8, LANES), 0)
    tail0 = jnp.zeros((8, LANES), F32)
    for i in range(FOUR):
        tail0 = jnp.where(sub == i, came[i, LANES : LANES + 1, :], tail0)
    between = jnp.where(first, own[TAIL:, :], near[TAIL:, :])
    keep = keep_of(between)
    tail1 = joined_tail(tail0, between)
    for x in range(NX):

        @pl.when(place[1] == x)
        def _(x=x):
            for dz in range(NL):
                order = [(x - j) % NX for j in range(NX)]
                tails = [tables[dz][k][TAIL:, :] for k in order[:-1]]
                keeps = [keep_of(t) for t in tails]
                late = first if dz else jnp.logical_not(first)
                for i in range(FOUR):
                    at = slice(i * LANES, (i + 1) * LANES)
                    state = came[i, :LANES, :]
                    second = joined_sums(
                        keep, FOUR + i, state, jnp.where(first, own[at, :], near[at, :])
                    )
                    state = jnp.where(late, second, state)
                    for j, k in enumerate(order):
                        outs[dz][k][at, :] = state
                        if j < NX - 1:
                            state = joined_sums(
                                keeps[j], FOUR + i, state, sums_of(tables[dz][k], i)
                            )
                tail = jnp.where(late, tail1, tail0)
                for j, k in enumerate(order):
                    outs[dz][k][TAIL:, :] = tail
                    if j < NX - 1:
                        tail = joined_tail(tail, tails[j])


def cores_back_kernel(place, ready, *refs):
    parts, mine, got = refs[:4], refs[4:6], refs[6:8]
    keep_out, send = refs[8:]
    first = place[0] == 0
    counts_only = iota((8, LANES), 0) < FOUR
    for d in range(2):
        for dz in range(NL):
            part, at = parts[2 * d + dz], 2 * d + dz
            core0 = jnp.where(first, mine[d][dz, TAIL:, :], got[d][dz, TAIL:, :])
            keep = keep_of(core0)
            for i in range(FOUR):
                rows = slice(i * LANES, (i + 1) * LANES)
                state = part[rows, :]
                second = joined_sums(
                    keep, FOUR + i, state,
                    jnp.where(first, mine[d][dz, rows, :], got[d][dz, rows, :]),
                )
                keep_out[at, rows, :] = jnp.where(first, state, second)
                send[at, rows, :] = jnp.where(first, second, state)
            state = part[TAIL:, :]
            second = joined_tail(state, core0)
            keep_out[at, TAIL:, :] = jnp.where(counts_only, jnp.where(first, state, second), 0.0)
            send[at, TAIL:, :] = jnp.where(counts_only, jnp.where(first, second, state), 0.0)


BACK = ((2, 0), (1, 3))


def finish_kernel(place, users, run, count, is_open, home, account, *refs):
    sides, (out, table, picked, sems) = refs[:4], refs[4:]
    copies, held = [], []
    for s, side in enumerate(sides):
        half_of = place[0] if s < 2 else 1 - place[0]
        for d in range(2):
            for dz in range(NL):
                at = half_of * CHUNKS + chunk_of(place, dz, BACK[s % 2][d])
                held.append((side, 2 * d + dz, at))
                copies.append(
                    pltpu.make_async_copy(
                        side.at[2 * d + dz], table.at[at], sems.at[4 * s + 2 * d + dz]
                    )
                )
                copies[-1].start()
    lines = home.shape[0]
    flat = table.reshape(NC * CHUNKS * ROWS, LANES)
    scale = []
    for t in range(lines // 8):
        rows = slice(8 * t, 8 * t + 8)
        home8, account8 = home[rows, :], account[rows, :]
        came = jnp.zeros((8, LANES), F32)
        for side, index, at in held:
            for i in range(FOUR):
                row = jnp.broadcast_to(side[index, TAIL + i : TAIL + i + 1, :], (8, LANES))
                found = jnp.take_along_axis(row, account8, axis=1)
                came = jnp.where(home8 == at * FOUR + i, found, came)
        scale.append(1.0 / (count[rows, :] + is_open[rows, :] * came))
    scale = jnp.concatenate(scale, axis=0)
    if lines < LANES:
        scale = jnp.concatenate([scale, jnp.zeros((LANES - lines, LANES), F32)], axis=0)
    scale = scale.T
    for copy in copies:
        copy.wait()

    def pick(b, _):
        for j in range(LANES):
            picked[pl.ds(b * LANES + j, 1), :] = flat[pl.ds(users[b, j], 1), :]
        return 0

    lax.fori_loop(0, lines, pick, 0)
    for b in range(lines):
        at = pl.ds(b * LANES, LANES)
        factor = jnp.broadcast_to(scale[:, b : b + 1], (LANES, LANES))
        out[at, :] = (run[at, :] + picked[at, :]) * factor


def ring(n, k):
    return [(i, (i + k) % n) for i in range(n)]


def body(features, home, account, flags):
    rows = features.shape[0]
    lines = rows // LANES
    home = home.reshape(lines, LANES)
    account = account.reshape(lines, LANES)
    flags = flags.reshape(lines, LANES)
    spot, place = iota((8,), 0), jnp.zeros((8,), I32)
    for n, axis in enumerate(("c", "x", "l", "h", "y")):
        place = jnp.where(spot == n, lax.axis_index(axis).astype(I32), place)
    small = jax.ShapeDtypeStruct((lines, LANES), I32)
    small_f = jax.ShapeDtypeStruct((lines, LANES), F32)
    by_owner = functools.partial(jax.ShapeDtypeStruct, (OWNERS, LANES))
    by_slot = jax.ShapeDtypeStruct((OWNERS * LANES, LANES), F32)
    slot, acc_rows, flag_rows, cleared = call(
        rank_kernel,
        [small, by_owner(I32), by_owner(F32), by_slot],
        (jnp.concatenate([home, account, flags]),),
        [VMEM],
        cost=2_000_000_000,
    )
    grouped = call(
        spread_kernel,
        by_slot,
        (slot, features, cleared),
        [VMEM] * 3,
        scratch=[pltpu.SMEM((lines, LANES), I32), pltpu.SemaphoreType.DMA],
        cost=4_000_000_000,
        aliases={2: 0},
    )
    swap = ring(NC, 1)

    def exchange(v, dz, dx):
        if dz == 0 and dx == 0:
            return v
        pairs = [
            (row * NX + x, (row ^ dz) * NX + (x + dx) % NX) for row in range(NL) for x in range(NX)
        ]
        return lax.ppermute(v, ("l", "x"), pairs)

    order = (2, 1, 3, 0)
    mine, got = [None] * NX, [None] * NX
    tables = [[None] * NX for _ in range(NL)]

    def meet(dx):
        chunks = call(core_kernel, [block()] * NL, (place, mine[dx], got[dx]),
                      [SMEM, VMEM, VMEM], cost=500_000_000)
        for dz in reversed(range(NL)):
            tables[dz][dx] = exchange(chunks[dz], dz, dx)
        return chunks[0]

    met = [acc_rows]
    for at, dx in enumerate(order):
        other, mine[dx] = call(
            functools.partial(closing_kernel, dx),
            [block(NL)] * 2,
            (place, acc_rows, flag_rows, grouped, met[at]),
            [SMEM] + [VMEM] * 3 + [ANY],
            cost=1_500_000_000,
        )
        got[dx] = lax.ppermute(other, "c", swap)
        met.append(meet(order[at - 1]) if at else mine[dx])
    met.append(meet(order[-1]))
    run_slots, counts, opens = call(
        running_kernel,
        [by_slot, by_owner(F32), by_owner(F32)],
        (acc_rows, flag_rows, grouped, met[-1]),
        [VMEM] * 3 + [ANY],
        cost=8_000_000_000,
    )
    own, near, *pairs = call(
        row_kernel,
        [block()] * NL + [one_block()] * NH,
        (place, *tables[0], *tables[1], counts),
        [SMEM] + [VMEM] * (NL * NX) + [ANY],
        scratch=[pltpu.VMEM((NH, ONE, LANES), F32)],
    )
    rows_got = [pairs[0]] + [lax.ppermute(pairs[r], "h", ring(NH, r)) for r in range(1, NH)]
    plane = call(plane_kernel, one_block(), (place, *rows_got), [SMEM] + [VMEM] * NH)
    ny = lax.axis_size("y")
    planes = [
        lax.ppermute(plane, "y", [(i, i + r) for i in range(ny - r)]) for r in range(1, ny)
    ]
    came = call(rows_back_kernel, [one_block()] * NH, (place, *planes, *rows_got),
                [SMEM] + [VMEM] * (3 + NH))
    came = [came[0]] + [lax.ppermute(came[r], "h", ring(NH, -r)) for r in range(1, NH)]
    parts = call(
        chips_back_kernel,
        [block()] * (NL * NX),
        (place, *came, own, near, *tables[0], *tables[1]),
        [SMEM] + [VMEM] * (NH + NL + NL * NX),
        scratch=[pltpu.VMEM((NH, ONE, LANES), F32)],
    )
    parts = [list(parts[:NX]), list(parts[NX:])]
    kept = parts[0][0]
    for dx in (2, 0, 1, 3):
        for dz in reversed(range(NL)):
            parts[dz][dx] = exchange(parts[dz][dx], dz, (NX - dx) % NX)
    run, count, is_open, users = call(
        in_time_kernel,
        [jax.ShapeDtypeStruct((rows, LANES), F32), small_f, small_f, small],
        (slot, slot, home, account, run_slots, counts, opens, kept),
        [SMEM] + [VMEM] * 6 + [ANY],
        cost=10_000_000_000,
    )
    keep, last = [], []
    for dxs in BACK:
        stay, send = call(
            cores_back_kernel,
            [block(4)] * 2,
            (place, keep[-1] if keep else count, *[parts[dz][dx] for dx in dxs for dz in range(NL)],
             *[mine[dx] for dx in dxs], *[got[dx] for dx in dxs]),
            [SMEM, ANY] + [VMEM] * 8,
            cost=500_000_000,
        )
        keep.append(stay)
        last.append(lax.ppermute(send, "c", swap))
    return call(
        finish_kernel,
        jax.ShapeDtypeStruct((rows, LANES), F32),
        (place, users, run, count, is_open, home, account, *keep, *last),
        [SMEM, SMEM] + [VMEM] * 9,
        scratch=[pltpu.VMEM((NC * CHUNKS, ROWS, LANES), F32), pltpu.VMEM((rows, LANES), F32),
                 pltpu.SemaphoreType.DMA((16,))],
    )


def solution(mesh):
    axes = ("y", "h", "l", "x", "c")
    split = Mesh(mesh.devices.reshape(-1, NH, NL, NX, NC), axes)
    return jax.shard_map(
        body,
        mesh=split,
        in_specs=(P(axes, None), P(axes, None), P(axes), P(axes)),
        out_specs=P(axes, None),
        check_vma=False,
    )
```

time: 170 us -> 139 us (0.82)
  blocking collectives: 30.2 us -> 0 us
  starting transfers between devices: 39.2 us -> 60.4 us
  local copies, waits for them, and re-layouts: 19 us -> 0.02 us
  Pallas kernels: 50.6 us -> 41.9 us
  waiting for transfers between devices: 27.7 us -> 34.7 us
    ppermute x16 -> x24, starting transfers between devices: 13 us -> 43.7 us  [the longest x14 20.5 us: exchange(): return lax.ppermute(v, ('l', 'x'), pairs)]
    all_to_all x2 -> x0, blocking collectives: 30.2 us -> none  [the longest x1 18 us: body(): row_totals.append(lax.all_to_all(total, 'z', 0, 0, tiled=True))]
    ppermute x16 -> x24, waiting for transfers between devices: 5.28 us -> 31 us  [the longest x14 23.3 us: exchange(): return lax.ppermute(v, ('l', 'x'), pairs)]
    unnamed x78 -> x6, local copies, waits for them, and re-layouts: 19 us -> 0.02 us
    all_to_all x2 -> x0, waiting for transfers between devices: 17.5 us -> none  [the longest x1 9.26 us: body(): row_totals.append(lax.all_to_all(total, 'z', 0, 0, tiled=True))]
    all_to_all x2 -> x0, starting transfers between devices: 12.2 us -> none  [the longest x1 8.19 us: body(): row_totals.append(lax.all_to_all(total, 'z', 0, 0, tiled=True))]
    pallas_call x27 -> x19, Pallas kernels: 50.6 us -> 41.9 us  [call(): pl.pallas_call(kernel, out_shape=out, in_specs=specs, out_specs=out_specs...]
    ppermute x2, starting transfers between devices: 5.52 us -> 7.68 us  [body(): last.append(lax.ppermute(send, 'c', swap))]
  transfers between devices with their start and end apart: 23 -> 29, of which waited for: 7 -> 11; matrix products, arithmetic and copies ran while one was open for 0% -> 0% of each run, Pallas kernels for 16% -> 15%
where the time goes in v4:
time: 139 us; the launch traced here: 138 us
  starting transfers between devices  60.4 us (43%)
  Pallas kernels  41.9 us (30%)
  waiting for transfers between devices  34.7 us (25%)
    pallas_call x19, Pallas kernels, call(): pl.pallas_call(kernel, out_shape=out, in_specs=specs, out_specs=out_specs...  41.9 us
    ppermute x14, waiting for transfers between devices, exchange(): return lax.ppermute(v, ('l', 'x'), pairs)  23.3 us
    ppermute x14, starting transfers between devices, exchange(): return lax.ppermute(v, ('l', 'x'), pairs)  20.5 us
    ppermute x3, starting transfers between devices, body(): lax.ppermute(pairs[r], 'h', ring(NH, r))  11.2 us
    ppermute x3, starting transfers between devices, body(): lax.ppermute(plane, 'y', [(i, i + r) for i in range(ny - r)])  9.03 us
    ppermute x3, starting transfers between devices, body(): lax.ppermute(came[r], 'h', ring(NH, -r))  7.95 us
    ppermute x2, starting transfers between devices, body(): last.append(lax.ppermute(send, 'c', swap))  7.68 us
    ppermute x3, waiting for transfers between devices, body(): lax.ppermute(came[r], 'h', ring(NH, -r))  5.3 us
  transfers between devices with their start and end apart: 29, of which 11 were waited for; matrix products, arithmetic and copies ran while one was open for 0% of the time, Pallas kernels for 15%

profile of v4, /device:TPU:1, one launch (start us, length us, event | category | flops | bytes accessed | tf_op | source)
XLA Modules:
  0.0 138.3 jit_solution(411170110778529638)
XLA Ops:
  0.0 0.8 pad_add_fusion.events
  0.8 2.7 %shard_map.46 = (s32[32,128]{1,0:T(8,128)S(1)}, s32[64,128]{1,0:T(8,128)S(1)}, f32[64,128]{1,0:T(8,128)S(1)}, f32[8192,128]{1,0:T(8,128)S(1)}) custom-call(s32[96,128]{1,0:T(8,128)S(1)} %pad_add_fusion.events), custom_call_target="tpu_custom_call" | custom-call | flops 2000000000 | bytes 1000000 | tf_op jit(solution)/shard_map/pallas_call | solution.py:55
  3.5 4.2 %shard_map.47.grouped = f32[8192,128]{1,0:T(8,128)S(1)} custom-call(s32[32,128]{1,0:T(8,128)S(1)} %get-tuple-element.54.slot_rows.slots, f32[4096,128]{1,0:T(8,128)S(1)} %copy-done.2, f32[8192,128]{1,0:T(8,128)S(1)} %get-tuple-element.57.cleared), custom_call_target="tpu_custom_call", output_to_operand_aliasing={{}: (2, {})} | custom-call | flops 4000000000 | bytes 1000000 | tf_op jit(solution)/shard_map/pallas_call | solution.py:55
  7.7 1.6 %shard_map.48 = (f32[2,520,128]{2,1,0:T(8,128)S(1)}, f32[2,520,128]{2,1,0:T(8,128)S(1)}) custom-call(s32[8]{0:T(128)S(1)} %compare_select_fusion.4.place, s32[64,128]{1,0:T(8,128)S(1)} %get-tuple-element.55.acc_rows.ready, f32[64,128]{1,0:T(8,128)S(1)} %get-tuple-element.56.flag_rows, f32[8192,128]{1,0:T(8,128)S(1)} %shard_map.47.grouped, ...), custom_call_target="tpu_custom_call" | custom-call | flops 1500000000 | bytes 1000000 | tf_op jit(solution)/shard_map/pallas_call | solution.py:55
  9.4 3.3 %collective-permute-start.3 = (f32[2,520,128]{2,1,0:T(8,128)S(1)}, f32[2,520,128]{2,1,0:T(8,128)S(1)}, u32[]{:S(2)}, u32[]{:S(2)}) collective-permute-start(f32[2,520,128]{2,1,0:T(8,128)S(1)} %get-tuple-element.68), channel_id=1, source_target_pairs={{0,1},{1,0},{2,3},{3,2},{4,5},{5,4},{6,7},{7,6},{8,9},{9,8},{10,11... | collective-permute-start | bytes 1597448 | tf_op jit(solution)/shard_map/ppermute | solution.py:527
  12.6 1.6 %shard_map.49 = (f32[2,520,128]{2,1,0:T(8,128)S(1)}, f32[2,520,128]{2,1,0:T(8,128)S(1)}) custom-call(s32[8]{0:T(128)S(1)} %compare_select_fusion.4.place, s32[64,128]{1,0:T(8,128)S(1)} %get-tuple-element.55.acc_rows.ready, f32[64,128]{1,0:T(8,128)S(1)} %get-tuple-element.56.flag_rows, f32[8192,128]{1,0:T(8,128)S(1)} %shard_map.47.grouped, ...), custom_call_target="tpu_custom_call" | custom-call | flops 1500000000 | bytes 1000000 | tf_op jit(solution)/shard_map/pallas_call | solution.py:55
  14.4 0.8 shard_map.54
  15.2 1.6 %shard_map.55 = (f32[2,520,128]{2,1,0:T(8,128)S(1)}, f32[2,520,128]{2,1,0:T(8,128)S(1)}) custom-call(s32[8]{0:T(128)S(1)} %compare_select_fusion.4.place, s32[64,128]{1,0:T(8,128)S(1)} %get-tuple-element.55.acc_rows.ready, f32[64,128]{1,0:T(8,128)S(1)} %get-tuple-element.56.flag_rows, f32[8192,128]{1,0:T(8,128)S(1)} %shard_map.47.grouped, ...), custom_call_target="tpu_custom_call" | custom-call | flops 1500000000 | bytes 1000000 | tf_op jit(solution)/shard_map/pallas_call | solution.py:55
  17.4 0.8 shard_map.50
  18.3 1.6 %shard_map.51 = (f32[2,520,128]{2,1,0:T(8,128)S(1)}, f32[2,520,128]{2,1,0:T(8,128)S(1)}) custom-call(s32[8]{0:T(128)S(1)} %compare_select_fusion.4.place, s32[64,128]{1,0:T(8,128)S(1)} %get-tuple-element.55.acc_rows.ready, f32[64,128]{1,0:T(8,128)S(1)} %get-tuple-element.56.flag_rows, f32[8192,128]{1,0:T(8,128)S(1)} %shard_map.47.grouped, ...), custom_call_target="tpu_custom_call" | custom-call | flops 1500000000 | bytes 1000000 | tf_op jit(solution)/shard_map/pallas_call | solution.py:55
  20.1 1.9 %collective-permute-start.4 = (f32[520,128]{1,0:T(8,128)S(1)}, f32[520,128]{1,0:T(8,128)S(1)}, u32[]{:S(2)}, u32[]{:S(2)}) collective-permute-start(f32[520,128]{1,0:T(8,128)S(1)} %get-tuple-element.69.ready), channel_id=1, source_target_pairs={{0,4},{2,6},{4,0},{6,2},{8,12},{10,14},{12,8},{14,10},{1,5},{3,7},... | collective-permute-start | bytes 798728 | tf_op jit(solution)/shard_map/ppermute | solution.py:505
  22.0 0.9 collective-permute-start.8
  23.0 2.3 %collective-permute-start.9 = (f32[520,128]{1,0:T(8,128)S(1)}, f32[520,128]{1,0:T(8,128)S(1)}, u32[]{:S(2)}, u32[]{:S(2)}) collective-permute-start(f32[520,128]{1,0:T(8,128)S(1)} %get-tuple-element.75), channel_id=1, source_target_pairs={{0,12},{2,14},{4,8},{6,10},{8,4},{10,6},{12,0},{14,2},{1,13},{3,15... | collective-permute-start | bytes 798728 | tf_op jit(solution)/shard_map/ppermute | solution.py:505
  25.3 0.8 shard_map.56
  26.1 1.1 collective-permute-start.6
  27.2 0.8 shard_map.52
  28.1 12.9 %collective-permute-done.2.refs_1_ = f32[520,128]{1,0:T(8,128)S(1)} collective-permute-done((f32[520,128]{1,0:T(8,128)S(1)}, f32[520,128]{1,0:T(8,128)S(1)}, u32[]{:S(2)}, u32[]{:S(2)}) %collective-permute-start.2) | collective-permute-done | bytes 266272 | tf_op jit(solution)/shard_map/ppermute | solution.py:505
  40.9 4.3 %collective-permute-done.4.refs_2_ = f32[520,128]{1,0:T(8,128)S(1)} collective-permute-done((f32[520,128]{1,0:T(8,128)S(1)}, f32[520,128]{1,0:T(8,128)S(1)}, u32[]{:S(2)}, u32[]{:S(2)}) %collective-permute-start.4) | collective-permute-done | bytes 266272 | tf_op jit(solution)/shard_map/ppermute | solution.py:505
  45.3 5.7 %shard_map.53 = (f32[8192,128]{1,0:T(8,128)S(1)}, f32[64,128]{1,0:T(8,128)S(1)}, f32[64,128]{1,0:T(8,128)S(1)}) custom-call(s32[64,128]{1,0:T(8,128)S(1)} %get-tuple-element.55.acc_rows.ready, f32[64,128]{1,0:T(8,128)S(1)} %get-tuple-element.56.flag_rows, f32[8192,128]{1,0:T(8,128)S(1)} %shard_map.47.grouped, f32[520,128]{1,0:T(8,128)S(1)} %get-tuple-element.64.ready.refs_0_), custom_call_target="tpu_custom_call" | custom-call | flops 8000000000 | bytes 1000000 | tf_op jit(solution)/shard_map/pallas_call | solution.py:55
  51.0 1.1 collective-permute-done.10.refs_7_
  52.1 1.5 %shard_map.57 = (f32[520,128]{1,0:T(8,128)S(1)}, f32[520,128]{1,0:T(8,128)S(1)}, f32[136,128]{1,0:T(8,128)S(1)}, f32[136,128]{1,0:T(8,128)S(1)}, f32[136,128]{1,0:T(8,128)S(1)}, /*index=5*/f32[136,128]{1,0:T(8,128)S(1)}) custom-call(s32[8]{0:T(128)S(1)} %compare_select_fusion.4.place, f32[520,128]{1,0:T(8,128)S(1)} %get-tuple-element.64.ready.refs_0_, ...), custom_call_target="tpu_custom_call" | custom-call | flops 1000000 | bytes 1000000 | tf_op jit(solution)/shard_map/pallas_call | solution.py:55
  53.7 3.7 %collective-permute-start.11 = (f32[136,128]{1,0:T(8,128)S(1)}, f32[136,128]{1,0:T(8,128)S(1)}, u32[]{:S(2)}, u32[]{:S(2)}) collective-permute-start(f32[136,128]{1,0:T(8,128)S(1)} %get-tuple-element.78), channel_id=1, source_target_pairs={{0,16},{16,32},{32,48},{48,0},{1,17},{17,33},{33,49},{49,1},{2,18}... | collective-permute-start | bytes 208904 | tf_op jit(solution)/shard_map/ppermute | solution.py:544
  57.4 5.1 %collective-permute-start.12 = (f32[136,128]{1,0:T(8,128)S(1)}, f32[136,128]{1,0:T(8,128)S(1)}, u32[]{:S(2)}, u32[]{:S(2)}) collective-permute-start(f32[136,128]{1,0:T(8,128)S(1)} %get-tuple-element.79), channel_id=1, source_target_pairs={{0,32},{16,48},{32,0},{48,16},{1,33},{17,49},{33,1},{49,17},{2,34}... | collective-permute-start | bytes 208904 | tf_op jit(solution)/shard_map/ppermute | solution.py:544
  62.5 2.4 %collective-permute-start.13 = (f32[136,128]{1,0:T(8,128)S(1)}, f32[136,128]{1,0:T(8,128)S(1)}, u32[]{:S(2)}, u32[]{:S(2)}) collective-permute-start(f32[136,128]{1,0:T(8,128)S(1)} %get-tuple-element.80), channel_id=1, source_target_pairs={{0,48},{16,0},{32,16},{48,32},{1,49},{17,1},{33,17},{49,33},{2,50}... | collective-permute-start | bytes 208904 | tf_op jit(solution)/shard_map/ppermute | solution.py:544
  65.3 2.1 %collective-permute-done.13.r3 = f32[136,128]{1,0:T(8,128)S(1)} collective-permute-done((f32[136,128]{1,0:T(8,128)S(1)}, f32[136,128]{1,0:T(8,128)S(1)}, u32[]{:S(2)}, u32[]{:S(2)}) %collective-permute-start.13) | collective-permute-done | bytes 69664 | tf_op jit(solution)/shard_map/ppermute | solution.py:544
  67.3 0.8 shard_map.58
  68.2 3.2 %collective-permute-start.14 = (f32[136,128]{1,0:T(8,128)S(1)}, f32[136,128]{1,0:T(8,128)S(1)}, u32[]{:S(2)}, u32[]{:S(2)}) collective-permute-start(f32[136,128]{1,0:T(8,128)S(1)} %shard_map.58), channel_id=1, source_target_pairs={{0,64},{64,128},{128,192},{1,65},{65,129},{129,193},{2,66},{66,130... | collective-permute-start | bytes 208904 | tf_op jit(solution)/shard_map/ppermute | solution.py:548
  71.4 4.5 %collective-permute-start.15 = (f32[136,128]{1,0:T(8,128)S(1)}, f32[136,128]{1,0:T(8,128)S(1)}, u32[]{:S(2)}, u32[]{:S(2)}) collective-permute-start(f32[136,128]{1,0:T(8,128)S(1)} %shard_map.58), channel_id=1, source_target_pairs={{0,128},{64,192},{1,129},{65,193},{2,130},{66,194},{3,131},{67,195... | collective-permute-start | bytes 208904 | tf_op jit(solution)/shard_map/ppermute | solution.py:548
  75.9 1.3 collective-permute-start.16
  77.6 0.9 collective-permute-done.16.p3
  78.6 1.0 shard_map.59
  79.6 5.8 %collective-permute-start.17 = (f32[136,128]{1,0:T(8,128)S(1)}, f32[136,128]{1,0:T(8,128)S(1)}, u32[]{:S(2)}, u32[]{:S(2)}) collective-permute-start(f32[136,128]{1,0:T(8,128)S(1)} %get-tuple-element.82), channel_id=1, source_target_pairs={{0,48},{16,0},{32,16},{48,32},{1,49},{17,1},{33,17},{49,33},{2,50}... | collective-permute-start | bytes 208904 | tf_op jit(solution)/shard_map/ppermute | solution.py:552
  85.4 2.2 %collective-permute-start.19 = (f32[136,128]{1,0:T(8,128)S(1)}, f32[136,128]{1,0:T(8,128)S(1)}, u32[]{:S(2)}, u32[]{:S(2)}) collective-permute-start(f32[136,128]{1,0:T(8,128)S(1)} %get-tuple-element.84), channel_id=1, source_target_pairs={{0,16},{16,32},{32,48},{48,0},{1,17},{17,33},{33,49},{49,1},{2,18}... | collective-permute-start | bytes 208904 | tf_op jit(solution)/shard_map/ppermute | solution.py:552
  87.5 1.0 collective-permute-done.17.e1
  88.6 4.3 %collective-permute-done.18.e2 = f32[136,128]{1,0:T(8,128)S(1)} collective-permute-done((f32[136,128]{1,0:T(8,128)S(1)}, f32[136,128]{1,0:T(8,128)S(1)}, u32[]{:S(2)}, u32[]{:S(2)}) %collective-permute-start.18) | collective-permute-done | bytes 69664 | tf_op jit(solution)/shard_map/ppermute | solution.py:552
  92.8 1.6 %shard_map.60 = (f32[520,128]{1,0:T(8,128)S(1)}, f32[520,128]{1,0:T(8,128)S(1)}, f32[520,128]{1,0:T(8,128)S(1)}, f32[520,128]{1,0:T(8,128)S(1)}, f32[520,128]{1,...) custom-call(s32[8]{0:T(128)S(1)} %compare_select_fusion.4.place, ...), custom_call_target="tpu_custom_call" | custom-call | flops 1000000 | bytes 1000000 | tf_op jit(solution)/shard_map/pallas_call | solution.py:55
  95.0 3.0 %collective-permute-start.21 = (f32[520,128]{1,0:T(8,128)S(1)}, f32[520,128]{1,0:T(8,128)S(1)}, u32[]{:S(2)}, u32[]{:S(2)}) collective-permute-start(f32[520,128]{1,0:T(8,128)S(1)} %get-tuple-element.93), channel_id=1, source_target_pairs={{0,12},{2,14},{4,8},{6,10},{8,4},{10,6},{12,0},{14,2},{1,13},{3,15... | collective-permute-start | bytes 798728 | tf_op jit(solution)/shard_map/ppermute | solution.py:505
  98.7 1.0 collective-permute-start.23
  99.7 0.8 collective-permute-start.24
  100.6 4.9 %collective-permute-done.20.refs_0_ = f32[520,128]{1,0:T(8,128)S(1)} collective-permute-done((f32[520,128]{1,0:T(8,128)S(1)}, f32[520,128]{1,0:T(8,128)S(1)}, u32[]{:S(2)}, u32[]{:S(2)}) %collective-permute-start.20) | collective-permute-done | bytes 266272 | tf_op jit(solution)/shard_map/ppermute | solution.py:505
  105.5 8.1 %collective-permute-start.25 = (f32[520,128]{1,0:T(8,128)S(1)}, f32[520,128]{1,0:T(8,128)S(1)}, u32[]{:S(2)}, u32[]{:S(2)}) collective-permute-start(f32[520,128]{1,0:T(8,128)S(1)} %get-tuple-element.98), channel_id=1, source_target_pairs={{0,2},{2,4},{4,6},{6,0},{8,10},{10,12},{12,14},{14,8},{1,3},{3,5},... | collective-permute-start | bytes 798728 | tf_op jit(solution)/shard_map/ppermute | solution.py:505
  113.6 5.0 %shard_map.61 = (f32[4096,128]{1,0:T(8,128)S(1)}, f32[32,128]{1,0:T(8,128)S(1)}, f32[32,128]{1,0:T(8,128)S(1)}, s32[32,128]{1,0:T(8,128)S(1)}) custom-call(s32[32,128]{1,0:T(8,128)S(1)} %get-tuple-element.54.slot_rows.slots, s32[32,128]{1,0:T(8,128)S(1)} %get-tuple-element.54.slot_rows.slots, s32[32,128]{1,0:T(8,128)S(1)} %bitcast.7, s32[32,128]{1,0:T(8,128)S(1)} %bitcast.4, ...), custom_call_target="tpu_custom_call" | custom-call | flops 10000000000 | bytes 1000000 | tf_op jit(solution)/shard_map/pallas_call | solution.py:55
  118.6 1.1 shard_map.62
  119.7 4.0 %collective-permute-start.27 = (f32[4,520,128]{2,1,0:T(8,128)S(1)}, f32[4,520,128]{2,1,0:T(8,128)S(1)}, u32[]{:S(2)}, u32[]{:S(2)}) collective-permute-start(f32[4,520,128]{2,1,0:T(8,128)S(1)} %get-tuple-element.101), channel_id=1, source_target_pairs={{0,1},{1,0},{2,3},{3,2},{4,5},{5,4},{6,7},{7,6},{8,9},{9,8},{10,11... | collective-permute-start | bytes 3194888 | tf_op jit(solution)/shard_map/ppermute | solution.py:583
  123.7 1.1 shard_map.63
  124.8 3.7 %collective-permute-start.28 = (f32[4,520,128]{2,1,0:T(8,128)S(1)}, f32[4,520,128]{2,1,0:T(8,128)S(1)}, u32[]{:S(2)}, u32[]{:S(2)}) collective-permute-start(f32[4,520,128]{2,1,0:T(8,128)S(1)} %get-tuple-element.102), channel_id=1, source_target_pairs={{0,1},{1,0},{2,3},{3,2},{4,5},{5,4},{6,7},{7,6},{8,9},{9,8},{10,11... | collective-permute-start | bytes 3194888 | tf_op jit(solution)/shard_map/ppermute | solution.py:583
  128.5 2.3 %collective-permute-done.28.refs_3_ = f32[4,520,128]{2,1,0:T(8,128)S(1)} collective-permute-done((f32[4,520,128]{2,1,0:T(8,128)S(1)}, f32[4,520,128]{2,1,0:T(8,128)S(1)}, u32[]{:S(2)}, u32[]{:S(2)}) %collective-permute-start.28) | collective-permute-done | bytes 1064992 | tf_op jit(solution)/shard_map/ppermute | solution.py:583
  130.8 7.3 %shard_map.64 = f32[4096,128]{1,0:T(8,128)} custom-call(s32[8]{0:T(128)S(1)} %compare_select_fusion.4.place, s32[32,128]{1,0:T(8,128)S(1)} %get-tuple-element.88.users, f32[4096,128]{1,0:T(8,128)S(1)} %get-tuple-element.89.run, f32[32,128]{1,0:T(8,128)S(1)} %get-tuple-element.90.ready.count, f32[32,128]{1,0:T(8,128)S(1)} %get-tuple-element.91.is_open, ...), custom_call_target="tpu_custom_call" | custom-call | flops 1000000 | bytes 1000000 | tf_op jit(solution)/shard_map/pallas_call | solution.py:55
  (37 shorter events, 2.9 us)
Async XLA Ops:
  0.8 2.8 %copy-start.2 = (f32[4096,128]{1,0:T(8,128)S(1)}, f32[4096,128]{1,0:T(8,128)}, u32[]{:S(2)}) copy-start(f32[4096,128]{1,0:T(8,128)} %features.1) | copy-start | bytes 6291460
  9.4 5.0 %collective-permute-start.3 = (f32[2,520,128]{2,1,0:T(8,128)S(1)}, f32[2,520,128]{2,1,0:T(8,128)S(1)}, u32[]{:S(2)}, u32[]{:S(2)}) collective-permute-start(f32[2,520,128]{2,1,0:T(8,128)S(1)} %get-tuple-element.68), channel_id=1, source_target_pairs={{0,1},{1,0},{2,3},{3,2},{4,5},{5,4},{6,7},{7,6},{8,9},{9,8},{10,11... | collective-permute-start | bytes 1597448 | tf_op jit(solution)/shard_map/ppermute | solution.py:527
  14.3 3.2 %collective-permute-start = (f32[2,520,128]{2,1,0:T(8,128)S(1)}, f32[2,520,128]{2,1,0:T(8,128)S(1)}, u32[]{:S(2)}, u32[]{:S(2)}) collective-permute-start(f32[2,520,128]{2,1,0:T(8,128)S(1)} %get-tuple-element.60), channel_id=1, source_target_pairs={{0,1},{1,0},{2,3},{3,2},{4,5},{5,4},{6,7},{7,6},{8,9},{9,8},{10,11... | collective-permute-start | bytes 1597448 | tf_op jit(solution)/shard_map/ppermute | solution.py:527
  16.9 6.1 %collective-permute-start.5 = (f32[2,520,128]{2,1,0:T(8,128)S(1)}, f32[2,520,128]{2,1,0:T(8,128)S(1)}, u32[]{:S(2)}, u32[]{:S(2)}) collective-permute-start(f32[2,520,128]{2,1,0:T(8,128)S(1)} %get-tuple-element.71), channel_id=1, source_target_pairs={{0,1},{1,0},{2,3},{3,2},{4,5},{5,4},{6,7},{7,6},{8,9},{9,8},{10,11... | collective-permute-start | bytes 1597448 | tf_op jit(solution)/shard_map/ppermute | solution.py:527
  19.9 6.2 %collective-permute-start.1 = (f32[2,520,128]{2,1,0:T(8,128)S(1)}, f32[2,520,128]{2,1,0:T(8,128)S(1)}, u32[]{:S(2)}, u32[]{:S(2)}) collective-permute-start(f32[2,520,128]{2,1,0:T(8,128)S(1)} %get-tuple-element.63), channel_id=1, source_target_pairs={{0,1},{1,0},{2,3},{3,2},{4,5},{5,4},{6,7},{7,6},{8,9},{9,8},{10,11... | collective-permute-start | bytes 1597448 | tf_op jit(solution)/shard_map/ppermute | solution.py:527
  20.0 20.9 %collective-permute-start.2 = (f32[520,128]{1,0:T(8,128)S(1)}, f32[520,128]{1,0:T(8,128)S(1)}, u32[]{:S(2)}, u32[]{:S(2)}) collective-permute-start(f32[520,128]{1,0:T(8,128)S(1)} %get-tuple-element.61.ready), channel_id=1, source_target_pairs={{0,2},{2,4},{4,6},{6,0},{8,10},{10,12},{12,14},{14,8},{1,3},{3,5},... | collective-permute-start | bytes 798728 | tf_op jit(solution)/shard_map/ppermute | solution.py:505
  20.1 25.2 %collective-permute-start.4 = (f32[520,128]{1,0:T(8,128)S(1)}, f32[520,128]{1,0:T(8,128)S(1)}, u32[]{:S(2)}, u32[]{:S(2)}) collective-permute-start(f32[520,128]{1,0:T(8,128)S(1)} %get-tuple-element.69.ready), channel_id=1, source_target_pairs={{0,4},{2,6},{4,0},{6,2},{8,12},{10,14},{12,8},{14,10},{1,5},{3,7},... | collective-permute-start | bytes 798728 | tf_op jit(solution)/shard_map/ppermute | solution.py:505
  22.0 28.9 %collective-permute-start.8 = (f32[520,128]{1,0:T(8,128)S(1)}, f32[520,128]{1,0:T(8,128)S(1)}, u32[]{:S(2)}, u32[]{:S(2)}) collective-permute-start(f32[520,128]{1,0:T(8,128)S(1)} %get-tuple-element.74), channel_id=1, source_target_pairs={{0,10},{2,12},{4,14},{6,8},{8,2},{10,4},{12,6},{14,0},{1,11},{3,13... | collective-permute-start | bytes 798728 | tf_op jit(solution)/shard_map/ppermute | solution.py:505
  23.0 28.0 %collective-permute-start.9 = (f32[520,128]{1,0:T(8,128)S(1)}, f32[520,128]{1,0:T(8,128)S(1)}, u32[]{:S(2)}, u32[]{:S(2)}) collective-permute-start(f32[520,128]{1,0:T(8,128)S(1)} %get-tuple-element.75), channel_id=1, source_target_pairs={{0,12},{2,14},{4,8},{6,10},{8,4},{10,6},{12,0},{14,2},{1,13},{3,15... | collective-permute-start | bytes 798728 | tf_op jit(solution)/shard_map/ppermute | solution.py:505
  26.1 24.9 %collective-permute-start.6 = (f32[520,128]{1,0:T(8,128)S(1)}, f32[520,128]{1,0:T(8,128)S(1)}, u32[]{:S(2)}, u32[]{:S(2)}) collective-permute-start(f32[520,128]{1,0:T(8,128)S(1)} %get-tuple-element.72), channel_id=1, source_target_pairs={{0,6},{2,0},{4,2},{6,4},{8,14},{10,8},{12,10},{14,12},{1,7},{3,1},... | collective-permute-start | bytes 798728 | tf_op jit(solution)/shard_map/ppermute | solution.py:505
  40.9 10.1 %collective-permute-start.7 = (f32[520,128]{1,0:T(8,128)S(1)}, f32[520,128]{1,0:T(8,128)S(1)}, u32[]{:S(2)}, u32[]{:S(2)}) collective-permute-start(f32[520,128]{1,0:T(8,128)S(1)} %get-tuple-element.73), channel_id=1, source_target_pairs={{0,8},{2,10},{4,12},{6,14},{8,0},{10,2},{12,4},{14,6},{1,9},{3,11}... | collective-permute-start | bytes 798728 | tf_op jit(solution)/shard_map/ppermute | solution.py:505
  45.3 6.9 %collective-permute-start.10 = (f32[520,128]{1,0:T(8,128)S(1)}, f32[520,128]{1,0:T(8,128)S(1)}, u32[]{:S(2)}, u32[]{:S(2)}) collective-permute-start(f32[520,128]{1,0:T(8,128)S(1)} %get-tuple-element.76), channel_id=1, source_target_pairs={{0,14},{2,8},{4,10},{6,12},{8,6},{10,0},{12,2},{14,4},{1,15},{3,9}... | collective-permute-start | bytes 798728 | tf_op jit(solution)/shard_map/ppermute | solution.py:505
  53.7 59.9 %copy-start = (s32[4096]{0:T(1024)S(1)}, s32[4096]{0:T(1024)}, u32[]{:S(2)}) copy-start(s32[4096]{0:T(1024)} %param.6) | copy-start | bytes 49156
  53.7 59.9 %copy-start.1 = (s32[4096,1]{0,1:T(1,128)S(1)}, s32[4096,1]{0,1:T(1,128)}, u32[]{:S(2)}) copy-start(s32[4096,1]{0,1:T(1,128)} %param.5) | copy-start | bytes 49156
  53.7 11.2 %collective-permute-start.11 = (f32[136,128]{1,0:T(8,128)S(1)}, f32[136,128]{1,0:T(8,128)S(1)}, u32[]{:S(2)}, u32[]{:S(2)}) collective-permute-start(f32[136,128]{1,0:T(8,128)S(1)} %get-tuple-element.78), channel_id=1, source_target_pairs={{0,16},{16,32},{32,48},{48,0},{1,17},{17,33},{33,49},{49,1},{2,18}... | collective-permute-start | bytes 208904 | tf_op jit(solution)/shard_map/ppermute | solution.py:544
  57.4 7.9 %collective-permute-start.12 = (f32[136,128]{1,0:T(8,128)S(1)}, f32[136,128]{1,0:T(8,128)S(1)}, u32[]{:S(2)}, u32[]{:S(2)}) collective-permute-start(f32[136,128]{1,0:T(8,128)S(1)} %get-tuple-element.79), channel_id=1, source_target_pairs={{0,32},{16,48},{32,0},{48,16},{1,33},{17,49},{33,1},{49,17},{2,34}... | collective-permute-start | bytes 208904 | tf_op jit(solution)/shard_map/ppermute | solution.py:544
  62.5 4.8 %collective-permute-start.13 = (f32[136,128]{1,0:T(8,128)S(1)}, f32[136,128]{1,0:T(8,128)S(1)}, u32[]{:S(2)}, u32[]{:S(2)}) collective-permute-start(f32[136,128]{1,0:T(8,128)S(1)} %get-tuple-element.80), channel_id=1, source_target_pairs={{0,48},{16,0},{32,16},{48,32},{1,49},{17,1},{33,17},{49,33},{2,50}... | collective-permute-start | bytes 208904 | tf_op jit(solution)/shard_map/ppermute | solution.py:544
  68.2 9.1 %collective-permute-start.14 = (f32[136,128]{1,0:T(8,128)S(1)}, f32[136,128]{1,0:T(8,128)S(1)}, u32[]{:S(2)}, u32[]{:S(2)}) collective-permute-start(f32[136,128]{1,0:T(8,128)S(1)} %shard_map.58), channel_id=1, source_target_pairs={{0,64},{64,128},{128,192},{1,65},{65,129},{129,193},{2,66},{66,130... | collective-permute-start | bytes 208904 | tf_op jit(solution)/shard_map/ppermute | solution.py:548
  71.4 6.3 %collective-permute-start.15 = (f32[136,128]{1,0:T(8,128)S(1)}, f32[136,128]{1,0:T(8,128)S(1)}, u32[]{:S(2)}, u32[]{:S(2)}) collective-permute-start(f32[136,128]{1,0:T(8,128)S(1)} %shard_map.58), channel_id=1, source_target_pairs={{0,128},{64,192},{1,129},{65,193},{2,130},{66,194},{3,131},{67,195... | collective-permute-start | bytes 208904 | tf_op jit(solution)/shard_map/ppermute | solution.py:548
  75.9 2.7 %collective-permute-start.16 = (f32[136,128]{1,0:T(8,128)S(1)}, f32[136,128]{1,0:T(8,128)S(1)}, u32[]{:S(2)}, u32[]{:S(2)}) collective-permute-start(f32[136,128]{1,0:T(8,128)S(1)} %shard_map.58), channel_id=1, source_target_pairs={{0,192},{1,193},{2,194},{3,195},{4,196},{5,197},{6,198},{7,199},{8... | collective-permute-start | bytes 208904 | tf_op jit(solution)/shard_map/ppermute | solution.py:548
  79.6 9.0 %collective-permute-start.17 = (f32[136,128]{1,0:T(8,128)S(1)}, f32[136,128]{1,0:T(8,128)S(1)}, u32[]{:S(2)}, u32[]{:S(2)}) collective-permute-start(f32[136,128]{1,0:T(8,128)S(1)} %get-tuple-element.82), channel_id=1, source_target_pairs={{0,48},{16,0},{32,16},{48,32},{1,49},{17,1},{33,17},{49,33},{2,50}... | collective-permute-start | bytes 208904 | tf_op jit(solution)/shard_map/ppermute | solution.py:552
  85.4 7.5 %collective-permute-start.18 = (f32[136,128]{1,0:T(8,128)S(1)}, f32[136,128]{1,0:T(8,128)S(1)}, u32[]{:S(2)}, u32[]{:S(2)}) collective-permute-start(f32[136,128]{1,0:T(8,128)S(1)} %get-tuple-element.83), channel_id=1, source_target_pairs={{0,32},{16,48},{32,0},{48,16},{1,33},{17,49},{33,1},{49,17},{2,34}... | collective-permute-start | bytes 208904 | tf_op jit(solution)/shard_map/ppermute | solution.py:552
  85.4 7.5 %collective-permute-start.19 = (f32[136,128]{1,0:T(8,128)S(1)}, f32[136,128]{1,0:T(8,128)S(1)}, u32[]{:S(2)}, u32[]{:S(2)}) collective-permute-start(f32[136,128]{1,0:T(8,128)S(1)} %get-tuple-element.84), channel_id=1, source_target_pairs={{0,16},{16,32},{32,48},{48,0},{1,17},{17,33},{33,49},{49,1},{2,18}... | collective-permute-start | bytes 208904 | tf_op jit(solution)/shard_map/ppermute | solution.py:552
  94.5 11.0 %collective-permute-start.20 = (f32[520,128]{1,0:T(8,128)S(1)}, f32[520,128]{1,0:T(8,128)S(1)}, u32[]{:S(2)}, u32[]{:S(2)}) collective-permute-start(f32[520,128]{1,0:T(8,128)S(1)} %get-tuple-element.92), channel_id=1, source_target_pairs={{0,4},{2,6},{4,0},{6,2},{8,12},{10,14},{12,8},{14,10},{1,5},{3,7},... | collective-permute-start | bytes 798728 | tf_op jit(solution)/shard_map/ppermute | solution.py:505
  95.0 18.5 %collective-permute-start.21 = (f32[520,128]{1,0:T(8,128)S(1)}, f32[520,128]{1,0:T(8,128)S(1)}, u32[]{:S(2)}, u32[]{:S(2)}) collective-permute-start(f32[520,128]{1,0:T(8,128)S(1)} %get-tuple-element.93), channel_id=1, source_target_pairs={{0,12},{2,14},{4,8},{6,10},{8,4},{10,6},{12,0},{14,2},{1,13},{3,15... | collective-permute-start | bytes 798728 | tf_op jit(solution)/shard_map/ppermute | solution.py:505
  98.1 20.5 %collective-permute-start.22 = (f32[520,128]{1,0:T(8,128)S(1)}, f32[520,128]{1,0:T(8,128)S(1)}, u32[]{:S(2)}, u32[]{:S(2)}) collective-permute-start(f32[520,128]{1,0:T(8,128)S(1)} %get-tuple-element.94), channel_id=1, source_target_pairs={{0,8},{2,10},{4,12},{6,14},{8,0},{10,2},{12,4},{14,6},{1,9},{3,11}... | collective-permute-start | bytes 798728 | tf_op jit(solution)/shard_map/ppermute | solution.py:505
  98.7 24.9 %collective-permute-start.23 = (f32[520,128]{1,0:T(8,128)S(1)}, f32[520,128]{1,0:T(8,128)S(1)}, u32[]{:S(2)}, u32[]{:S(2)}) collective-permute-start(f32[520,128]{1,0:T(8,128)S(1)} %get-tuple-element.96), channel_id=1, source_target_pairs={{0,6},{2,0},{4,2},{6,4},{8,14},{10,8},{12,10},{14,12},{1,7},{3,1},... | collective-permute-start | bytes 798728 | tf_op jit(solution)/shard_map/ppermute | solution.py:505
  99.7 23.9 %collective-permute-start.24 = (f32[520,128]{1,0:T(8,128)S(1)}, f32[520,128]{1,0:T(8,128)S(1)}, u32[]{:S(2)}, u32[]{:S(2)}) collective-permute-start(f32[520,128]{1,0:T(8,128)S(1)} %get-tuple-element.97), channel_id=1, source_target_pairs={{0,14},{2,8},{4,10},{6,12},{8,6},{10,0},{12,2},{14,4},{1,15},{3,9}... | collective-permute-start | bytes 798728 | tf_op jit(solution)/shard_map/ppermute | solution.py:505
  105.5 18.2 %collective-permute-start.25 = (f32[520,128]{1,0:T(8,128)S(1)}, f32[520,128]{1,0:T(8,128)S(1)}, u32[]{:S(2)}, u32[]{:S(2)}) collective-permute-start(f32[520,128]{1,0:T(8,128)S(1)} %get-tuple-element.98), channel_id=1, source_target_pairs={{0,2},{2,4},{4,6},{6,0},{8,10},{10,12},{12,14},{14,8},{1,3},{3,5},... | collective-permute-start | bytes 798728 | tf_op jit(solution)/shard_map/ppermute | solution.py:505
  113.5 10.1 %collective-permute-start.26 = (f32[520,128]{1,0:T(8,128)S(1)}, f32[520,128]{1,0:T(8,128)S(1)}, u32[]{:S(2)}, u32[]{:S(2)}) collective-permute-start(f32[520,128]{1,0:T(8,128)S(1)} %get-tuple-element.99), channel_id=1, source_target_pairs={{0,10},{2,12},{4,14},{6,8},{8,2},{10,4},{12,6},{14,0},{1,11},{3,13... | collective-permute-start | bytes 798728 | tf_op jit(solution)/shard_map/ppermute | solution.py:505
  119.7 8.8 %collective-permute-start.27 = (f32[4,520,128]{2,1,0:T(8,128)S(1)}, f32[4,520,128]{2,1,0:T(8,128)S(1)}, u32[]{:S(2)}, u32[]{:S(2)}) collective-permute-start(f32[4,520,128]{2,1,0:T(8,128)S(1)} %get-tuple-element.101), channel_id=1, source_target_pairs={{0,1},{1,0},{2,3},{3,2},{4,5},{5,4},{6,7},{7,6},{8,9},{9,8},{10,11... | collective-permute-start | bytes 3194888 | tf_op jit(solution)/shard_map/ppermute | solution.py:583
  124.8 6.0 %collective-permute-start.28 = (f32[4,520,128]{2,1,0:T(8,128)S(1)}, f32[4,520,128]{2,1,0:T(8,128)S(1)}, u32[]{:S(2)}, u32[]{:S(2)}) collective-permute-start(f32[4,520,128]{2,1,0:T(8,128)S(1)} %get-tuple-element.102), channel_id=1, source_target_pairs={{0,1},{1,0},{2,3},{3,2},{4,5},{5,4},{6,7},{7,6},{8,9},{9,8},{10,11... | collective-permute-start | bytes 3194888 | tf_op jit(solution)/shard_map/ppermute | solution.py:583

commit v5 on v4

--- a/solution.py
+++ b/solution.py
@@ -12,7 +12,8 @@
 FOUR = 4
 TAIL = FOUR * LANES
 ROWS = TAIL + 8
-ONE = LANES + 8
+QUARTER = LANES // 4
+PIECE = QUARTER + 8
 NH, NL, NX, NC = 4, 2, 4, 2
 OWNERS = NH * NL * NX * NC
 HALF = OWNERS // NC
@@ -68,8 +69,8 @@
     return jax.ShapeDtypeStruct((*lead, ROWS, LANES), F32)
 
 
-def one_block(*lead):
-    return jax.ShapeDtypeStruct((*lead, ONE, LANES), F32)
+def pieces(n):
+    return jax.ShapeDtypeStruct((n, PIECE, LANES), F32)
 
 
 def chunk_of(place, dz, dx):
@@ -77,47 +78,55 @@
     return row * NX + lax.rem(place[1] + dx, NX)
 
 
-def rank_kernel(events, slot_out, acc_out, flag_out, cleared):
+def rank_kernel(events, slot_out, cleared):
     lines = slot_out.shape[0]
     zero = jnp.zeros((LANES, LANES), F32)
     below = as_bf16(iota((LANES, LANES), 0) < iota((LANES, LANES), 1))
     with_total = jnp.concatenate([below, jnp.ones((LANES, LANES), BF16)], axis=1)
     owner_ids = iota((OWNERS, LANES), 0)
     before = jnp.zeros((OWNERS, LANES), F32)
-    codes = jnp.zeros((OWNERS, LANES), F32)
     each = cleared.shape[0] // LANES // lines
-    for b in range(lines):
-        home_row = events[b : b + 1, :]
-        account_row = events[lines + b : lines + b + 1, :]
-        flag_row = events[2 * lines + b : 2 * lines + b + 1, :]
-        chosen = owner_ids == home_row
-        counted = dot(as_bf16(chosen), with_total)
-        rank = jnp.sum(
-            jnp.where(chosen, counted[:, :LANES] + before, 0.0), axis=0, keepdims=True
-        )
-        before = before + counted[:, LANES:]
-        slot_out[b : b + 1, :] = home_row * LANES + rank.astype(I32)
-        code = (account_row * 2 + flag_row + 1).astype(F32)
-        rank_of = as_bf16(iota((LANES, LANES), 0) == rank.astype(I32))
-        codes = codes + dot_nt(jnp.where(chosen, code, 0.0).astype(BF16), rank_of)
-        for i in range(each):
-            cleared[(b * each + i) * LANES : (b * each + i + 1) * LANES, :] = zero
-    code_ids = codes.astype(I32) - 1
-    acc_out[...] = jnp.right_shift(code_ids, 1)
-    flag_out[...] = jnp.where(code_ids >= 0, jnp.bitwise_and(code_ids, 1), 0).astype(F32)
-
-
-def spread_kernel(slot_rows, features, cleared, grouped, slots, sem):
+    step = 8
+    for b in range(0, lines, step):
+        homes = [events[b + i : b + i + 1, :] for i in range(step)]
+        chosen = [owner_ids == home for home in homes]
+        counted = dot(jnp.concatenate([as_bf16(c) for c in chosen], axis=0), with_total)
+        for i in range(step):
+            some = counted[i * OWNERS : (i + 1) * OWNERS, :]
+            rank = jnp.sum(
+                jnp.where(chosen[i], some[:, :LANES] + before, 0.0), axis=0, keepdims=True
+            )
+            before = before + some[:, LANES:]
+            slot_out[b + i : b + i + 1, :] = homes[i] * LANES + rank.astype(I32)
+        for i in range(step * each):
+            at = (b * each + i) * LANES
+            cleared[at : at + LANES, :] = zero
+
+
+def spread_kernel(
+    events, slot_rows, features, cleared, grouped, acc_out, flag_out, slots, codes, sem
+):
     copy = pltpu.make_async_copy(slot_rows, slots, sem)
     copy.start()
+    lines = slot_rows.shape[0]
+    codes[...] = jnp.zeros_like(codes)
     copy.wait()
 
     def spread(b, _):
+        home_row = events[pl.ds(b, 1), :]
+        code = (events[pl.ds(lines + b, 1), :] * 2 + events[pl.ds(2 * lines + b, 1), :] + 1)
+        rank = slot_rows[pl.ds(b, 1), :] - home_row * LANES
+        chosen = iota((OWNERS, LANES), 0) == home_row
+        rank_of = as_bf16(iota((LANES, LANES), 0) == rank)
+        codes[...] += dot_nt(jnp.where(chosen, code.astype(F32), 0.0).astype(BF16), rank_of)
         for j in range(LANES):
             grouped[pl.ds(slots[b, j], 1), :] = features[pl.ds(b * LANES + j, 1), :]
         return 0
 
-    lax.fori_loop(0, slot_rows.shape[0], spread, 0)
+    lax.fori_loop(0, lines, spread, 0)
+    code_ids = codes[...].astype(I32) - 1
+    acc_out[...] = jnp.right_shift(code_ids, 1)
+    flag_out[...] = jnp.where(code_ids >= 0, jnp.bitwise_and(code_ids, 1), 0).astype(F32)
 
 
 def after_and_ones():
@@ -139,9 +148,10 @@
     return both.T
 
 
-def closing_kernel(dx, place, acc_rows, flag_rows, grouped, ready, other, mine):
+def closing_kernel(dx, halves, place, acc_rows, flag_rows, grouped, ready, *outs):
     sides = after_and_ones()
-    for out, half_of in ((other, 1 - place[0]), (mine, place[0])):
+    for out, own_half in zip(outs, halves):
+        half_of = place[0] if own_half else 1 - place[0]
         bases = [half_of * HALF + chunk_of(place, dz, dx) * FOUR for dz in range(NL)]
         acc8 = jnp.concatenate([acc_rows[pl.ds(b, FOUR), :] for b in bases], axis=0)
         flag8 = jnp.concatenate([flag_rows[pl.ds(b, FOUR), :] for b in bases], axis=0)
@@ -247,17 +257,6 @@
     )
 
 
-def joined_one(earlier, later):
-    tail, first = later[LANES:, :], earlier[LANES:, :]
-    mark = tail[1:2, :]
-    sub = iota((8, LANES), 0)
-    sums = joined_sums(keep_of(tail), 1, earlier[:LANES, :], later[:LANES, :])
-    tail = jnp.where(
-        sub == 0, tail + (1.0 - mark) * first, jnp.where(sub == 1, jnp.maximum(tail, first), 0.0)
-    )
-    return jnp.concatenate([sums, tail], axis=0)
-
-
 def core_kernel(place, mine, got, *outs):
     first = place[0] == 0
     for dz in range(NL):
@@ -275,8 +274,7 @@
 
 def row_kernel(place, *refs):
     tables = (refs[:NX], refs[NX : 2 * NX])
-    totals = refs[2 * NX + 1 : 2 * NX + 3]
-    outs, pair = refs[2 * NX + 3 : 2 * NX + 3 + NH], refs[-1]
+    totals, out = refs[2 * NX + 1 : 2 * NX + 3], refs[-1]
     for x in range(NX):
 
         @pl.when(place[1] == x)
@@ -304,56 +302,38 @@
     sub = iota((8, LANES), 0)
     for i in range(FOUR):
         a, b = sums_of(own, i), sums_of(near, i)
-        pair[i, :LANES, :] = joined_sums(
-            keep, FOUR + i, jnp.where(first, a, b), jnp.where(first, b, a)
-        )
-        pair[i, LANES:, :] = jnp.where(
+        total = joined_sums(keep, FOUR + i, jnp.where(first, a, b), jnp.where(first, b, a))
+        ends = jnp.where(
             sub == 0, tail[i : i + 1, :],
             jnp.where(sub == 1, tail[FOUR + i : FOUR + i + 1, :], 0.0),
         )
-    for r in range(NH):
-        outs[r][...] = pair[lax.rem(place[3] + r, NH)]
-
-
-def plane_kernel(place, r0, r1, r2, r3, out):
-    rows = (r0, r1, r2, r3)
-    for h in range(NH):
-
-        @pl.when(place[3] == h)
-        def _(h=h):
-            total = rows[h][...]
-            for j in range(1, NH):
-                total = joined_one(total, rows[(h - j) % NH][...])
-            out[...] = total
-
-
-def rows_back_kernel(place, p1, p2, p3, r0, r1, r2, r3, *outs):
-    rows = (r0, r1, r2, r3)
-    start = jnp.zeros((ONE, LANES), F32)
-    for r, plane in ((2, p3), (1, p2), (0, p1)):
-        start = jnp.where(place[4] > r, joined_one(start, plane[...]), start)
-    for h in range(NH):
-
-        @pl.when(place[3] == h)
-        def _(h=h):
-            state = start
-            for j in range(NH):
-                k = (h - j) % NH
-                outs[k][...] = state
-                if j < NH - 1:
-                    state = joined_one(state, rows[k][...])
-
-
-def chips_back_kernel(place, e0, e1, e2, e3, own, near, *refs):
+        for q in range(4):
+            out[4 * i + q, :QUARTER, :] = total[q * QUARTER : (q + 1) * QUARTER, :]
+            out[4 * i + q, QUARTER:, :] = ends
+
+
+def scan_kernel(place, rows, out, keeps):
+    n = rows.shape[0]
+    marks = jnp.concatenate([rows[r, QUARTER + 1 : QUARTER + 2, :] for r in range(n)], axis=0)
+    keeps[...] = (1.0 - marks).T
+    keep = keeps[pl.ds(pl.multiple_of(place[3] * QUARTER, QUARTER), QUARTER), :]
+    sub = iota((8, LANES), 0)
+    state, tail = jnp.zeros((QUARTER, LANES), F32), jnp.zeros((8, LANES), F32)
+    for r in range(n):
+        out[r, :QUARTER, :] = state
+        out[r, QUARTER:, :] = tail
+        ends = rows[r, QUARTER:, :]
+        state = rows[r, :QUARTER, :] + jnp.broadcast_to(keep[:, r : r + 1], state.shape) * state
+        tail = jnp.where(sub == 0, ends + (1.0 - ends[1:2, :]) * tail, 0.0)
+
+
+def chips_back_kernel(place, came, own, near, *refs):
     tables, outs = (refs[:NX], refs[NX : 2 * NX]), (refs[2 * NX : 3 * NX], refs[3 * NX : 4 * NX])
-    came = refs[-1]
-    for r, e in enumerate((e0, e1, e2, e3)):
-        came[lax.rem(place[3] + r, NH)] = e[...]
     first = place[2] == 0
     sub = iota((8, LANES), 0)
     tail0 = jnp.zeros((8, LANES), F32)
     for i in range(FOUR):
-        tail0 = jnp.where(sub == i, came[i, LANES : LANES + 1, :], tail0)
+        tail0 = jnp.where(sub == i, came[4 * i, QUARTER : QUARTER + 1, :], tail0)
     between = jnp.where(first, own[TAIL:, :], near[TAIL:, :])
     keep = keep_of(between)
     tail1 = joined_tail(tail0, between)
@@ -368,7 +348,9 @@
                 late = first if dz else jnp.logical_not(first)
                 for i in range(FOUR):
                     at = slice(i * LANES, (i + 1) * LANES)
-                    state = came[i, :LANES, :]
+                    state = jnp.concatenate(
+                        [came[4 * i + q, :QUARTER, :] for q in range(4)], axis=0
+                    )
                     second = joined_sums(
                         keep, FOUR + i, state, jnp.where(first, own[at, :], near[at, :])
                     )
@@ -387,11 +369,12 @@
 
 
 def cores_back_kernel(place, ready, *refs):
-    parts, mine, got = refs[:4], refs[4:6], refs[6:8]
-    keep_out, send = refs[8:]
+    n = (len(refs) - 2) // 4
+    parts, mine, got = refs[: 2 * n], refs[2 * n : 3 * n], refs[3 * n : 4 * n]
+    keep_out, send = refs[4 * n :]
     first = place[0] == 0
     counts_only = iota((8, LANES), 0) < FOUR
-    for d in range(2):
+    for d in range(n):
         for dz in range(NL):
             part, at = parts[2 * d + dz], 2 * d + dz
             core0 = jnp.where(first, mine[d][dz, TAIL:, :], got[d][dz, TAIL:, :])
@@ -411,27 +394,28 @@
             send[at, TAIL:, :] = jnp.where(counts_only, jnp.where(first, second, state), 0.0)
 
 
-BACK = ((2, 0), (1, 3))
+BACK = ((2, 0), (1,), (3,))
 
 
 def finish_kernel(place, users, run, count, is_open, home, account, *refs):
-    sides, (out, table, picked, sems) = refs[:4], refs[4:]
+    n = len(BACK)
+    sides = refs[: 2 * n]
+    out, table, scale, even, odd, even_out, odd_out, sems, out_sems = refs[2 * n :]
     copies, held = [], []
     for s, side in enumerate(sides):
-        half_of = place[0] if s < 2 else 1 - place[0]
-        for d in range(2):
+        half_of = place[0] if s < n else 1 - place[0]
+        for d, dx in enumerate(BACK[s % n]):
             for dz in range(NL):
-                at = half_of * CHUNKS + chunk_of(place, dz, BACK[s % 2][d])
+                at = half_of * CHUNKS + chunk_of(place, dz, dx)
                 held.append((side, 2 * d + dz, at))
                 copies.append(
                     pltpu.make_async_copy(
-                        side.at[2 * d + dz], table.at[at], sems.at[4 * s + 2 * d + dz]
+                        side.at[2 * d + dz], table.at[at], sems.at[len(copies)]
                     )
                 )
                 copies[-1].start()
     lines = home.shape[0]
     flat = table.reshape(NC * CHUNKS * ROWS, LANES)
-    scale = []
     for t in range(lines // 8):
         rows = slice(8 * t, 8 * t + 8)
         home8, account8 = home[rows, :], account[rows, :]
@@ -441,24 +425,45 @@
                 row = jnp.broadcast_to(side[index, TAIL + i : TAIL + i + 1, :], (8, LANES))
                 found = jnp.take_along_axis(row, account8, axis=1)
                 came = jnp.where(home8 == at * FOUR + i, found, came)
-        scale.append(1.0 / (count[rows, :] + is_open[rows, :] * came))
-    scale = jnp.concatenate(scale, axis=0)
-    if lines < LANES:
-        scale = jnp.concatenate([scale, jnp.zeros((LANES - lines, LANES), F32)], axis=0)
-    scale = scale.T
+        scale[rows, :] = 1.0 / (count[rows, :] + is_open[rows, :] * came)
     for copy in copies:
         copy.wait()
 
-    def pick(b, _):
+    def pick(b, to):
         for j in range(LANES):
-            picked[pl.ds(b * LANES + j, 1), :] = flat[pl.ds(users[b, j], 1), :]
+            to[j : j + 1, :] = flat[pl.ds(users[b, j], 1), :]
+
+    def leave(b, k):
+        at = pl.multiple_of(b * LANES, LANES)
+        return pltpu.make_async_copy(
+            (even_out, odd_out)[k], out.at[pl.ds(at, LANES), :], out_sems.at[k]
+        )
+
+    def scaled(b, picked, k):
+        at = pl.ds(pl.multiple_of(b * LANES, LANES), LANES)
+        factor = jnp.broadcast_to(scale[pl.ds(b, 1), :], (LANES, LANES)).T
+        (even_out, odd_out)[k][...] = (run[at, :] + picked[...]) * factor
+        leave(b, k).start()
+
+    pick(0, even)
+    pick(1, odd)
+    scaled(0, even, 0)
+
+    def two(g, _):
+        b = 2 * g
+        pick(b, even)
+        pl.when(g > 1)(lambda: leave(b - 3, 1).wait())
+        scaled(b - 1, odd, 1)
+        pick(b + 1, odd)
+        leave(b - 2, 0).wait()
+        scaled(b, even, 0)
         return 0
 
-    lax.fori_loop(0, lines, pick, 0)
-    for b in range(lines):
-        at = pl.ds(b * LANES, LANES)
-        factor = jnp.broadcast_to(scale[:, b : b + 1], (LANES, LANES))
-        out[at, :] = (run[at, :] + picked[at, :]) * factor
+    lax.fori_loop(1, lines // 2, two, 0)
+    leave(lines - 3, 1).wait()
+    scaled(lines - 1, odd, 1)
+    leave(lines - 2, 0).wait()
+    leave(lines - 1, 1).wait()
 
 
 def ring(n, k):
@@ -478,21 +483,17 @@
     small_f = jax.ShapeDtypeStruct((lines, LANES), F32)
     by_owner = functools.partial(jax.ShapeDtypeStruct, (OWNERS, LANES))
     by_slot = jax.ShapeDtypeStruct((OWNERS * LANES, LANES), F32)
-    slot, acc_rows, flag_rows, cleared = call(
-        rank_kernel,
-        [small, by_owner(I32), by_owner(F32), by_slot],
-        (jnp.concatenate([home, account, flags]),),
-        [VMEM],
-        cost=2_000_000_000,
-    )
-    grouped = call(
+    events = jnp.concatenate([home, account, flags])
+    slot, cleared = call(rank_kernel, [small, by_slot], (events,), [VMEM], cost=2_000_000_000)
+    grouped, acc_rows, flag_rows = call(
         spread_kernel,
-        by_slot,
-        (slot, features, cleared),
-        [VMEM] * 3,
-        scratch=[pltpu.SMEM((lines, LANES), I32), pltpu.SemaphoreType.DMA],
+        [by_slot, by_owner(I32), by_owner(F32)],
+        (events, slot, features, cleared),
+        [VMEM] * 4,
+        scratch=[pltpu.SMEM((lines, LANES), I32), pltpu.VMEM((OWNERS, LANES), F32),
+                 pltpu.SemaphoreType.DMA],
         cost=4_000_000_000,
-        aliases={2: 0},
+        aliases={3: 0},
     )
     swap = ring(NC, 1)
 
@@ -515,16 +516,24 @@
             tables[dz][dx] = exchange(chunks[dz], dz, dx)
         return chunks[0]
 
+    def close(dx, halves, ready):
+        return call(
+            functools.partial(closing_kernel, dx, halves),
+            [block(NL)] * len(halves),
+            (place, acc_rows, flag_rows, grouped, ready),
+            [SMEM] + [VMEM] * 3 + [ANY],
+            cost=800_000_000 * len(halves),
+        )
+
     met = [acc_rows]
     for at, dx in enumerate(order):
-        other, mine[dx] = call(
-            functools.partial(closing_kernel, dx),
-            [block(NL)] * 2,
-            (place, acc_rows, flag_rows, grouped, met[at]),
-            [SMEM] + [VMEM] * 3 + [ANY],
-            cost=1_500_000_000,
-        )
+        if at:
+            other, mine[dx] = close(dx, (0, 1), met[at])
+        else:
+            (other,) = close(dx, (0,), met[at])
         got[dx] = lax.ppermute(other, "c", swap)
+        if at == 0:
+            (mine[dx],) = close(dx, (1,), other)
         met.append(meet(order[at - 1]) if at else mine[dx])
     met.append(meet(order[-1]))
     run_slots, counts, opens = call(
@@ -534,28 +543,21 @@
         [VMEM] * 3 + [ANY],
         cost=8_000_000_000,
     )
-    own, near, *pairs = call(
+    own, near, total = call(
         row_kernel,
-        [block()] * NL + [one_block()] * NH,
+        [block()] * NL + [pieces(16)],
         (place, *tables[0], *tables[1], counts),
         [SMEM] + [VMEM] * (NL * NX) + [ANY],
-        scratch=[pltpu.VMEM((NH, ONE, LANES), F32)],
-    )
-    rows_got = [pairs[0]] + [lax.ppermute(pairs[r], "h", ring(NH, r)) for r in range(1, NH)]
-    plane = call(plane_kernel, one_block(), (place, *rows_got), [SMEM] + [VMEM] * NH)
-    ny = lax.axis_size("y")
-    planes = [
-        lax.ppermute(plane, "y", [(i, i + r) for i in range(ny - r)]) for r in range(1, ny)
-    ]
-    came = call(rows_back_kernel, [one_block()] * NH, (place, *planes, *rows_got),
-                [SMEM] + [VMEM] * (3 + NH))
-    came = [came[0]] + [lax.ppermute(came[r], "h", ring(NH, -r)) for r in range(1, NH)]
+    )
+    total = lax.all_to_all(total, ("y", "h"), 0, 0, tiled=True)
+    came = call(scan_kernel, pieces(16), (place, total), [SMEM, VMEM],
+                scratch=[pltpu.VMEM((LANES, 16), F32)])
+    came = lax.all_to_all(came, ("y", "h"), 0, 0, tiled=True)
     parts = call(
         chips_back_kernel,
         [block()] * (NL * NX),
-        (place, *came, own, near, *tables[0], *tables[1]),
-        [SMEM] + [VMEM] * (NH + NL + NL * NX),
-        scratch=[pltpu.VMEM((NH, ONE, LANES), F32)],
+        (place, came, own, near, *tables[0], *tables[1]),
+        [SMEM] + [VMEM] * (1 + NL + NL * NX),
     )
     parts = [list(parts[:NX]), list(parts[NX:])]
     kept = parts[0][0]
@@ -573,21 +575,24 @@
     for dxs in BACK:
         stay, send = call(
             cores_back_kernel,
-            [block(4)] * 2,
+            [block(2 * len(dxs))] * 2,
             (place, keep[-1] if keep else count, *[parts[dz][dx] for dx in dxs for dz in range(NL)],
              *[mine[dx] for dx in dxs], *[got[dx] for dx in dxs]),
-            [SMEM, ANY] + [VMEM] * 8,
+            [SMEM, ANY] + [VMEM] * (4 * len(dxs)),
             cost=500_000_000,
         )
         keep.append(stay)
         last.append(lax.ppermute(send, "c", swap))
+    line = pltpu.VMEM((LANES, LANES), F32)
     return call(
         finish_kernel,
         jax.ShapeDtypeStruct((rows, LANES), F32),
         (place, users, run, count, is_open, home, account, *keep, *last),
-        [SMEM, SMEM] + [VMEM] * 9,
-        scratch=[pltpu.VMEM((NC * CHUNKS, ROWS, LANES), F32), pltpu.VMEM((rows, LANES), F32),
-                 pltpu.SemaphoreType.DMA((16,))],
+        [SMEM, SMEM] + [VMEM] * (5 + 2 * len(BACK)),
+        out_specs=ANY,
+        scratch=[pltpu.VMEM((NC * CHUNKS, ROWS, LANES), F32), pltpu.VMEM((lines, LANES), F32),
+                 line, line, line, line, pltpu.SemaphoreType.DMA((16,)),
+                 pltpu.SemaphoreType.DMA((2,))],
     )
 
 

time: 139 us -> 150 us (1.079)
  blocking collectives: 0 us -> 38.1 us
  starting transfers between devices: 60.4 us -> 26.6 us
  Pallas kernels: 41.9 us -> 48.4 us
    all_to_all x0 -> x2, blocking collectives: none -> 38.1 us  [the longest x1 24.4 us: body(): total = lax.all_to_all(total, ('y', 'h'), 0, 0, tiled=True)]
    ppermute x9 -> x0, starting transfers between devices: 28.2 us -> none  [the longest x3 11.2 us: body(): lax.ppermute(pairs[r], 'h', ring(NH, r))]
    ppermute x14, waiting for transfers between devices: 23.3 us -> 32.5 us  [exchange(): return lax.ppermute(v, ('l', 'x'), pairs)]
    ppermute x9 -> x0, waiting for transfers between devices: 9.09 us -> none  [the longest x3 5.3 us: body(): lax.ppermute(came[r], 'h', ring(NH, -r))]
    pallas_call x19 -> x20, Pallas kernels: 41.9 us -> 48.4 us  [call(): pl.pallas_call(kernel, out_shape=out, in_specs=specs, out_specs=out_specs...]
    ppermute x14, starting transfers between devices: 20.5 us -> 15.3 us  [exchange(): return lax.ppermute(v, ('l', 'x'), pairs)]
    ppermute x2 -> x3, starting transfers between devices: 7.68 us -> 7.26 us  [body(): last.append(lax.ppermute(send, 'c', swap))]
  transfers between devices with their start and end apart: 29 -> 21, of which waited for: 11 -> 7; matrix products, arithmetic and copies ran while one was open for 0% -> 0% of each run, Pallas kernels for 15% -> 15%
where the time goes in v5:
time: 150 us; the launch traced here: 149 us
  Pallas kernels  48.4 us (32%)
  blocking collectives  38.1 us (25%)
  waiting for transfers between devices  34 us (23%)
  starting transfers between devices  26.6 us (18%)
    pallas_call x20, Pallas kernels, call(): pl.pallas_call(kernel, out_shape=out, in_specs=specs, out_specs=out_specs...  48.4 us
    ppermute x14, waiting for transfers between devices, exchange(): return lax.ppermute(v, ('l', 'x'), pairs)  32.5 us
    all_to_all x1, blocking collectives, body(): total = lax.all_to_all(total, ('y', 'h'), 0, 0, tiled=True)  24.4 us
    ppermute x14, starting transfers between devices, exchange(): return lax.ppermute(v, ('l', 'x'), pairs)  15.3 us
    all_to_all x1, blocking collectives, body(): came = lax.all_to_all(came, ('y', 'h'), 0, 0, tiled=True)  13.8 us
    ppermute x3, starting transfers between devices, body(): last.append(lax.ppermute(send, 'c', swap))  7.26 us
    ppermute x4, starting transfers between devices, body(): got[dx] = lax.ppermute(other, 'c', swap)  4.07 us
  transfers between devices with their start and end apart: 21, of which 7 were waited for; matrix products, arithmetic and copies ran while one was open for 0% of the time, Pallas kernels for 15%

profile of v5, /device:TPU:1, one launch (start us, length us, event | category | flops | bytes accessed | tf_op | source)
XLA Modules:
  0.0 149.2 jit_solution(3213979602317484264)
XLA Ops:
  0.0 0.8 pad_add_fusion.events
  0.8 0.7 shard_map.46
  1.5 0.8 copy-done.2
  2.3 5.8 %shard_map.47 = (f32[8192,128]{1,0:T(8,128)S(1)}, s32[64,128]{1,0:T(8,128)S(1)}, f32[64,128]{1,0:T(8,128)S(1)}) custom-call(s32[96,128]{1,0:T(8,128)S(1)} %pad_add_fusion.events, s32[32,128]{1,0:T(8,128)S(1)} %get-tuple-element.48.slot_rows.slots, f32[4096,128]{1,0:T(8,128)S(1)} %copy-done.2, ...), custom_call_target="tpu_custom_call", output_to_operand_aliasing={{0}: (3, {})} | custom-call | flops 4000000000 | bytes 1000000 | tf_op jit(solution)/shard_map/pallas_call | solution.py:56
  8.2 1.3 shard_map.48.ready
  9.4 3.3 %collective-permute-start.3 = (f32[2,520,128]{2,1,0:T(8,128)S(1)}, f32[2,520,128]{2,1,0:T(8,128)S(1)}, u32[]{:S(2)}, u32[]{:S(2)}) collective-permute-start(f32[2,520,128]{2,1,0:T(8,128)S(1)} %shard_map.48.ready), channel_id=1, source_target_pairs={{0,1},{1,0},{2,3},{3,2},{4,5},{5,4},{6,7},{7,6},{8,9},{9,8},{10,11... | collective-permute-start | bytes 1597448 | tf_op jit(solution)/shard_map/ppermute | solution.py:534
  12.7 1.3 shard_map.49.ready.mine.refs_4_
  14.0 1.6 %shard_map.50 = (f32[2,520,128]{2,1,0:T(8,128)S(1)}, f32[2,520,128]{2,1,0:T(8,128)S(1)}) custom-call(s32[8]{0:T(128)S(1)} %compare_select_fusion.4.place, s32[64,128]{1,0:T(8,128)S(1)} %get-tuple-element.50.acc_rows.ready, f32[64,128]{1,0:T(8,128)S(1)} %get-tuple-element.51.flag_rows, f32[8192,128]{1,0:T(8,128)S(1)} %get-tuple-element.52.grouped, ...), custom_call_target="tpu_custom_call" | custom-call | flops 1600000000 | bytes 1000000 | tf_op jit(solution)/shard_map/pallas_call | solution.py:56
  15.7 0.8 shard_map.55
  16.6 1.6 %shard_map.56 = (f32[2,520,128]{2,1,0:T(8,128)S(1)}, f32[2,520,128]{2,1,0:T(8,128)S(1)}) custom-call(s32[8]{0:T(128)S(1)} %compare_select_fusion.4.place, s32[64,128]{1,0:T(8,128)S(1)} %get-tuple-element.50.acc_rows.ready, f32[64,128]{1,0:T(8,128)S(1)} %get-tuple-element.51.flag_rows, f32[8192,128]{1,0:T(8,128)S(1)} %get-tuple-element.52.grouped, ...), custom_call_target="tpu_custom_call" | custom-call | flops 1600000000 | bytes 1000000 | tf_op jit(solution)/shard_map/pallas_call | solution.py:56
  18.2 0.6 collective-permute-start.5
  18.8 0.8 shard_map.51
  19.6 1.6 %shard_map.52 = (f32[2,520,128]{2,1,0:T(8,128)S(1)}, f32[2,520,128]{2,1,0:T(8,128)S(1)}) custom-call(s32[8]{0:T(128)S(1)} %compare_select_fusion.4.place, s32[64,128]{1,0:T(8,128)S(1)} %get-tuple-element.50.acc_rows.ready, f32[64,128]{1,0:T(8,128)S(1)} %get-tuple-element.51.flag_rows, f32[8192,128]{1,0:T(8,128)S(1)} %get-tuple-element.52.grouped, ...), custom_call_target="tpu_custom_call" | custom-call | flops 1600000000 | bytes 1000000 | tf_op jit(solution)/shard_map/pallas_call | solution.py:56
  21.3 0.1 collective-permute-start.1
  21.5 1.9 %collective-permute-start.4 = (f32[520,128]{1,0:T(8,128)S(1)}, f32[520,128]{1,0:T(8,128)S(1)}, u32[]{:S(2)}, u32[]{:S(2)}) collective-permute-start(f32[520,128]{1,0:T(8,128)S(1)} %get-tuple-element.62.ready), channel_id=1, source_target_pairs={{0,4},{2,6},{4,0},{6,2},{8,12},{10,14},{12,8},{14,10},{1,5},{3,7},... | collective-permute-start | bytes 798728 | tf_op jit(solution)/shard_map/ppermute | solution.py:506
  23.4 1.0 collective-permute-start.8
  24.3 2.3 %collective-permute-start.9 = (f32[520,128]{1,0:T(8,128)S(1)}, f32[520,128]{1,0:T(8,128)S(1)}, u32[]{:S(2)}, u32[]{:S(2)}) collective-permute-start(f32[520,128]{1,0:T(8,128)S(1)} %get-tuple-element.68), channel_id=1, source_target_pairs={{0,12},{2,14},{4,8},{6,10},{8,4},{10,6},{12,0},{14,2},{1,13},{3,15... | collective-permute-start | bytes 798728 | tf_op jit(solution)/shard_map/ppermute | solution.py:506
  26.6 0.8 shard_map.57
  27.5 0.9 collective-permute-start.6
  28.4 0.8 shard_map.53
  29.2 13.1 %collective-permute-done.2.refs_1_ = f32[520,128]{1,0:T(8,128)S(1)} collective-permute-done((f32[520,128]{1,0:T(8,128)S(1)}, f32[520,128]{1,0:T(8,128)S(1)}, u32[]{:S(2)}, u32[]{:S(2)}) %collective-permute-start.2) | collective-permute-done | bytes 266272 | tf_op jit(solution)/shard_map/ppermute | solution.py:506
  42.3 4.3 %collective-permute-done.4.refs_2_ = f32[520,128]{1,0:T(8,128)S(1)} collective-permute-done((f32[520,128]{1,0:T(8,128)S(1)}, f32[520,128]{1,0:T(8,128)S(1)}, u32[]{:S(2)}, u32[]{:S(2)}) %collective-permute-start.4) | collective-permute-done | bytes 266272 | tf_op jit(solution)/shard_map/ppermute | solution.py:506
  46.6 5.7 %shard_map.54 = (f32[8192,128]{1,0:T(8,128)S(1)}, f32[64,128]{1,0:T(8,128)S(1)}, f32[64,128]{1,0:T(8,128)S(1)}) custom-call(s32[64,128]{1,0:T(8,128)S(1)} %get-tuple-element.50.acc_rows.ready, f32[64,128]{1,0:T(8,128)S(1)} %get-tuple-element.51.flag_rows, f32[8192,128]{1,0:T(8,128)S(1)} %get-tuple-element.52.grouped, ...), custom_call_target="tpu_custom_call" | custom-call | flops 8000000000 | bytes 1000000 | tf_op jit(solution)/shard_map/pallas_call | solution.py:56
  52.4 1.1 collective-permute-done.10.refs_7_
  53.5 1.5 %shard_map.58 = (f32[520,128]{1,0:T(8,128)S(1)}, f32[520,128]{1,0:T(8,128)S(1)}, f32[16,40,128]{2,1,0:T(8,128)S(1)}) custom-call(s32[8]{0:T(128)S(1)} %compare_select_fusion.4.place, f32[520,128]{1,0:T(8,128)S(1)} %get-tuple-element.58.ready.refs_0_, f32[520,128]{1,0:T(8,128)S(1)} %collective-permute-done.2.refs_1_, ...), custom_call_target="tpu_custom_call" | custom-call | flops 1000000 | bytes 1000000 | tf_op jit(solution)/shard_map/pallas_call | solution.py:56
  55.0 24.4 %all_to_all.10.rows = f32[16,40,128]{2,1,0:T(8,128)S(1)} all-to-all(f32[16,40,128]{2,1,0:T(8,128)S(1)} %get-tuple-element.70), channel_id=1, replica_groups=mesh['y'=4,'h'=4,'l'=2,'x'=4,'c'=2] {'y','h'}, dimensions={0} | all-to-all | bytes 655360 | tf_op jit(solution)/shard_map/all_to_all | solution.py:552
  79.4 0.8 shard_map.59
  80.2 13.8 %all_to_all.11.came = f32[16,40,128]{2,1,0:T(8,128)S(1)} all-to-all(f32[16,40,128]{2,1,0:T(8,128)S(1)} %shard_map.59), channel_id=1, replica_groups=mesh['y'=4,'h'=4,'l'=2,'x'=4,'c'=2] {'y','h'}, dimensions={0} | all-to-all | bytes 655360 | tf_op jit(solution)/shard_map/all_to_all | solution.py:555
  94.0 1.4 shard_map.60
  95.4 0.6 collective-permute-start.11
  96.0 2.1 %collective-permute-start.12 = (f32[520,128]{1,0:T(8,128)S(1)}, f32[520,128]{1,0:T(8,128)S(1)}, u32[]{:S(2)}, u32[]{:S(2)}) collective-permute-start(f32[520,128]{1,0:T(8,128)S(1)} %get-tuple-element.79), channel_id=1, source_target_pairs={{0,12},{2,14},{4,8},{6,10},{8,4},{10,6},{12,0},{14,2},{1,13},{3,15... | collective-permute-start | bytes 798728 | tf_op jit(solution)/shard_map/ppermute | solution.py:506
  98.1 1.5 %collective-permute-start.13 = (f32[520,128]{1,0:T(8,128)S(1)}, f32[520,128]{1,0:T(8,128)S(1)}, u32[]{:S(2)}, u32[]{:S(2)}) collective-permute-start(f32[520,128]{1,0:T(8,128)S(1)} %get-tuple-element.80), channel_id=1, source_target_pairs={{0,8},{2,10},{4,12},{6,14},{8,0},{10,2},{12,4},{14,6},{1,9},{3,11}... | collective-permute-start | bytes 798728 | tf_op jit(solution)/shard_map/ppermute | solution.py:506
  99.6 5.0 %shard_map.61 = (f32[4096,128]{1,0:T(8,128)S(1)}, f32[32,128]{1,0:T(8,128)S(1)}, f32[32,128]{1,0:T(8,128)S(1)}, s32[32,128]{1,0:T(8,128)S(1)}) custom-call(s32[32,128]{1,0:T(8,128)S(1)} %get-tuple-element.48.slot_rows.slots, s32[32,128]{1,0:T(8,128)S(1)} %get-tuple-element.48.slot_rows.slots, s32[32,128]{1,0:T(8,128)S(1)} %bitcast.7, s32[32,128]{1,0:T(8,128)S(1)} %bitcast.4, ...), custom_call_target="tpu_custom_call" | custom-call | flops 10000000000 | bytes 1000000 | tf_op jit(solution)/shard_map/pallas_call | solution.py:56
  104.7 3.3 %collective-permute-done.11.refs_0_ = f32[520,128]{1,0:T(8,128)S(1)} collective-permute-done((f32[520,128]{1,0:T(8,128)S(1)}, f32[520,128]{1,0:T(8,128)S(1)}, u32[]{:S(2)}, u32[]{:S(2)}) %collective-permute-start.11) | collective-permute-done | bytes 266272 | tf_op jit(solution)/shard_map/ppermute | solution.py:506
  108.0 1.1 shard_map.62
  109.1 4.8 %collective-permute-start.18 = (f32[4,520,128]{2,1,0:T(8,128)S(1)}, f32[4,520,128]{2,1,0:T(8,128)S(1)}, u32[]{:S(2)}, u32[]{:S(2)}) collective-permute-start(f32[4,520,128]{2,1,0:T(8,128)S(1)} %get-tuple-element.88), channel_id=1, source_target_pairs={{0,1},{1,0},{2,3},{3,2},{4,5},{5,4},{6,7},{7,6},{8,9},{9,8},{10,11... | collective-permute-start | bytes 3194888 | tf_op jit(solution)/shard_map/ppermute | solution.py:585
  113.9 2.0 %collective-permute-start.14 = (f32[520,128]{1,0:T(8,128)S(1)}, f32[520,128]{1,0:T(8,128)S(1)}, u32[]{:S(2)}, u32[]{:S(2)}) collective-permute-start(f32[520,128]{1,0:T(8,128)S(1)} %get-tuple-element.82), channel_id=1, source_target_pairs={{0,6},{2,0},{4,2},{6,4},{8,14},{10,8},{12,10},{14,12},{1,7},{3,1},... | collective-permute-start | bytes 798728 | tf_op jit(solution)/shard_map/ppermute | solution.py:506
  116.0 0.9 collective-permute-start.15
  116.9 1.5 collective-permute-start.16
  118.4 0.4 collective-permute-start.17
  118.8 9.7 %collective-permute-done.14.refs_0_ = f32[520,128]{1,0:T(8,128)S(1)} collective-permute-done((f32[520,128]{1,0:T(8,128)S(1)}, f32[520,128]{1,0:T(8,128)S(1)}, u32[]{:S(2)}, u32[]{:S(2)}) %collective-permute-start.14) | collective-permute-done | bytes 266272 | tf_op jit(solution)/shard_map/ppermute | solution.py:506
  128.6 0.9 shard_map.63
  129.4 0.8 collective-permute-start.19
  130.2 0.9 collective-permute-done.17.refs_1_
  131.1 0.9 shard_map.64
  131.9 1.7 %collective-permute-start.20 = (f32[2,520,128]{2,1,0:T(8,128)S(1)}, f32[2,520,128]{2,1,0:T(8,128)S(1)}, u32[]{:S(2)}, u32[]{:S(2)}) collective-permute-start(f32[2,520,128]{2,1,0:T(8,128)S(1)} %get-tuple-element.90), channel_id=1, source_target_pairs={{0,1},{1,0},{2,3},{3,2},{4,5},{5,4},{6,7},{7,6},{8,9},{9,8},{10,11... | collective-permute-start | bytes 1597448 | tf_op jit(solution)/shard_map/ppermute | solution.py:585
  133.6 1.5 %collective-permute-done.20.refs_5_ = f32[2,520,128]{2,1,0:T(8,128)S(1)} collective-permute-done((f32[2,520,128]{2,1,0:T(8,128)S(1)}, f32[2,520,128]{2,1,0:T(8,128)S(1)}, u32[]{:S(2)}, u32[]{:S(2)}) %collective-permute-start.20) | collective-permute-done | bytes 532512 | tf_op jit(solution)/shard_map/ppermute | solution.py:585
  135.1 13.9 %shard_map.65 = f32[4096,128]{1,0:T(8,128)} custom-call(s32[8]{0:T(128)S(1)} %compare_select_fusion.4.place, s32[32,128]{1,0:T(8,128)S(1)} %get-tuple-element.74.users, f32[4096,128]{1,0:T(8,128)S(1)} %get-tuple-element.75.run, f32[32,128]{1,0:T(8,128)S(1)} %get-tuple-element.76.ready.count, f32[32,128]{1,0:T(8,128)S(1)} %get-tuple-element.77.is_open, ...), custom_call_target="tpu_custom_call" | custom-call | flops 1000000 | bytes 1000000 | tf_op jit(solution)/shard_map/pallas_call | solution.py:56
  (24 shorter events, 0.2 us)
Async XLA Ops:
  0.8 1.6 %copy-start.2 = (f32[4096,128]{1,0:T(8,128)S(1)}, f32[4096,128]{1,0:T(8,128)}, u32[]{:S(2)}) copy-start(f32[4096,128]{1,0:T(8,128)} %features.1) | copy-start | bytes 6291460
  9.4 6.3 %collective-permute-start.3 = (f32[2,520,128]{2,1,0:T(8,128)S(1)}, f32[2,520,128]{2,1,0:T(8,128)S(1)}, u32[]{:S(2)}, u32[]{:S(2)}) collective-permute-start(f32[2,520,128]{2,1,0:T(8,128)S(1)} %shard_map.48.ready), channel_id=1, source_target_pairs={{0,1},{1,0},{2,3},{3,2},{4,5},{5,4},{6,7},{7,6},{8,9},{9,8},{10,11... | collective-permute-start | bytes 1597448 | tf_op jit(solution)/shard_map/ppermute | solution.py:534
  15.6 3.2 %collective-permute-start = (f32[2,520,128]{2,1,0:T(8,128)S(1)}, f32[2,520,128]{2,1,0:T(8,128)S(1)}, u32[]{:S(2)}, u32[]{:S(2)}) collective-permute-start(f32[2,520,128]{2,1,0:T(8,128)S(1)} %get-tuple-element.54), channel_id=1, source_target_pairs={{0,1},{1,0},{2,3},{3,2},{4,5},{5,4},{6,7},{7,6},{8,9},{9,8},{10,11... | collective-permute-start | bytes 1597448 | tf_op jit(solution)/shard_map/ppermute | solution.py:534
  18.2 6.1 %collective-permute-start.5 = (f32[2,520,128]{2,1,0:T(8,128)S(1)}, f32[2,520,128]{2,1,0:T(8,128)S(1)}, u32[]{:S(2)}, u32[]{:S(2)}) collective-permute-start(f32[2,520,128]{2,1,0:T(8,128)S(1)} %get-tuple-element.64), channel_id=1, source_target_pairs={{0,1},{1,0},{2,3},{3,2},{4,5},{5,4},{6,7},{7,6},{8,9},{9,8},{10,11... | collective-permute-start | bytes 1597448 | tf_op jit(solution)/shard_map/ppermute | solution.py:534
  21.3 6.2 %collective-permute-start.1 = (f32[2,520,128]{2,1,0:T(8,128)S(1)}, f32[2,520,128]{2,1,0:T(8,128)S(1)}, u32[]{:S(2)}, u32[]{:S(2)}) collective-permute-start(f32[2,520,128]{2,1,0:T(8,128)S(1)} %get-tuple-element.57), channel_id=1, source_target_pairs={{0,1},{1,0},{2,3},{3,2},{4,5},{5,4},{6,7},{7,6},{8,9},{9,8},{10,11... | collective-permute-start | bytes 1597448 | tf_op jit(solution)/shard_map/ppermute | solution.py:534
  21.4 20.9 %collective-permute-start.2 = (f32[520,128]{1,0:T(8,128)S(1)}, f32[520,128]{1,0:T(8,128)S(1)}, u32[]{:S(2)}, u32[]{:S(2)}) collective-permute-start(f32[520,128]{1,0:T(8,128)S(1)} %get-tuple-element.55.ready), channel_id=1, source_target_pairs={{0,2},{2,4},{4,6},{6,0},{8,10},{10,12},{12,14},{14,8},{1,3},{3,5},... | collective-permute-start | bytes 798728 | tf_op jit(solution)/shard_map/ppermute | solution.py:506
  21.5 25.2 %collective-permute-start.4 = (f32[520,128]{1,0:T(8,128)S(1)}, f32[520,128]{1,0:T(8,128)S(1)}, u32[]{:S(2)}, u32[]{:S(2)}) collective-permute-start(f32[520,128]{1,0:T(8,128)S(1)} %get-tuple-element.62.ready), channel_id=1, source_target_pairs={{0,4},{2,6},{4,0},{6,2},{8,12},{10,14},{12,8},{14,10},{1,5},{3,7},... | collective-permute-start | bytes 798728 | tf_op jit(solution)/shard_map/ppermute | solution.py:506
  23.4 28.9 %collective-permute-start.8 = (f32[520,128]{1,0:T(8,128)S(1)}, f32[520,128]{1,0:T(8,128)S(1)}, u32[]{:S(2)}, u32[]{:S(2)}) collective-permute-start(f32[520,128]{1,0:T(8,128)S(1)} %get-tuple-element.67), channel_id=1, source_target_pairs={{0,10},{2,12},{4,14},{6,8},{8,2},{10,4},{12,6},{14,0},{1,11},{3,13... | collective-permute-start | bytes 798728 | tf_op jit(solution)/shard_map/ppermute | solution.py:506
  24.3 28.0 %collective-permute-start.9 = (f32[520,128]{1,0:T(8,128)S(1)}, f32[520,128]{1,0:T(8,128)S(1)}, u32[]{:S(2)}, u32[]{:S(2)}) collective-permute-start(f32[520,128]{1,0:T(8,128)S(1)} %get-tuple-element.68), channel_id=1, source_target_pairs={{0,12},{2,14},{4,8},{6,10},{8,4},{10,6},{12,0},{14,2},{1,13},{3,15... | collective-permute-start | bytes 798728 | tf_op jit(solution)/shard_map/ppermute | solution.py:506
  27.5 24.9 %collective-permute-start.6 = (f32[520,128]{1,0:T(8,128)S(1)}, f32[520,128]{1,0:T(8,128)S(1)}, u32[]{:S(2)}, u32[]{:S(2)}) collective-permute-start(f32[520,128]{1,0:T(8,128)S(1)} %get-tuple-element.65), channel_id=1, source_target_pairs={{0,6},{2,0},{4,2},{6,4},{8,14},{10,8},{12,10},{14,12},{1,7},{3,1},... | collective-permute-start | bytes 798728 | tf_op jit(solution)/shard_map/ppermute | solution.py:506
  42.3 10.1 %collective-permute-start.7 = (f32[520,128]{1,0:T(8,128)S(1)}, f32[520,128]{1,0:T(8,128)S(1)}, u32[]{:S(2)}, u32[]{:S(2)}) collective-permute-start(f32[520,128]{1,0:T(8,128)S(1)} %get-tuple-element.66), channel_id=1, source_target_pairs={{0,8},{2,10},{4,12},{6,14},{8,0},{10,2},{12,4},{14,6},{1,9},{3,11}... | collective-permute-start | bytes 798728 | tf_op jit(solution)/shard_map/ppermute | solution.py:506
  46.6 6.9 %collective-permute-start.10 = (f32[520,128]{1,0:T(8,128)S(1)}, f32[520,128]{1,0:T(8,128)S(1)}, u32[]{:S(2)}, u32[]{:S(2)}) collective-permute-start(f32[520,128]{1,0:T(8,128)S(1)} %get-tuple-element.69), channel_id=1, source_target_pairs={{0,14},{2,8},{4,10},{6,12},{8,6},{10,0},{12,2},{14,4},{1,15},{3,9}... | collective-permute-start | bytes 798728 | tf_op jit(solution)/shard_map/ppermute | solution.py:506
  79.4 20.3 %copy-start = (s32[4096]{0:T(1024)S(1)}, s32[4096]{0:T(1024)}, u32[]{:S(2)}) copy-start(s32[4096]{0:T(1024)} %param.6) | copy-start | bytes 49156
  79.4 20.3 %copy-start.1 = (s32[4096,1]{0,1:T(1,128)S(1)}, s32[4096,1]{0,1:T(1,128)}, u32[]{:S(2)}) copy-start(s32[4096,1]{0,1:T(1,128)} %param.5) | copy-start | bytes 49156
  95.4 12.6 %collective-permute-start.11 = (f32[520,128]{1,0:T(8,128)S(1)}, f32[520,128]{1,0:T(8,128)S(1)}, u32[]{:S(2)}, u32[]{:S(2)}) collective-permute-start(f32[520,128]{1,0:T(8,128)S(1)} %get-tuple-element.78), channel_id=1, source_target_pairs={{0,4},{2,6},{4,0},{6,2},{8,12},{10,14},{12,8},{14,10},{1,5},{3,7},... | collective-permute-start | bytes 798728 | tf_op jit(solution)/shard_map/ppermute | solution.py:506
  96.0 12.0 %collective-permute-start.12 = (f32[520,128]{1,0:T(8,128)S(1)}, f32[520,128]{1,0:T(8,128)S(1)}, u32[]{:S(2)}, u32[]{:S(2)}) collective-permute-start(f32[520,128]{1,0:T(8,128)S(1)} %get-tuple-element.79), channel_id=1, source_target_pairs={{0,12},{2,14},{4,8},{6,10},{8,4},{10,6},{12,0},{14,2},{1,13},{3,15... | collective-permute-start | bytes 798728 | tf_op jit(solution)/shard_map/ppermute | solution.py:506
  98.1 9.9 %collective-permute-start.13 = (f32[520,128]{1,0:T(8,128)S(1)}, f32[520,128]{1,0:T(8,128)S(1)}, u32[]{:S(2)}, u32[]{:S(2)}) collective-permute-start(f32[520,128]{1,0:T(8,128)S(1)} %get-tuple-element.80), channel_id=1, source_target_pairs={{0,8},{2,10},{4,12},{6,14},{8,0},{10,2},{12,4},{14,6},{1,9},{3,11}... | collective-permute-start | bytes 798728 | tf_op jit(solution)/shard_map/ppermute | solution.py:506
  109.1 26.0 %collective-permute-start.18 = (f32[4,520,128]{2,1,0:T(8,128)S(1)}, f32[4,520,128]{2,1,0:T(8,128)S(1)}, u32[]{:S(2)}, u32[]{:S(2)}) collective-permute-start(f32[4,520,128]{2,1,0:T(8,128)S(1)} %get-tuple-element.88), channel_id=1, source_target_pairs={{0,1},{1,0},{2,3},{3,2},{4,5},{5,4},{6,7},{7,6},{8,9},{9,8},{10,11... | collective-permute-start | bytes 3194888 | tf_op jit(solution)/shard_map/ppermute | solution.py:585
  113.9 14.6 %collective-permute-start.14 = (f32[520,128]{1,0:T(8,128)S(1)}, f32[520,128]{1,0:T(8,128)S(1)}, u32[]{:S(2)}, u32[]{:S(2)}) collective-permute-start(f32[520,128]{1,0:T(8,128)S(1)} %get-tuple-element.82), channel_id=1, source_target_pairs={{0,6},{2,0},{4,2},{6,4},{8,14},{10,8},{12,10},{14,12},{1,7},{3,1},... | collective-permute-start | bytes 798728 | tf_op jit(solution)/shard_map/ppermute | solution.py:506
  116.0 12.6 %collective-permute-start.15 = (f32[520,128]{1,0:T(8,128)S(1)}, f32[520,128]{1,0:T(8,128)S(1)}, u32[]{:S(2)}, u32[]{:S(2)}) collective-permute-start(f32[520,128]{1,0:T(8,128)S(1)} %get-tuple-element.83), channel_id=1, source_target_pairs={{0,14},{2,8},{4,10},{6,12},{8,6},{10,0},{12,2},{14,4},{1,15},{3,9}... | collective-permute-start | bytes 798728 | tf_op jit(solution)/shard_map/ppermute | solution.py:506
  116.9 13.3 %collective-permute-start.16 = (f32[520,128]{1,0:T(8,128)S(1)}, f32[520,128]{1,0:T(8,128)S(1)}, u32[]{:S(2)}, u32[]{:S(2)}) collective-permute-start(f32[520,128]{1,0:T(8,128)S(1)} %get-tuple-element.85), channel_id=1, source_target_pairs={{0,2},{2,4},{4,6},{6,0},{8,10},{10,12},{12,14},{14,8},{1,3},{3,5},... | collective-permute-start | bytes 798728 | tf_op jit(solution)/shard_map/ppermute | solution.py:506
  118.4 12.7 %collective-permute-start.17 = (f32[520,128]{1,0:T(8,128)S(1)}, f32[520,128]{1,0:T(8,128)S(1)}, u32[]{:S(2)}, u32[]{:S(2)}) collective-permute-start(f32[520,128]{1,0:T(8,128)S(1)} %get-tuple-element.86), channel_id=1, source_target_pairs={{0,10},{2,12},{4,14},{6,8},{8,2},{10,4},{12,6},{14,0},{1,11},{3,13... | collective-permute-start | bytes 798728 | tf_op jit(solution)/shard_map/ppermute | solution.py:506
  129.4 4.2 %collective-permute-start.19 = (f32[2,520,128]{2,1,0:T(8,128)S(1)}, f32[2,520,128]{2,1,0:T(8,128)S(1)}, u32[]{:S(2)}, u32[]{:S(2)}) collective-permute-start(f32[2,520,128]{2,1,0:T(8,128)S(1)} %get-tuple-element.89), channel_id=1, source_target_pairs={{0,1},{1,0},{2,3},{3,2},{4,5},{5,4},{6,7},{7,6},{8,9},{9,8},{10,11... | collective-permute-start | bytes 1597448 | tf_op jit(solution)/shard_map/ppermute | solution.py:585
  131.9 3.2 %collective-permute-start.20 = (f32[2,520,128]{2,1,0:T(8,128)S(1)}, f32[2,520,128]{2,1,0:T(8,128)S(1)}, u32[]{:S(2)}, u32[]{:S(2)}) collective-permute-start(f32[2,520,128]{2,1,0:T(8,128)S(1)} %get-tuple-element.90), channel_id=1, source_target_pairs={{0,1},{1,0},{2,3},{3,2},{4,5},{5,4},{6,7},{7,6},{8,9},{9,8},{10,11... | collective-permute-start | bytes 1597448 | tf_op jit(solution)/shard_map/ppermute | solution.py:585

commit v6 on v4

--- a/solution.py
+++ b/solution.py
@@ -86,22 +86,30 @@
     before = jnp.zeros((OWNERS, LANES), F32)
     codes = jnp.zeros((OWNERS, LANES), F32)
     each = cleared.shape[0] // LANES // lines
-    for b in range(lines):
-        home_row = events[b : b + 1, :]
-        account_row = events[lines + b : lines + b + 1, :]
-        flag_row = events[2 * lines + b : 2 * lines + b + 1, :]
-        chosen = owner_ids == home_row
-        counted = dot(as_bf16(chosen), with_total)
-        rank = jnp.sum(
-            jnp.where(chosen, counted[:, :LANES] + before, 0.0), axis=0, keepdims=True
+    step = 8
+    for b in range(0, lines, step):
+        homes = [events[b + i : b + i + 1, :] for i in range(step)]
+        chosen = [owner_ids == home for home in homes]
+        counted = dot(jnp.concatenate([as_bf16(c) for c in chosen], axis=0), with_total)
+        coded, rank_of = [], []
+        for i in range(step):
+            some = counted[i * OWNERS : (i + 1) * OWNERS, :]
+            rank = jnp.sum(
+                jnp.where(chosen[i], some[:, :LANES] + before, 0.0), axis=0, keepdims=True
+            ).astype(I32)
+            before = before + some[:, LANES:]
+            slot_out[b + i : b + i + 1, :] = homes[i] * LANES + rank
+            account = events[lines + b + i : lines + b + i + 1, :]
+            flag = events[2 * lines + b + i : 2 * lines + b + i + 1, :]
+            code = (account * 2 + flag + 1).astype(F32)
+            coded.append(jnp.where(chosen[i], code, 0.0).astype(BF16))
+            rank_of.append(as_bf16(iota((LANES, LANES), 0) == rank))
+        codes = codes + dot_nt(
+            jnp.concatenate(coded, axis=1), jnp.concatenate(rank_of, axis=1)
         )
-        before = before + counted[:, LANES:]
-        slot_out[b : b + 1, :] = home_row * LANES + rank.astype(I32)
-        code = (account_row * 2 + flag_row + 1).astype(F32)
-        rank_of = as_bf16(iota((LANES, LANES), 0) == rank.astype(I32))
-        codes = codes + dot_nt(jnp.where(chosen, code, 0.0).astype(BF16), rank_of)
-        for i in range(each):
-            cleared[(b * each + i) * LANES : (b * each + i + 1) * LANES, :] = zero
+        for i in range(step * each):
+            at = (b * each + i) * LANES
+            cleared[at : at + LANES, :] = zero
     code_ids = codes.astype(I32) - 1
     acc_out[...] = jnp.right_shift(code_ids, 1)
     flag_out[...] = jnp.where(code_ids >= 0, jnp.bitwise_and(code_ids, 1), 0).astype(F32)
@@ -387,11 +395,12 @@
 
 
 def cores_back_kernel(place, ready, *refs):
-    parts, mine, got = refs[:4], refs[4:6], refs[6:8]
-    keep_out, send = refs[8:]
+    n = (len(refs) - 2) // 4
+    parts, mine, got = refs[: 2 * n], refs[2 * n : 3 * n], refs[3 * n : 4 * n]
+    keep_out, send = refs[4 * n :]
     first = place[0] == 0
     counts_only = iota((8, LANES), 0) < FOUR
-    for d in range(2):
+    for d in range(n):
         for dz in range(NL):
             part, at = parts[2 * d + dz], 2 * d + dz
             core0 = jnp.where(first, mine[d][dz, TAIL:, :], got[d][dz, TAIL:, :])
@@ -411,36 +420,69 @@
             send[at, TAIL:, :] = jnp.where(counts_only, jnp.where(first, second, state), 0.0)
 
 
-BACK = ((2, 0), (1, 3))
-
-
-def finish_kernel(place, users, run, count, is_open, home, account, *refs):
-    sides, (out, table, picked, sems) = refs[:4], refs[4:]
-    copies, held = [], []
+BACK = ((2, 0), (1,), (3,))
+
+
+def lookup(home8, account8, held, came):
+    for tail, at in held:
+        for i in range(FOUR):
+            row = jnp.broadcast_to(tail[i : i + 1, :], (8, LANES))
+            found = jnp.take_along_axis(row, account8, axis=1)
+            came = jnp.where(home8 == at * FOUR + i, found, came)
+    return came
+
+
+def held_parts(place, dxs, side, own_half):
+    half_of = place[0] if own_half else 1 - place[0]
+    return [
+        (side, 2 * d + dz, half_of * CHUNKS + chunk_of(place, dz, dx))
+        for d, dx in enumerate(dxs)
+        for dz in range(NL)
+    ]
+
+
+def gather_kernel(place, home, account, *refs):
+    n = len(BACK)
+    sides, (table, counts, sems) = refs[: n + 1], refs[n + 1 :]
+    held = []
     for s, side in enumerate(sides):
-        half_of = place[0] if s < 2 else 1 - place[0]
-        for d in range(2):
-            for dz in range(NL):
-                at = half_of * CHUNKS + chunk_of(place, dz, BACK[s % 2][d])
-                held.append((side, 2 * d + dz, at))
-                copies.append(
-                    pltpu.make_async_copy(
-                        side.at[2 * d + dz], table.at[at], sems.at[4 * s + 2 * d + dz]
-                    )
-                )
-                copies[-1].start()
+        held += held_parts(place, BACK[s % n], side, s < n)
+    copies = [
+        pltpu.make_async_copy(side.at[k], table.at[at], sems.at[i])
+        for i, (side, k, at) in enumerate(held)
+    ]
+    for copy in copies:
+        copy.start()
+    tails = [(side[k, TAIL:, :], at) for side, k, at in held]
+    for t in range(home.shape[0] // 8):
+        rows = slice(8 * t, 8 * t + 8)
+        counts[rows, :] = lookup(
+            home[rows, :], account[rows, :], tails, jnp.zeros((8, LANES), F32)
+        )
+    for copy in copies:
+        copy.wait()
+
+
+def finish_kernel(
+    place, users, run, count, is_open, home, account, counts, table_in, got1, got2,
+    table, out, picked, sems, out_sems,
+):
+    held = []
+    for s, side in ((1, got1), (2, got2)):
+        held += held_parts(place, BACK[s], side, False)
+    copies = [
+        pltpu.make_async_copy(side.at[k], table.at[at], sems.at[i])
+        for i, (side, k, at) in enumerate(held)
+    ]
+    for copy in copies:
+        copy.start()
     lines = home.shape[0]
     flat = table.reshape(NC * CHUNKS * ROWS, LANES)
+    tails = [(side[k, TAIL:, :], at) for side, k, at in held]
     scale = []
     for t in range(lines // 8):
         rows = slice(8 * t, 8 * t + 8)
-        home8, account8 = home[rows, :], account[rows, :]
-        came = jnp.zeros((8, LANES), F32)
-        for side, index, at in held:
-            for i in range(FOUR):
-                row = jnp.broadcast_to(side[index, TAIL + i : TAIL + i + 1, :], (8, LANES))
-                found = jnp.take_along_axis(row, account8, axis=1)
-                came = jnp.where(home8 == at * FOUR + i, found, came)
+        came = lookup(home[rows, :], account[rows, :], tails, counts[rows, :])
         scale.append(1.0 / (count[rows, :] + is_open[rows, :] * came))
     scale = jnp.concatenate(scale, axis=0)
     if lines < LANES:
@@ -455,10 +497,22 @@
         return 0
 
     lax.fori_loop(0, lines, pick, 0)
+    group = lines // 8
+    leaving = []
     for b in range(lines):
         at = pl.ds(b * LANES, LANES)
         factor = jnp.broadcast_to(scale[:, b : b + 1], (LANES, LANES))
-        out[at, :] = (run[at, :] + picked[at, :]) * factor
+        picked[at, :] = (run[at, :] + picked[at, :]) * factor
+        if b % group == group - 1:
+            rows = pl.ds((b - group + 1) * LANES, group * LANES)
+            leaving.append(
+                pltpu.make_async_copy(
+                    picked.at[rows, :], out.at[rows, :], out_sems.at[len(leaving)]
+                )
+            )
+            leaving[-1].start()
+    for copy in leaving:
+        copy.wait()
 
 
 def ring(n, k):
@@ -541,7 +595,9 @@
         [SMEM] + [VMEM] * (NL * NX) + [ANY],
         scratch=[pltpu.VMEM((NH, ONE, LANES), F32)],
     )
-    rows_got = [pairs[0]] + [lax.ppermute(pairs[r], "h", ring(NH, r)) for r in range(1, NH)]
+    rows_got = list(pairs)
+    for r in (1, 3, 2):
+        rows_got[r] = lax.ppermute(pairs[r], "h", ring(NH, r))
     plane = call(plane_kernel, one_block(), (place, *rows_got), [SMEM] + [VMEM] * NH)
     ny = lax.axis_size("y")
     planes = [
@@ -549,7 +605,9 @@
     ]
     came = call(rows_back_kernel, [one_block()] * NH, (place, *planes, *rows_got),
                 [SMEM] + [VMEM] * (3 + NH))
-    came = [came[0]] + [lax.ppermute(came[r], "h", ring(NH, -r)) for r in range(1, NH)]
+    came = list(came)
+    for r in (1, 3, 2):
+        came[r] = lax.ppermute(came[r], "h", ring(NH, -r))
     parts = call(
         chips_back_kernel,
         [block()] * (NL * NX),
@@ -573,22 +631,33 @@
     for dxs in BACK:
         stay, send = call(
             cores_back_kernel,
-            [block(4)] * 2,
+            [block(2 * len(dxs))] * 2,
             (place, keep[-1] if keep else count, *[parts[dz][dx] for dx in dxs for dz in range(NL)],
              *[mine[dx] for dx in dxs], *[got[dx] for dx in dxs]),
-            [SMEM, ANY] + [VMEM] * 8,
+            [SMEM, ANY] + [VMEM] * (4 * len(dxs)),
             cost=500_000_000,
         )
         keep.append(stay)
         last.append(lax.ppermute(send, "c", swap))
-    return call(
+    table, came_counts = call(
+        gather_kernel,
+        [block(NC * CHUNKS), small_f],
+        (place, home, account, *keep, last[0]),
+        [SMEM] + [VMEM] * 6,
+        scratch=[pltpu.SemaphoreType.DMA((12,))],
+        cost=2_000_000_000,
+    )
+    _, result = call(
         finish_kernel,
-        jax.ShapeDtypeStruct((rows, LANES), F32),
-        (place, users, run, count, is_open, home, account, *keep, *last),
+        [block(NC * CHUNKS), jax.ShapeDtypeStruct((rows, LANES), F32)],
+        (place, users, run, count, is_open, home, account, came_counts, table, *last[1:]),
         [SMEM, SMEM] + [VMEM] * 9,
-        scratch=[pltpu.VMEM((NC * CHUNKS, ROWS, LANES), F32), pltpu.VMEM((rows, LANES), F32),
-                 pltpu.SemaphoreType.DMA((16,))],
-    )
+        out_specs=[VMEM, ANY],
+        scratch=[pltpu.VMEM((rows, LANES), F32), pltpu.SemaphoreType.DMA((4,)),
+                 pltpu.SemaphoreType.DMA((8,))],
+        aliases={8: 0},
+    )
+    return result
 
 
 def solution(mesh):

time: 139 us -> 138 us (level)
  waiting for transfers between devices: 34.7 us -> 41.1 us
  starting transfers between devices: 60.4 us -> 54.7 us
    ppermute x14, waiting for transfers between devices: 23.3 us -> 31.7 us  [exchange(): return lax.ppermute(v, ('l', 'x'), pairs)]
    ppermute x14, starting transfers between devices: 20.5 us -> 14.5 us  [exchange(): return lax.ppermute(v, ('l', 'x'), pairs)]
    ppermute x2 -> x3, waiting for transfers between devices: 2.31 us -> 0.26 us  [body(): last.append(lax.ppermute(send, 'c', swap))]
    pallas_call x19 -> x21, Pallas kernels: 41.9 us -> 40.9 us  [call(): pl.pallas_call(kernel, out_shape=out, in_specs=specs, out_specs=out_specs...]
    ppermute x2 -> x3, starting transfers between devices: 7.68 us -> 7.95 us  [body(): last.append(lax.ppermute(send, 'c', swap))]
  transfers between devices with their start and end apart: 29 -> 30, of which waited for: 11 -> 14; matrix products, arithmetic and copies ran while one was open for 0% -> 0% of each run, Pallas kernels for 15% -> 16%
where the time goes in v6:
time: 138 us
  starting transfers between devices  54.7 us (40%)
  waiting for transfers between devices  41.1 us (30%)
  Pallas kernels  40.9 us (30%)
    pallas_call x21, Pallas kernels, call(): pl.pallas_call(kernel, out_shape=out, in_specs=specs, out_specs=out_specs...  40.9 us
    ppermute x14, waiting for transfers between devices, exchange(): return lax.ppermute(v, ('l', 'x'), pairs)  31.7 us
    ppermute x14, starting transfers between devices, exchange(): return lax.ppermute(v, ('l', 'x'), pairs)  14.5 us
    ppermute x3, starting transfers between devices, body(): rows_got[r] = lax.ppermute(pairs[r], 'h', ring(NH, r))  11.2 us
    ppermute x3, starting transfers between devices, body(): lax.ppermute(plane, 'y', [(i, i + r) for i in range(ny - r)])  9.02 us
    ppermute x3, starting transfers between devices, body(): came[r] = lax.ppermute(came[r], 'h', ring(NH, -r))  7.96 us
    ppermute x3, starting transfers between devices, body(): last.append(lax.ppermute(send, 'c', swap))  7.95 us
    ppermute x3, waiting for transfers between devices, body(): came[r] = lax.ppermute(came[r], 'h', ring(NH, -r))  5.3 us
  transfers between devices with their start and end apart: 30, of which 14 were waited for; matrix products, arithmetic and copies ran while one was open for 0% of the time, Pallas kernels for 16%

profile of v6, /device:TPU:1, one launch (start us, length us, event | category | flops | bytes accessed | tf_op | source)
XLA Modules:
  0.0 138.2 jit_solution(10645466194894415325)
XLA Ops:
  0.8 1.3 shard_map.46
  2.3 4.2 %shard_map.47.grouped = f32[8192,128]{1,0:T(8,128)S(1)} custom-call(s32[32,128]{1,0:T(8,128)S(1)} %get-tuple-element.59.slot_rows.slots, f32[4096,128]{1,0:T(8,128)S(1)} %copy-done.2, f32[8192,128]{1,0:T(8,128)S(1)} %get-tuple-element.62.cleared), custom_call_target="tpu_custom_call", output_to_operand_aliasing={{}: (2, {})} | custom-call | flops 4000000000 | bytes 1000000 | tf_op jit(solution)/shard_map/pallas_call | solution.py:55
  6.6 1.6 %shard_map.48 = (f32[2,520,128]{2,1,0:T(8,128)S(1)}, f32[2,520,128]{2,1,0:T(8,128)S(1)}) custom-call(s32[8]{0:T(128)S(1)} %compare_select_fusion.4.place, s32[64,128]{1,0:T(8,128)S(1)} %get-tuple-element.60.acc_rows.ready, f32[64,128]{1,0:T(8,128)S(1)} %get-tuple-element.61.flag_rows, f32[8192,128]{1,0:T(8,128)S(1)} %shard_map.47.grouped, ...), custom_call_target="tpu_custom_call" | custom-call | flops 1500000000 | bytes 1000000 | tf_op jit(solution)/shard_map/pallas_call | solution.py:55
  8.2 3.3 %collective-permute-start.3 = (f32[2,520,128]{2,1,0:T(8,128)S(1)}, f32[2,520,128]{2,1,0:T(8,128)S(1)}, u32[]{:S(2)}, u32[]{:S(2)}) collective-permute-start(f32[2,520,128]{2,1,0:T(8,128)S(1)} %get-tuple-element.73), channel_id=1, source_target_pairs={{0,1},{1,0},{2,3},{3,2},{4,5},{5,4},{6,7},{7,6},{8,9},{9,8},{10,11... | collective-permute-start | bytes 1597448 | tf_op jit(solution)/shard_map/ppermute | solution.py:581
  11.5 1.6 %shard_map.49 = (f32[2,520,128]{2,1,0:T(8,128)S(1)}, f32[2,520,128]{2,1,0:T(8,128)S(1)}) custom-call(s32[8]{0:T(128)S(1)} %compare_select_fusion.4.place, s32[64,128]{1,0:T(8,128)S(1)} %get-tuple-element.60.acc_rows.ready, f32[64,128]{1,0:T(8,128)S(1)} %get-tuple-element.61.flag_rows, f32[8192,128]{1,0:T(8,128)S(1)} %shard_map.47.grouped, ...), custom_call_target="tpu_custom_call" | custom-call | flops 1500000000 | bytes 1000000 | tf_op jit(solution)/shard_map/pallas_call | solution.py:55
  13.2 0.8 shard_map.54
  14.0 1.6 %shard_map.55 = (f32[2,520,128]{2,1,0:T(8,128)S(1)}, f32[2,520,128]{2,1,0:T(8,128)S(1)}) custom-call(s32[8]{0:T(128)S(1)} %compare_select_fusion.4.place, s32[64,128]{1,0:T(8,128)S(1)} %get-tuple-element.60.acc_rows.ready, f32[64,128]{1,0:T(8,128)S(1)} %get-tuple-element.61.flag_rows, f32[8192,128]{1,0:T(8,128)S(1)} %shard_map.47.grouped, ...), custom_call_target="tpu_custom_call" | custom-call | flops 1500000000 | bytes 1000000 | tf_op jit(solution)/shard_map/pallas_call | solution.py:55
  16.3 0.8 shard_map.50
  17.1 1.6 %shard_map.51 = (f32[2,520,128]{2,1,0:T(8,128)S(1)}, f32[2,520,128]{2,1,0:T(8,128)S(1)}) custom-call(s32[8]{0:T(128)S(1)} %compare_select_fusion.4.place, s32[64,128]{1,0:T(8,128)S(1)} %get-tuple-element.60.acc_rows.ready, f32[64,128]{1,0:T(8,128)S(1)} %get-tuple-element.61.flag_rows, f32[8192,128]{1,0:T(8,128)S(1)} %shard_map.47.grouped, ...), custom_call_target="tpu_custom_call" | custom-call | flops 1500000000 | bytes 1000000 | tf_op jit(solution)/shard_map/pallas_call | solution.py:55
  18.9 1.9 %collective-permute-start.4 = (f32[520,128]{1,0:T(8,128)S(1)}, f32[520,128]{1,0:T(8,128)S(1)}, u32[]{:S(2)}, u32[]{:S(2)}) collective-permute-start(f32[520,128]{1,0:T(8,128)S(1)} %get-tuple-element.74.ready), channel_id=1, source_target_pairs={{0,4},{2,6},{4,0},{6,2},{8,12},{10,14},{12,8},{14,10},{1,5},{3,7},... | collective-permute-start | bytes 798728 | tf_op jit(solution)/shard_map/ppermute | solution.py:559
  20.9 0.9 collective-permute-start.8
  21.8 2.3 %collective-permute-start.9 = (f32[520,128]{1,0:T(8,128)S(1)}, f32[520,128]{1,0:T(8,128)S(1)}, u32[]{:S(2)}, u32[]{:S(2)}) collective-permute-start(f32[520,128]{1,0:T(8,128)S(1)} %get-tuple-element.80), channel_id=1, source_target_pairs={{0,12},{2,14},{4,8},{6,10},{8,4},{10,6},{12,0},{14,2},{1,13},{3,15... | collective-permute-start | bytes 798728 | tf_op jit(solution)/shard_map/ppermute | solution.py:559
  24.9 0.9 collective-permute-start.6
  25.9 0.8 shard_map.52
  26.7 13.1 %collective-permute-done.2.refs_1_ = f32[520,128]{1,0:T(8,128)S(1)} collective-permute-done((f32[520,128]{1,0:T(8,128)S(1)}, f32[520,128]{1,0:T(8,128)S(1)}, u32[]{:S(2)}, u32[]{:S(2)}) %collective-permute-start.2) | collective-permute-done | bytes 266272 | tf_op jit(solution)/shard_map/ppermute | solution.py:559
  39.8 4.3 %collective-permute-done.4.refs_2_ = f32[520,128]{1,0:T(8,128)S(1)} collective-permute-done((f32[520,128]{1,0:T(8,128)S(1)}, f32[520,128]{1,0:T(8,128)S(1)}, u32[]{:S(2)}, u32[]{:S(2)}) %collective-permute-start.4) | collective-permute-done | bytes 266272 | tf_op jit(solution)/shard_map/ppermute | solution.py:559
  44.1 5.7 %shard_map.53 = (f32[8192,128]{1,0:T(8,128)S(1)}, f32[64,128]{1,0:T(8,128)S(1)}, f32[64,128]{1,0:T(8,128)S(1)}) custom-call(s32[64,128]{1,0:T(8,128)S(1)} %get-tuple-element.60.acc_rows.ready, f32[64,128]{1,0:T(8,128)S(1)} %get-tuple-element.61.flag_rows, f32[8192,128]{1,0:T(8,128)S(1)} %shard_map.47.grouped, f32[520,128]{1,0:T(8,128)S(1)} %get-tuple-element.69.ready.refs_0_), custom_call_target="tpu_custom_call" | custom-call | flops 8000000000 | bytes 1000000 | tf_op jit(solution)/shard_map/pallas_call | solution.py:55
  49.8 1.1 collective-permute-done.10.refs_7_
  51.0 1.5 %shard_map.57 = (f32[520,128]{1,0:T(8,128)S(1)}, f32[520,128]{1,0:T(8,128)S(1)}, f32[136,128]{1,0:T(8,128)S(1)}, f32[136,128]{1,0:T(8,128)S(1)}, f32[136,128]{1,0:T(8,128)S(1)}, /*index=5*/f32[136,128]{1,0:T(8,128)S(1)}) custom-call(s32[8]{0:T(128)S(1)} %compare_select_fusion.4.place, f32[520,128]{1,0:T(8,128)S(1)} %get-tuple-element.69.ready.refs_0_, ...), custom_call_target="tpu_custom_call" | custom-call | flops 1000000 | bytes 1000000 | tf_op jit(solution)/shard_map/pallas_call | solution.py:55
  52.5 3.7 %collective-permute-start.11 = (f32[136,128]{1,0:T(8,128)S(1)}, f32[136,128]{1,0:T(8,128)S(1)}, u32[]{:S(2)}, u32[]{:S(2)}) collective-permute-start(f32[136,128]{1,0:T(8,128)S(1)} %get-tuple-element.83), channel_id=1, source_target_pairs={{0,16},{16,32},{32,48},{48,0},{1,17},{17,33},{33,49},{49,1},{2,18}... | collective-permute-start | bytes 208904 | tf_op jit(solution)/shard_map/ppermute | solution.py:600
  56.2 5.1 %collective-permute-start.12 = (f32[136,128]{1,0:T(8,128)S(1)}, f32[136,128]{1,0:T(8,128)S(1)}, u32[]{:S(2)}, u32[]{:S(2)}) collective-permute-start(f32[136,128]{1,0:T(8,128)S(1)} %get-tuple-element.84), channel_id=1, source_target_pairs={{0,32},{16,48},{32,0},{48,16},{1,33},{17,49},{33,1},{49,17},{2,34}... | collective-permute-start | bytes 208904 | tf_op jit(solution)/shard_map/ppermute | solution.py:600
  61.3 2.4 %collective-permute-start.13 = (f32[136,128]{1,0:T(8,128)S(1)}, f32[136,128]{1,0:T(8,128)S(1)}, u32[]{:S(2)}, u32[]{:S(2)}) collective-permute-start(f32[136,128]{1,0:T(8,128)S(1)} %get-tuple-element.85), channel_id=1, source_target_pairs={{0,48},{16,0},{32,16},{48,32},{1,49},{17,1},{33,17},{49,33},{2,50}... | collective-permute-start | bytes 208904 | tf_op jit(solution)/shard_map/ppermute | solution.py:600
  64.1 2.1 %collective-permute-done.13.r3 = f32[136,128]{1,0:T(8,128)S(1)} collective-permute-done((f32[136,128]{1,0:T(8,128)S(1)}, f32[136,128]{1,0:T(8,128)S(1)}, u32[]{:S(2)}, u32[]{:S(2)}) %collective-permute-start.13) | collective-permute-done | bytes 69664 | tf_op jit(solution)/shard_map/ppermute | solution.py:600
  67.0 3.2 %collective-permute-start.14 = (f32[136,128]{1,0:T(8,128)S(1)}, f32[136,128]{1,0:T(8,128)S(1)}, u32[]{:S(2)}, u32[]{:S(2)}) collective-permute-start(f32[136,128]{1,0:T(8,128)S(1)} %shard_map.58), channel_id=1, source_target_pairs={{0,64},{64,128},{128,192},{1,65},{65,129},{129,193},{2,66},{66,130... | collective-permute-start | bytes 208904 | tf_op jit(solution)/shard_map/ppermute | solution.py:604
  70.2 4.5 %collective-permute-start.15 = (f32[136,128]{1,0:T(8,128)S(1)}, f32[136,128]{1,0:T(8,128)S(1)}, u32[]{:S(2)}, u32[]{:S(2)}) collective-permute-start(f32[136,128]{1,0:T(8,128)S(1)} %shard_map.58), channel_id=1, source_target_pairs={{0,128},{64,192},{1,129},{65,193},{2,130},{66,194},{3,131},{67,195... | collective-permute-start | bytes 208904 | tf_op jit(solution)/shard_map/ppermute | solution.py:604
  74.7 1.3 collective-permute-start.16
  76.4 0.9 collective-permute-done.16.p3
  77.4 1.0 shard_map.59
  78.4 5.8 %collective-permute-start.17 = (f32[136,128]{1,0:T(8,128)S(1)}, f32[136,128]{1,0:T(8,128)S(1)}, u32[]{:S(2)}, u32[]{:S(2)}) collective-permute-start(f32[136,128]{1,0:T(8,128)S(1)} %get-tuple-element.87), channel_id=1, source_target_pairs={{0,48},{16,0},{32,16},{48,32},{1,49},{17,1},{33,17},{49,33},{2,50}... | collective-permute-start | bytes 208904 | tf_op jit(solution)/shard_map/ppermute | solution.py:610
  84.2 2.2 %collective-permute-start.19 = (f32[136,128]{1,0:T(8,128)S(1)}, f32[136,128]{1,0:T(8,128)S(1)}, u32[]{:S(2)}, u32[]{:S(2)}) collective-permute-start(f32[136,128]{1,0:T(8,128)S(1)} %get-tuple-element.89), channel_id=1, source_target_pairs={{0,16},{16,32},{32,48},{48,0},{1,17},{17,33},{33,49},{49,1},{2,18}... | collective-permute-start | bytes 208904 | tf_op jit(solution)/shard_map/ppermute | solution.py:610
  86.4 1.0 collective-permute-done.17.e1
  87.4 4.3 %collective-permute-done.18.e2 = f32[136,128]{1,0:T(8,128)S(1)} collective-permute-done((f32[136,128]{1,0:T(8,128)S(1)}, f32[136,128]{1,0:T(8,128)S(1)}, u32[]{:S(2)}, u32[]{:S(2)}) %collective-permute-start.18) | collective-permute-done | bytes 69664 | tf_op jit(solution)/shard_map/ppermute | solution.py:610
  91.7 1.4 %shard_map.60 = (f32[520,128]{1,0:T(8,128)S(1)}, f32[520,128]{1,0:T(8,128)S(1)}, f32[520,128]{1,0:T(8,128)S(1)}, f32[520,128]{1,0:T(8,128)S(1)}, f32[520,128]{1,...) custom-call(s32[8]{0:T(128)S(1)} %compare_select_fusion.4.place, ...), custom_call_target="tpu_custom_call" | custom-call | flops 1000000 | bytes 1000000 | tf_op jit(solution)/shard_map/pallas_call | solution.py:55
  93.9 3.0 %collective-permute-start.21 = (f32[520,128]{1,0:T(8,128)S(1)}, f32[520,128]{1,0:T(8,128)S(1)}, u32[]{:S(2)}, u32[]{:S(2)}) collective-permute-start(f32[520,128]{1,0:T(8,128)S(1)} %get-tuple-element.98), channel_id=1, source_target_pairs={{0,12},{2,14},{4,8},{6,10},{8,4},{10,6},{12,0},{14,2},{1,13},{3,15... | collective-permute-start | bytes 798728 | tf_op jit(solution)/shard_map/ppermute | solution.py:559
  97.6 5.0 %shard_map.61 = (f32[4096,128]{1,0:T(8,128)S(1)}, f32[32,128]{1,0:T(8,128)S(1)}, f32[32,128]{1,0:T(8,128)S(1)}, s32[32,128]{1,0:T(8,128)S(1)}) custom-call(s32[32,128]{1,0:T(8,128)S(1)} %get-tuple-element.59.slot_rows.slots, s32[32,128]{1,0:T(8,128)S(1)} %get-tuple-element.59.slot_rows.slots, s32[32,128]{1,0:T(8,128)S(1)} %bitcast.8, s32[32,128]{1,0:T(8,128)S(1)} %bitcast.4, ...), custom_call_target="tpu_custom_call" | custom-call | flops 10000000000 | bytes 1000000 | tf_op jit(solution)/shard_map/pallas_call | solution.py:55
  102.6 1.7 %collective-permute-done.20.refs_0_ = f32[520,128]{1,0:T(8,128)S(1)} collective-permute-done((f32[520,128]{1,0:T(8,128)S(1)}, f32[520,128]{1,0:T(8,128)S(1)}, u32[]{:S(2)}, u32[]{:S(2)}) %collective-permute-start.20) | collective-permute-done | bytes 266272 | tf_op jit(solution)/shard_map/ppermute | solution.py:559
  105.1 1.1 shard_map.62
  106.2 5.6 %collective-permute-start.27 = (f32[4,520,128]{2,1,0:T(8,128)S(1)}, f32[4,520,128]{2,1,0:T(8,128)S(1)}, u32[]{:S(2)}, u32[]{:S(2)}) collective-permute-start(f32[4,520,128]{2,1,0:T(8,128)S(1)} %get-tuple-element.107), channel_id=1, source_target_pairs={{0,1},{1,0},{2,3},{3,2},{4,5},{5,4},{6,7},{7,6},{8,9},{9,8},{10,11... | collective-permute-start | bytes 3194888 | tf_op jit(solution)/shard_map/ppermute | solution.py:641
  111.8 1.1 collective-permute-start.23
  113.7 1.5 %collective-permute-start.25 = (f32[520,128]{1,0:T(8,128)S(1)}, f32[520,128]{1,0:T(8,128)S(1)}, u32[]{:S(2)}, u32[]{:S(2)}) collective-permute-start(f32[520,128]{1,0:T(8,128)S(1)} %get-tuple-element.104), channel_id=1, source_target_pairs={{0,2},{2,4},{4,6},{6,0},{8,10},{10,12},{12,14},{14,8},{1,3},{3,5},... | collective-permute-start | bytes 798728 | tf_op jit(solution)/shard_map/ppermute | solution.py:559
  115.7 9.8 %collective-permute-done.23.refs_0_ = f32[520,128]{1,0:T(8,128)S(1)} collective-permute-done((f32[520,128]{1,0:T(8,128)S(1)}, f32[520,128]{1,0:T(8,128)S(1)}, u32[]{:S(2)}, u32[]{:S(2)}) %collective-permute-start.23) | collective-permute-done | bytes 266272 | tf_op jit(solution)/shard_map/ppermute | solution.py:559
  125.4 0.9 shard_map.63
  126.3 1.0 collective-permute-start.28
  127.3 0.8 collective-permute-done.26.refs_1_
  128.1 0.8 shard_map.64
  129.0 1.4 collective-permute-start.29
  130.4 1.3 shard_map.65
  131.9 6.1 %shard_map.66 = (f32[16,520,128]{2,1,0:T(8,128)S(1)}, f32[4096,128]{1,0:T(8,128)}) custom-call(s32[8]{0:T(128)S(1)} %compare_select_fusion.4.place, s32[32,128]{1,0:T(8,128)S(1)} %get-tuple-element.93.users, f32[4096,128]{1,0:T(8,128)S(1)} %get-tuple-element.94.run, f32[32,128]{1,0:T(8,128)S(1)} %get-tuple-element.95.ready.count, ...), custom_call_target="tpu_custom_call", output_to_operand_aliasing={{0}: (8, {})} | custom-call | flops 1000000 | bytes 1000000 | tf_op jit(solution)/shard_map/pallas_call | solution.py:55
  (41 shorter events, 8.1 us)
Async XLA Ops:
  0.8 1.6 %copy-start.2 = (f32[4096,128]{1,0:T(8,128)S(1)}, f32[4096,128]{1,0:T(8,128)}, u32[]{:S(2)}) copy-start(f32[4096,128]{1,0:T(8,128)} %features.1) | copy-start | bytes 6291460
  8.2 5.0 %collective-permute-start.3 = (f32[2,520,128]{2,1,0:T(8,128)S(1)}, f32[2,520,128]{2,1,0:T(8,128)S(1)}, u32[]{:S(2)}, u32[]{:S(2)}) collective-permute-start(f32[2,520,128]{2,1,0:T(8,128)S(1)} %get-tuple-element.73), channel_id=1, source_target_pairs={{0,1},{1,0},{2,3},{3,2},{4,5},{5,4},{6,7},{7,6},{8,9},{9,8},{10,11... | collective-permute-start | bytes 1597448 | tf_op jit(solution)/shard_map/ppermute | solution.py:581
  13.1 3.2 %collective-permute-start = (f32[2,520,128]{2,1,0:T(8,128)S(1)}, f32[2,520,128]{2,1,0:T(8,128)S(1)}, u32[]{:S(2)}, u32[]{:S(2)}) collective-permute-start(f32[2,520,128]{2,1,0:T(8,128)S(1)} %get-tuple-element.65), channel_id=1, source_target_pairs={{0,1},{1,0},{2,3},{3,2},{4,5},{5,4},{6,7},{7,6},{8,9},{9,8},{10,11... | collective-permute-start | bytes 1597448 | tf_op jit(solution)/shard_map/ppermute | solution.py:581
  15.7 6.1 %collective-permute-start.5 = (f32[2,520,128]{2,1,0:T(8,128)S(1)}, f32[2,520,128]{2,1,0:T(8,128)S(1)}, u32[]{:S(2)}, u32[]{:S(2)}) collective-permute-start(f32[2,520,128]{2,1,0:T(8,128)S(1)} %get-tuple-element.76), channel_id=1, source_target_pairs={{0,1},{1,0},{2,3},{3,2},{4,5},{5,4},{6,7},{7,6},{8,9},{9,8},{10,11... | collective-permute-start | bytes 1597448 | tf_op jit(solution)/shard_map/ppermute | solution.py:581
  18.7 6.2 %collective-permute-start.1 = (f32[2,520,128]{2,1,0:T(8,128)S(1)}, f32[2,520,128]{2,1,0:T(8,128)S(1)}, u32[]{:S(2)}, u32[]{:S(2)}) collective-permute-start(f32[2,520,128]{2,1,0:T(8,128)S(1)} %get-tuple-element.68), channel_id=1, source_target_pairs={{0,1},{1,0},{2,3},{3,2},{4,5},{5,4},{6,7},{7,6},{8,9},{9,8},{10,11... | collective-permute-start | bytes 1597448 | tf_op jit(solution)/shard_map/ppermute | solution.py:581
  18.8 20.9 %collective-permute-start.2 = (f32[520,128]{1,0:T(8,128)S(1)}, f32[520,128]{1,0:T(8,128)S(1)}, u32[]{:S(2)}, u32[]{:S(2)}) collective-permute-start(f32[520,128]{1,0:T(8,128)S(1)} %get-tuple-element.66.ready), channel_id=1, source_target_pairs={{0,2},{2,4},{4,6},{6,0},{8,10},{10,12},{12,14},{14,8},{1,3},{3,5},... | collective-permute-start | bytes 798728 | tf_op jit(solution)/shard_map/ppermute | solution.py:559
  18.9 25.2 %collective-permute-start.4 = (f32[520,128]{1,0:T(8,128)S(1)}, f32[520,128]{1,0:T(8,128)S(1)}, u32[]{:S(2)}, u32[]{:S(2)}) collective-permute-start(f32[520,128]{1,0:T(8,128)S(1)} %get-tuple-element.74.ready), channel_id=1, source_target_pairs={{0,4},{2,6},{4,0},{6,2},{8,12},{10,14},{12,8},{14,10},{1,5},{3,7},... | collective-permute-start | bytes 798728 | tf_op jit(solution)/shard_map/ppermute | solution.py:559
  20.9 28.9 %collective-permute-start.8 = (f32[520,128]{1,0:T(8,128)S(1)}, f32[520,128]{1,0:T(8,128)S(1)}, u32[]{:S(2)}, u32[]{:S(2)}) collective-permute-start(f32[520,128]{1,0:T(8,128)S(1)} %get-tuple-element.79), channel_id=1, source_target_pairs={{0,10},{2,12},{4,14},{6,8},{8,2},{10,4},{12,6},{14,0},{1,11},{3,13... | collective-permute-start | bytes 798728 | tf_op jit(solution)/shard_map/ppermute | solution.py:559
  21.8 28.0 %collective-permute-start.9 = (f32[520,128]{1,0:T(8,128)S(1)}, f32[520,128]{1,0:T(8,128)S(1)}, u32[]{:S(2)}, u32[]{:S(2)}) collective-permute-start(f32[520,128]{1,0:T(8,128)S(1)} %get-tuple-element.80), channel_id=1, source_target_pairs={{0,12},{2,14},{4,8},{6,10},{8,4},{10,6},{12,0},{14,2},{1,13},{3,15... | collective-permute-start | bytes 798728 | tf_op jit(solution)/shard_map/ppermute | solution.py:559
  24.9 24.9 %collective-permute-start.6 = (f32[520,128]{1,0:T(8,128)S(1)}, f32[520,128]{1,0:T(8,128)S(1)}, u32[]{:S(2)}, u32[]{:S(2)}) collective-permute-start(f32[520,128]{1,0:T(8,128)S(1)} %get-tuple-element.77), channel_id=1, source_target_pairs={{0,6},{2,0},{4,2},{6,4},{8,14},{10,8},{12,10},{14,12},{1,7},{3,1},... | collective-permute-start | bytes 798728 | tf_op jit(solution)/shard_map/ppermute | solution.py:559
  39.8 10.1 %collective-permute-start.7 = (f32[520,128]{1,0:T(8,128)S(1)}, f32[520,128]{1,0:T(8,128)S(1)}, u32[]{:S(2)}, u32[]{:S(2)}) collective-permute-start(f32[520,128]{1,0:T(8,128)S(1)} %get-tuple-element.78), channel_id=1, source_target_pairs={{0,8},{2,10},{4,12},{6,14},{8,0},{10,2},{12,4},{14,6},{1,9},{3,11}... | collective-permute-start | bytes 798728 | tf_op jit(solution)/shard_map/ppermute | solution.py:559
  44.1 6.9 %collective-permute-start.10 = (f32[520,128]{1,0:T(8,128)S(1)}, f32[520,128]{1,0:T(8,128)S(1)}, u32[]{:S(2)}, u32[]{:S(2)}) collective-permute-start(f32[520,128]{1,0:T(8,128)S(1)} %get-tuple-element.81), channel_id=1, source_target_pairs={{0,14},{2,8},{4,10},{6,12},{8,6},{10,0},{12,2},{14,4},{1,15},{3,9}... | collective-permute-start | bytes 798728 | tf_op jit(solution)/shard_map/ppermute | solution.py:559
  52.5 45.1 %copy-start = (s32[4096]{0:T(1024)S(1)}, s32[4096]{0:T(1024)}, u32[]{:S(2)}) copy-start(s32[4096]{0:T(1024)} %param.6) | copy-start | bytes 49156
  52.5 45.1 %copy-start.1 = (s32[4096,1]{0,1:T(1,128)S(1)}, s32[4096,1]{0,1:T(1,128)}, u32[]{:S(2)}) copy-start(s32[4096,1]{0,1:T(1,128)} %param.5) | copy-start | bytes 49156
  52.5 11.2 %collective-permute-start.11 = (f32[136,128]{1,0:T(8,128)S(1)}, f32[136,128]{1,0:T(8,128)S(1)}, u32[]{:S(2)}, u32[]{:S(2)}) collective-permute-start(f32[136,128]{1,0:T(8,128)S(1)} %get-tuple-element.83), channel_id=1, source_target_pairs={{0,16},{16,32},{32,48},{48,0},{1,17},{17,33},{33,49},{49,1},{2,18}... | collective-permute-start | bytes 208904 | tf_op jit(solution)/shard_map/ppermute | solution.py:600
  56.2 7.9 %collective-permute-start.12 = (f32[136,128]{1,0:T(8,128)S(1)}, f32[136,128]{1,0:T(8,128)S(1)}, u32[]{:S(2)}, u32[]{:S(2)}) collective-permute-start(f32[136,128]{1,0:T(8,128)S(1)} %get-tuple-element.84), channel_id=1, source_target_pairs={{0,32},{16,48},{32,0},{48,16},{1,33},{17,49},{33,1},{49,17},{2,34}... | collective-permute-start | bytes 208904 | tf_op jit(solution)/shard_map/ppermute | solution.py:600
  61.3 4.8 %collective-permute-start.13 = (f32[136,128]{1,0:T(8,128)S(1)}, f32[136,128]{1,0:T(8,128)S(1)}, u32[]{:S(2)}, u32[]{:S(2)}) collective-permute-start(f32[136,128]{1,0:T(8,128)S(1)} %get-tuple-element.85), channel_id=1, source_target_pairs={{0,48},{16,0},{32,16},{48,32},{1,49},{17,1},{33,17},{49,33},{2,50}... | collective-permute-start | bytes 208904 | tf_op jit(solution)/shard_map/ppermute | solution.py:600
  67.0 9.0 %collective-permute-start.14 = (f32[136,128]{1,0:T(8,128)S(1)}, f32[136,128]{1,0:T(8,128)S(1)}, u32[]{:S(2)}, u32[]{:S(2)}) collective-permute-start(f32[136,128]{1,0:T(8,128)S(1)} %shard_map.58), channel_id=1, source_target_pairs={{0,64},{64,128},{128,192},{1,65},{65,129},{129,193},{2,66},{66,130... | collective-permute-start | bytes 208904 | tf_op jit(solution)/shard_map/ppermute | solution.py:604
  70.2 6.3 %collective-permute-start.15 = (f32[136,128]{1,0:T(8,128)S(1)}, f32[136,128]{1,0:T(8,128)S(1)}, u32[]{:S(2)}, u32[]{:S(2)}) collective-permute-start(f32[136,128]{1,0:T(8,128)S(1)} %shard_map.58), channel_id=1, source_target_pairs={{0,128},{64,192},{1,129},{65,193},{2,130},{66,194},{3,131},{67,195... | collective-permute-start | bytes 208904 | tf_op jit(solution)/shard_map/ppermute | solution.py:604
  74.7 2.7 %collective-permute-start.16 = (f32[136,128]{1,0:T(8,128)S(1)}, f32[136,128]{1,0:T(8,128)S(1)}, u32[]{:S(2)}, u32[]{:S(2)}) collective-permute-start(f32[136,128]{1,0:T(8,128)S(1)} %shard_map.58), channel_id=1, source_target_pairs={{0,192},{1,193},{2,194},{3,195},{4,196},{5,197},{6,198},{7,199},{8... | collective-permute-start | bytes 208904 | tf_op jit(solution)/shard_map/ppermute | solution.py:604
  78.4 9.0 %collective-permute-start.17 = (f32[136,128]{1,0:T(8,128)S(1)}, f32[136,128]{1,0:T(8,128)S(1)}, u32[]{:S(2)}, u32[]{:S(2)}) collective-permute-start(f32[136,128]{1,0:T(8,128)S(1)} %get-tuple-element.87), channel_id=1, source_target_pairs={{0,48},{16,0},{32,16},{48,32},{1,49},{17,1},{33,17},{49,33},{2,50}... | collective-permute-start | bytes 208904 | tf_op jit(solution)/shard_map/ppermute | solution.py:610
  84.2 7.5 %collective-permute-start.18 = (f32[136,128]{1,0:T(8,128)S(1)}, f32[136,128]{1,0:T(8,128)S(1)}, u32[]{:S(2)}, u32[]{:S(2)}) collective-permute-start(f32[136,128]{1,0:T(8,128)S(1)} %get-tuple-element.88), channel_id=1, source_target_pairs={{0,32},{16,48},{32,0},{48,16},{1,33},{17,49},{33,1},{49,17},{2,34}... | collective-permute-start | bytes 208904 | tf_op jit(solution)/shard_map/ppermute | solution.py:610
  84.2 7.5 %collective-permute-start.19 = (f32[136,128]{1,0:T(8,128)S(1)}, f32[136,128]{1,0:T(8,128)S(1)}, u32[]{:S(2)}, u32[]{:S(2)}) collective-permute-start(f32[136,128]{1,0:T(8,128)S(1)} %get-tuple-element.89), channel_id=1, source_target_pairs={{0,16},{16,32},{32,48},{48,0},{1,17},{17,33},{33,49},{49,1},{2,18}... | collective-permute-start | bytes 208904 | tf_op jit(solution)/shard_map/ppermute | solution.py:610
  93.1 11.2 %collective-permute-start.20 = (f32[520,128]{1,0:T(8,128)S(1)}, f32[520,128]{1,0:T(8,128)S(1)}, u32[]{:S(2)}, u32[]{:S(2)}) collective-permute-start(f32[520,128]{1,0:T(8,128)S(1)} %get-tuple-element.97), channel_id=1, source_target_pairs={{0,4},{2,6},{4,0},{6,2},{8,12},{10,14},{12,8},{14,10},{1,5},{3,7},... | collective-permute-start | bytes 798728 | tf_op jit(solution)/shard_map/ppermute | solution.py:559
  93.9 10.4 %collective-permute-start.21 = (f32[520,128]{1,0:T(8,128)S(1)}, f32[520,128]{1,0:T(8,128)S(1)}, u32[]{:S(2)}, u32[]{:S(2)}) collective-permute-start(f32[520,128]{1,0:T(8,128)S(1)} %get-tuple-element.98), channel_id=1, source_target_pairs={{0,12},{2,14},{4,8},{6,10},{8,4},{10,6},{12,0},{14,2},{1,13},{3,15... | collective-permute-start | bytes 798728 | tf_op jit(solution)/shard_map/ppermute | solution.py:559
  96.9 8.2 %collective-permute-start.22 = (f32[520,128]{1,0:T(8,128)S(1)}, f32[520,128]{1,0:T(8,128)S(1)}, u32[]{:S(2)}, u32[]{:S(2)}) collective-permute-start(f32[520,128]{1,0:T(8,128)S(1)} %get-tuple-element.99), channel_id=1, source_target_pairs={{0,8},{2,10},{4,12},{6,14},{8,0},{10,2},{12,4},{14,6},{1,9},{3,11}... | collective-permute-start | bytes 798728 | tf_op jit(solution)/shard_map/ppermute | solution.py:559
  106.2 24.1 %collective-permute-start.27 = (f32[4,520,128]{2,1,0:T(8,128)S(1)}, f32[4,520,128]{2,1,0:T(8,128)S(1)}, u32[]{:S(2)}, u32[]{:S(2)}) collective-permute-start(f32[4,520,128]{2,1,0:T(8,128)S(1)} %get-tuple-element.107), channel_id=1, source_target_pairs={{0,1},{1,0},{2,3},{3,2},{4,5},{5,4},{6,7},{7,6},{8,9},{9,8},{10,11... | collective-permute-start | bytes 3194888 | tf_op jit(solution)/shard_map/ppermute | solution.py:641
  111.8 13.6 %collective-permute-start.23 = (f32[520,128]{1,0:T(8,128)S(1)}, f32[520,128]{1,0:T(8,128)S(1)}, u32[]{:S(2)}, u32[]{:S(2)}) collective-permute-start(f32[520,128]{1,0:T(8,128)S(1)} %get-tuple-element.101), channel_id=1, source_target_pairs={{0,6},{2,0},{4,2},{6,4},{8,14},{10,8},{12,10},{14,12},{1,7},{3,1},... | collective-permute-start | bytes 798728 | tf_op jit(solution)/shard_map/ppermute | solution.py:559
  112.9 12.5 %collective-permute-start.24 = (f32[520,128]{1,0:T(8,128)S(1)}, f32[520,128]{1,0:T(8,128)S(1)}, u32[]{:S(2)}, u32[]{:S(2)}) collective-permute-start(f32[520,128]{1,0:T(8,128)S(1)} %get-tuple-element.102), channel_id=1, source_target_pairs={{0,14},{2,8},{4,10},{6,12},{8,6},{10,0},{12,2},{14,4},{1,15},{3,9}... | collective-permute-start | bytes 798728 | tf_op jit(solution)/shard_map/ppermute | solution.py:559
  113.7 13.6 %collective-permute-start.25 = (f32[520,128]{1,0:T(8,128)S(1)}, f32[520,128]{1,0:T(8,128)S(1)}, u32[]{:S(2)}, u32[]{:S(2)}) collective-permute-start(f32[520,128]{1,0:T(8,128)S(1)} %get-tuple-element.104), channel_id=1, source_target_pairs={{0,2},{2,4},{4,6},{6,0},{8,10},{10,12},{12,14},{14,8},{1,3},{3,5},... | collective-permute-start | bytes 798728 | tf_op jit(solution)/shard_map/ppermute | solution.py:559
  115.2 13.0 %collective-permute-start.26 = (f32[520,128]{1,0:T(8,128)S(1)}, f32[520,128]{1,0:T(8,128)S(1)}, u32[]{:S(2)}, u32[]{:S(2)}) collective-permute-start(f32[520,128]{1,0:T(8,128)S(1)} %get-tuple-element.105), channel_id=1, source_target_pairs={{0,10},{2,12},{4,14},{6,8},{8,2},{10,4},{12,6},{14,0},{1,11},{3,13... | collective-permute-start | bytes 798728 | tf_op jit(solution)/shard_map/ppermute | solution.py:559
  126.3 5.4 %collective-permute-start.28 = (f32[2,520,128]{2,1,0:T(8,128)S(1)}, f32[2,520,128]{2,1,0:T(8,128)S(1)}, u32[]{:S(2)}, u32[]{:S(2)}) collective-permute-start(f32[2,520,128]{2,1,0:T(8,128)S(1)} %get-tuple-element.110), channel_id=1, source_target_pairs={{0,1},{1,0},{2,3},{3,2},{4,5},{5,4},{6,7},{7,6},{8,9},{9,8},{10,11... | collective-permute-start | bytes 1597448 | tf_op jit(solution)/shard_map/ppermute | solution.py:641
  129.0 2.9 %collective-permute-start.29 = (f32[2,520,128]{2,1,0:T(8,128)S(1)}, f32[2,520,128]{2,1,0:T(8,128)S(1)}, u32[]{:S(2)}, u32[]{:S(2)}) collective-permute-start(f32[2,520,128]{2,1,0:T(8,128)S(1)} %get-tuple-element.111), channel_id=1, source_target_pairs={{0,1},{1,0},{2,3},{3,2},{4,5},{5,4},{6,7},{7,6},{8,9},{9,8},{10,11... | collective-permute-start | bytes 1597448 | tf_op jit(solution)/shard_map/ppermute | solution.py:641

commit v7 on v6

--- a/solution.py
+++ b/solution.py
@@ -64,6 +64,14 @@
     )(*args)
 
 
+class Place:
+    def __getitem__(self, n):
+        return lax.axis_index(("c", "x", "l", "h", "y")[n])
+
+
+PLACE = Place()
+
+
 def block(*lead):
     return jax.ShapeDtypeStruct((*lead, ROWS, LANES), F32)
 
@@ -72,9 +80,9 @@
     return jax.ShapeDtypeStruct((*lead, ONE, LANES), F32)
 
 
-def chunk_of(place, dz, dx):
-    row = jnp.where(place[2] == 0, dz, 1 - dz)
-    return row * NX + lax.rem(place[1] + dx, NX)
+def chunk_of(dz, dx):
+    row = jnp.where(PLACE[2] == 0, dz, 1 - dz)
+    return row * NX + lax.rem(PLACE[1] + dx, NX)
 
 
 def rank_kernel(events, slot_out, acc_out, flag_out, cleared):
@@ -147,10 +155,10 @@
     return both.T
 
 
-def closing_kernel(dx, place, acc_rows, flag_rows, grouped, ready, other, mine):
+def closing_kernel(dx, acc_rows, flag_rows, grouped, ready, other, mine):
     sides = after_and_ones()
-    for out, half_of in ((other, 1 - place[0]), (mine, place[0])):
-        bases = [half_of * HALF + chunk_of(place, dz, dx) * FOUR for dz in range(NL)]
+    for out, half_of in ((other, 1 - PLACE[0]), (mine, PLACE[0])):
+        bases = [half_of * HALF + chunk_of(dz, dx) * FOUR for dz in range(NL)]
         acc8 = jnp.concatenate([acc_rows[pl.ds(b, FOUR), :] for b in bases], axis=0)
         flag8 = jnp.concatenate([flag_rows[pl.ds(b, FOUR), :] for b in bases], axis=0)
         member = [iota((LANES, LANES), 0) == acc8[i : i + 1, :] for i in range(8)]
@@ -266,8 +274,8 @@
     return jnp.concatenate([sums, tail], axis=0)
 
 
-def core_kernel(place, mine, got, *outs):
-    first = place[0] == 0
+def core_kernel(mine, got, *outs):
+    first = PLACE[0] == 0
     for dz in range(NL):
         a, b = mine[dz, TAIL:, :], got[dz, TAIL:, :]
         early, late = jnp.where(first, a, b), jnp.where(first, b, a)
@@ -281,13 +289,13 @@
         outs[dz][TAIL:, :] = joined_tail(early, late)
 
 
-def row_kernel(place, *refs):
+def row_kernel(*refs):
     tables = (refs[:NX], refs[NX : 2 * NX])
     totals = refs[2 * NX + 1 : 2 * NX + 3]
     outs, pair = refs[2 * NX + 3 : 2 * NX + 3 + NH], refs[-1]
     for x in range(NX):
 
-        @pl.when(place[1] == x)
+        @pl.when(PLACE[1] == x)
         def _(x=x):
             for dz in range(NL):
                 order = [tables[dz][(x - j) % NX] for j in range(NX)]
@@ -304,7 +312,7 @@
                 totals[dz][TAIL:, :] = tail
 
     own, near = totals
-    first = place[2] == 0
+    first = PLACE[2] == 0
     a, b = own[TAIL:, :], near[TAIL:, :]
     early, late = jnp.where(first, a, b), jnp.where(first, b, a)
     keep = keep_of(late)
@@ -320,14 +328,14 @@
             jnp.where(sub == 1, tail[FOUR + i : FOUR + i + 1, :], 0.0),
         )
     for r in range(NH):
-        outs[r][...] = pair[lax.rem(place[3] + r, NH)]
-
-
-def plane_kernel(place, r0, r1, r2, r3, out):
+        outs[r][...] = pair[lax.rem(PLACE[3] + r, NH)]
+
+
+def plane_kernel(r0, r1, r2, r3, out):
     rows = (r0, r1, r2, r3)
     for h in range(NH):
 
-        @pl.when(place[3] == h)
+        @pl.when(PLACE[3] == h)
         def _(h=h):
             total = rows[h][...]
             for j in range(1, NH):
@@ -335,14 +343,14 @@
             out[...] = total
 
 
-def rows_back_kernel(place, p1, p2, p3, r0, r1, r2, r3, *outs):
+def rows_back_kernel(p1, p2, p3, r0, r1, r2, r3, *outs):
     rows = (r0, r1, r2, r3)
     start = jnp.zeros((ONE, LANES), F32)
     for r, plane in ((2, p3), (1, p2), (0, p1)):
-        start = jnp.where(place[4] > r, joined_one(start, plane[...]), start)
+        start = jnp.where(PLACE[4] > r, joined_one(start, plane[...]), start)
     for h in range(NH):
 
-        @pl.when(place[3] == h)
+        @pl.when(PLACE[3] == h)
         def _(h=h):
             state = start
             for j in range(NH):
@@ -352,12 +360,12 @@
                     state = joined_one(state, rows[k][...])
 
 
-def chips_back_kernel(place, e0, e1, e2, e3, own, near, *refs):
+def chips_back_kernel(e0, e1, e2, e3, own, near, *refs):
     tables, outs = (refs[:NX], refs[NX : 2 * NX]), (refs[2 * NX : 3 * NX], refs[3 * NX : 4 * NX])
     came = refs[-1]
     for r, e in enumerate((e0, e1, e2, e3)):
-        came[lax.rem(place[3] + r, NH)] = e[...]
-    first = place[2] == 0
+        came[lax.rem(PLACE[3] + r, NH)] = e[...]
+    first = PLACE[2] == 0
     sub = iota((8, LANES), 0)
     tail0 = jnp.zeros((8, LANES), F32)
     for i in range(FOUR):
@@ -367,7 +375,7 @@
     tail1 = joined_tail(tail0, between)
     for x in range(NX):
 
-        @pl.when(place[1] == x)
+        @pl.when(PLACE[1] == x)
         def _(x=x):
             for dz in range(NL):
                 order = [(x - j) % NX for j in range(NX)]
@@ -394,11 +402,11 @@
                         tail = joined_tail(tail, tails[j])
 
 
-def cores_back_kernel(place, ready, *refs):
+def cores_back_kernel(ready, *refs):
     n = (len(refs) - 2) // 4
     parts, mine, got = refs[: 2 * n], refs[2 * n : 3 * n], refs[3 * n : 4 * n]
     keep_out, send = refs[4 * n :]
-    first = place[0] == 0
+    first = PLACE[0] == 0
     counts_only = iota((8, LANES), 0) < FOUR
     for d in range(n):
         for dz in range(NL):
@@ -432,21 +440,21 @@
     return came
 
 
-def held_parts(place, dxs, side, own_half):
-    half_of = place[0] if own_half else 1 - place[0]
+def held_parts(dxs, side, own_half):
+    half_of = PLACE[0] if own_half else 1 - PLACE[0]
     return [
-        (side, 2 * d + dz, half_of * CHUNKS + chunk_of(place, dz, dx))
+        (side, 2 * d + dz, half_of * CHUNKS + chunk_of(dz, dx))
         for d, dx in enumerate(dxs)
         for dz in range(NL)
     ]
 
 
-def gather_kernel(place, home, account, *refs):
+def gather_kernel(home, account, *refs):
     n = len(BACK)
     sides, (table, counts, sems) = refs[: n + 1], refs[n + 1 :]
     held = []
     for s, side in enumerate(sides):
-        held += held_parts(place, BACK[s % n], side, s < n)
+        held += held_parts(BACK[s % n], side, s < n)
     copies = [
         pltpu.make_async_copy(side.at[k], table.at[at], sems.at[i])
         for i, (side, k, at) in enumerate(held)
@@ -464,12 +472,14 @@
 
 
 def finish_kernel(
-    place, users, run, count, is_open, home, account, counts, table_in, got1, got2,
-    table, out, picked, sems, out_sems,
+    user_rows, run, count, is_open, home, account, counts, table_in, got1, got2,
+    table, out, picked, users, sems, out_sems,
 ):
+    listed = pltpu.make_async_copy(user_rows, users, sems.at[4])
+    listed.start()
     held = []
     for s, side in ((1, got1), (2, got2)):
-        held += held_parts(place, BACK[s], side, False)
+        held += held_parts(BACK[s], side, False)
     copies = [
         pltpu.make_async_copy(side.at[k], table.at[at], sems.at[i])
         for i, (side, k, at) in enumerate(held)
@@ -488,7 +498,7 @@
     if lines < LANES:
         scale = jnp.concatenate([scale, jnp.zeros((LANES - lines, LANES), F32)], axis=0)
     scale = scale.T
-    for copy in copies:
+    for copy in (*copies, listed):
         copy.wait()
 
     def pick(b, _):
@@ -525,9 +535,6 @@
     home = home.reshape(lines, LANES)
     account = account.reshape(lines, LANES)
     flags = flags.reshape(lines, LANES)
-    spot, place = iota((8,), 0), jnp.zeros((8,), I32)
-    for n, axis in enumerate(("c", "x", "l", "h", "y")):
-        place = jnp.where(spot == n, lax.axis_index(axis).astype(I32), place)
     small = jax.ShapeDtypeStruct((lines, LANES), I32)
     small_f = jax.ShapeDtypeStruct((lines, LANES), F32)
     by_owner = functools.partial(jax.ShapeDtypeStruct, (OWNERS, LANES))
@@ -563,8 +570,8 @@
     tables = [[None] * NX for _ in range(NL)]
 
     def meet(dx):
-        chunks = call(core_kernel, [block()] * NL, (place, mine[dx], got[dx]),
-                      [SMEM, VMEM, VMEM], cost=500_000_000)
+        chunks = call(core_kernel, [block()] * NL, (mine[dx], got[dx]),
+                      [VMEM, VMEM], cost=500_000_000)
         for dz in reversed(range(NL)):
             tables[dz][dx] = exchange(chunks[dz], dz, dx)
         return chunks[0]
@@ -574,8 +581,8 @@
         other, mine[dx] = call(
             functools.partial(closing_kernel, dx),
             [block(NL)] * 2,
-            (place, acc_rows, flag_rows, grouped, met[at]),
-            [SMEM] + [VMEM] * 3 + [ANY],
+            (acc_rows, flag_rows, grouped, met[at]),
+            [VMEM] * 3 + [ANY],
             cost=1_500_000_000,
         )
         got[dx] = lax.ppermute(other, "c", swap)
@@ -591,28 +598,28 @@
     own, near, *pairs = call(
         row_kernel,
         [block()] * NL + [one_block()] * NH,
-        (place, *tables[0], *tables[1], counts),
-        [SMEM] + [VMEM] * (NL * NX) + [ANY],
+        (*tables[0], *tables[1], counts),
+        [VMEM] * (NL * NX) + [ANY],
         scratch=[pltpu.VMEM((NH, ONE, LANES), F32)],
     )
     rows_got = list(pairs)
     for r in (1, 3, 2):
         rows_got[r] = lax.ppermute(pairs[r], "h", ring(NH, r))
-    plane = call(plane_kernel, one_block(), (place, *rows_got), [SMEM] + [VMEM] * NH)
+    plane = call(plane_kernel, one_block(), tuple(rows_got), [VMEM] * NH)
     ny = lax.axis_size("y")
     planes = [
         lax.ppermute(plane, "y", [(i, i + r) for i in range(ny - r)]) for r in range(1, ny)
     ]
-    came = call(rows_back_kernel, [one_block()] * NH, (place, *planes, *rows_got),
-                [SMEM] + [VMEM] * (3 + NH))
+    came = call(rows_back_kernel, [one_block()] * NH, (*planes, *rows_got),
+                [VMEM] * (3 + NH))
     came = list(came)
     for r in (1, 3, 2):
         came[r] = lax.ppermute(came[r], "h", ring(NH, -r))
     parts = call(
         chips_back_kernel,
         [block()] * (NL * NX),
-        (place, *came, own, near, *tables[0], *tables[1]),
-        [SMEM] + [VMEM] * (NH + NL + NL * NX),
+        (*came, own, near, *tables[0], *tables[1]),
+        [VMEM] * (NH + NL + NL * NX),
         scratch=[pltpu.VMEM((NH, ONE, LANES), F32)],
     )
     parts = [list(parts[:NX]), list(parts[NX:])]
@@ -632,9 +639,9 @@
         stay, send = call(
             cores_back_kernel,
             [block(2 * len(dxs))] * 2,
-            (place, keep[-1] if keep else count, *[parts[dz][dx] for dx in dxs for dz in range(NL)],
+            (keep[-1] if keep else count, *[parts[dz][dx] for dx in dxs for dz in range(NL)],
              *[mine[dx] for dx in dxs], *[got[dx] for dx in dxs]),
-            [SMEM, ANY] + [VMEM] * (4 * len(dxs)),
+            [ANY] + [VMEM] * (4 * len(dxs)),
             cost=500_000_000,
         )
         keep.append(stay)
@@ -642,20 +649,21 @@
     table, came_counts = call(
         gather_kernel,
         [block(NC * CHUNKS), small_f],
-        (place, home, account, *keep, last[0]),
-        [SMEM] + [VMEM] * 6,
+        (home, account, *keep, last[0]),
+        [VMEM] * 6,
         scratch=[pltpu.SemaphoreType.DMA((12,))],
         cost=2_000_000_000,
     )
     _, result = call(
         finish_kernel,
         [block(NC * CHUNKS), jax.ShapeDtypeStruct((rows, LANES), F32)],
-        (place, users, run, count, is_open, home, account, came_counts, table, *last[1:]),
-        [SMEM, SMEM] + [VMEM] * 9,
+        (users, run, count, is_open, home, account, came_counts, table, *last[1:]),
+        [VMEM] * 10,
         out_specs=[VMEM, ANY],
-        scratch=[pltpu.VMEM((rows, LANES), F32), pltpu.SemaphoreType.DMA((4,)),
+        scratch=[pltpu.VMEM((rows, LANES), F32), pltpu.SMEM((lines, LANES), I32),
+                 pltpu.SemaphoreType.DMA((5,)),
                  pltpu.SemaphoreType.DMA((8,))],
-        aliases={8: 0},
+        aliases={7: 0},
     )
     return result
 

time: 138 us -> 132 us (0.957)
  Pallas kernels: 40.9 us -> 31.9 us
  waiting for transfers between devices: 41.1 us -> 44.1 us
    pallas_call x21, Pallas kernels: 40.9 us -> 31.9 us  [call(): pl.pallas_call(kernel, out_shape=out, in_specs=specs, out_specs=out_specs...]
    ppermute x14, waiting for transfers between devices: 31.7 us -> 33.4 us  [exchange(): return lax.ppermute(v, ('l', 'x'), pairs)]
  transfers between devices with their start and end apart: 30 -> 30, of which waited for: 14 -> 15; matrix products, arithmetic and copies ran while one was open for 0% -> 0% of each run, Pallas kernels for 16% -> 13%
where the time goes in v7:
time: 132 us
  starting transfers between devices  54.1 us (41%)
  waiting for transfers between devices  44.1 us (33%)
  Pallas kernels  31.9 us (24%)
    ppermute x14, waiting for transfers between devices, exchange(): return lax.ppermute(v, ('l', 'x'), pairs)  33.4 us
    pallas_call x21, Pallas kernels, call(): pl.pallas_call(kernel, out_shape=out, in_specs=specs, out_specs=out_specs...  31.9 us
    ppermute x14, starting transfers between devices, exchange(): return lax.ppermute(v, ('l', 'x'), pairs)  14.4 us
    ppermute x3, starting transfers between devices, body(): rows_got[r] = lax.ppermute(pairs[r], 'h', ring(NH, r))  11.2 us
    ppermute x3, starting transfers between devices, body(): lax.ppermute(plane, 'y', [(i, i + r) for i in range(ny - r)])  9.04 us
    ppermute x3, starting transfers between devices, body(): last.append(lax.ppermute(send, 'c', swap))  7.81 us
    ppermute x3, starting transfers between devices, body(): came[r] = lax.ppermute(came[r], 'h', ring(NH, -r))  7.64 us
    ppermute x3, waiting for transfers between devices, body(): came[r] = lax.ppermute(came[r], 'h', ring(NH, -r))  5.51 us
  transfers between devices with their start and end apart: 30, of which 15 were waited for; matrix products, arithmetic and copies ran while one was open for 0% of the time, Pallas kernels for 13%

profile of v7, /device:TPU:1, one launch (start us, length us, event | category | flops | bytes accessed | tf_op | source)
XLA Modules:
  0.0 131.6 jit_solution(219212473829289670)
XLA Ops:
  0.0 0.8 pad_add_fusion.events
  0.8 1.3 shard_map.46
  2.3 4.2 %shard_map.47.grouped = f32[8192,128]{1,0:T(8,128)S(1)} custom-call(s32[32,128]{1,0:T(8,128)S(1)} %get-tuple-element.59.slot_rows.slots, f32[4096,128]{1,0:T(8,128)S(1)} %copy-done.2, f32[8192,128]{1,0:T(8,128)S(1)} %get-tuple-element.62.cleared), custom_call_target="tpu_custom_call", output_to_operand_aliasing={{}: (2, {})} | custom-call | flops 4000000000 | bytes 1000000 | tf_op jit(solution)/shard_map/pallas_call | solution.py:55
  6.5 1.1 shard_map.48
  7.6 3.3 %collective-permute-start.3 = (f32[2,520,128]{2,1,0:T(8,128)S(1)}, f32[2,520,128]{2,1,0:T(8,128)S(1)}, u32[]{:S(2)}, u32[]{:S(2)}) collective-permute-start(f32[2,520,128]{2,1,0:T(8,128)S(1)} %get-tuple-element.73), channel_id=1, source_target_pairs={{0,1},{1,0},{2,3},{3,2},{4,5},{5,4},{6,7},{7,6},{8,9},{9,8},{10,11... | collective-permute-start | bytes 1597448 | tf_op jit(solution)/shard_map/ppermute | solution.py:588
  10.9 1.1 shard_map.49
  12.8 1.1 shard_map.55
  14.6 1.1 shard_map.51
  15.9 2.0 %collective-permute-start.4 = (f32[520,128]{1,0:T(8,128)S(1)}, f32[520,128]{1,0:T(8,128)S(1)}, u32[]{:S(2)}, u32[]{:S(2)}) collective-permute-start(f32[520,128]{1,0:T(8,128)S(1)} %get-tuple-element.74.ready), channel_id=1, source_target_pairs={{0,4},{2,6},{4,0},{6,2},{8,12},{10,14},{12,8},{14,10},{1,5},{3,7},... | collective-permute-start | bytes 798728 | tf_op jit(solution)/shard_map/ppermute | solution.py:566
  17.9 0.9 collective-permute-start.8
  18.8 2.3 %collective-permute-start.9 = (f32[520,128]{1,0:T(8,128)S(1)}, f32[520,128]{1,0:T(8,128)S(1)}, u32[]{:S(2)}, u32[]{:S(2)}) collective-permute-start(f32[520,128]{1,0:T(8,128)S(1)} %get-tuple-element.80), channel_id=1, source_target_pairs={{0,12},{2,14},{4,8},{6,10},{8,4},{10,6},{12,0},{14,2},{1,13},{3,15... | collective-permute-start | bytes 798728 | tf_op jit(solution)/shard_map/ppermute | solution.py:566
  21.4 0.9 collective-permute-start.6
  22.6 14.2 %collective-permute-done.2.refs_1_ = f32[520,128]{1,0:T(8,128)S(1)} collective-permute-done((f32[520,128]{1,0:T(8,128)S(1)}, f32[520,128]{1,0:T(8,128)S(1)}, u32[]{:S(2)}, u32[]{:S(2)}) %collective-permute-start.2) | collective-permute-done | bytes 266272 | tf_op jit(solution)/shard_map/ppermute | solution.py:566
  36.8 4.3 %collective-permute-done.4.refs_2_ = f32[520,128]{1,0:T(8,128)S(1)} collective-permute-done((f32[520,128]{1,0:T(8,128)S(1)}, f32[520,128]{1,0:T(8,128)S(1)}, u32[]{:S(2)}, u32[]{:S(2)}) %collective-permute-start.4) | collective-permute-done | bytes 266272 | tf_op jit(solution)/shard_map/ppermute | solution.py:566
  41.2 5.7 %shard_map.53 = (f32[8192,128]{1,0:T(8,128)S(1)}, f32[64,128]{1,0:T(8,128)S(1)}, f32[64,128]{1,0:T(8,128)S(1)}) custom-call(s32[64,128]{1,0:T(8,128)S(1)} %get-tuple-element.60.acc_rows.ready, f32[64,128]{1,0:T(8,128)S(1)} %get-tuple-element.61.flag_rows, f32[8192,128]{1,0:T(8,128)S(1)} %shard_map.47.grouped, f32[520,128]{1,0:T(8,128)S(1)} %get-tuple-element.69.ready.refs_0_), custom_call_target="tpu_custom_call" | custom-call | flops 8000000000 | bytes 1000000 | tf_op jit(solution)/shard_map/pallas_call | solution.py:55
  46.9 1.2 collective-permute-done.10.refs_7_
  48.1 1.0 shard_map.57
  49.1 3.7 %collective-permute-start.11 = (f32[136,128]{1,0:T(8,128)S(1)}, f32[136,128]{1,0:T(8,128)S(1)}, u32[]{:S(2)}, u32[]{:S(2)}) collective-permute-start(f32[136,128]{1,0:T(8,128)S(1)} %get-tuple-element.83), channel_id=1, source_target_pairs={{0,16},{16,32},{32,48},{48,0},{1,17},{17,33},{33,49},{49,1},{2,18}... | collective-permute-start | bytes 208904 | tf_op jit(solution)/shard_map/ppermute | solution.py:607
  52.8 5.1 %collective-permute-start.12 = (f32[136,128]{1,0:T(8,128)S(1)}, f32[136,128]{1,0:T(8,128)S(1)}, u32[]{:S(2)}, u32[]{:S(2)}) collective-permute-start(f32[136,128]{1,0:T(8,128)S(1)} %get-tuple-element.84), channel_id=1, source_target_pairs={{0,32},{16,48},{32,0},{48,16},{1,33},{17,49},{33,1},{49,17},{2,34}... | collective-permute-start | bytes 208904 | tf_op jit(solution)/shard_map/ppermute | solution.py:607
  57.9 2.4 %collective-permute-start.13 = (f32[136,128]{1,0:T(8,128)S(1)}, f32[136,128]{1,0:T(8,128)S(1)}, u32[]{:S(2)}, u32[]{:S(2)}) collective-permute-start(f32[136,128]{1,0:T(8,128)S(1)} %get-tuple-element.85), channel_id=1, source_target_pairs={{0,48},{16,0},{32,16},{48,32},{1,49},{17,1},{33,17},{49,33},{2,50}... | collective-permute-start | bytes 208904 | tf_op jit(solution)/shard_map/ppermute | solution.py:607
  60.6 2.3 %collective-permute-done.13.r3 = f32[136,128]{1,0:T(8,128)S(1)} collective-permute-done((f32[136,128]{1,0:T(8,128)S(1)}, f32[136,128]{1,0:T(8,128)S(1)}, u32[]{:S(2)}, u32[]{:S(2)}) %collective-permute-start.13) | collective-permute-done | bytes 69664 | tf_op jit(solution)/shard_map/ppermute | solution.py:607
  63.2 3.2 %collective-permute-start.14 = (f32[136,128]{1,0:T(8,128)S(1)}, f32[136,128]{1,0:T(8,128)S(1)}, u32[]{:S(2)}, u32[]{:S(2)}) collective-permute-start(f32[136,128]{1,0:T(8,128)S(1)} %shard_map.58), channel_id=1, source_target_pairs={{0,64},{64,128},{128,192},{1,65},{65,129},{129,193},{2,66},{66,130... | collective-permute-start | bytes 208904 | tf_op jit(solution)/shard_map/ppermute | solution.py:611
  66.4 4.5 %collective-permute-start.15 = (f32[136,128]{1,0:T(8,128)S(1)}, f32[136,128]{1,0:T(8,128)S(1)}, u32[]{:S(2)}, u32[]{:S(2)}) collective-permute-start(f32[136,128]{1,0:T(8,128)S(1)} %shard_map.58), channel_id=1, source_target_pairs={{0,128},{64,192},{1,129},{65,193},{2,130},{66,194},{3,131},{67,195... | collective-permute-start | bytes 208904 | tf_op jit(solution)/shard_map/ppermute | solution.py:611
  71.0 1.3 collective-permute-start.16
  72.3 0.6 collective-permute-done.15.p2
  72.9 0.7 collective-permute-done.16.p3
  74.1 5.5 %collective-permute-start.17 = (f32[136,128]{1,0:T(8,128)S(1)}, f32[136,128]{1,0:T(8,128)S(1)}, u32[]{:S(2)}, u32[]{:S(2)}) collective-permute-start(f32[136,128]{1,0:T(8,128)S(1)} %get-tuple-element.87), channel_id=1, source_target_pairs={{0,48},{16,0},{32,16},{48,32},{1,49},{17,1},{33,17},{49,33},{2,50}... | collective-permute-start | bytes 208904 | tf_op jit(solution)/shard_map/ppermute | solution.py:617
  79.6 2.2 %collective-permute-start.19 = (f32[136,128]{1,0:T(8,128)S(1)}, f32[136,128]{1,0:T(8,128)S(1)}, u32[]{:S(2)}, u32[]{:S(2)}) collective-permute-start(f32[136,128]{1,0:T(8,128)S(1)} %get-tuple-element.89), channel_id=1, source_target_pairs={{0,16},{16,32},{32,48},{48,0},{1,17},{17,33},{33,49},{49,1},{2,18}... | collective-permute-start | bytes 208904 | tf_op jit(solution)/shard_map/ppermute | solution.py:617
  81.7 1.1 collective-permute-done.17.e1
  82.8 4.4 %collective-permute-done.18.e2 = f32[136,128]{1,0:T(8,128)S(1)} collective-permute-done((f32[136,128]{1,0:T(8,128)S(1)}, f32[136,128]{1,0:T(8,128)S(1)}, u32[]{:S(2)}, u32[]{:S(2)}) %collective-permute-start.18) | collective-permute-done | bytes 69664 | tf_op jit(solution)/shard_map/ppermute | solution.py:617
  87.2 0.9 shard_map.60
  88.1 0.8 collective-permute-start.20
  88.9 2.9 %collective-permute-start.21 = (f32[520,128]{1,0:T(8,128)S(1)}, f32[520,128]{1,0:T(8,128)S(1)}, u32[]{:S(2)}, u32[]{:S(2)}) collective-permute-start(f32[520,128]{1,0:T(8,128)S(1)} %get-tuple-element.98), channel_id=1, source_target_pairs={{0,12},{2,14},{4,8},{6,10},{8,4},{10,6},{12,0},{14,2},{1,13},{3,15... | collective-permute-start | bytes 798728 | tf_op jit(solution)/shard_map/ppermute | solution.py:566
  91.8 0.8 collective-permute-start.22
  92.6 5.0 %shard_map.61 = (f32[4096,128]{1,0:T(8,128)S(1)}, f32[32,128]{1,0:T(8,128)S(1)}, f32[32,128]{1,0:T(8,128)S(1)}, s32[32,128]{1,0:T(8,128)S(1)}) custom-call(s32[32,128]{1,0:T(8,128)S(1)} %get-tuple-element.59.slot_rows.slots, s32[32,128]{1,0:T(8,128)S(1)} %get-tuple-element.59.slot_rows.slots, s32[32,128]{1,0:T(8,128)S(1)} %bitcast.8, s32[32,128]{1,0:T(8,128)S(1)} %bitcast.4, ...), custom_call_target="tpu_custom_call" | custom-call | flops 10000000000 | bytes 1000000 | tf_op jit(solution)/shard_map/pallas_call | solution.py:55
  97.6 2.3 %collective-permute-done.20.refs_0_ = f32[520,128]{1,0:T(8,128)S(1)} collective-permute-done((f32[520,128]{1,0:T(8,128)S(1)}, f32[520,128]{1,0:T(8,128)S(1)}, u32[]{:S(2)}, u32[]{:S(2)}) %collective-permute-start.20) | collective-permute-done | bytes 266272 | tf_op jit(solution)/shard_map/ppermute | solution.py:566
  100.9 5.4 %collective-permute-start.27 = (f32[4,520,128]{2,1,0:T(8,128)S(1)}, f32[4,520,128]{2,1,0:T(8,128)S(1)}, u32[]{:S(2)}, u32[]{:S(2)}) collective-permute-start(f32[4,520,128]{2,1,0:T(8,128)S(1)} %get-tuple-element.107), channel_id=1, source_target_pairs={{0,1},{1,0},{2,3},{3,2},{4,5},{5,4},{6,7},{7,6},{8,9},{9,8},{10,11... | collective-permute-start | bytes 3194888 | tf_op jit(solution)/shard_map/ppermute | solution.py:648
  106.3 0.9 collective-permute-start.23
  107.2 0.8 collective-permute-start.24
  108.0 1.5 %collective-permute-start.25 = (f32[520,128]{1,0:T(8,128)S(1)}, f32[520,128]{1,0:T(8,128)S(1)}, u32[]{:S(2)}, u32[]{:S(2)}) collective-permute-start(f32[520,128]{1,0:T(8,128)S(1)} %get-tuple-element.104), channel_id=1, source_target_pairs={{0,2},{2,4},{4,6},{6,0},{8,10},{10,12},{12,14},{14,8},{1,3},{3,5},... | collective-permute-start | bytes 798728 | tf_op jit(solution)/shard_map/ppermute | solution.py:566
  109.5 0.7 collective-permute-start.26
  110.1 9.7 %collective-permute-done.23.refs_0_ = f32[520,128]{1,0:T(8,128)S(1)} collective-permute-done((f32[520,128]{1,0:T(8,128)S(1)}, f32[520,128]{1,0:T(8,128)S(1)}, u32[]{:S(2)}, u32[]{:S(2)}) %collective-permute-start.23) | collective-permute-done | bytes 266272 | tf_op jit(solution)/shard_map/ppermute | solution.py:566
  120.2 1.0 collective-permute-start.28
  121.2 1.2 collective-permute-done.26.refs_1_
  122.8 1.4 %collective-permute-start.29 = (f32[2,520,128]{2,1,0:T(8,128)S(1)}, f32[2,520,128]{2,1,0:T(8,128)S(1)}, u32[]{:S(2)}, u32[]{:S(2)}) collective-permute-start(f32[2,520,128]{2,1,0:T(8,128)S(1)} %get-tuple-element.111), channel_id=1, source_target_pairs={{0,1},{1,0},{2,3},{3,2},{4,5},{5,4},{6,7},{7,6},{8,9},{9,8},{10,11... | collective-permute-start | bytes 1597448 | tf_op jit(solution)/shard_map/ppermute | solution.py:648
  124.1 0.7 shard_map.65
  124.9 0.8 collective-permute-done.29.got2
  125.7 5.7 %shard_map.66 = (f32[16,520,128]{2,1,0:T(8,128)S(1)}, f32[4096,128]{1,0:T(8,128)}) custom-call(s32[32,128]{1,0:T(8,128)S(1)} %get-tuple-element.93.user_rows, f32[4096,128]{1,0:T(8,128)S(1)} %get-tuple-element.94.run, f32[32,128]{1,0:T(8,128)S(1)} %get-tuple-element.95.ready.count, ...), custom_call_target="tpu_custom_call", output_to_operand_aliasing={{0}: (7, {})} | custom-call | flops 1000000 | bytes 1000000 | tf_op jit(solution)/shard_map/pallas_call | solution.py:55
  (40 shorter events, 5.4 us)
Async XLA Ops:
  0.8 1.6 %copy-start.2 = (f32[4096,128]{1,0:T(8,128)S(1)}, f32[4096,128]{1,0:T(8,128)}, u32[]{:S(2)}) copy-start(f32[4096,128]{1,0:T(8,128)} %features.1) | copy-start | bytes 6291460
  7.6 4.8 %collective-permute-start.3 = (f32[2,520,128]{2,1,0:T(8,128)S(1)}, f32[2,520,128]{2,1,0:T(8,128)S(1)}, u32[]{:S(2)}, u32[]{:S(2)}) collective-permute-start(f32[2,520,128]{2,1,0:T(8,128)S(1)} %get-tuple-element.73), channel_id=1, source_target_pairs={{0,1},{1,0},{2,3},{3,2},{4,5},{5,4},{6,7},{7,6},{8,9},{9,8},{10,11... | collective-permute-start | bytes 1597448 | tf_op jit(solution)/shard_map/ppermute | solution.py:588
  12.0 2.3 %collective-permute-start = (f32[2,520,128]{2,1,0:T(8,128)S(1)}, f32[2,520,128]{2,1,0:T(8,128)S(1)}, u32[]{:S(2)}, u32[]{:S(2)}) collective-permute-start(f32[2,520,128]{2,1,0:T(8,128)S(1)} %get-tuple-element.65), channel_id=1, source_target_pairs={{0,1},{1,0},{2,3},{3,2},{4,5},{5,4},{6,7},{7,6},{8,9},{9,8},{10,11... | collective-permute-start | bytes 1597448 | tf_op jit(solution)/shard_map/ppermute | solution.py:588
  13.9 5.0 %collective-permute-start.5 = (f32[2,520,128]{2,1,0:T(8,128)S(1)}, f32[2,520,128]{2,1,0:T(8,128)S(1)}, u32[]{:S(2)}, u32[]{:S(2)}) collective-permute-start(f32[2,520,128]{2,1,0:T(8,128)S(1)} %get-tuple-element.76), channel_id=1, source_target_pairs={{0,1},{1,0},{2,3},{3,2},{4,5},{5,4},{6,7},{7,6},{8,9},{9,8},{10,11... | collective-permute-start | bytes 1597448 | tf_op jit(solution)/shard_map/ppermute | solution.py:588
  15.7 5.7 %collective-permute-start.1 = (f32[2,520,128]{2,1,0:T(8,128)S(1)}, f32[2,520,128]{2,1,0:T(8,128)S(1)}, u32[]{:S(2)}, u32[]{:S(2)}) collective-permute-start(f32[2,520,128]{2,1,0:T(8,128)S(1)} %get-tuple-element.68), channel_id=1, source_target_pairs={{0,1},{1,0},{2,3},{3,2},{4,5},{5,4},{6,7},{7,6},{8,9},{9,8},{10,11... | collective-permute-start | bytes 1597448 | tf_op jit(solution)/shard_map/ppermute | solution.py:588
  15.9 20.9 %collective-permute-start.2 = (f32[520,128]{1,0:T(8,128)S(1)}, f32[520,128]{1,0:T(8,128)S(1)}, u32[]{:S(2)}, u32[]{:S(2)}) collective-permute-start(f32[520,128]{1,0:T(8,128)S(1)} %get-tuple-element.66.ready), channel_id=1, source_target_pairs={{0,2},{2,4},{4,6},{6,0},{8,10},{10,12},{12,14},{14,8},{1,3},{3,5},... | collective-permute-start | bytes 798728 | tf_op jit(solution)/shard_map/ppermute | solution.py:566
  15.9 25.2 %collective-permute-start.4 = (f32[520,128]{1,0:T(8,128)S(1)}, f32[520,128]{1,0:T(8,128)S(1)}, u32[]{:S(2)}, u32[]{:S(2)}) collective-permute-start(f32[520,128]{1,0:T(8,128)S(1)} %get-tuple-element.74.ready), channel_id=1, source_target_pairs={{0,4},{2,6},{4,0},{6,2},{8,12},{10,14},{12,8},{14,10},{1,5},{3,7},... | collective-permute-start | bytes 798728 | tf_op jit(solution)/shard_map/ppermute | solution.py:566
  17.9 29.0 %collective-permute-start.8 = (f32[520,128]{1,0:T(8,128)S(1)}, f32[520,128]{1,0:T(8,128)S(1)}, u32[]{:S(2)}, u32[]{:S(2)}) collective-permute-start(f32[520,128]{1,0:T(8,128)S(1)} %get-tuple-element.79), channel_id=1, source_target_pairs={{0,10},{2,12},{4,14},{6,8},{8,2},{10,4},{12,6},{14,0},{1,11},{3,13... | collective-permute-start | bytes 798728 | tf_op jit(solution)/shard_map/ppermute | solution.py:566
  18.8 28.0 %collective-permute-start.9 = (f32[520,128]{1,0:T(8,128)S(1)}, f32[520,128]{1,0:T(8,128)S(1)}, u32[]{:S(2)}, u32[]{:S(2)}) collective-permute-start(f32[520,128]{1,0:T(8,128)S(1)} %get-tuple-element.80), channel_id=1, source_target_pairs={{0,12},{2,14},{4,8},{6,10},{8,4},{10,6},{12,0},{14,2},{1,13},{3,15... | collective-permute-start | bytes 798728 | tf_op jit(solution)/shard_map/ppermute | solution.py:566
  21.4 25.5 %collective-permute-start.6 = (f32[520,128]{1,0:T(8,128)S(1)}, f32[520,128]{1,0:T(8,128)S(1)}, u32[]{:S(2)}, u32[]{:S(2)}) collective-permute-start(f32[520,128]{1,0:T(8,128)S(1)} %get-tuple-element.77), channel_id=1, source_target_pairs={{0,6},{2,0},{4,2},{6,4},{8,14},{10,8},{12,10},{14,12},{1,7},{3,1},... | collective-permute-start | bytes 798728 | tf_op jit(solution)/shard_map/ppermute | solution.py:566
  36.8 10.1 %collective-permute-start.7 = (f32[520,128]{1,0:T(8,128)S(1)}, f32[520,128]{1,0:T(8,128)S(1)}, u32[]{:S(2)}, u32[]{:S(2)}) collective-permute-start(f32[520,128]{1,0:T(8,128)S(1)} %get-tuple-element.78), channel_id=1, source_target_pairs={{0,8},{2,10},{4,12},{6,14},{8,0},{10,2},{12,4},{14,6},{1,9},{3,11}... | collective-permute-start | bytes 798728 | tf_op jit(solution)/shard_map/ppermute | solution.py:566
  41.2 6.9 %collective-permute-start.10 = (f32[520,128]{1,0:T(8,128)S(1)}, f32[520,128]{1,0:T(8,128)S(1)}, u32[]{:S(2)}, u32[]{:S(2)}) collective-permute-start(f32[520,128]{1,0:T(8,128)S(1)} %get-tuple-element.81), channel_id=1, source_target_pairs={{0,14},{2,8},{4,10},{6,12},{8,6},{10,0},{12,2},{14,4},{1,15},{3,9}... | collective-permute-start | bytes 798728 | tf_op jit(solution)/shard_map/ppermute | solution.py:566
  49.1 43.5 %copy-start = (s32[4096]{0:T(1024)S(1)}, s32[4096]{0:T(1024)}, u32[]{:S(2)}) copy-start(s32[4096]{0:T(1024)} %param.6) | copy-start | bytes 49156
  49.1 43.5 %copy-start.1 = (s32[4096,1]{0,1:T(1,128)S(1)}, s32[4096,1]{0,1:T(1,128)}, u32[]{:S(2)}) copy-start(s32[4096,1]{0,1:T(1,128)} %param.5) | copy-start | bytes 49156
  49.1 11.2 %collective-permute-start.11 = (f32[136,128]{1,0:T(8,128)S(1)}, f32[136,128]{1,0:T(8,128)S(1)}, u32[]{:S(2)}, u32[]{:S(2)}) collective-permute-start(f32[136,128]{1,0:T(8,128)S(1)} %get-tuple-element.83), channel_id=1, source_target_pairs={{0,16},{16,32},{32,48},{48,0},{1,17},{17,33},{33,49},{49,1},{2,18}... | collective-permute-start | bytes 208904 | tf_op jit(solution)/shard_map/ppermute | solution.py:607
  52.8 7.8 %collective-permute-start.12 = (f32[136,128]{1,0:T(8,128)S(1)}, f32[136,128]{1,0:T(8,128)S(1)}, u32[]{:S(2)}, u32[]{:S(2)}) collective-permute-start(f32[136,128]{1,0:T(8,128)S(1)} %get-tuple-element.84), channel_id=1, source_target_pairs={{0,32},{16,48},{32,0},{48,16},{1,33},{17,49},{33,1},{49,17},{2,34}... | collective-permute-start | bytes 208904 | tf_op jit(solution)/shard_map/ppermute | solution.py:607
  57.9 5.0 %collective-permute-start.13 = (f32[136,128]{1,0:T(8,128)S(1)}, f32[136,128]{1,0:T(8,128)S(1)}, u32[]{:S(2)}, u32[]{:S(2)}) collective-permute-start(f32[136,128]{1,0:T(8,128)S(1)} %get-tuple-element.85), channel_id=1, source_target_pairs={{0,48},{16,0},{32,16},{48,32},{1,49},{17,1},{33,17},{49,33},{2,50}... | collective-permute-start | bytes 208904 | tf_op jit(solution)/shard_map/ppermute | solution.py:607
  63.2 9.1 %collective-permute-start.14 = (f32[136,128]{1,0:T(8,128)S(1)}, f32[136,128]{1,0:T(8,128)S(1)}, u32[]{:S(2)}, u32[]{:S(2)}) collective-permute-start(f32[136,128]{1,0:T(8,128)S(1)} %shard_map.58), channel_id=1, source_target_pairs={{0,64},{64,128},{128,192},{1,65},{65,129},{129,193},{2,66},{66,130... | collective-permute-start | bytes 208904 | tf_op jit(solution)/shard_map/ppermute | solution.py:611
  66.4 6.5 %collective-permute-start.15 = (f32[136,128]{1,0:T(8,128)S(1)}, f32[136,128]{1,0:T(8,128)S(1)}, u32[]{:S(2)}, u32[]{:S(2)}) collective-permute-start(f32[136,128]{1,0:T(8,128)S(1)} %shard_map.58), channel_id=1, source_target_pairs={{0,128},{64,192},{1,129},{65,193},{2,130},{66,194},{3,131},{67,195... | collective-permute-start | bytes 208904 | tf_op jit(solution)/shard_map/ppermute | solution.py:611
  71.0 2.7 %collective-permute-start.16 = (f32[136,128]{1,0:T(8,128)S(1)}, f32[136,128]{1,0:T(8,128)S(1)}, u32[]{:S(2)}, u32[]{:S(2)}) collective-permute-start(f32[136,128]{1,0:T(8,128)S(1)} %shard_map.58), channel_id=1, source_target_pairs={{0,192},{1,193},{2,194},{3,195},{4,196},{5,197},{6,198},{7,199},{8... | collective-permute-start | bytes 208904 | tf_op jit(solution)/shard_map/ppermute | solution.py:611
  74.1 8.7 %collective-permute-start.17 = (f32[136,128]{1,0:T(8,128)S(1)}, f32[136,128]{1,0:T(8,128)S(1)}, u32[]{:S(2)}, u32[]{:S(2)}) collective-permute-start(f32[136,128]{1,0:T(8,128)S(1)} %get-tuple-element.87), channel_id=1, source_target_pairs={{0,48},{16,0},{32,16},{48,32},{1,49},{17,1},{33,17},{49,33},{2,50}... | collective-permute-start | bytes 208904 | tf_op jit(solution)/shard_map/ppermute | solution.py:617
  79.6 7.7 %collective-permute-start.18 = (f32[136,128]{1,0:T(8,128)S(1)}, f32[136,128]{1,0:T(8,128)S(1)}, u32[]{:S(2)}, u32[]{:S(2)}) collective-permute-start(f32[136,128]{1,0:T(8,128)S(1)} %get-tuple-element.88), channel_id=1, source_target_pairs={{0,32},{16,48},{32,0},{48,16},{1,33},{17,49},{33,1},{49,17},{2,34}... | collective-permute-start | bytes 208904 | tf_op jit(solution)/shard_map/ppermute | solution.py:617
  79.6 7.7 %collective-permute-start.19 = (f32[136,128]{1,0:T(8,128)S(1)}, f32[136,128]{1,0:T(8,128)S(1)}, u32[]{:S(2)}, u32[]{:S(2)}) collective-permute-start(f32[136,128]{1,0:T(8,128)S(1)} %get-tuple-element.89), channel_id=1, source_target_pairs={{0,16},{16,32},{32,48},{48,0},{1,17},{17,33},{33,49},{49,1},{2,18}... | collective-permute-start | bytes 208904 | tf_op jit(solution)/shard_map/ppermute | solution.py:617
  88.1 11.7 %collective-permute-start.20 = (f32[520,128]{1,0:T(8,128)S(1)}, f32[520,128]{1,0:T(8,128)S(1)}, u32[]{:S(2)}, u32[]{:S(2)}) collective-permute-start(f32[520,128]{1,0:T(8,128)S(1)} %get-tuple-element.97), channel_id=1, source_target_pairs={{0,4},{2,6},{4,0},{6,2},{8,12},{10,14},{12,8},{14,10},{1,5},{3,7},... | collective-permute-start | bytes 798728 | tf_op jit(solution)/shard_map/ppermute | solution.py:566
  88.9 11.0 %collective-permute-start.21 = (f32[520,128]{1,0:T(8,128)S(1)}, f32[520,128]{1,0:T(8,128)S(1)}, u32[]{:S(2)}, u32[]{:S(2)}) collective-permute-start(f32[520,128]{1,0:T(8,128)S(1)} %get-tuple-element.98), channel_id=1, source_target_pairs={{0,12},{2,14},{4,8},{6,10},{8,4},{10,6},{12,0},{14,2},{1,13},{3,15... | collective-permute-start | bytes 798728 | tf_op jit(solution)/shard_map/ppermute | solution.py:566
  91.8 8.6 %collective-permute-start.22 = (f32[520,128]{1,0:T(8,128)S(1)}, f32[520,128]{1,0:T(8,128)S(1)}, u32[]{:S(2)}, u32[]{:S(2)}) collective-permute-start(f32[520,128]{1,0:T(8,128)S(1)} %get-tuple-element.99), channel_id=1, source_target_pairs={{0,8},{2,10},{4,12},{6,14},{8,0},{10,2},{12,4},{14,6},{1,9},{3,11}... | collective-permute-start | bytes 798728 | tf_op jit(solution)/shard_map/ppermute | solution.py:566
  100.9 23.2 %collective-permute-start.27 = (f32[4,520,128]{2,1,0:T(8,128)S(1)}, f32[4,520,128]{2,1,0:T(8,128)S(1)}, u32[]{:S(2)}, u32[]{:S(2)}) collective-permute-start(f32[4,520,128]{2,1,0:T(8,128)S(1)} %get-tuple-element.107), channel_id=1, source_target_pairs={{0,1},{1,0},{2,3},{3,2},{4,5},{5,4},{6,7},{7,6},{8,9},{9,8},{10,11... | collective-permute-start | bytes 3194888 | tf_op jit(solution)/shard_map/ppermute | solution.py:648
  106.3 13.6 %collective-permute-start.23 = (f32[520,128]{1,0:T(8,128)S(1)}, f32[520,128]{1,0:T(8,128)S(1)}, u32[]{:S(2)}, u32[]{:S(2)}) collective-permute-start(f32[520,128]{1,0:T(8,128)S(1)} %get-tuple-element.101), channel_id=1, source_target_pairs={{0,6},{2,0},{4,2},{6,4},{8,14},{10,8},{12,10},{14,12},{1,7},{3,1},... | collective-permute-start | bytes 798728 | tf_op jit(solution)/shard_map/ppermute | solution.py:566
  107.2 12.7 %collective-permute-start.24 = (f32[520,128]{1,0:T(8,128)S(1)}, f32[520,128]{1,0:T(8,128)S(1)}, u32[]{:S(2)}, u32[]{:S(2)}) collective-permute-start(f32[520,128]{1,0:T(8,128)S(1)} %get-tuple-element.102), channel_id=1, source_target_pairs={{0,14},{2,8},{4,10},{6,12},{8,6},{10,0},{12,2},{14,4},{1,15},{3,9}... | collective-permute-start | bytes 798728 | tf_op jit(solution)/shard_map/ppermute | solution.py:566
  108.0 13.2 %collective-permute-start.25 = (f32[520,128]{1,0:T(8,128)S(1)}, f32[520,128]{1,0:T(8,128)S(1)}, u32[]{:S(2)}, u32[]{:S(2)}) collective-permute-start(f32[520,128]{1,0:T(8,128)S(1)} %get-tuple-element.104), channel_id=1, source_target_pairs={{0,2},{2,4},{4,6},{6,0},{8,10},{10,12},{12,14},{14,8},{1,3},{3,5},... | collective-permute-start | bytes 798728 | tf_op jit(solution)/shard_map/ppermute | solution.py:566
  109.5 13.0 %collective-permute-start.26 = (f32[520,128]{1,0:T(8,128)S(1)}, f32[520,128]{1,0:T(8,128)S(1)}, u32[]{:S(2)}, u32[]{:S(2)}) collective-permute-start(f32[520,128]{1,0:T(8,128)S(1)} %get-tuple-element.105), channel_id=1, source_target_pairs={{0,10},{2,12},{4,14},{6,8},{8,2},{10,4},{12,6},{14,0},{1,11},{3,13... | collective-permute-start | bytes 798728 | tf_op jit(solution)/shard_map/ppermute | solution.py:566
  120.2 4.7 %collective-permute-start.28 = (f32[2,520,128]{2,1,0:T(8,128)S(1)}, f32[2,520,128]{2,1,0:T(8,128)S(1)}, u32[]{:S(2)}, u32[]{:S(2)}) collective-permute-start(f32[2,520,128]{2,1,0:T(8,128)S(1)} %get-tuple-element.110), channel_id=1, source_target_pairs={{0,1},{1,0},{2,3},{3,2},{4,5},{5,4},{6,7},{7,6},{8,9},{9,8},{10,11... | collective-permute-start | bytes 1597448 | tf_op jit(solution)/shard_map/ppermute | solution.py:648
  122.8 2.9 %collective-permute-start.29 = (f32[2,520,128]{2,1,0:T(8,128)S(1)}, f32[2,520,128]{2,1,0:T(8,128)S(1)}, u32[]{:S(2)}, u32[]{:S(2)}) collective-permute-start(f32[2,520,128]{2,1,0:T(8,128)S(1)} %get-tuple-element.111), channel_id=1, source_target_pairs={{0,1},{1,0},{2,3},{3,2},{4,5},{5,4},{6,7},{7,6},{8,9},{9,8},{10,11... | collective-permute-start | bytes 1597448 | tf_op jit(solution)/shard_map/ppermute | solution.py:648

commit v8 on v7

--- a/solution.py
+++ b/solution.py
@@ -81,19 +81,16 @@
 
 
 def chunk_of(dz, dx):
-    row = jnp.where(PLACE[2] == 0, dz, 1 - dz)
-    return row * NX + lax.rem(PLACE[1] + dx, NX)
-
-
-def rank_kernel(events, slot_out, acc_out, flag_out, cleared):
+    return (PLACE[2] ^ dz) * NX + (PLACE[1] ^ dx)
+
+
+def rank_kernel(events, slot_out, acc_out, flag_out):
     lines = slot_out.shape[0]
-    zero = jnp.zeros((LANES, LANES), F32)
     below = as_bf16(iota((LANES, LANES), 0) < iota((LANES, LANES), 1))
     with_total = jnp.concatenate([below, jnp.ones((LANES, LANES), BF16)], axis=1)
     owner_ids = iota((OWNERS, LANES), 0)
     before = jnp.zeros((OWNERS, LANES), F32)
     codes = jnp.zeros((OWNERS, LANES), F32)
-    each = cleared.shape[0] // LANES // lines
     step = 8
     for b in range(0, lines, step):
         homes = [events[b + i : b + i + 1, :] for i in range(step)]
@@ -115,17 +112,21 @@
         codes = codes + dot_nt(
             jnp.concatenate(coded, axis=1), jnp.concatenate(rank_of, axis=1)
         )
-        for i in range(step * each):
-            at = (b * each + i) * LANES
-            cleared[at : at + LANES, :] = zero
     code_ids = codes.astype(I32) - 1
     acc_out[...] = jnp.right_shift(code_ids, 1)
     flag_out[...] = jnp.where(code_ids >= 0, jnp.bitwise_and(code_ids, 1), 0).astype(F32)
 
 
-def spread_kernel(slot_rows, features, cleared, grouped, slots, sem):
+def spread_kernel(slot_rows, features, grouped, slots, sem):
     copy = pltpu.make_async_copy(slot_rows, slots, sem)
     copy.start()
+    zero = jnp.zeros((LANES, LANES), F32)
+
+    def clear(o, _):
+        grouped[pl.ds(pl.multiple_of(o * LANES, LANES), LANES), :] = zero
+        return 0
+
+    lax.fori_loop(0, OWNERS, clear, 0)
     copy.wait()
 
     def spread(b, _):
@@ -298,7 +299,7 @@
         @pl.when(PLACE[1] == x)
         def _(x=x):
             for dz in range(NL):
-                order = [tables[dz][(x - j) % NX] for j in range(NX)]
+                order = [tables[dz][x ^ j] for j in range(NX)]
                 tails = [t[TAIL:, :] for t in order]
                 keep = [keep_of(t) for t in tails]
                 for i in range(FOUR):
@@ -328,7 +329,7 @@
             jnp.where(sub == 1, tail[FOUR + i : FOUR + i + 1, :], 0.0),
         )
     for r in range(NH):
-        outs[r][...] = pair[lax.rem(PLACE[3] + r, NH)]
+        outs[r][...] = pair[PLACE[3] ^ r]
 
 
 def plane_kernel(r0, r1, r2, r3, out):
@@ -339,7 +340,7 @@
         def _(h=h):
             total = rows[h][...]
             for j in range(1, NH):
-                total = joined_one(total, rows[(h - j) % NH][...])
+                total = joined_one(total, rows[h ^ j][...])
             out[...] = total
 
 
@@ -354,7 +355,7 @@
         def _(h=h):
             state = start
             for j in range(NH):
-                k = (h - j) % NH
+                k = h ^ j
                 outs[k][...] = state
                 if j < NH - 1:
                     state = joined_one(state, rows[k][...])
@@ -364,7 +365,7 @@
     tables, outs = (refs[:NX], refs[NX : 2 * NX]), (refs[2 * NX : 3 * NX], refs[3 * NX : 4 * NX])
     came = refs[-1]
     for r, e in enumerate((e0, e1, e2, e3)):
-        came[lax.rem(PLACE[3] + r, NH)] = e[...]
+        came[PLACE[3] ^ r] = e[...]
     first = PLACE[2] == 0
     sub = iota((8, LANES), 0)
     tail0 = jnp.zeros((8, LANES), F32)
@@ -378,7 +379,7 @@
         @pl.when(PLACE[1] == x)
         def _(x=x):
             for dz in range(NL):
-                order = [(x - j) % NX for j in range(NX)]
+                order = [x ^ j for j in range(NX)]
                 tails = [tables[dz][k][TAIL:, :] for k in order[:-1]]
                 keeps = [keep_of(t) for t in tails]
                 late = first if dz else jnp.logical_not(first)
@@ -501,32 +502,31 @@
     for copy in (*copies, listed):
         copy.wait()
 
-    def pick(b, _):
-        for j in range(LANES):
-            picked[pl.ds(b * LANES + j, 1), :] = flat[pl.ds(users[b, j], 1), :]
-        return 0
-
-    lax.fori_loop(0, lines, pick, 0)
-    group = lines // 8
-    leaving = []
-    for b in range(lines):
-        at = pl.ds(b * LANES, LANES)
-        factor = jnp.broadcast_to(scale[:, b : b + 1], (LANES, LANES))
-        picked[at, :] = (run[at, :] + picked[at, :]) * factor
-        if b % group == group - 1:
-            rows = pl.ds((b - group + 1) * LANES, group * LANES)
-            leaving.append(
-                pltpu.make_async_copy(
-                    picked.at[rows, :], out.at[rows, :], out_sems.at[len(leaving)]
-                )
-            )
-            leaving[-1].start()
-    for copy in leaving:
-        copy.wait()
-
-
-def ring(n, k):
-    return [(i, (i + k) % n) for i in range(n)]
+    group = 4
+
+    def leave(g):
+        rows = pl.ds(pl.multiple_of(g * group * LANES, group * LANES), group * LANES)
+        return pltpu.make_async_copy(picked.at[rows, :], out.at[rows, :], out_sems.at[g])
+
+    def lines_of(g, scale):
+        for b in range(group):
+            for j in range(LANES):
+                at = (g * group + b) * LANES + j
+                picked[pl.ds(at, 1), :] = flat[pl.ds(users[g * group + b, j], 1), :]
+        for b in range(group):
+            at = pl.ds(pl.multiple_of((g * group + b) * LANES, LANES), LANES)
+            factor = jnp.broadcast_to(scale[:, b : b + 1], (LANES, LANES))
+            picked[at, :] = (run[at, :] + picked[at, :]) * factor
+        leave(g).start()
+        return pltpu.roll(scale, LANES - group, 1)
+
+    lax.fori_loop(0, lines // group, lines_of, scale)
+    for g in range(lines // group):
+        leave(g).wait()
+
+
+def swapped(n, k):
+    return [(i, i ^ k) for i in range(n)]
 
 
 def body(features, home, account, flags):
@@ -539,9 +539,9 @@
     small_f = jax.ShapeDtypeStruct((lines, LANES), F32)
     by_owner = functools.partial(jax.ShapeDtypeStruct, (OWNERS, LANES))
     by_slot = jax.ShapeDtypeStruct((OWNERS * LANES, LANES), F32)
-    slot, acc_rows, flag_rows, cleared = call(
+    slot, acc_rows, flag_rows = call(
         rank_kernel,
-        [small, by_owner(I32), by_owner(F32), by_slot],
+        [small, by_owner(I32), by_owner(F32)],
         (jnp.concatenate([home, account, flags]),),
         [VMEM],
         cost=2_000_000_000,
@@ -549,21 +549,17 @@
     grouped = call(
         spread_kernel,
         by_slot,
-        (slot, features, cleared),
-        [VMEM] * 3,
+        (slot, features),
+        [VMEM] * 2,
         scratch=[pltpu.SMEM((lines, LANES), I32), pltpu.SemaphoreType.DMA],
         cost=4_000_000_000,
-        aliases={2: 0},
-    )
-    swap = ring(NC, 1)
+    )
+    swap = swapped(NC, 1)
 
     def exchange(v, dz, dx):
         if dz == 0 and dx == 0:
             return v
-        pairs = [
-            (row * NX + x, (row ^ dz) * NX + (x + dx) % NX) for row in range(NL) for x in range(NX)
-        ]
-        return lax.ppermute(v, ("l", "x"), pairs)
+        return lax.ppermute(v, ("l", "x"), swapped(NL * NX, dz * NX + dx))
 
     order = (2, 1, 3, 0)
     mine, got = [None] * NX, [None] * NX
@@ -604,7 +600,7 @@
     )
     rows_got = list(pairs)
     for r in (1, 3, 2):
-        rows_got[r] = lax.ppermute(pairs[r], "h", ring(NH, r))
+        rows_got[r] = lax.ppermute(pairs[r], "h", swapped(NH, r))
     plane = call(plane_kernel, one_block(), tuple(rows_got), [VMEM] * NH)
     ny = lax.axis_size("y")
     planes = [
@@ -614,7 +610,7 @@
                 [VMEM] * (3 + NH))
     came = list(came)
     for r in (1, 3, 2):
-        came[r] = lax.ppermute(came[r], "h", ring(NH, -r))
+        came[r] = lax.ppermute(came[r], "h", swapped(NH, r))
     parts = call(
         chips_back_kernel,
         [block()] * (NL * NX),
@@ -626,7 +622,7 @@
     kept = parts[0][0]
     for dx in (2, 0, 1, 3):
         for dz in reversed(range(NL)):
-            parts[dz][dx] = exchange(parts[dz][dx], dz, (NX - dx) % NX)
+            parts[dz][dx] = exchange(parts[dz][dx], dz, dx)
     run, count, is_open, users = call(
         in_time_kernel,
         [jax.ShapeDtypeStruct((rows, LANES), F32), small_f, small_f, small],

time: 132 us -> 132 us (level)
  transfers between devices with their start and end apart: 30 -> 30, of which waited for: 15 -> 13; matrix products, arithmetic and copies ran while one was open for 0% -> 0% of each run, Pallas kernels for 13% -> 12%
where the time goes in v8:
time: 132 us
  starting transfers between devices  54.2 us (41%)
  waiting for transfers between devices  44.3 us (34%)
  Pallas kernels  31.6 us (24%)
    pallas_call x21, Pallas kernels, call(): pl.pallas_call(kernel, out_shape=out, in_specs=specs, out_specs=out_specs...  31.6 us
    ppermute x14, waiting for transfers between devices, exchange(): return lax.ppermute(v, ('l', 'x'), swapped(NL * NX, dz * NX + dx))  31.5 us
    ppermute x14, starting transfers between devices, exchange(): return lax.ppermute(v, ('l', 'x'), swapped(NL * NX, dz * NX + dx))  17.6 us
    ppermute x3, starting transfers between devices, body(): lax.ppermute(plane, 'y', [(i, i + r) for i in range(ny - r)])  9.03 us
    ppermute x3, starting transfers between devices, body(): last.append(lax.ppermute(send, 'c', swap))  8.6 us
    ppermute x3, starting transfers between devices, body(): rows_got[r] = lax.ppermute(pairs[r], 'h', swapped(NH, r))  8.19 us
    ppermute x3, starting transfers between devices, body(): came[r] = lax.ppermute(came[r], 'h', swapped(NH, r))  6.72 us
    ppermute x3, waiting for transfers between devices, body(): rows_got[r] = lax.ppermute(pairs[r], 'h', swapped(NH, r))  6.04 us
  transfers between devices with their start and end apart: 30, of which 13 were waited for; matrix products, arithmetic and copies ran while one was open for 0% of the time, Pallas kernels for 12%

profile of v8, /device:TPU:1, one launch (start us, length us, event | category | flops | bytes accessed | tf_op | source)
XLA Modules:
  0.0 131.8 jit_solution(7692942561888000878)
XLA Ops:
  0.0 0.8 pad_add_fusion.events
  0.8 1.0 shard_map.46
  1.8 0.5 copy-done.2
  2.3 4.2 %shard_map.47.grouped = f32[8192,128]{1,0:T(8,128)S(1)} custom-call(s32[32,128]{1,0:T(8,128)S(1)} %get-tuple-element.58.slot_rows.slots, f32[4096,128]{1,0:T(8,128)S(1)} %copy-done.2), custom_call_target="tpu_custom_call" | custom-call | flops 4000000000 | bytes 1000000 | tf_op jit(solution)/shard_map/pallas_call | solution.py:55
  6.5 1.1 shard_map.48
  7.6 3.3 %collective-permute-start.3 = (f32[2,520,128]{2,1,0:T(8,128)S(1)}, f32[2,520,128]{2,1,0:T(8,128)S(1)}, u32[]{:S(2)}, u32[]{:S(2)}) collective-permute-start(f32[2,520,128]{2,1,0:T(8,128)S(1)} %get-tuple-element.71), channel_id=1, source_target_pairs={{0,1},{1,0},{2,3},{3,2},{4,5},{5,4},{6,7},{7,6},{8,9},{9,8},{10,11... | collective-permute-start | bytes 1597448 | tf_op jit(solution)/shard_map/ppermute | solution.py:584
  10.9 1.1 shard_map.49
  12.8 1.1 shard_map.55
  14.6 1.1 shard_map.51
  15.9 1.9 %collective-permute-start.4 = (f32[520,128]{1,0:T(8,128)S(1)}, f32[520,128]{1,0:T(8,128)S(1)}, u32[]{:S(2)}, u32[]{:S(2)}) collective-permute-start(f32[520,128]{1,0:T(8,128)S(1)} %get-tuple-element.72.ready), channel_id=1, source_target_pairs={{0,4},{2,6},{4,0},{6,2},{8,12},{10,14},{12,8},{14,10},{1,5},{3,7},... | collective-permute-start | bytes 798728 | tf_op jit(solution)/shard_map/ppermute | solution.py:562
  17.9 1.3 collective-permute-start.8
  19.2 2.7 %collective-permute-start.9 = (f32[520,128]{1,0:T(8,128)S(1)}, f32[520,128]{1,0:T(8,128)S(1)}, u32[]{:S(2)}, u32[]{:S(2)}) collective-permute-start(f32[520,128]{1,0:T(8,128)S(1)} %get-tuple-element.78), channel_id=1, source_target_pairs={{0,12},{2,14},{4,8},{6,10},{8,4},{10,6},{12,0},{14,2},{1,13},{3,15... | collective-permute-start | bytes 798728 | tf_op jit(solution)/shard_map/ppermute | solution.py:562
  22.2 0.9 collective-permute-start.6
  23.3 11.6 %collective-permute-done.2.refs_1_ = f32[520,128]{1,0:T(8,128)S(1)} collective-permute-done((f32[520,128]{1,0:T(8,128)S(1)}, f32[520,128]{1,0:T(8,128)S(1)}, u32[]{:S(2)}, u32[]{:S(2)}) %collective-permute-start.2) | collective-permute-done | bytes 266272 | tf_op jit(solution)/shard_map/ppermute | solution.py:562
  34.9 6.2 %collective-permute-done.4.refs_2_ = f32[520,128]{1,0:T(8,128)S(1)} collective-permute-done((f32[520,128]{1,0:T(8,128)S(1)}, f32[520,128]{1,0:T(8,128)S(1)}, u32[]{:S(2)}, u32[]{:S(2)}) %collective-permute-start.4) | collective-permute-done | bytes 266272 | tf_op jit(solution)/shard_map/ppermute | solution.py:562
  41.1 1.5 %collective-permute-start.10 = (f32[520,128]{1,0:T(8,128)S(1)}, f32[520,128]{1,0:T(8,128)S(1)}, u32[]{:S(2)}, u32[]{:S(2)}) collective-permute-start(f32[520,128]{1,0:T(8,128)S(1)} %get-tuple-element.79), channel_id=1, source_target_pairs={{0,14},{2,12},{4,10},{6,8},{8,6},{10,4},{12,2},{14,0},{1,15},{3,13... | collective-permute-start | bytes 798728 | tf_op jit(solution)/shard_map/ppermute | solution.py:562
  42.7 5.7 %shard_map.53 = (f32[8192,128]{1,0:T(8,128)S(1)}, f32[64,128]{1,0:T(8,128)S(1)}, f32[64,128]{1,0:T(8,128)S(1)}) custom-call(s32[64,128]{1,0:T(8,128)S(1)} %get-tuple-element.59.acc_rows.ready, f32[64,128]{1,0:T(8,128)S(1)} %get-tuple-element.60.flag_rows, f32[8192,128]{1,0:T(8,128)S(1)} %shard_map.47.grouped, f32[520,128]{1,0:T(8,128)S(1)} %get-tuple-element.67.ready.refs_0_), custom_call_target="tpu_custom_call" | custom-call | flops 8000000000 | bytes 1000000 | tf_op jit(solution)/shard_map/pallas_call | solution.py:55
  48.4 1.5 %collective-permute-done.10.refs_7_ = f32[520,128]{1,0:T(8,128)S(1)} collective-permute-done((f32[520,128]{1,0:T(8,128)S(1)}, f32[520,128]{1,0:T(8,128)S(1)}, u32[]{:S(2)}, u32[]{:S(2)}) %collective-permute-start.10) | collective-permute-done | bytes 266272 | tf_op jit(solution)/shard_map/ppermute | solution.py:562
  49.9 1.0 shard_map.57
  50.9 3.1 %collective-permute-start.11 = (f32[136,128]{1,0:T(8,128)S(1)}, f32[136,128]{1,0:T(8,128)S(1)}, u32[]{:S(2)}, u32[]{:S(2)}) collective-permute-start(f32[136,128]{1,0:T(8,128)S(1)} %get-tuple-element.81), channel_id=1, source_target_pairs={{0,16},{16,0},{32,48},{48,32},{1,17},{17,1},{33,49},{49,33},{2,18}... | collective-permute-start | bytes 208904 | tf_op jit(solution)/shard_map/ppermute | solution.py:603
  54.0 5.1 %collective-permute-start.12 = (f32[136,128]{1,0:T(8,128)S(1)}, f32[136,128]{1,0:T(8,128)S(1)}, u32[]{:S(2)}, u32[]{:S(2)}) collective-permute-start(f32[136,128]{1,0:T(8,128)S(1)} %get-tuple-element.82), channel_id=1, source_target_pairs={{0,32},{16,48},{32,0},{48,16},{1,33},{17,49},{33,1},{49,17},{2,34}... | collective-permute-start | bytes 208904 | tf_op jit(solution)/shard_map/ppermute | solution.py:603
  59.1 2.5 %collective-permute-done.12.r2 = f32[136,128]{1,0:T(8,128)S(1)} collective-permute-done((f32[136,128]{1,0:T(8,128)S(1)}, f32[136,128]{1,0:T(8,128)S(1)}, u32[]{:S(2)}, u32[]{:S(2)}) %collective-permute-start.12) | collective-permute-done | bytes 69664 | tf_op jit(solution)/shard_map/ppermute | solution.py:603
  61.7 3.5 %collective-permute-done.13.r3 = f32[136,128]{1,0:T(8,128)S(1)} collective-permute-done((f32[136,128]{1,0:T(8,128)S(1)}, f32[136,128]{1,0:T(8,128)S(1)}, u32[]{:S(2)}, u32[]{:S(2)}) %collective-permute-start.13) | collective-permute-done | bytes 69664 | tf_op jit(solution)/shard_map/ppermute | solution.py:603
  65.4 3.2 %collective-permute-start.14 = (f32[136,128]{1,0:T(8,128)S(1)}, f32[136,128]{1,0:T(8,128)S(1)}, u32[]{:S(2)}, u32[]{:S(2)}) collective-permute-start(f32[136,128]{1,0:T(8,128)S(1)} %shard_map.58), channel_id=1, source_target_pairs={{0,64},{64,128},{128,192},{1,65},{65,129},{129,193},{2,66},{66,130... | collective-permute-start | bytes 208904 | tf_op jit(solution)/shard_map/ppermute | solution.py:607
  68.6 4.5 %collective-permute-start.15 = (f32[136,128]{1,0:T(8,128)S(1)}, f32[136,128]{1,0:T(8,128)S(1)}, u32[]{:S(2)}, u32[]{:S(2)}) collective-permute-start(f32[136,128]{1,0:T(8,128)S(1)} %shard_map.58), channel_id=1, source_target_pairs={{0,128},{64,192},{1,129},{65,193},{2,130},{66,194},{3,131},{67,195... | collective-permute-start | bytes 208904 | tf_op jit(solution)/shard_map/ppermute | solution.py:607
  73.2 1.3 collective-permute-start.16
  74.5 1.3 collective-permute-done.16.p3
  76.3 3.3 %collective-permute-start.17 = (f32[136,128]{1,0:T(8,128)S(1)}, f32[136,128]{1,0:T(8,128)S(1)}, u32[]{:S(2)}, u32[]{:S(2)}) collective-permute-start(f32[136,128]{1,0:T(8,128)S(1)} %get-tuple-element.85), channel_id=1, source_target_pairs={{0,16},{16,0},{32,48},{48,32},{1,17},{17,1},{33,49},{49,33},{2,18}... | collective-permute-start | bytes 208904 | tf_op jit(solution)/shard_map/ppermute | solution.py:613
  79.6 0.8 collective-permute-start.18
  80.4 2.6 %collective-permute-start.19 = (f32[136,128]{1,0:T(8,128)S(1)}, f32[136,128]{1,0:T(8,128)S(1)}, u32[]{:S(2)}, u32[]{:S(2)}) collective-permute-start(f32[136,128]{1,0:T(8,128)S(1)} %get-tuple-element.87), channel_id=1, source_target_pairs={{0,48},{16,32},{32,16},{48,0},{1,49},{17,33},{33,17},{49,1},{2,50}... | collective-permute-start | bytes 208904 | tf_op jit(solution)/shard_map/ppermute | solution.py:613
  83.0 4.2 %collective-permute-done.18.e2 = f32[136,128]{1,0:T(8,128)S(1)} collective-permute-done((f32[136,128]{1,0:T(8,128)S(1)}, f32[136,128]{1,0:T(8,128)S(1)}, u32[]{:S(2)}, u32[]{:S(2)}) %collective-permute-start.18) | collective-permute-done | bytes 69664 | tf_op jit(solution)/shard_map/ppermute | solution.py:613
  87.2 0.9 shard_map.60
  88.2 3.3 %collective-permute-start.21 = (f32[520,128]{1,0:T(8,128)S(1)}, f32[520,128]{1,0:T(8,128)S(1)}, u32[]{:S(2)}, u32[]{:S(2)}) collective-permute-start(f32[520,128]{1,0:T(8,128)S(1)} %get-tuple-element.96), channel_id=1, source_target_pairs={{0,12},{2,14},{4,8},{6,10},{8,4},{10,6},{12,0},{14,2},{1,13},{3,15... | collective-permute-start | bytes 798728 | tf_op jit(solution)/shard_map/ppermute | solution.py:562
  91.5 0.9 collective-permute-start.22
  92.4 5.0 %shard_map.61 = (f32[4096,128]{1,0:T(8,128)S(1)}, f32[32,128]{1,0:T(8,128)S(1)}, f32[32,128]{1,0:T(8,128)S(1)}, s32[32,128]{1,0:T(8,128)S(1)}) custom-call(s32[32,128]{1,0:T(8,128)S(1)} %get-tuple-element.58.slot_rows.slots, s32[32,128]{1,0:T(8,128)S(1)} %get-tuple-element.58.slot_rows.slots, s32[32,128]{1,0:T(8,128)S(1)} %bitcast.8, s32[32,128]{1,0:T(8,128)S(1)} %bitcast.4, ...), custom_call_target="tpu_custom_call" | custom-call | flops 10000000000 | bytes 1000000 | tf_op jit(solution)/shard_map/pallas_call | solution.py:55
  97.4 1.2 collective-permute-done.20.refs_0_
  98.6 1.0 collective-permute-done.22.refs_3_
  99.6 0.6 shard_map.62
  100.2 6.0 %collective-permute-start.27 = (f32[4,520,128]{2,1,0:T(8,128)S(1)}, f32[4,520,128]{2,1,0:T(8,128)S(1)}, u32[]{:S(2)}, u32[]{:S(2)}) collective-permute-start(f32[4,520,128]{2,1,0:T(8,128)S(1)} %get-tuple-element.105), channel_id=1, source_target_pairs={{0,1},{1,0},{2,3},{3,2},{4,5},{5,4},{6,7},{7,6},{8,9},{9,8},{10,11... | collective-permute-start | bytes 3194888 | tf_op jit(solution)/shard_map/ppermute | solution.py:644
  106.1 2.2 %collective-permute-start.24 = (f32[520,128]{1,0:T(8,128)S(1)}, f32[520,128]{1,0:T(8,128)S(1)}, u32[]{:S(2)}, u32[]{:S(2)}) collective-permute-start(f32[520,128]{1,0:T(8,128)S(1)} %get-tuple-element.100), channel_id=1, source_target_pairs={{0,10},{2,8},{4,14},{6,12},{8,2},{10,0},{12,6},{14,4},{1,11},{3,9}... | collective-permute-start | bytes 798728 | tf_op jit(solution)/shard_map/ppermute | solution.py:562
  108.5 2.7 %collective-permute-start.26 = (f32[520,128]{1,0:T(8,128)S(1)}, f32[520,128]{1,0:T(8,128)S(1)}, u32[]{:S(2)}, u32[]{:S(2)}) collective-permute-start(f32[520,128]{1,0:T(8,128)S(1)} %get-tuple-element.103), channel_id=1, source_target_pairs={{0,14},{2,12},{4,10},{6,8},{8,6},{10,4},{12,2},{14,0},{1,15},{3,13... | collective-permute-start | bytes 798728 | tf_op jit(solution)/shard_map/ppermute | solution.py:562
  111.2 8.5 %collective-permute-done.23.refs_0_ = f32[520,128]{1,0:T(8,128)S(1)} collective-permute-done((f32[520,128]{1,0:T(8,128)S(1)}, f32[520,128]{1,0:T(8,128)S(1)}, u32[]{:S(2)}, u32[]{:S(2)}) %collective-permute-start.23) | collective-permute-done | bytes 266272 | tf_op jit(solution)/shard_map/ppermute | solution.py:562
  120.0 1.0 collective-permute-start.28
  121.0 1.5 %collective-permute-done.25.refs_0_ = f32[520,128]{1,0:T(8,128)S(1)} collective-permute-done((f32[520,128]{1,0:T(8,128)S(1)}, f32[520,128]{1,0:T(8,128)S(1)}, u32[]{:S(2)}, u32[]{:S(2)}) %collective-permute-start.25) | collective-permute-done | bytes 266272 | tf_op jit(solution)/shard_map/ppermute | solution.py:562
  122.8 1.6 %collective-permute-start.29 = (f32[2,520,128]{2,1,0:T(8,128)S(1)}, f32[2,520,128]{2,1,0:T(8,128)S(1)}, u32[]{:S(2)}, u32[]{:S(2)}) collective-permute-start(f32[2,520,128]{2,1,0:T(8,128)S(1)} %get-tuple-element.109), channel_id=1, source_target_pairs={{0,1},{1,0},{2,3},{3,2},{4,5},{5,4},{6,7},{7,6},{8,9},{9,8},{10,11... | collective-permute-start | bytes 1597448 | tf_op jit(solution)/shard_map/ppermute | solution.py:644
  124.4 0.7 shard_map.65
  125.2 0.8 collective-permute-done.29.got2
  126.0 5.7 %shard_map.66 = (f32[16,520,128]{2,1,0:T(8,128)S(1)}, f32[4096,128]{1,0:T(8,128)}) custom-call(s32[32,128]{1,0:T(8,128)S(1)} %get-tuple-element.91.user_rows, f32[4096,128]{1,0:T(8,128)S(1)} %get-tuple-element.92.run, f32[32,128]{1,0:T(8,128)S(1)} %get-tuple-element.93.ready.count, ...), custom_call_target="tpu_custom_call", output_to_operand_aliasing={{0}: (7, {})} | custom-call | flops 1000000 | bytes 1000000 | tf_op jit(solution)/shard_map/pallas_call | solution.py:55
  (40 shorter events, 4.0 us)
Async XLA Ops:
  0.8 1.6 %copy-start.2 = (f32[4096,128]{1,0:T(8,128)S(1)}, f32[4096,128]{1,0:T(8,128)}, u32[]{:S(2)}) copy-start(f32[4096,128]{1,0:T(8,128)} %features.1) | copy-start | bytes 6291460
  7.6 4.8 %collective-permute-start.3 = (f32[2,520,128]{2,1,0:T(8,128)S(1)}, f32[2,520,128]{2,1,0:T(8,128)S(1)}, u32[]{:S(2)}, u32[]{:S(2)}) collective-permute-start(f32[2,520,128]{2,1,0:T(8,128)S(1)} %get-tuple-element.71), channel_id=1, source_target_pairs={{0,1},{1,0},{2,3},{3,2},{4,5},{5,4},{6,7},{7,6},{8,9},{9,8},{10,11... | collective-permute-start | bytes 1597448 | tf_op jit(solution)/shard_map/ppermute | solution.py:584
  12.0 2.3 %collective-permute-start = (f32[2,520,128]{2,1,0:T(8,128)S(1)}, f32[2,520,128]{2,1,0:T(8,128)S(1)}, u32[]{:S(2)}, u32[]{:S(2)}) collective-permute-start(f32[2,520,128]{2,1,0:T(8,128)S(1)} %get-tuple-element.63), channel_id=1, source_target_pairs={{0,1},{1,0},{2,3},{3,2},{4,5},{5,4},{6,7},{7,6},{8,9},{9,8},{10,11... | collective-permute-start | bytes 1597448 | tf_op jit(solution)/shard_map/ppermute | solution.py:584
  13.9 5.3 %collective-permute-start.5 = (f32[2,520,128]{2,1,0:T(8,128)S(1)}, f32[2,520,128]{2,1,0:T(8,128)S(1)}, u32[]{:S(2)}, u32[]{:S(2)}) collective-permute-start(f32[2,520,128]{2,1,0:T(8,128)S(1)} %get-tuple-element.74), channel_id=1, source_target_pairs={{0,1},{1,0},{2,3},{3,2},{4,5},{5,4},{6,7},{7,6},{8,9},{9,8},{10,11... | collective-permute-start | bytes 1597448 | tf_op jit(solution)/shard_map/ppermute | solution.py:584
  15.7 6.5 %collective-permute-start.1 = (f32[2,520,128]{2,1,0:T(8,128)S(1)}, f32[2,520,128]{2,1,0:T(8,128)S(1)}, u32[]{:S(2)}, u32[]{:S(2)}) collective-permute-start(f32[2,520,128]{2,1,0:T(8,128)S(1)} %get-tuple-element.66), channel_id=1, source_target_pairs={{0,1},{1,0},{2,3},{3,2},{4,5},{5,4},{6,7},{7,6},{8,9},{9,8},{10,11... | collective-permute-start | bytes 1597448 | tf_op jit(solution)/shard_map/ppermute | solution.py:584
  15.9 19.0 %collective-permute-start.2 = (f32[520,128]{1,0:T(8,128)S(1)}, f32[520,128]{1,0:T(8,128)S(1)}, u32[]{:S(2)}, u32[]{:S(2)}) collective-permute-start(f32[520,128]{1,0:T(8,128)S(1)} %get-tuple-element.64.ready), channel_id=1, source_target_pairs={{0,2},{2,0},{4,6},{6,4},{8,10},{10,8},{12,14},{14,12},{1,3},{3,1},... | collective-permute-start | bytes 798728 | tf_op jit(solution)/shard_map/ppermute | solution.py:562
  15.9 25.2 %collective-permute-start.4 = (f32[520,128]{1,0:T(8,128)S(1)}, f32[520,128]{1,0:T(8,128)S(1)}, u32[]{:S(2)}, u32[]{:S(2)}) collective-permute-start(f32[520,128]{1,0:T(8,128)S(1)} %get-tuple-element.72.ready), channel_id=1, source_target_pairs={{0,4},{2,6},{4,0},{6,2},{8,12},{10,14},{12,8},{14,10},{1,5},{3,7},... | collective-permute-start | bytes 798728 | tf_op jit(solution)/shard_map/ppermute | solution.py:562
  17.9 30.5 %collective-permute-start.8 = (f32[520,128]{1,0:T(8,128)S(1)}, f32[520,128]{1,0:T(8,128)S(1)}, u32[]{:S(2)}, u32[]{:S(2)}) collective-permute-start(f32[520,128]{1,0:T(8,128)S(1)} %get-tuple-element.77), channel_id=1, source_target_pairs={{0,10},{2,8},{4,14},{6,12},{8,2},{10,0},{12,6},{14,4},{1,11},{3,9}... | collective-permute-start | bytes 798728 | tf_op jit(solution)/shard_map/ppermute | solution.py:562
  19.2 29.2 %collective-permute-start.9 = (f32[520,128]{1,0:T(8,128)S(1)}, f32[520,128]{1,0:T(8,128)S(1)}, u32[]{:S(2)}, u32[]{:S(2)}) collective-permute-start(f32[520,128]{1,0:T(8,128)S(1)} %get-tuple-element.78), channel_id=1, source_target_pairs={{0,12},{2,14},{4,8},{6,10},{8,4},{10,6},{12,0},{14,2},{1,13},{3,15... | collective-permute-start | bytes 798728 | tf_op jit(solution)/shard_map/ppermute | solution.py:562
  22.2 26.2 %collective-permute-start.6 = (f32[520,128]{1,0:T(8,128)S(1)}, f32[520,128]{1,0:T(8,128)S(1)}, u32[]{:S(2)}, u32[]{:S(2)}) collective-permute-start(f32[520,128]{1,0:T(8,128)S(1)} %get-tuple-element.75), channel_id=1, source_target_pairs={{0,6},{2,4},{4,2},{6,0},{8,14},{10,12},{12,10},{14,8},{1,7},{3,5},... | collective-permute-start | bytes 798728 | tf_op jit(solution)/shard_map/ppermute | solution.py:562
  34.9 13.5 %collective-permute-start.7 = (f32[520,128]{1,0:T(8,128)S(1)}, f32[520,128]{1,0:T(8,128)S(1)}, u32[]{:S(2)}, u32[]{:S(2)}) collective-permute-start(f32[520,128]{1,0:T(8,128)S(1)} %get-tuple-element.76), channel_id=1, source_target_pairs={{0,8},{2,10},{4,12},{6,14},{8,0},{10,2},{12,4},{14,6},{1,9},{3,11}... | collective-permute-start | bytes 798728 | tf_op jit(solution)/shard_map/ppermute | solution.py:562
  41.1 8.8 %collective-permute-start.10 = (f32[520,128]{1,0:T(8,128)S(1)}, f32[520,128]{1,0:T(8,128)S(1)}, u32[]{:S(2)}, u32[]{:S(2)}) collective-permute-start(f32[520,128]{1,0:T(8,128)S(1)} %get-tuple-element.79), channel_id=1, source_target_pairs={{0,14},{2,12},{4,10},{6,8},{8,6},{10,4},{12,2},{14,0},{1,15},{3,13... | collective-permute-start | bytes 798728 | tf_op jit(solution)/shard_map/ppermute | solution.py:562
  50.9 41.5 %copy-start = (s32[4096]{0:T(1024)S(1)}, s32[4096]{0:T(1024)}, u32[]{:S(2)}) copy-start(s32[4096]{0:T(1024)} %param.6) | copy-start | bytes 49156
  50.9 41.5 %copy-start.1 = (s32[4096,1]{0,1:T(1,128)S(1)}, s32[4096,1]{0,1:T(1,128)}, u32[]{:S(2)}) copy-start(s32[4096,1]{0,1:T(1,128)} %param.5) | copy-start | bytes 49156
  50.9 8.2 %collective-permute-start.11 = (f32[136,128]{1,0:T(8,128)S(1)}, f32[136,128]{1,0:T(8,128)S(1)}, u32[]{:S(2)}, u32[]{:S(2)}) collective-permute-start(f32[136,128]{1,0:T(8,128)S(1)} %get-tuple-element.81), channel_id=1, source_target_pairs={{0,16},{16,0},{32,48},{48,32},{1,17},{17,1},{33,49},{49,33},{2,18}... | collective-permute-start | bytes 208904 | tf_op jit(solution)/shard_map/ppermute | solution.py:603
  54.0 7.7 %collective-permute-start.12 = (f32[136,128]{1,0:T(8,128)S(1)}, f32[136,128]{1,0:T(8,128)S(1)}, u32[]{:S(2)}, u32[]{:S(2)}) collective-permute-start(f32[136,128]{1,0:T(8,128)S(1)} %get-tuple-element.82), channel_id=1, source_target_pairs={{0,32},{16,48},{32,0},{48,16},{1,33},{17,49},{33,1},{49,17},{2,34}... | collective-permute-start | bytes 208904 | tf_op jit(solution)/shard_map/ppermute | solution.py:603
  59.1 6.0 %collective-permute-start.13 = (f32[136,128]{1,0:T(8,128)S(1)}, f32[136,128]{1,0:T(8,128)S(1)}, u32[]{:S(2)}, u32[]{:S(2)}) collective-permute-start(f32[136,128]{1,0:T(8,128)S(1)} %get-tuple-element.83), channel_id=1, source_target_pairs={{0,48},{16,32},{32,16},{48,0},{1,49},{17,33},{33,17},{49,1},{2,50}... | collective-permute-start | bytes 208904 | tf_op jit(solution)/shard_map/ppermute | solution.py:603
  65.4 9.1 %collective-permute-start.14 = (f32[136,128]{1,0:T(8,128)S(1)}, f32[136,128]{1,0:T(8,128)S(1)}, u32[]{:S(2)}, u32[]{:S(2)}) collective-permute-start(f32[136,128]{1,0:T(8,128)S(1)} %shard_map.58), channel_id=1, source_target_pairs={{0,64},{64,128},{128,192},{1,65},{65,129},{129,193},{2,66},{66,130... | collective-permute-start | bytes 208904 | tf_op jit(solution)/shard_map/ppermute | solution.py:607
  68.6 5.9 %collective-permute-start.15 = (f32[136,128]{1,0:T(8,128)S(1)}, f32[136,128]{1,0:T(8,128)S(1)}, u32[]{:S(2)}, u32[]{:S(2)}) collective-permute-start(f32[136,128]{1,0:T(8,128)S(1)} %shard_map.58), channel_id=1, source_target_pairs={{0,128},{64,192},{1,129},{65,193},{2,130},{66,194},{3,131},{67,195... | collective-permute-start | bytes 208904 | tf_op jit(solution)/shard_map/ppermute | solution.py:607
  73.2 2.7 %collective-permute-start.16 = (f32[136,128]{1,0:T(8,128)S(1)}, f32[136,128]{1,0:T(8,128)S(1)}, u32[]{:S(2)}, u32[]{:S(2)}) collective-permute-start(f32[136,128]{1,0:T(8,128)S(1)} %shard_map.58), channel_id=1, source_target_pairs={{0,192},{1,193},{2,194},{3,195},{4,196},{5,197},{6,198},{7,199},{8... | collective-permute-start | bytes 208904 | tf_op jit(solution)/shard_map/ppermute | solution.py:607
  76.3 6.7 %collective-permute-start.17 = (f32[136,128]{1,0:T(8,128)S(1)}, f32[136,128]{1,0:T(8,128)S(1)}, u32[]{:S(2)}, u32[]{:S(2)}) collective-permute-start(f32[136,128]{1,0:T(8,128)S(1)} %get-tuple-element.85), channel_id=1, source_target_pairs={{0,16},{16,0},{32,48},{48,32},{1,17},{17,1},{33,49},{49,33},{2,18}... | collective-permute-start | bytes 208904 | tf_op jit(solution)/shard_map/ppermute | solution.py:613
  79.6 7.6 %collective-permute-start.18 = (f32[136,128]{1,0:T(8,128)S(1)}, f32[136,128]{1,0:T(8,128)S(1)}, u32[]{:S(2)}, u32[]{:S(2)}) collective-permute-start(f32[136,128]{1,0:T(8,128)S(1)} %get-tuple-element.86), channel_id=1, source_target_pairs={{0,32},{16,48},{32,0},{48,16},{1,33},{17,49},{33,1},{49,17},{2,34}... | collective-permute-start | bytes 208904 | tf_op jit(solution)/shard_map/ppermute | solution.py:613
  80.4 6.8 %collective-permute-start.19 = (f32[136,128]{1,0:T(8,128)S(1)}, f32[136,128]{1,0:T(8,128)S(1)}, u32[]{:S(2)}, u32[]{:S(2)}) collective-permute-start(f32[136,128]{1,0:T(8,128)S(1)} %get-tuple-element.87), channel_id=1, source_target_pairs={{0,48},{16,32},{32,16},{48,0},{1,49},{17,33},{33,17},{49,1},{2,50}... | collective-permute-start | bytes 208904 | tf_op jit(solution)/shard_map/ppermute | solution.py:613
  88.1 10.5 %collective-permute-start.20 = (f32[520,128]{1,0:T(8,128)S(1)}, f32[520,128]{1,0:T(8,128)S(1)}, u32[]{:S(2)}, u32[]{:S(2)}) collective-permute-start(f32[520,128]{1,0:T(8,128)S(1)} %get-tuple-element.95), channel_id=1, source_target_pairs={{0,4},{2,6},{4,0},{6,2},{8,12},{10,14},{12,8},{14,10},{1,5},{3,7},... | collective-permute-start | bytes 798728 | tf_op jit(solution)/shard_map/ppermute | solution.py:562
  88.2 10.4 %collective-permute-start.21 = (f32[520,128]{1,0:T(8,128)S(1)}, f32[520,128]{1,0:T(8,128)S(1)}, u32[]{:S(2)}, u32[]{:S(2)}) collective-permute-start(f32[520,128]{1,0:T(8,128)S(1)} %get-tuple-element.96), channel_id=1, source_target_pairs={{0,12},{2,14},{4,8},{6,10},{8,4},{10,6},{12,0},{14,2},{1,13},{3,15... | collective-permute-start | bytes 798728 | tf_op jit(solution)/shard_map/ppermute | solution.py:562
  91.5 8.1 %collective-permute-start.22 = (f32[520,128]{1,0:T(8,128)S(1)}, f32[520,128]{1,0:T(8,128)S(1)}, u32[]{:S(2)}, u32[]{:S(2)}) collective-permute-start(f32[520,128]{1,0:T(8,128)S(1)} %get-tuple-element.97), channel_id=1, source_target_pairs={{0,8},{2,10},{4,12},{6,14},{8,0},{10,2},{12,4},{14,6},{1,9},{3,11}... | collective-permute-start | bytes 798728 | tf_op jit(solution)/shard_map/ppermute | solution.py:562
  100.2 24.3 %collective-permute-start.27 = (f32[4,520,128]{2,1,0:T(8,128)S(1)}, f32[4,520,128]{2,1,0:T(8,128)S(1)}, u32[]{:S(2)}, u32[]{:S(2)}) collective-permute-start(f32[4,520,128]{2,1,0:T(8,128)S(1)} %get-tuple-element.105), channel_id=1, source_target_pairs={{0,1},{1,0},{2,3},{3,2},{4,5},{5,4},{6,7},{7,6},{8,9},{9,8},{10,11... | collective-permute-start | bytes 3194888 | tf_op jit(solution)/shard_map/ppermute | solution.py:644
  106.1 13.6 %collective-permute-start.23 = (f32[520,128]{1,0:T(8,128)S(1)}, f32[520,128]{1,0:T(8,128)S(1)}, u32[]{:S(2)}, u32[]{:S(2)}) collective-permute-start(f32[520,128]{1,0:T(8,128)S(1)} %get-tuple-element.99), channel_id=1, source_target_pairs={{0,2},{2,0},{4,6},{6,4},{8,10},{10,8},{12,14},{14,12},{1,3},{3,1},... | collective-permute-start | bytes 798728 | tf_op jit(solution)/shard_map/ppermute | solution.py:562
  106.1 13.6 %collective-permute-start.24 = (f32[520,128]{1,0:T(8,128)S(1)}, f32[520,128]{1,0:T(8,128)S(1)}, u32[]{:S(2)}, u32[]{:S(2)}) collective-permute-start(f32[520,128]{1,0:T(8,128)S(1)} %get-tuple-element.100), channel_id=1, source_target_pairs={{0,10},{2,8},{4,14},{6,12},{8,2},{10,0},{12,6},{14,4},{1,11},{3,9}... | collective-permute-start | bytes 798728 | tf_op jit(solution)/shard_map/ppermute | solution.py:562
  108.3 14.2 %collective-permute-start.25 = (f32[520,128]{1,0:T(8,128)S(1)}, f32[520,128]{1,0:T(8,128)S(1)}, u32[]{:S(2)}, u32[]{:S(2)}) collective-permute-start(f32[520,128]{1,0:T(8,128)S(1)} %get-tuple-element.102), channel_id=1, source_target_pairs={{0,6},{2,4},{4,2},{6,0},{8,14},{10,12},{12,10},{14,8},{1,7},{3,5},... | collective-permute-start | bytes 798728 | tf_op jit(solution)/shard_map/ppermute | solution.py:562
  108.5 14.0 %collective-permute-start.26 = (f32[520,128]{1,0:T(8,128)S(1)}, f32[520,128]{1,0:T(8,128)S(1)}, u32[]{:S(2)}, u32[]{:S(2)}) collective-permute-start(f32[520,128]{1,0:T(8,128)S(1)} %get-tuple-element.103), channel_id=1, source_target_pairs={{0,14},{2,12},{4,10},{6,8},{8,6},{10,4},{12,2},{14,0},{1,15},{3,13... | collective-permute-start | bytes 798728 | tf_op jit(solution)/shard_map/ppermute | solution.py:562
  120.0 5.2 %collective-permute-start.28 = (f32[2,520,128]{2,1,0:T(8,128)S(1)}, f32[2,520,128]{2,1,0:T(8,128)S(1)}, u32[]{:S(2)}, u32[]{:S(2)}) collective-permute-start(f32[2,520,128]{2,1,0:T(8,128)S(1)} %get-tuple-element.108), channel_id=1, source_target_pairs={{0,1},{1,0},{2,3},{3,2},{4,5},{5,4},{6,7},{7,6},{8,9},{9,8},{10,11... | collective-permute-start | bytes 1597448 | tf_op jit(solution)/shard_map/ppermute | solution.py:644
  122.8 3.2 %collective-permute-start.29 = (f32[2,520,128]{2,1,0:T(8,128)S(1)}, f32[2,520,128]{2,1,0:T(8,128)S(1)}, u32[]{:S(2)}, u32[]{:S(2)}) collective-permute-start(f32[2,520,128]{2,1,0:T(8,128)S(1)} %get-tuple-element.109), channel_id=1, source_target_pairs={{0,1},{1,0},{2,3},{3,2},{4,5},{5,4},{6,7},{7,6},{8,9},{9,8},{10,11... | collective-permute-start | bytes 1597448 | tf_op jit(solution)/shard_map/ppermute | solution.py:644

commit v9 on v8

--- a/solution.py
+++ b/solution.py
@@ -81,7 +81,7 @@
 
 
 def chunk_of(dz, dx):
-    return (PLACE[2] ^ dz) * NX + (PLACE[1] ^ dx)
+    return (PLACE[2] ^ dz) * NX + lax.rem(PLACE[1] + dx, NX)
 
 
 def rank_kernel(events, slot_out, acc_out, flag_out):
@@ -129,12 +129,10 @@
     lax.fori_loop(0, OWNERS, clear, 0)
     copy.wait()
 
-    def spread(b, _):
+    for b in range(slot_rows.shape[0]):
         for j in range(LANES):
-            grouped[pl.ds(slots[b, j], 1), :] = features[pl.ds(b * LANES + j, 1), :]
-        return 0
-
-    lax.fori_loop(0, slot_rows.shape[0], spread, 0)
+            at = b * LANES + j
+            grouped[pl.ds(slots[b, j], 1), :] = features[at : at + 1, :]
 
 
 def after_and_ones():
@@ -299,7 +297,7 @@
         @pl.when(PLACE[1] == x)
         def _(x=x):
             for dz in range(NL):
-                order = [tables[dz][x ^ j] for j in range(NX)]
+                order = [tables[dz][(x - j) % NX] for j in range(NX)]
                 tails = [t[TAIL:, :] for t in order]
                 keep = [keep_of(t) for t in tails]
                 for i in range(FOUR):
@@ -379,7 +377,7 @@
         @pl.when(PLACE[1] == x)
         def _(x=x):
             for dz in range(NL):
-                order = [x ^ j for j in range(NX)]
+                order = [(x - j) % NX for j in range(NX)]
                 tails = [tables[dz][k][TAIL:, :] for k in order[:-1]]
                 keeps = [keep_of(t) for t in tails]
                 late = first if dz else jnp.logical_not(first)
@@ -559,7 +557,10 @@
     def exchange(v, dz, dx):
         if dz == 0 and dx == 0:
             return v
-        return lax.ppermute(v, ("l", "x"), swapped(NL * NX, dz * NX + dx))
+        pairs = [
+            (row * NX + x, (row ^ dz) * NX + (x + dx) % NX) for row in range(NL) for x in range(NX)
+        ]
+        return lax.ppermute(v, ("l", "x"), pairs)
 
     order = (2, 1, 3, 0)
     mine, got = [None] * NX, [None] * NX
@@ -622,7 +623,7 @@
     kept = parts[0][0]
     for dx in (2, 0, 1, 3):
         for dz in reversed(range(NL)):
-            parts[dz][dx] = exchange(parts[dz][dx], dz, dx)
+            parts[dz][dx] = exchange(parts[dz][dx], dz, (NX - dx) % NX)
     run, count, is_open, users = call(
         in_time_kernel,
         [jax.ShapeDtypeStruct((rows, LANES), F32), small_f, small_f, small],

time: 132 us -> 130 us (0.985)
  starting transfers between devices: 54.2 us -> 52.1 us
    ppermute x14, starting transfers between devices: 17.6 us -> 14.8 us  [exchange(): return lax.ppermute(v, ('l', 'x'), pairs)]
  transfers between devices with their start and end apart: 30 -> 30, of which waited for: 13 -> 13; matrix products, arithmetic and copies ran while one was open for 0% -> 0% of each run, Pallas kernels for 12% -> 13%
where the time goes in v9:
time: 130 us
  starting transfers between devices  52.1 us (40%)
  waiting for transfers between devices  45.2 us (35%)
  Pallas kernels  30.6 us (24%)
    ppermute x14, waiting for transfers between devices, exchange(): return lax.ppermute(v, ('l', 'x'), pairs)  32.4 us
    pallas_call x21, Pallas kernels, call(): pl.pallas_call(kernel, out_shape=out, in_specs=specs, out_specs=out_specs...  30.6 us
    ppermute x14, starting transfers between devices, exchange(): return lax.ppermute(v, ('l', 'x'), pairs)  14.8 us
    ppermute x3, starting transfers between devices, body(): lax.ppermute(plane, 'y', [(i, i + r) for i in range(ny - r)])  9.03 us
    ppermute x3, starting transfers between devices, body(): rows_got[r] = lax.ppermute(pairs[r], 'h', swapped(NH, r))  8.84 us
    ppermute x3, starting transfers between devices, body(): last.append(lax.ppermute(send, 'c', swap))  8.64 us
    ppermute x3, starting transfers between devices, body(): came[r] = lax.ppermute(came[r], 'h', swapped(NH, r))  6.72 us
    ppermute x3, waiting for transfers between devices, body(): rows_got[r] = lax.ppermute(pairs[r], 'h', swapped(NH, r))  6.04 us
  transfers between devices with their start and end apart: 30, of which 13 were waited for; matrix products, arithmetic and copies ran while one was open for 0% of the time, Pallas kernels for 13%

profile of v9, /device:TPU:1, one launch (start us, length us, event | category | flops | bytes accessed | tf_op | source)
XLA Modules:
  0.0 129.6 jit_solution(6365322655773790034)
XLA Ops:
  0.0 0.8 pad_add_fusion.events
  0.8 1.0 shard_map.46
  2.3 3.0 %shard_map.47.grouped = f32[8192,128]{1,0:T(8,128)S(1)} custom-call(s32[32,128]{1,0:T(8,128)S(1)} %get-tuple-element.58.slot_rows.slots, f32[4096,128]{1,0:T(8,128)S(1)} %copy-done.2), custom_call_target="tpu_custom_call" | custom-call | flops 4000000000 | bytes 1000000 | tf_op jit(solution)/shard_map/pallas_call | solution.py:55
  5.3 1.1 shard_map.48
  6.4 3.3 %collective-permute-start.3 = (f32[2,520,128]{2,1,0:T(8,128)S(1)}, f32[2,520,128]{2,1,0:T(8,128)S(1)}, u32[]{:S(2)}, u32[]{:S(2)}) collective-permute-start(f32[2,520,128]{2,1,0:T(8,128)S(1)} %get-tuple-element.71), channel_id=1, source_target_pairs={{0,1},{1,0},{2,3},{3,2},{4,5},{5,4},{6,7},{7,6},{8,9},{9,8},{10,11... | collective-permute-start | bytes 1597448 | tf_op jit(solution)/shard_map/ppermute | solution.py:585
  9.7 1.1 shard_map.49
  11.6 1.1 shard_map.55
  13.4 1.1 shard_map.51
  14.7 2.0 %collective-permute-start.4 = (f32[520,128]{1,0:T(8,128)S(1)}, f32[520,128]{1,0:T(8,128)S(1)}, u32[]{:S(2)}, u32[]{:S(2)}) collective-permute-start(f32[520,128]{1,0:T(8,128)S(1)} %get-tuple-element.72.ready), channel_id=1, source_target_pairs={{0,4},{2,6},{4,0},{6,2},{8,12},{10,14},{12,8},{14,10},{1,5},{3,7},... | collective-permute-start | bytes 798728 | tf_op jit(solution)/shard_map/ppermute | solution.py:563
  16.7 0.9 collective-permute-start.8
  17.6 2.3 %collective-permute-start.9 = (f32[520,128]{1,0:T(8,128)S(1)}, f32[520,128]{1,0:T(8,128)S(1)}, u32[]{:S(2)}, u32[]{:S(2)}) collective-permute-start(f32[520,128]{1,0:T(8,128)S(1)} %get-tuple-element.78), channel_id=1, source_target_pairs={{0,12},{2,14},{4,8},{6,10},{8,4},{10,6},{12,0},{14,2},{1,13},{3,15... | collective-permute-start | bytes 798728 | tf_op jit(solution)/shard_map/ppermute | solution.py:563
  20.2 0.9 collective-permute-start.6
  21.4 14.2 %collective-permute-done.2.refs_1_ = f32[520,128]{1,0:T(8,128)S(1)} collective-permute-done((f32[520,128]{1,0:T(8,128)S(1)}, f32[520,128]{1,0:T(8,128)S(1)}, u32[]{:S(2)}, u32[]{:S(2)}) %collective-permute-start.2) | collective-permute-done | bytes 266272 | tf_op jit(solution)/shard_map/ppermute | solution.py:563
  35.6 4.3 %collective-permute-done.4.refs_2_ = f32[520,128]{1,0:T(8,128)S(1)} collective-permute-done((f32[520,128]{1,0:T(8,128)S(1)}, f32[520,128]{1,0:T(8,128)S(1)}, u32[]{:S(2)}, u32[]{:S(2)}) %collective-permute-start.4) | collective-permute-done | bytes 266272 | tf_op jit(solution)/shard_map/ppermute | solution.py:563
  40.0 5.7 %shard_map.53 = (f32[8192,128]{1,0:T(8,128)S(1)}, f32[64,128]{1,0:T(8,128)S(1)}, f32[64,128]{1,0:T(8,128)S(1)}) custom-call(s32[64,128]{1,0:T(8,128)S(1)} %get-tuple-element.59.acc_rows.ready, f32[64,128]{1,0:T(8,128)S(1)} %get-tuple-element.60.flag_rows, f32[8192,128]{1,0:T(8,128)S(1)} %shard_map.47.grouped, f32[520,128]{1,0:T(8,128)S(1)} %get-tuple-element.67.ready.refs_0_), custom_call_target="tpu_custom_call" | custom-call | flops 8000000000 | bytes 1000000 | tf_op jit(solution)/shard_map/pallas_call | solution.py:55
  45.7 1.2 collective-permute-done.10.refs_7_
  46.9 1.0 shard_map.57
  47.9 3.7 %collective-permute-start.11 = (f32[136,128]{1,0:T(8,128)S(1)}, f32[136,128]{1,0:T(8,128)S(1)}, u32[]{:S(2)}, u32[]{:S(2)}) collective-permute-start(f32[136,128]{1,0:T(8,128)S(1)} %get-tuple-element.81), channel_id=1, source_target_pairs={{0,16},{16,0},{32,48},{48,32},{1,17},{17,1},{33,49},{49,33},{2,18}... | collective-permute-start | bytes 208904 | tf_op jit(solution)/shard_map/ppermute | solution.py:604
  51.6 5.1 %collective-permute-start.12 = (f32[136,128]{1,0:T(8,128)S(1)}, f32[136,128]{1,0:T(8,128)S(1)}, u32[]{:S(2)}, u32[]{:S(2)}) collective-permute-start(f32[136,128]{1,0:T(8,128)S(1)} %get-tuple-element.82), channel_id=1, source_target_pairs={{0,32},{16,48},{32,0},{48,16},{1,33},{17,49},{33,1},{49,17},{2,34}... | collective-permute-start | bytes 208904 | tf_op jit(solution)/shard_map/ppermute | solution.py:604
  56.7 2.5 %collective-permute-done.12.r2 = f32[136,128]{1,0:T(8,128)S(1)} collective-permute-done((f32[136,128]{1,0:T(8,128)S(1)}, f32[136,128]{1,0:T(8,128)S(1)}, u32[]{:S(2)}, u32[]{:S(2)}) %collective-permute-start.12) | collective-permute-done | bytes 69664 | tf_op jit(solution)/shard_map/ppermute | solution.py:604
  59.3 3.5 %collective-permute-done.13.r3 = f32[136,128]{1,0:T(8,128)S(1)} collective-permute-done((f32[136,128]{1,0:T(8,128)S(1)}, f32[136,128]{1,0:T(8,128)S(1)}, u32[]{:S(2)}, u32[]{:S(2)}) %collective-permute-start.13) | collective-permute-done | bytes 69664 | tf_op jit(solution)/shard_map/ppermute | solution.py:604
  63.0 3.2 %collective-permute-start.14 = (f32[136,128]{1,0:T(8,128)S(1)}, f32[136,128]{1,0:T(8,128)S(1)}, u32[]{:S(2)}, u32[]{:S(2)}) collective-permute-start(f32[136,128]{1,0:T(8,128)S(1)} %shard_map.58), channel_id=1, source_target_pairs={{0,64},{64,128},{128,192},{1,65},{65,129},{129,193},{2,66},{66,130... | collective-permute-start | bytes 208904 | tf_op jit(solution)/shard_map/ppermute | solution.py:608
  66.2 4.5 %collective-permute-start.15 = (f32[136,128]{1,0:T(8,128)S(1)}, f32[136,128]{1,0:T(8,128)S(1)}, u32[]{:S(2)}, u32[]{:S(2)}) collective-permute-start(f32[136,128]{1,0:T(8,128)S(1)} %shard_map.58), channel_id=1, source_target_pairs={{0,128},{64,192},{1,129},{65,193},{2,130},{66,194},{3,131},{67,195... | collective-permute-start | bytes 208904 | tf_op jit(solution)/shard_map/ppermute | solution.py:608
  70.8 1.3 collective-permute-start.16
  72.1 1.3 %collective-permute-done.16.p3 = f32[136,128]{1,0:T(8,128)S(1)} collective-permute-done((f32[136,128]{1,0:T(8,128)S(1)}, f32[136,128]{1,0:T(8,128)S(1)}, u32[]{:S(2)}, u32[]{:S(2)}) %collective-permute-start.16) | collective-permute-done | bytes 69664 | tf_op jit(solution)/shard_map/ppermute | solution.py:608
  73.9 3.3 %collective-permute-start.17 = (f32[136,128]{1,0:T(8,128)S(1)}, f32[136,128]{1,0:T(8,128)S(1)}, u32[]{:S(2)}, u32[]{:S(2)}) collective-permute-start(f32[136,128]{1,0:T(8,128)S(1)} %get-tuple-element.85), channel_id=1, source_target_pairs={{0,16},{16,0},{32,48},{48,32},{1,17},{17,1},{33,49},{49,33},{2,18}... | collective-permute-start | bytes 208904 | tf_op jit(solution)/shard_map/ppermute | solution.py:614
  77.2 0.8 collective-permute-start.18
  78.0 2.6 %collective-permute-start.19 = (f32[136,128]{1,0:T(8,128)S(1)}, f32[136,128]{1,0:T(8,128)S(1)}, u32[]{:S(2)}, u32[]{:S(2)}) collective-permute-start(f32[136,128]{1,0:T(8,128)S(1)} %get-tuple-element.87), channel_id=1, source_target_pairs={{0,48},{16,32},{32,16},{48,0},{1,49},{17,33},{33,17},{49,1},{2,50}... | collective-permute-start | bytes 208904 | tf_op jit(solution)/shard_map/ppermute | solution.py:614
  80.6 4.2 %collective-permute-done.18.e2 = f32[136,128]{1,0:T(8,128)S(1)} collective-permute-done((f32[136,128]{1,0:T(8,128)S(1)}, f32[136,128]{1,0:T(8,128)S(1)}, u32[]{:S(2)}, u32[]{:S(2)}) %collective-permute-start.18) | collective-permute-done | bytes 69664 | tf_op jit(solution)/shard_map/ppermute | solution.py:614
  84.9 1.1 shard_map.60
  86.0 0.6 collective-permute-start.20
  86.6 1.6 %collective-permute-start.21 = (f32[520,128]{1,0:T(8,128)S(1)}, f32[520,128]{1,0:T(8,128)S(1)}, u32[]{:S(2)}, u32[]{:S(2)}) collective-permute-start(f32[520,128]{1,0:T(8,128)S(1)} %get-tuple-element.96), channel_id=1, source_target_pairs={{0,12},{2,14},{4,8},{6,10},{8,4},{10,6},{12,0},{14,2},{1,13},{3,15... | collective-permute-start | bytes 798728 | tf_op jit(solution)/shard_map/ppermute | solution.py:563
  88.2 2.0 %collective-permute-start.22 = (f32[520,128]{1,0:T(8,128)S(1)}, f32[520,128]{1,0:T(8,128)S(1)}, u32[]{:S(2)}, u32[]{:S(2)}) collective-permute-start(f32[520,128]{1,0:T(8,128)S(1)} %get-tuple-element.97), channel_id=1, source_target_pairs={{0,8},{2,10},{4,12},{6,14},{8,0},{10,2},{12,4},{14,6},{1,9},{3,11}... | collective-permute-start | bytes 798728 | tf_op jit(solution)/shard_map/ppermute | solution.py:563
  90.2 5.0 %shard_map.61 = (f32[4096,128]{1,0:T(8,128)S(1)}, f32[32,128]{1,0:T(8,128)S(1)}, f32[32,128]{1,0:T(8,128)S(1)}, s32[32,128]{1,0:T(8,128)S(1)}) custom-call(s32[32,128]{1,0:T(8,128)S(1)} %get-tuple-element.58.slot_rows.slots, s32[32,128]{1,0:T(8,128)S(1)} %get-tuple-element.58.slot_rows.slots, s32[32,128]{1,0:T(8,128)S(1)} %bitcast.8, s32[32,128]{1,0:T(8,128)S(1)} %bitcast.4, ...), custom_call_target="tpu_custom_call" | custom-call | flops 10000000000 | bytes 1000000 | tf_op jit(solution)/shard_map/pallas_call | solution.py:55
  95.2 1.3 collective-permute-done.20.refs_0_
  96.5 0.9 collective-permute-done.22.refs_3_
  97.4 0.6 shard_map.62
  98.0 6.0 %collective-permute-start.27 = (f32[4,520,128]{2,1,0:T(8,128)S(1)}, f32[4,520,128]{2,1,0:T(8,128)S(1)}, u32[]{:S(2)}, u32[]{:S(2)}) collective-permute-start(f32[4,520,128]{2,1,0:T(8,128)S(1)} %get-tuple-element.105), channel_id=1, source_target_pairs={{0,1},{1,0},{2,3},{3,2},{4,5},{5,4},{6,7},{7,6},{8,9},{9,8},{10,11... | collective-permute-start | bytes 3194888 | tf_op jit(solution)/shard_map/ppermute | solution.py:645
  103.9 2.2 %collective-permute-start.23 = (f32[520,128]{1,0:T(8,128)S(1)}, f32[520,128]{1,0:T(8,128)S(1)}, u32[]{:S(2)}, u32[]{:S(2)}) collective-permute-start(f32[520,128]{1,0:T(8,128)S(1)} %get-tuple-element.99), channel_id=1, source_target_pairs={{0,6},{2,0},{4,2},{6,4},{8,14},{10,8},{12,10},{14,12},{1,7},{3,1},... | collective-permute-start | bytes 798728 | tf_op jit(solution)/shard_map/ppermute | solution.py:563
  106.1 1.3 %collective-permute-start.25 = (f32[520,128]{1,0:T(8,128)S(1)}, f32[520,128]{1,0:T(8,128)S(1)}, u32[]{:S(2)}, u32[]{:S(2)}) collective-permute-start(f32[520,128]{1,0:T(8,128)S(1)} %get-tuple-element.102), channel_id=1, source_target_pairs={{0,2},{2,4},{4,6},{6,0},{8,10},{10,12},{12,14},{14,8},{1,3},{3,5},... | collective-permute-start | bytes 798728 | tf_op jit(solution)/shard_map/ppermute | solution.py:563
  107.4 1.0 collective-permute-start.26
  108.4 9.0 %collective-permute-done.23.refs_0_ = f32[520,128]{1,0:T(8,128)S(1)} collective-permute-done((f32[520,128]{1,0:T(8,128)S(1)}, f32[520,128]{1,0:T(8,128)S(1)}, u32[]{:S(2)}, u32[]{:S(2)}) %collective-permute-start.23) | collective-permute-done | bytes 266272 | tf_op jit(solution)/shard_map/ppermute | solution.py:563
  117.8 1.0 collective-permute-start.28
  118.8 1.4 %collective-permute-done.26.refs_1_ = f32[520,128]{1,0:T(8,128)S(1)} collective-permute-done((f32[520,128]{1,0:T(8,128)S(1)}, f32[520,128]{1,0:T(8,128)S(1)}, u32[]{:S(2)}, u32[]{:S(2)}) %collective-permute-start.26) | collective-permute-done | bytes 266272 | tf_op jit(solution)/shard_map/ppermute | solution.py:563
  120.6 1.6 %collective-permute-start.29 = (f32[2,520,128]{2,1,0:T(8,128)S(1)}, f32[2,520,128]{2,1,0:T(8,128)S(1)}, u32[]{:S(2)}, u32[]{:S(2)}) collective-permute-start(f32[2,520,128]{2,1,0:T(8,128)S(1)} %get-tuple-element.109), channel_id=1, source_target_pairs={{0,1},{1,0},{2,3},{3,2},{4,5},{5,4},{6,7},{7,6},{8,9},{9,8},{10,11... | collective-permute-start | bytes 1597448 | tf_op jit(solution)/shard_map/ppermute | solution.py:645
  122.2 0.7 shard_map.65
  122.9 0.8 collective-permute-done.29.got2
  123.8 5.7 %shard_map.66 = (f32[16,520,128]{2,1,0:T(8,128)S(1)}, f32[4096,128]{1,0:T(8,128)}) custom-call(s32[32,128]{1,0:T(8,128)S(1)} %get-tuple-element.91.user_rows, f32[4096,128]{1,0:T(8,128)S(1)} %get-tuple-element.92.run, f32[32,128]{1,0:T(8,128)S(1)} %get-tuple-element.93.ready.count, ...), custom_call_target="tpu_custom_call", output_to_operand_aliasing={{0}: (7, {})} | custom-call | flops 1000000 | bytes 1000000 | tf_op jit(solution)/shard_map/pallas_call | solution.py:55
  (40 shorter events, 4.3 us)
Async XLA Ops:
  0.8 1.6 %copy-start.2 = (f32[4096,128]{1,0:T(8,128)S(1)}, f32[4096,128]{1,0:T(8,128)}, u32[]{:S(2)}) copy-start(f32[4096,128]{1,0:T(8,128)} %features.1) | copy-start | bytes 6291460
  6.4 4.8 %collective-permute-start.3 = (f32[2,520,128]{2,1,0:T(8,128)S(1)}, f32[2,520,128]{2,1,0:T(8,128)S(1)}, u32[]{:S(2)}, u32[]{:S(2)}) collective-permute-start(f32[2,520,128]{2,1,0:T(8,128)S(1)} %get-tuple-element.71), channel_id=1, source_target_pairs={{0,1},{1,0},{2,3},{3,2},{4,5},{5,4},{6,7},{7,6},{8,9},{9,8},{10,11... | collective-permute-start | bytes 1597448 | tf_op jit(solution)/shard_map/ppermute | solution.py:585
  10.8 2.3 %collective-permute-start = (f32[2,520,128]{2,1,0:T(8,128)S(1)}, f32[2,520,128]{2,1,0:T(8,128)S(1)}, u32[]{:S(2)}, u32[]{:S(2)}) collective-permute-start(f32[2,520,128]{2,1,0:T(8,128)S(1)} %get-tuple-element.63), channel_id=1, source_target_pairs={{0,1},{1,0},{2,3},{3,2},{4,5},{5,4},{6,7},{7,6},{8,9},{9,8},{10,11... | collective-permute-start | bytes 1597448 | tf_op jit(solution)/shard_map/ppermute | solution.py:585
  12.6 5.0 %collective-permute-start.5 = (f32[2,520,128]{2,1,0:T(8,128)S(1)}, f32[2,520,128]{2,1,0:T(8,128)S(1)}, u32[]{:S(2)}, u32[]{:S(2)}) collective-permute-start(f32[2,520,128]{2,1,0:T(8,128)S(1)} %get-tuple-element.74), channel_id=1, source_target_pairs={{0,1},{1,0},{2,3},{3,2},{4,5},{5,4},{6,7},{7,6},{8,9},{9,8},{10,11... | collective-permute-start | bytes 1597448 | tf_op jit(solution)/shard_map/ppermute | solution.py:585
  14.5 5.7 %collective-permute-start.1 = (f32[2,520,128]{2,1,0:T(8,128)S(1)}, f32[2,520,128]{2,1,0:T(8,128)S(1)}, u32[]{:S(2)}, u32[]{:S(2)}) collective-permute-start(f32[2,520,128]{2,1,0:T(8,128)S(1)} %get-tuple-element.66), channel_id=1, source_target_pairs={{0,1},{1,0},{2,3},{3,2},{4,5},{5,4},{6,7},{7,6},{8,9},{9,8},{10,11... | collective-permute-start | bytes 1597448 | tf_op jit(solution)/shard_map/ppermute | solution.py:585
  14.7 20.9 %collective-permute-start.2 = (f32[520,128]{1,0:T(8,128)S(1)}, f32[520,128]{1,0:T(8,128)S(1)}, u32[]{:S(2)}, u32[]{:S(2)}) collective-permute-start(f32[520,128]{1,0:T(8,128)S(1)} %get-tuple-element.64.ready), channel_id=1, source_target_pairs={{0,2},{2,4},{4,6},{6,0},{8,10},{10,12},{12,14},{14,8},{1,3},{3,5},... | collective-permute-start | bytes 798728 | tf_op jit(solution)/shard_map/ppermute | solution.py:563
  14.7 25.2 %collective-permute-start.4 = (f32[520,128]{1,0:T(8,128)S(1)}, f32[520,128]{1,0:T(8,128)S(1)}, u32[]{:S(2)}, u32[]{:S(2)}) collective-permute-start(f32[520,128]{1,0:T(8,128)S(1)} %get-tuple-element.72.ready), channel_id=1, source_target_pairs={{0,4},{2,6},{4,0},{6,2},{8,12},{10,14},{12,8},{14,10},{1,5},{3,7},... | collective-permute-start | bytes 798728 | tf_op jit(solution)/shard_map/ppermute | solution.py:563
  16.7 29.0 %collective-permute-start.8 = (f32[520,128]{1,0:T(8,128)S(1)}, f32[520,128]{1,0:T(8,128)S(1)}, u32[]{:S(2)}, u32[]{:S(2)}) collective-permute-start(f32[520,128]{1,0:T(8,128)S(1)} %get-tuple-element.77), channel_id=1, source_target_pairs={{0,10},{2,12},{4,14},{6,8},{8,2},{10,4},{12,6},{14,0},{1,11},{3,13... | collective-permute-start | bytes 798728 | tf_op jit(solution)/shard_map/ppermute | solution.py:563
  17.6 28.0 %collective-permute-start.9 = (f32[520,128]{1,0:T(8,128)S(1)}, f32[520,128]{1,0:T(8,128)S(1)}, u32[]{:S(2)}, u32[]{:S(2)}) collective-permute-start(f32[520,128]{1,0:T(8,128)S(1)} %get-tuple-element.78), channel_id=1, source_target_pairs={{0,12},{2,14},{4,8},{6,10},{8,4},{10,6},{12,0},{14,2},{1,13},{3,15... | collective-permute-start | bytes 798728 | tf_op jit(solution)/shard_map/ppermute | solution.py:563
  20.2 25.5 %collective-permute-start.6 = (f32[520,128]{1,0:T(8,128)S(1)}, f32[520,128]{1,0:T(8,128)S(1)}, u32[]{:S(2)}, u32[]{:S(2)}) collective-permute-start(f32[520,128]{1,0:T(8,128)S(1)} %get-tuple-element.75), channel_id=1, source_target_pairs={{0,6},{2,0},{4,2},{6,4},{8,14},{10,8},{12,10},{14,12},{1,7},{3,1},... | collective-permute-start | bytes 798728 | tf_op jit(solution)/shard_map/ppermute | solution.py:563
  35.6 10.0 %collective-permute-start.7 = (f32[520,128]{1,0:T(8,128)S(1)}, f32[520,128]{1,0:T(8,128)S(1)}, u32[]{:S(2)}, u32[]{:S(2)}) collective-permute-start(f32[520,128]{1,0:T(8,128)S(1)} %get-tuple-element.76), channel_id=1, source_target_pairs={{0,8},{2,10},{4,12},{6,14},{8,0},{10,2},{12,4},{14,6},{1,9},{3,11}... | collective-permute-start | bytes 798728 | tf_op jit(solution)/shard_map/ppermute | solution.py:563
  40.0 6.9 %collective-permute-start.10 = (f32[520,128]{1,0:T(8,128)S(1)}, f32[520,128]{1,0:T(8,128)S(1)}, u32[]{:S(2)}, u32[]{:S(2)}) collective-permute-start(f32[520,128]{1,0:T(8,128)S(1)} %get-tuple-element.79), channel_id=1, source_target_pairs={{0,14},{2,8},{4,10},{6,12},{8,6},{10,0},{12,2},{14,4},{1,15},{3,9}... | collective-permute-start | bytes 798728 | tf_op jit(solution)/shard_map/ppermute | solution.py:563
  47.9 42.4 %copy-start = (s32[4096]{0:T(1024)S(1)}, s32[4096]{0:T(1024)}, u32[]{:S(2)}) copy-start(s32[4096]{0:T(1024)} %param.6) | copy-start | bytes 49156
  47.9 42.3 %copy-start.1 = (s32[4096,1]{0,1:T(1,128)S(1)}, s32[4096,1]{0,1:T(1,128)}, u32[]{:S(2)}) copy-start(s32[4096,1]{0,1:T(1,128)} %param.5) | copy-start | bytes 49156
  47.9 8.8 %collective-permute-start.11 = (f32[136,128]{1,0:T(8,128)S(1)}, f32[136,128]{1,0:T(8,128)S(1)}, u32[]{:S(2)}, u32[]{:S(2)}) collective-permute-start(f32[136,128]{1,0:T(8,128)S(1)} %get-tuple-element.81), channel_id=1, source_target_pairs={{0,16},{16,0},{32,48},{48,32},{1,17},{17,1},{33,49},{49,33},{2,18}... | collective-permute-start | bytes 208904 | tf_op jit(solution)/shard_map/ppermute | solution.py:604
  51.6 7.7 %collective-permute-start.12 = (f32[136,128]{1,0:T(8,128)S(1)}, f32[136,128]{1,0:T(8,128)S(1)}, u32[]{:S(2)}, u32[]{:S(2)}) collective-permute-start(f32[136,128]{1,0:T(8,128)S(1)} %get-tuple-element.82), channel_id=1, source_target_pairs={{0,32},{16,48},{32,0},{48,16},{1,33},{17,49},{33,1},{49,17},{2,34}... | collective-permute-start | bytes 208904 | tf_op jit(solution)/shard_map/ppermute | solution.py:604
  56.7 6.0 %collective-permute-start.13 = (f32[136,128]{1,0:T(8,128)S(1)}, f32[136,128]{1,0:T(8,128)S(1)}, u32[]{:S(2)}, u32[]{:S(2)}) collective-permute-start(f32[136,128]{1,0:T(8,128)S(1)} %get-tuple-element.83), channel_id=1, source_target_pairs={{0,48},{16,32},{32,16},{48,0},{1,49},{17,33},{33,17},{49,1},{2,50}... | collective-permute-start | bytes 208904 | tf_op jit(solution)/shard_map/ppermute | solution.py:604
  63.0 9.1 %collective-permute-start.14 = (f32[136,128]{1,0:T(8,128)S(1)}, f32[136,128]{1,0:T(8,128)S(1)}, u32[]{:S(2)}, u32[]{:S(2)}) collective-permute-start(f32[136,128]{1,0:T(8,128)S(1)} %shard_map.58), channel_id=1, source_target_pairs={{0,64},{64,128},{128,192},{1,65},{65,129},{129,193},{2,66},{66,130... | collective-permute-start | bytes 208904 | tf_op jit(solution)/shard_map/ppermute | solution.py:608
  66.2 5.9 %collective-permute-start.15 = (f32[136,128]{1,0:T(8,128)S(1)}, f32[136,128]{1,0:T(8,128)S(1)}, u32[]{:S(2)}, u32[]{:S(2)}) collective-permute-start(f32[136,128]{1,0:T(8,128)S(1)} %shard_map.58), channel_id=1, source_target_pairs={{0,128},{64,192},{1,129},{65,193},{2,130},{66,194},{3,131},{67,195... | collective-permute-start | bytes 208904 | tf_op jit(solution)/shard_map/ppermute | solution.py:608
  70.8 2.7 %collective-permute-start.16 = (f32[136,128]{1,0:T(8,128)S(1)}, f32[136,128]{1,0:T(8,128)S(1)}, u32[]{:S(2)}, u32[]{:S(2)}) collective-permute-start(f32[136,128]{1,0:T(8,128)S(1)} %shard_map.58), channel_id=1, source_target_pairs={{0,192},{1,193},{2,194},{3,195},{4,196},{5,197},{6,198},{7,199},{8... | collective-permute-start | bytes 208904 | tf_op jit(solution)/shard_map/ppermute | solution.py:608
  73.9 6.7 %collective-permute-start.17 = (f32[136,128]{1,0:T(8,128)S(1)}, f32[136,128]{1,0:T(8,128)S(1)}, u32[]{:S(2)}, u32[]{:S(2)}) collective-permute-start(f32[136,128]{1,0:T(8,128)S(1)} %get-tuple-element.85), channel_id=1, source_target_pairs={{0,16},{16,0},{32,48},{48,32},{1,17},{17,1},{33,49},{49,33},{2,18}... | collective-permute-start | bytes 208904 | tf_op jit(solution)/shard_map/ppermute | solution.py:614
  77.2 7.6 %collective-permute-start.18 = (f32[136,128]{1,0:T(8,128)S(1)}, f32[136,128]{1,0:T(8,128)S(1)}, u32[]{:S(2)}, u32[]{:S(2)}) collective-permute-start(f32[136,128]{1,0:T(8,128)S(1)} %get-tuple-element.86), channel_id=1, source_target_pairs={{0,32},{16,48},{32,0},{48,16},{1,33},{17,49},{33,1},{49,17},{2,34}... | collective-permute-start | bytes 208904 | tf_op jit(solution)/shard_map/ppermute | solution.py:614
  78.0 6.9 %collective-permute-start.19 = (f32[136,128]{1,0:T(8,128)S(1)}, f32[136,128]{1,0:T(8,128)S(1)}, u32[]{:S(2)}, u32[]{:S(2)}) collective-permute-start(f32[136,128]{1,0:T(8,128)S(1)} %get-tuple-element.87), channel_id=1, source_target_pairs={{0,48},{16,32},{32,16},{48,0},{1,49},{17,33},{33,17},{49,1},{2,50}... | collective-permute-start | bytes 208904 | tf_op jit(solution)/shard_map/ppermute | solution.py:614
  86.0 10.5 %collective-permute-start.20 = (f32[520,128]{1,0:T(8,128)S(1)}, f32[520,128]{1,0:T(8,128)S(1)}, u32[]{:S(2)}, u32[]{:S(2)}) collective-permute-start(f32[520,128]{1,0:T(8,128)S(1)} %get-tuple-element.95), channel_id=1, source_target_pairs={{0,4},{2,6},{4,0},{6,2},{8,12},{10,14},{12,8},{14,10},{1,5},{3,7},... | collective-permute-start | bytes 798728 | tf_op jit(solution)/shard_map/ppermute | solution.py:563
  86.6 9.9 %collective-permute-start.21 = (f32[520,128]{1,0:T(8,128)S(1)}, f32[520,128]{1,0:T(8,128)S(1)}, u32[]{:S(2)}, u32[]{:S(2)}) collective-permute-start(f32[520,128]{1,0:T(8,128)S(1)} %get-tuple-element.96), channel_id=1, source_target_pairs={{0,12},{2,14},{4,8},{6,10},{8,4},{10,6},{12,0},{14,2},{1,13},{3,15... | collective-permute-start | bytes 798728 | tf_op jit(solution)/shard_map/ppermute | solution.py:563
  88.2 9.2 %collective-permute-start.22 = (f32[520,128]{1,0:T(8,128)S(1)}, f32[520,128]{1,0:T(8,128)S(1)}, u32[]{:S(2)}, u32[]{:S(2)}) collective-permute-start(f32[520,128]{1,0:T(8,128)S(1)} %get-tuple-element.97), channel_id=1, source_target_pairs={{0,8},{2,10},{4,12},{6,14},{8,0},{10,2},{12,4},{14,6},{1,9},{3,11}... | collective-permute-start | bytes 798728 | tf_op jit(solution)/shard_map/ppermute | solution.py:563
  98.0 24.3 %collective-permute-start.27 = (f32[4,520,128]{2,1,0:T(8,128)S(1)}, f32[4,520,128]{2,1,0:T(8,128)S(1)}, u32[]{:S(2)}, u32[]{:S(2)}) collective-permute-start(f32[4,520,128]{2,1,0:T(8,128)S(1)} %get-tuple-element.105), channel_id=1, source_target_pairs={{0,1},{1,0},{2,3},{3,2},{4,5},{5,4},{6,7},{7,6},{8,9},{9,8},{10,11... | collective-permute-start | bytes 3194888 | tf_op jit(solution)/shard_map/ppermute | solution.py:645
  103.9 13.6 %collective-permute-start.23 = (f32[520,128]{1,0:T(8,128)S(1)}, f32[520,128]{1,0:T(8,128)S(1)}, u32[]{:S(2)}, u32[]{:S(2)}) collective-permute-start(f32[520,128]{1,0:T(8,128)S(1)} %get-tuple-element.99), channel_id=1, source_target_pairs={{0,6},{2,0},{4,2},{6,4},{8,14},{10,8},{12,10},{14,12},{1,7},{3,1},... | collective-permute-start | bytes 798728 | tf_op jit(solution)/shard_map/ppermute | solution.py:563
  106.1 11.4 %collective-permute-start.24 = (f32[520,128]{1,0:T(8,128)S(1)}, f32[520,128]{1,0:T(8,128)S(1)}, u32[]{:S(2)}, u32[]{:S(2)}) collective-permute-start(f32[520,128]{1,0:T(8,128)S(1)} %get-tuple-element.100), channel_id=1, source_target_pairs={{0,14},{2,8},{4,10},{6,12},{8,6},{10,0},{12,2},{14,4},{1,15},{3,9}... | collective-permute-start | bytes 798728 | tf_op jit(solution)/shard_map/ppermute | solution.py:563
  106.1 12.8 %collective-permute-start.25 = (f32[520,128]{1,0:T(8,128)S(1)}, f32[520,128]{1,0:T(8,128)S(1)}, u32[]{:S(2)}, u32[]{:S(2)}) collective-permute-start(f32[520,128]{1,0:T(8,128)S(1)} %get-tuple-element.102), channel_id=1, source_target_pairs={{0,2},{2,4},{4,6},{6,0},{8,10},{10,12},{12,14},{14,8},{1,3},{3,5},... | collective-permute-start | bytes 798728 | tf_op jit(solution)/shard_map/ppermute | solution.py:563
  107.4 12.8 %collective-permute-start.26 = (f32[520,128]{1,0:T(8,128)S(1)}, f32[520,128]{1,0:T(8,128)S(1)}, u32[]{:S(2)}, u32[]{:S(2)}) collective-permute-start(f32[520,128]{1,0:T(8,128)S(1)} %get-tuple-element.103), channel_id=1, source_target_pairs={{0,10},{2,12},{4,14},{6,8},{8,2},{10,4},{12,6},{14,0},{1,11},{3,13... | collective-permute-start | bytes 798728 | tf_op jit(solution)/shard_map/ppermute | solution.py:563
  117.8 5.1 %collective-permute-start.28 = (f32[2,520,128]{2,1,0:T(8,128)S(1)}, f32[2,520,128]{2,1,0:T(8,128)S(1)}, u32[]{:S(2)}, u32[]{:S(2)}) collective-permute-start(f32[2,520,128]{2,1,0:T(8,128)S(1)} %get-tuple-element.108), channel_id=1, source_target_pairs={{0,1},{1,0},{2,3},{3,2},{4,5},{5,4},{6,7},{7,6},{8,9},{9,8},{10,11... | collective-permute-start | bytes 1597448 | tf_op jit(solution)/shard_map/ppermute | solution.py:645
  120.6 3.2 %collective-permute-start.29 = (f32[2,520,128]{2,1,0:T(8,128)S(1)}, f32[2,520,128]{2,1,0:T(8,128)S(1)}, u32[]{:S(2)}, u32[]{:S(2)}) collective-permute-start(f32[2,520,128]{2,1,0:T(8,128)S(1)} %get-tuple-element.109), channel_id=1, source_target_pairs={{0,1},{1,0},{2,3},{3,2},{4,5},{5,4},{6,7},{7,6},{8,9},{9,8},{10,11... | collective-permute-start | bytes 1597448 | tf_op jit(solution)/shard_map/ppermute | solution.py:645

commit v10 on v9

--- a/solution.py
+++ b/solution.py
@@ -230,7 +230,10 @@
         open_out[rows, :] = is_open
         chunk = jnp.right_shift(home8, 2)
         row = (home8 - chunk * FOUR) * LANES + account[rows, :]
-        user_out[rows, :] = chunk * ROWS + jnp.where(is_open > 0.5, row, TAIL + FOUR)
+        user = chunk * ROWS + jnp.where(is_open > 0.5, row, TAIL + FOUR)
+        for half in range(2):
+            at = pl.ds(pl.multiple_of(t * 16 + half * 8, 8), 4)
+            user_out[at, :] = user[half * 4 : half * 4 + 4, :]
         return 0
 
     lax.fori_loop(0, lines // 8, scalars, 0)
@@ -472,10 +475,17 @@
 
 def finish_kernel(
     user_rows, run, count, is_open, home, account, counts, table_in, got1, got2,
-    table, out, picked, users, sems, out_sems,
+    table, out, picked, u0, u1, u2, u3, sems, out_sems, list_sems,
 ):
-    listed = pltpu.make_async_copy(user_rows, users, sems.at[4])
-    listed.start()
+    users = (u0, u1, u2, u3)
+
+    def listed(g, q):
+        return pltpu.make_async_copy(
+            user_rows.at[pl.ds(pl.multiple_of(g * 8, 8), 4), :], users[q], list_sems.at[q]
+        )
+
+    for q in range(4):
+        listed(q, q).start()
     held = []
     for s, side in ((1, got1), (2, got2)):
         held += held_parts(BACK[s], side, False)
@@ -497,7 +507,7 @@
     if lines < LANES:
         scale = jnp.concatenate([scale, jnp.zeros((LANES - lines, LANES), F32)], axis=0)
     scale = scale.T
-    for copy in (*copies, listed):
+    for copy in copies:
         copy.wait()
 
     group = 4
@@ -506,19 +516,24 @@
         rows = pl.ds(pl.multiple_of(g * group * LANES, group * LANES), group * LANES)
         return pltpu.make_async_copy(picked.at[rows, :], out.at[rows, :], out_sems.at[g])
 
-    def lines_of(g, scale):
-        for b in range(group):
-            for j in range(LANES):
-                at = (g * group + b) * LANES + j
-                picked[pl.ds(at, 1), :] = flat[pl.ds(users[g * group + b, j], 1), :]
-        for b in range(group):
-            at = pl.ds(pl.multiple_of((g * group + b) * LANES, LANES), LANES)
-            factor = jnp.broadcast_to(scale[:, b : b + 1], (LANES, LANES))
-            picked[at, :] = (run[at, :] + picked[at, :]) * factor
-        leave(g).start()
-        return pltpu.roll(scale, LANES - group, 1)
-
-    lax.fori_loop(0, lines // group, lines_of, scale)
+    def some(turn, scale):
+        for q in range(4):
+            g = turn * 4 + q
+            listed(g, q).wait()
+            for b in range(group):
+                for j in range(LANES):
+                    at = (g * group + b) * LANES + j
+                    picked[pl.ds(at, 1), :] = flat[pl.ds(users[q][b, j], 1), :]
+            pl.when(g + 4 < lines // group)(lambda g=g, q=q: listed(g + 4, q).start())
+            for b in range(group):
+                at = pl.ds(pl.multiple_of((g * group + b) * LANES, LANES), LANES)
+                factor = jnp.broadcast_to(scale[:, b : b + 1], (LANES, LANES))
+                picked[at, :] = (run[at, :] + picked[at, :]) * factor
+            leave(g).start()
+            scale = pltpu.roll(scale, LANES - group, 1)
+        return scale
+
+    lax.fori_loop(0, lines // (4 * group), some, scale)
     for g in range(lines // group):
         leave(g).wait()
 
@@ -626,7 +641,8 @@
             parts[dz][dx] = exchange(parts[dz][dx], dz, (NX - dx) % NX)
     run, count, is_open, users = call(
         in_time_kernel,
-        [jax.ShapeDtypeStruct((rows, LANES), F32), small_f, small_f, small],
+        [jax.ShapeDtypeStruct((rows, LANES), F32), small_f, small_f,
+         jax.ShapeDtypeStruct((2 * lines, LANES), I32)],
         (slot, slot, home, account, run_slots, counts, opens, kept),
         [SMEM] + [VMEM] * 6 + [ANY],
         cost=10_000_000_000,
@@ -657,9 +673,9 @@
         (users, run, count, is_open, home, account, came_counts, table, *last[1:]),
         [VMEM] * 10,
         out_specs=[VMEM, ANY],
-        scratch=[pltpu.VMEM((rows, LANES), F32), pltpu.SMEM((lines, LANES), I32),
-                 pltpu.SemaphoreType.DMA((5,)),
-                 pltpu.SemaphoreType.DMA((8,))],
+        scratch=[pltpu.VMEM((rows, LANES), F32)] + [pltpu.SMEM((4, LANES), I32)] * 4
+        + [pltpu.SemaphoreType.DMA((4,)), pltpu.SemaphoreType.DMA((8,)),
+           pltpu.SemaphoreType.DMA((4,))],
         aliases={7: 0},
     )
     return result

time: 130 us -> 129 us (level)
  no operation moved by 1% of the time
where the time goes in v10:
time: 129 us; the launch traced here: 128 us
  starting transfers between devices  52.1 us (40%)
  waiting for transfers between devices  45.2 us (35%)
  Pallas kernels  29.4 us (23%)
    ppermute x14, waiting for transfers between devices, exchange(): return lax.ppermute(v, ('l', 'x'), pairs)  32.4 us
    pallas_call x21, Pallas kernels, call(): pl.pallas_call(kernel, out_shape=out, in_specs=specs, out_specs=out_specs...  29.4 us
    ppermute x14, starting transfers between devices, exchange(): return lax.ppermute(v, ('l', 'x'), pairs)  14.8 us
    ppermute x3, starting transfers between devices, body(): lax.ppermute(plane, 'y', [(i, i + r) for i in range(ny - r)])  9.03 us
    ppermute x3, starting transfers between devices, body(): rows_got[r] = lax.ppermute(pairs[r], 'h', swapped(NH, r))  8.84 us
    ppermute x3, starting transfers between devices, body(): last.append(lax.ppermute(send, 'c', swap))  8.64 us
    ppermute x3, starting transfers between devices, body(): came[r] = lax.ppermute(came[r], 'h', swapped(NH, r))  6.72 us
    ppermute x3, waiting for transfers between devices, body(): rows_got[r] = lax.ppermute(pairs[r], 'h', swapped(NH, r))  6.04 us
  transfers between devices with their start and end apart: 30, of which 13 were waited for; matrix products, arithmetic and copies ran while one was open for 0% of the time, Pallas kernels for 13%

profile of v10, /device:TPU:1, one launch (start us, length us, event | category | flops | bytes accessed | tf_op | source)
XLA Modules:
  0.0 128.4 jit_solution(14213017675029074493)
XLA Ops:
  0.0 0.8 pad_add_fusion.events
  0.8 1.0 shard_map.46
  2.3 3.0 %shard_map.47.grouped = f32[8192,128]{1,0:T(8,128)S(1)} custom-call(s32[32,128]{1,0:T(8,128)S(1)} %get-tuple-element.58.slot_rows.slots, f32[4096,128]{1,0:T(8,128)S(1)} %copy-done.2), custom_call_target="tpu_custom_call" | custom-call | flops 4000000000 | bytes 1000000 | tf_op jit(solution)/shard_map/pallas_call | solution.py:55
  5.3 1.1 shard_map.48
  6.4 3.3 %collective-permute-start.3 = (f32[2,520,128]{2,1,0:T(8,128)S(1)}, f32[2,520,128]{2,1,0:T(8,128)S(1)}, u32[]{:S(2)}, u32[]{:S(2)}) collective-permute-start(f32[2,520,128]{2,1,0:T(8,128)S(1)} %get-tuple-element.71), channel_id=1, source_target_pairs={{0,1},{1,0},{2,3},{3,2},{4,5},{5,4},{6,7},{7,6},{8,9},{9,8},{10,11... | collective-permute-start | bytes 1597448 | tf_op jit(solution)/shard_map/ppermute | solution.py:600
  9.7 1.1 shard_map.49
  11.6 1.1 shard_map.55
  13.4 1.1 shard_map.51
  14.7 2.0 %collective-permute-start.4 = (f32[520,128]{1,0:T(8,128)S(1)}, f32[520,128]{1,0:T(8,128)S(1)}, u32[]{:S(2)}, u32[]{:S(2)}) collective-permute-start(f32[520,128]{1,0:T(8,128)S(1)} %get-tuple-element.72.ready), channel_id=1, source_target_pairs={{0,4},{2,6},{4,0},{6,2},{8,12},{10,14},{12,8},{14,10},{1,5},{3,7},... | collective-permute-start | bytes 798728 | tf_op jit(solution)/shard_map/ppermute | solution.py:578
  16.7 0.9 collective-permute-start.8
  17.6 2.3 %collective-permute-start.9 = (f32[520,128]{1,0:T(8,128)S(1)}, f32[520,128]{1,0:T(8,128)S(1)}, u32[]{:S(2)}, u32[]{:S(2)}) collective-permute-start(f32[520,128]{1,0:T(8,128)S(1)} %get-tuple-element.78), channel_id=1, source_target_pairs={{0,12},{2,14},{4,8},{6,10},{8,4},{10,6},{12,0},{14,2},{1,13},{3,15... | collective-permute-start | bytes 798728 | tf_op jit(solution)/shard_map/ppermute | solution.py:578
  20.2 0.9 collective-permute-start.6
  21.4 14.2 %collective-permute-done.2.refs_1_ = f32[520,128]{1,0:T(8,128)S(1)} collective-permute-done((f32[520,128]{1,0:T(8,128)S(1)}, f32[520,128]{1,0:T(8,128)S(1)}, u32[]{:S(2)}, u32[]{:S(2)}) %collective-permute-start.2) | collective-permute-done | bytes 266272 | tf_op jit(solution)/shard_map/ppermute | solution.py:578
  35.6 4.3 %collective-permute-done.4.refs_2_ = f32[520,128]{1,0:T(8,128)S(1)} collective-permute-done((f32[520,128]{1,0:T(8,128)S(1)}, f32[520,128]{1,0:T(8,128)S(1)}, u32[]{:S(2)}, u32[]{:S(2)}) %collective-permute-start.4) | collective-permute-done | bytes 266272 | tf_op jit(solution)/shard_map/ppermute | solution.py:578
  40.0 5.7 %shard_map.53 = (f32[8192,128]{1,0:T(8,128)S(1)}, f32[64,128]{1,0:T(8,128)S(1)}, f32[64,128]{1,0:T(8,128)S(1)}) custom-call(s32[64,128]{1,0:T(8,128)S(1)} %get-tuple-element.59.acc_rows.ready, f32[64,128]{1,0:T(8,128)S(1)} %get-tuple-element.60.flag_rows, f32[8192,128]{1,0:T(8,128)S(1)} %shard_map.47.grouped, f32[520,128]{1,0:T(8,128)S(1)} %get-tuple-element.67.ready.refs_0_), custom_call_target="tpu_custom_call" | custom-call | flops 8000000000 | bytes 1000000 | tf_op jit(solution)/shard_map/pallas_call | solution.py:55
  45.7 1.2 collective-permute-done.10.refs_7_
  46.9 1.0 shard_map.57
  47.9 3.7 %collective-permute-start.11 = (f32[136,128]{1,0:T(8,128)S(1)}, f32[136,128]{1,0:T(8,128)S(1)}, u32[]{:S(2)}, u32[]{:S(2)}) collective-permute-start(f32[136,128]{1,0:T(8,128)S(1)} %get-tuple-element.81), channel_id=1, source_target_pairs={{0,16},{16,0},{32,48},{48,32},{1,17},{17,1},{33,49},{49,33},{2,18}... | collective-permute-start | bytes 208904 | tf_op jit(solution)/shard_map/ppermute | solution.py:619
  51.6 5.1 %collective-permute-start.12 = (f32[136,128]{1,0:T(8,128)S(1)}, f32[136,128]{1,0:T(8,128)S(1)}, u32[]{:S(2)}, u32[]{:S(2)}) collective-permute-start(f32[136,128]{1,0:T(8,128)S(1)} %get-tuple-element.82), channel_id=1, source_target_pairs={{0,32},{16,48},{32,0},{48,16},{1,33},{17,49},{33,1},{49,17},{2,34}... | collective-permute-start | bytes 208904 | tf_op jit(solution)/shard_map/ppermute | solution.py:619
  56.7 2.5 %collective-permute-done.12.r2 = f32[136,128]{1,0:T(8,128)S(1)} collective-permute-done((f32[136,128]{1,0:T(8,128)S(1)}, f32[136,128]{1,0:T(8,128)S(1)}, u32[]{:S(2)}, u32[]{:S(2)}) %collective-permute-start.12) | collective-permute-done | bytes 69664 | tf_op jit(solution)/shard_map/ppermute | solution.py:619
  59.3 3.5 %collective-permute-done.13.r3 = f32[136,128]{1,0:T(8,128)S(1)} collective-permute-done((f32[136,128]{1,0:T(8,128)S(1)}, f32[136,128]{1,0:T(8,128)S(1)}, u32[]{:S(2)}, u32[]{:S(2)}) %collective-permute-start.13) | collective-permute-done | bytes 69664 | tf_op jit(solution)/shard_map/ppermute | solution.py:619
  63.0 3.2 %collective-permute-start.14 = (f32[136,128]{1,0:T(8,128)S(1)}, f32[136,128]{1,0:T(8,128)S(1)}, u32[]{:S(2)}, u32[]{:S(2)}) collective-permute-start(f32[136,128]{1,0:T(8,128)S(1)} %shard_map.58), channel_id=1, source_target_pairs={{0,64},{64,128},{128,192},{1,65},{65,129},{129,193},{2,66},{66,130... | collective-permute-start | bytes 208904 | tf_op jit(solution)/shard_map/ppermute | solution.py:623
  66.2 4.5 %collective-permute-start.15 = (f32[136,128]{1,0:T(8,128)S(1)}, f32[136,128]{1,0:T(8,128)S(1)}, u32[]{:S(2)}, u32[]{:S(2)}) collective-permute-start(f32[136,128]{1,0:T(8,128)S(1)} %shard_map.58), channel_id=1, source_target_pairs={{0,128},{64,192},{1,129},{65,193},{2,130},{66,194},{3,131},{67,195... | collective-permute-start | bytes 208904 | tf_op jit(solution)/shard_map/ppermute | solution.py:623
  70.8 1.3 %collective-permute-start.16 = (f32[136,128]{1,0:T(8,128)S(1)}, f32[136,128]{1,0:T(8,128)S(1)}, u32[]{:S(2)}, u32[]{:S(2)}) collective-permute-start(f32[136,128]{1,0:T(8,128)S(1)} %shard_map.58), channel_id=1, source_target_pairs={{0,192},{1,193},{2,194},{3,195},{4,196},{5,197},{6,198},{7,199},{8... | collective-permute-start | bytes 208904 | tf_op jit(solution)/shard_map/ppermute | solution.py:623
  72.1 1.3 %collective-permute-done.16.p3 = f32[136,128]{1,0:T(8,128)S(1)} collective-permute-done((f32[136,128]{1,0:T(8,128)S(1)}, f32[136,128]{1,0:T(8,128)S(1)}, u32[]{:S(2)}, u32[]{:S(2)}) %collective-permute-start.16) | collective-permute-done | bytes 69664 | tf_op jit(solution)/shard_map/ppermute | solution.py:623
  73.9 3.3 %collective-permute-start.17 = (f32[136,128]{1,0:T(8,128)S(1)}, f32[136,128]{1,0:T(8,128)S(1)}, u32[]{:S(2)}, u32[]{:S(2)}) collective-permute-start(f32[136,128]{1,0:T(8,128)S(1)} %get-tuple-element.85), channel_id=1, source_target_pairs={{0,16},{16,0},{32,48},{48,32},{1,17},{17,1},{33,49},{49,33},{2,18}... | collective-permute-start | bytes 208904 | tf_op jit(solution)/shard_map/ppermute | solution.py:629
  77.2 0.8 collective-permute-start.18
  78.0 2.6 %collective-permute-start.19 = (f32[136,128]{1,0:T(8,128)S(1)}, f32[136,128]{1,0:T(8,128)S(1)}, u32[]{:S(2)}, u32[]{:S(2)}) collective-permute-start(f32[136,128]{1,0:T(8,128)S(1)} %get-tuple-element.87), channel_id=1, source_target_pairs={{0,48},{16,32},{32,16},{48,0},{1,49},{17,33},{33,17},{49,1},{2,50}... | collective-permute-start | bytes 208904 | tf_op jit(solution)/shard_map/ppermute | solution.py:629
  80.6 4.2 %collective-permute-done.18.e2 = f32[136,128]{1,0:T(8,128)S(1)} collective-permute-done((f32[136,128]{1,0:T(8,128)S(1)}, f32[136,128]{1,0:T(8,128)S(1)}, u32[]{:S(2)}, u32[]{:S(2)}) %collective-permute-start.18) | collective-permute-done | bytes 69664 | tf_op jit(solution)/shard_map/ppermute | solution.py:629
  84.9 1.1 shard_map.60
  86.0 0.6 collective-permute-start.20
  86.6 1.6 %collective-permute-start.21 = (f32[520,128]{1,0:T(8,128)S(1)}, f32[520,128]{1,0:T(8,128)S(1)}, u32[]{:S(2)}, u32[]{:S(2)}) collective-permute-start(f32[520,128]{1,0:T(8,128)S(1)} %get-tuple-element.96), channel_id=1, source_target_pairs={{0,12},{2,14},{4,8},{6,10},{8,4},{10,6},{12,0},{14,2},{1,13},{3,15... | collective-permute-start | bytes 798728 | tf_op jit(solution)/shard_map/ppermute | solution.py:578
  88.2 2.0 %collective-permute-start.22 = (f32[520,128]{1,0:T(8,128)S(1)}, f32[520,128]{1,0:T(8,128)S(1)}, u32[]{:S(2)}, u32[]{:S(2)}) collective-permute-start(f32[520,128]{1,0:T(8,128)S(1)} %get-tuple-element.97), channel_id=1, source_target_pairs={{0,8},{2,10},{4,12},{6,14},{8,0},{10,2},{12,4},{14,6},{1,9},{3,11}... | collective-permute-start | bytes 798728 | tf_op jit(solution)/shard_map/ppermute | solution.py:578
  90.2 5.0 %shard_map.61 = (f32[4096,128]{1,0:T(8,128)S(1)}, f32[32,128]{1,0:T(8,128)S(1)}, f32[32,128]{1,0:T(8,128)S(1)}, s32[64,128]{1,0:T(8,128)S(1)}) custom-call(s32[32,128]{1,0:T(8,128)S(1)} %get-tuple-element.58.slot_rows.slots, s32[32,128]{1,0:T(8,128)S(1)} %get-tuple-element.58.slot_rows.slots, s32[32,128]{1,0:T(8,128)S(1)} %bitcast.8, s32[32,128]{1,0:T(8,128)S(1)} %bitcast.4, ...), custom_call_target="tpu_custom_call" | custom-call | flops 10000000000 | bytes 1000000 | tf_op jit(solution)/shard_map/pallas_call | solution.py:55
  95.2 1.3 collective-permute-done.20.refs_0_
  96.5 0.9 collective-permute-done.22.refs_3_
  97.4 0.6 shard_map.62
  98.0 6.0 %collective-permute-start.27 = (f32[4,520,128]{2,1,0:T(8,128)S(1)}, f32[4,520,128]{2,1,0:T(8,128)S(1)}, u32[]{:S(2)}, u32[]{:S(2)}) collective-permute-start(f32[4,520,128]{2,1,0:T(8,128)S(1)} %get-tuple-element.105), channel_id=1, source_target_pairs={{0,1},{1,0},{2,3},{3,2},{4,5},{5,4},{6,7},{7,6},{8,9},{9,8},{10,11... | collective-permute-start | bytes 3194888 | tf_op jit(solution)/shard_map/ppermute | solution.py:661
  103.9 2.2 %collective-permute-start.23 = (f32[520,128]{1,0:T(8,128)S(1)}, f32[520,128]{1,0:T(8,128)S(1)}, u32[]{:S(2)}, u32[]{:S(2)}) collective-permute-start(f32[520,128]{1,0:T(8,128)S(1)} %get-tuple-element.99), channel_id=1, source_target_pairs={{0,6},{2,0},{4,2},{6,4},{8,14},{10,8},{12,10},{14,12},{1,7},{3,1},... | collective-permute-start | bytes 798728 | tf_op jit(solution)/shard_map/ppermute | solution.py:578
  106.1 1.3 %collective-permute-start.25 = (f32[520,128]{1,0:T(8,128)S(1)}, f32[520,128]{1,0:T(8,128)S(1)}, u32[]{:S(2)}, u32[]{:S(2)}) collective-permute-start(f32[520,128]{1,0:T(8,128)S(1)} %get-tuple-element.102), channel_id=1, source_target_pairs={{0,2},{2,4},{4,6},{6,0},{8,10},{10,12},{12,14},{14,8},{1,3},{3,5},... | collective-permute-start | bytes 798728 | tf_op jit(solution)/shard_map/ppermute | solution.py:578
  107.4 1.0 collective-permute-start.26
  108.4 9.0 %collective-permute-done.23.refs_0_ = f32[520,128]{1,0:T(8,128)S(1)} collective-permute-done((f32[520,128]{1,0:T(8,128)S(1)}, f32[520,128]{1,0:T(8,128)S(1)}, u32[]{:S(2)}, u32[]{:S(2)}) %collective-permute-start.23) | collective-permute-done | bytes 266272 | tf_op jit(solution)/shard_map/ppermute | solution.py:578
  117.8 1.0 collective-permute-start.28
  118.8 1.4 %collective-permute-done.26.refs_1_ = f32[520,128]{1,0:T(8,128)S(1)} collective-permute-done((f32[520,128]{1,0:T(8,128)S(1)}, f32[520,128]{1,0:T(8,128)S(1)}, u32[]{:S(2)}, u32[]{:S(2)}) %collective-permute-start.26) | collective-permute-done | bytes 266272 | tf_op jit(solution)/shard_map/ppermute | solution.py:578
  120.6 1.6 %collective-permute-start.29 = (f32[2,520,128]{2,1,0:T(8,128)S(1)}, f32[2,520,128]{2,1,0:T(8,128)S(1)}, u32[]{:S(2)}, u32[]{:S(2)}) collective-permute-start(f32[2,520,128]{2,1,0:T(8,128)S(1)} %get-tuple-element.109), channel_id=1, source_target_pairs={{0,1},{1,0},{2,3},{3,2},{4,5},{5,4},{6,7},{7,6},{8,9},{9,8},{10,11... | collective-permute-start | bytes 1597448 | tf_op jit(solution)/shard_map/ppermute | solution.py:661
  122.2 0.7 shard_map.65
  122.9 0.8 collective-permute-done.29.got2
  123.8 4.5 %shard_map.66 = (f32[16,520,128]{2,1,0:T(8,128)S(1)}, f32[4096,128]{1,0:T(8,128)}) custom-call(s32[64,128]{1,0:T(8,128)S(1)} %get-tuple-element.91.user_rows, f32[4096,128]{1,0:T(8,128)S(1)} %get-tuple-element.92.run, f32[32,128]{1,0:T(8,128)S(1)} %get-tuple-element.93.ready.count, ...), custom_call_target="tpu_custom_call", output_to_operand_aliasing={{0}: (7, {})} | custom-call | flops 1000000 | bytes 1000000 | tf_op jit(solution)/shard_map/pallas_call | solution.py:55
  (40 shorter events, 4.3 us)
Async XLA Ops:
  0.8 1.6 %copy-start.2 = (f32[4096,128]{1,0:T(8,128)S(1)}, f32[4096,128]{1,0:T(8,128)}, u32[]{:S(2)}) copy-start(f32[4096,128]{1,0:T(8,128)} %features.1) | copy-start | bytes 6291460
  6.4 4.8 %collective-permute-start.3 = (f32[2,520,128]{2,1,0:T(8,128)S(1)}, f32[2,520,128]{2,1,0:T(8,128)S(1)}, u32[]{:S(2)}, u32[]{:S(2)}) collective-permute-start(f32[2,520,128]{2,1,0:T(8,128)S(1)} %get-tuple-element.71), channel_id=1, source_target_pairs={{0,1},{1,0},{2,3},{3,2},{4,5},{5,4},{6,7},{7,6},{8,9},{9,8},{10,11... | collective-permute-start | bytes 1597448 | tf_op jit(solution)/shard_map/ppermute | solution.py:600
  10.8 2.3 %collective-permute-start = (f32[2,520,128]{2,1,0:T(8,128)S(1)}, f32[2,520,128]{2,1,0:T(8,128)S(1)}, u32[]{:S(2)}, u32[]{:S(2)}) collective-permute-start(f32[2,520,128]{2,1,0:T(8,128)S(1)} %get-tuple-element.63), channel_id=1, source_target_pairs={{0,1},{1,0},{2,3},{3,2},{4,5},{5,4},{6,7},{7,6},{8,9},{9,8},{10,11... | collective-permute-start | bytes 1597448 | tf_op jit(solution)/shard_map/ppermute | solution.py:600
  12.6 5.0 %collective-permute-start.5 = (f32[2,520,128]{2,1,0:T(8,128)S(1)}, f32[2,520,128]{2,1,0:T(8,128)S(1)}, u32[]{:S(2)}, u32[]{:S(2)}) collective-permute-start(f32[2,520,128]{2,1,0:T(8,128)S(1)} %get-tuple-element.74), channel_id=1, source_target_pairs={{0,1},{1,0},{2,3},{3,2},{4,5},{5,4},{6,7},{7,6},{8,9},{9,8},{10,11... | collective-permute-start | bytes 1597448 | tf_op jit(solution)/shard_map/ppermute | solution.py:600
  14.5 5.7 %collective-permute-start.1 = (f32[2,520,128]{2,1,0:T(8,128)S(1)}, f32[2,520,128]{2,1,0:T(8,128)S(1)}, u32[]{:S(2)}, u32[]{:S(2)}) collective-permute-start(f32[2,520,128]{2,1,0:T(8,128)S(1)} %get-tuple-element.66), channel_id=1, source_target_pairs={{0,1},{1,0},{2,3},{3,2},{4,5},{5,4},{6,7},{7,6},{8,9},{9,8},{10,11... | collective-permute-start | bytes 1597448 | tf_op jit(solution)/shard_map/ppermute | solution.py:600
  14.7 20.9 %collective-permute-start.2 = (f32[520,128]{1,0:T(8,128)S(1)}, f32[520,128]{1,0:T(8,128)S(1)}, u32[]{:S(2)}, u32[]{:S(2)}) collective-permute-start(f32[520,128]{1,0:T(8,128)S(1)} %get-tuple-element.64.ready), channel_id=1, source_target_pairs={{0,2},{2,4},{4,6},{6,0},{8,10},{10,12},{12,14},{14,8},{1,3},{3,5},... | collective-permute-start | bytes 798728 | tf_op jit(solution)/shard_map/ppermute | solution.py:578
  14.7 25.2 %collective-permute-start.4 = (f32[520,128]{1,0:T(8,128)S(1)}, f32[520,128]{1,0:T(8,128)S(1)}, u32[]{:S(2)}, u32[]{:S(2)}) collective-permute-start(f32[520,128]{1,0:T(8,128)S(1)} %get-tuple-element.72.ready), channel_id=1, source_target_pairs={{0,4},{2,6},{4,0},{6,2},{8,12},{10,14},{12,8},{14,10},{1,5},{3,7},... | collective-permute-start | bytes 798728 | tf_op jit(solution)/shard_map/ppermute | solution.py:578
  16.7 29.0 %collective-permute-start.8 = (f32[520,128]{1,0:T(8,128)S(1)}, f32[520,128]{1,0:T(8,128)S(1)}, u32[]{:S(2)}, u32[]{:S(2)}) collective-permute-start(f32[520,128]{1,0:T(8,128)S(1)} %get-tuple-element.77), channel_id=1, source_target_pairs={{0,10},{2,12},{4,14},{6,8},{8,2},{10,4},{12,6},{14,0},{1,11},{3,13... | collective-permute-start | bytes 798728 | tf_op jit(solution)/shard_map/ppermute | solution.py:578
  17.6 28.0 %collective-permute-start.9 = (f32[520,128]{1,0:T(8,128)S(1)}, f32[520,128]{1,0:T(8,128)S(1)}, u32[]{:S(2)}, u32[]{:S(2)}) collective-permute-start(f32[520,128]{1,0:T(8,128)S(1)} %get-tuple-element.78), channel_id=1, source_target_pairs={{0,12},{2,14},{4,8},{6,10},{8,4},{10,6},{12,0},{14,2},{1,13},{3,15... | collective-permute-start | bytes 798728 | tf_op jit(solution)/shard_map/ppermute | solution.py:578
  20.2 25.5 %collective-permute-start.6 = (f32[520,128]{1,0:T(8,128)S(1)}, f32[520,128]{1,0:T(8,128)S(1)}, u32[]{:S(2)}, u32[]{:S(2)}) collective-permute-start(f32[520,128]{1,0:T(8,128)S(1)} %get-tuple-element.75), channel_id=1, source_target_pairs={{0,6},{2,0},{4,2},{6,4},{8,14},{10,8},{12,10},{14,12},{1,7},{3,1},... | collective-permute-start | bytes 798728 | tf_op jit(solution)/shard_map/ppermute | solution.py:578
  35.6 10.0 %collective-permute-start.7 = (f32[520,128]{1,0:T(8,128)S(1)}, f32[520,128]{1,0:T(8,128)S(1)}, u32[]{:S(2)}, u32[]{:S(2)}) collective-permute-start(f32[520,128]{1,0:T(8,128)S(1)} %get-tuple-element.76), channel_id=1, source_target_pairs={{0,8},{2,10},{4,12},{6,14},{8,0},{10,2},{12,4},{14,6},{1,9},{3,11}... | collective-permute-start | bytes 798728 | tf_op jit(solution)/shard_map/ppermute | solution.py:578
  40.0 6.9 %collective-permute-start.10 = (f32[520,128]{1,0:T(8,128)S(1)}, f32[520,128]{1,0:T(8,128)S(1)}, u32[]{:S(2)}, u32[]{:S(2)}) collective-permute-start(f32[520,128]{1,0:T(8,128)S(1)} %get-tuple-element.79), channel_id=1, source_target_pairs={{0,14},{2,8},{4,10},{6,12},{8,6},{10,0},{12,2},{14,4},{1,15},{3,9}... | collective-permute-start | bytes 798728 | tf_op jit(solution)/shard_map/ppermute | solution.py:578
  47.9 42.4 %copy-start = (s32[4096]{0:T(1024)S(1)}, s32[4096]{0:T(1024)}, u32[]{:S(2)}) copy-start(s32[4096]{0:T(1024)} %param.6) | copy-start | bytes 49156
  47.9 42.3 %copy-start.1 = (s32[4096,1]{0,1:T(1,128)S(1)}, s32[4096,1]{0,1:T(1,128)}, u32[]{:S(2)}) copy-start(s32[4096,1]{0,1:T(1,128)} %param.5) | copy-start | bytes 49156
  47.9 8.8 %collective-permute-start.11 = (f32[136,128]{1,0:T(8,128)S(1)}, f32[136,128]{1,0:T(8,128)S(1)}, u32[]{:S(2)}, u32[]{:S(2)}) collective-permute-start(f32[136,128]{1,0:T(8,128)S(1)} %get-tuple-element.81), channel_id=1, source_target_pairs={{0,16},{16,0},{32,48},{48,32},{1,17},{17,1},{33,49},{49,33},{2,18}... | collective-permute-start | bytes 208904 | tf_op jit(solution)/shard_map/ppermute | solution.py:619
  51.6 7.7 %collective-permute-start.12 = (f32[136,128]{1,0:T(8,128)S(1)}, f32[136,128]{1,0:T(8,128)S(1)}, u32[]{:S(2)}, u32[]{:S(2)}) collective-permute-start(f32[136,128]{1,0:T(8,128)S(1)} %get-tuple-element.82), channel_id=1, source_target_pairs={{0,32},{16,48},{32,0},{48,16},{1,33},{17,49},{33,1},{49,17},{2,34}... | collective-permute-start | bytes 208904 | tf_op jit(solution)/shard_map/ppermute | solution.py:619
  56.7 6.0 %collective-permute-start.13 = (f32[136,128]{1,0:T(8,128)S(1)}, f32[136,128]{1,0:T(8,128)S(1)}, u32[]{:S(2)}, u32[]{:S(2)}) collective-permute-start(f32[136,128]{1,0:T(8,128)S(1)} %get-tuple-element.83), channel_id=1, source_target_pairs={{0,48},{16,32},{32,16},{48,0},{1,49},{17,33},{33,17},{49,1},{2,50}... | collective-permute-start | bytes 208904 | tf_op jit(solution)/shard_map/ppermute | solution.py:619
  63.0 9.1 %collective-permute-start.14 = (f32[136,128]{1,0:T(8,128)S(1)}, f32[136,128]{1,0:T(8,128)S(1)}, u32[]{:S(2)}, u32[]{:S(2)}) collective-permute-start(f32[136,128]{1,0:T(8,128)S(1)} %shard_map.58), channel_id=1, source_target_pairs={{0,64},{64,128},{128,192},{1,65},{65,129},{129,193},{2,66},{66,130... | collective-permute-start | bytes 208904 | tf_op jit(solution)/shard_map/ppermute | solution.py:623
  66.2 5.9 %collective-permute-start.15 = (f32[136,128]{1,0:T(8,128)S(1)}, f32[136,128]{1,0:T(8,128)S(1)}, u32[]{:S(2)}, u32[]{:S(2)}) collective-permute-start(f32[136,128]{1,0:T(8,128)S(1)} %shard_map.58), channel_id=1, source_target_pairs={{0,128},{64,192},{1,129},{65,193},{2,130},{66,194},{3,131},{67,195... | collective-permute-start | bytes 208904 | tf_op jit(solution)/shard_map/ppermute | solution.py:623
  70.8 2.7 %collective-permute-start.16 = (f32[136,128]{1,0:T(8,128)S(1)}, f32[136,128]{1,0:T(8,128)S(1)}, u32[]{:S(2)}, u32[]{:S(2)}) collective-permute-start(f32[136,128]{1,0:T(8,128)S(1)} %shard_map.58), channel_id=1, source_target_pairs={{0,192},{1,193},{2,194},{3,195},{4,196},{5,197},{6,198},{7,199},{8... | collective-permute-start | bytes 208904 | tf_op jit(solution)/shard_map/ppermute | solution.py:623
  73.9 6.7 %collective-permute-start.17 = (f32[136,128]{1,0:T(8,128)S(1)}, f32[136,128]{1,0:T(8,128)S(1)}, u32[]{:S(2)}, u32[]{:S(2)}) collective-permute-start(f32[136,128]{1,0:T(8,128)S(1)} %get-tuple-element.85), channel_id=1, source_target_pairs={{0,16},{16,0},{32,48},{48,32},{1,17},{17,1},{33,49},{49,33},{2,18}... | collective-permute-start | bytes 208904 | tf_op jit(solution)/shard_map/ppermute | solution.py:629
  77.2 7.6 %collective-permute-start.18 = (f32[136,128]{1,0:T(8,128)S(1)}, f32[136,128]{1,0:T(8,128)S(1)}, u32[]{:S(2)}, u32[]{:S(2)}) collective-permute-start(f32[136,128]{1,0:T(8,128)S(1)} %get-tuple-element.86), channel_id=1, source_target_pairs={{0,32},{16,48},{32,0},{48,16},{1,33},{17,49},{33,1},{49,17},{2,34}... | collective-permute-start | bytes 208904 | tf_op jit(solution)/shard_map/ppermute | solution.py:629
  78.0 6.9 %collective-permute-start.19 = (f32[136,128]{1,0:T(8,128)S(1)}, f32[136,128]{1,0:T(8,128)S(1)}, u32[]{:S(2)}, u32[]{:S(2)}) collective-permute-start(f32[136,128]{1,0:T(8,128)S(1)} %get-tuple-element.87), channel_id=1, source_target_pairs={{0,48},{16,32},{32,16},{48,0},{1,49},{17,33},{33,17},{49,1},{2,50}... | collective-permute-start | bytes 208904 | tf_op jit(solution)/shard_map/ppermute | solution.py:629
  86.0 10.5 %collective-permute-start.20 = (f32[520,128]{1,0:T(8,128)S(1)}, f32[520,128]{1,0:T(8,128)S(1)}, u32[]{:S(2)}, u32[]{:S(2)}) collective-permute-start(f32[520,128]{1,0:T(8,128)S(1)} %get-tuple-element.95), channel_id=1, source_target_pairs={{0,4},{2,6},{4,0},{6,2},{8,12},{10,14},{12,8},{14,10},{1,5},{3,7},... | collective-permute-start | bytes 798728 | tf_op jit(solution)/shard_map/ppermute | solution.py:578
  86.6 9.9 %collective-permute-start.21 = (f32[520,128]{1,0:T(8,128)S(1)}, f32[520,128]{1,0:T(8,128)S(1)}, u32[]{:S(2)}, u32[]{:S(2)}) collective-permute-start(f32[520,128]{1,0:T(8,128)S(1)} %get-tuple-element.96), channel_id=1, source_target_pairs={{0,12},{2,14},{4,8},{6,10},{8,4},{10,6},{12,0},{14,2},{1,13},{3,15... | collective-permute-start | bytes 798728 | tf_op jit(solution)/shard_map/ppermute | solution.py:578
  88.2 9.2 %collective-permute-start.22 = (f32[520,128]{1,0:T(8,128)S(1)}, f32[520,128]{1,0:T(8,128)S(1)}, u32[]{:S(2)}, u32[]{:S(2)}) collective-permute-start(f32[520,128]{1,0:T(8,128)S(1)} %get-tuple-element.97), channel_id=1, source_target_pairs={{0,8},{2,10},{4,12},{6,14},{8,0},{10,2},{12,4},{14,6},{1,9},{3,11}... | collective-permute-start | bytes 798728 | tf_op jit(solution)/shard_map/ppermute | solution.py:578
  98.0 24.3 %collective-permute-start.27 = (f32[4,520,128]{2,1,0:T(8,128)S(1)}, f32[4,520,128]{2,1,0:T(8,128)S(1)}, u32[]{:S(2)}, u32[]{:S(2)}) collective-permute-start(f32[4,520,128]{2,1,0:T(8,128)S(1)} %get-tuple-element.105), channel_id=1, source_target_pairs={{0,1},{1,0},{2,3},{3,2},{4,5},{5,4},{6,7},{7,6},{8,9},{9,8},{10,11... | collective-permute-start | bytes 3194888 | tf_op jit(solution)/shard_map/ppermute | solution.py:661
  103.9 13.6 %collective-permute-start.23 = (f32[520,128]{1,0:T(8,128)S(1)}, f32[520,128]{1,0:T(8,128)S(1)}, u32[]{:S(2)}, u32[]{:S(2)}) collective-permute-start(f32[520,128]{1,0:T(8,128)S(1)} %get-tuple-element.99), channel_id=1, source_target_pairs={{0,6},{2,0},{4,2},{6,4},{8,14},{10,8},{12,10},{14,12},{1,7},{3,1},... | collective-permute-start | bytes 798728 | tf_op jit(solution)/shard_map/ppermute | solution.py:578
  106.1 11.4 %collective-permute-start.24 = (f32[520,128]{1,0:T(8,128)S(1)}, f32[520,128]{1,0:T(8,128)S(1)}, u32[]{:S(2)}, u32[]{:S(2)}) collective-permute-start(f32[520,128]{1,0:T(8,128)S(1)} %get-tuple-element.100), channel_id=1, source_target_pairs={{0,14},{2,8},{4,10},{6,12},{8,6},{10,0},{12,2},{14,4},{1,15},{3,9}... | collective-permute-start | bytes 798728 | tf_op jit(solution)/shard_map/ppermute | solution.py:578
  106.1 12.8 %collective-permute-start.25 = (f32[520,128]{1,0:T(8,128)S(1)}, f32[520,128]{1,0:T(8,128)S(1)}, u32[]{:S(2)}, u32[]{:S(2)}) collective-permute-start(f32[520,128]{1,0:T(8,128)S(1)} %get-tuple-element.102), channel_id=1, source_target_pairs={{0,2},{2,4},{4,6},{6,0},{8,10},{10,12},{12,14},{14,8},{1,3},{3,5},... | collective-permute-start | bytes 798728 | tf_op jit(solution)/shard_map/ppermute | solution.py:578
  107.4 12.8 %collective-permute-start.26 = (f32[520,128]{1,0:T(8,128)S(1)}, f32[520,128]{1,0:T(8,128)S(1)}, u32[]{:S(2)}, u32[]{:S(2)}) collective-permute-start(f32[520,128]{1,0:T(8,128)S(1)} %get-tuple-element.103), channel_id=1, source_target_pairs={{0,10},{2,12},{4,14},{6,8},{8,2},{10,4},{12,6},{14,0},{1,11},{3,13... | collective-permute-start | bytes 798728 | tf_op jit(solution)/shard_map/ppermute | solution.py:578
  117.8 5.1 %collective-permute-start.28 = (f32[2,520,128]{2,1,0:T(8,128)S(1)}, f32[2,520,128]{2,1,0:T(8,128)S(1)}, u32[]{:S(2)}, u32[]{:S(2)}) collective-permute-start(f32[2,520,128]{2,1,0:T(8,128)S(1)} %get-tuple-element.108), channel_id=1, source_target_pairs={{0,1},{1,0},{2,3},{3,2},{4,5},{5,4},{6,7},{7,6},{8,9},{9,8},{10,11... | collective-permute-start | bytes 1597448 | tf_op jit(solution)/shard_map/ppermute | solution.py:661
  120.6 3.2 %collective-permute-start.29 = (f32[2,520,128]{2,1,0:T(8,128)S(1)}, f32[2,520,128]{2,1,0:T(8,128)S(1)}, u32[]{:S(2)}, u32[]{:S(2)}) collective-permute-start(f32[2,520,128]{2,1,0:T(8,128)S(1)} %get-tuple-element.109), channel_id=1, source_target_pairs={{0,1},{1,0},{2,3},{3,2},{4,5},{5,4},{6,7},{7,6},{8,9},{9,8},{10,11... | collective-permute-start | bytes 1597448 | tf_op jit(solution)/shard_map/ppermute | solution.py:661

commit v11 on v10

--- a/solution.py
+++ b/solution.py
@@ -619,9 +619,9 @@
         rows_got[r] = lax.ppermute(pairs[r], "h", swapped(NH, r))
     plane = call(plane_kernel, one_block(), tuple(rows_got), [VMEM] * NH)
     ny = lax.axis_size("y")
-    planes = [
-        lax.ppermute(plane, "y", [(i, i + r) for i in range(ny - r)]) for r in range(1, ny)
-    ]
+    planes = []
+    for r in range(1, ny):
+        planes.append(lax.ppermute(plane, "y", [(i, i + r) for i in range(ny - r)]))
     came = call(rows_back_kernel, [one_block()] * NH, (*planes, *rows_got),
                 [VMEM] * (3 + NH))
     came = list(came)

time: 129 us -> 129 us (level)
  no operation moved by 1% of the time
where the time goes in v11:
time: 129 us; the launch traced here: 128 us
  starting transfers between devices  52.1 us (40%)
  waiting for transfers between devices  45.2 us (35%)
  Pallas kernels  29.4 us (23%)
    ppermute x14, waiting for transfers between devices, exchange(): return lax.ppermute(v, ('l', 'x'), pairs)  32.4 us
    pallas_call x21, Pallas kernels, call(): pl.pallas_call(kernel, out_shape=out, in_specs=specs, out_specs=out_specs...  29.4 us
    ppermute x14, starting transfers between devices, exchange(): return lax.ppermute(v, ('l', 'x'), pairs)  14.8 us
    ppermute x3, starting transfers between devices, body(): planes.append(lax.ppermute(plane, 'y', [(i, i + r) for i in range(ny - r)]))  9.03 us
    ppermute x3, starting transfers between devices, body(): rows_got[r] = lax.ppermute(pairs[r], 'h', swapped(NH, r))  8.84 us
    ppermute x3, starting transfers between devices, body(): last.append(lax.ppermute(send, 'c', swap))  8.64 us
    ppermute x3, starting transfers between devices, body(): came[r] = lax.ppermute(came[r], 'h', swapped(NH, r))  6.72 us
    ppermute x3, waiting for transfers between devices, body(): rows_got[r] = lax.ppermute(pairs[r], 'h', swapped(NH, r))  6.04 us
  transfers between devices with their start and end apart: 30, of which 13 were waited for; matrix products, arithmetic and copies ran while one was open for 0% of the time, Pallas kernels for 13%

profile of v11, /device:TPU:1, one launch (start us, length us, event | category | flops | bytes accessed | tf_op | source)
XLA Modules:
  0.0 128.4 jit_solution(14213017675029074493)
XLA Ops:
  0.0 0.8 pad_add_fusion.events
  0.8 1.0 shard_map.46
  2.3 3.0 %shard_map.47.grouped = f32[8192,128]{1,0:T(8,128)S(1)} custom-call(s32[32,128]{1,0:T(8,128)S(1)} %get-tuple-element.58.slot_rows.slots, f32[4096,128]{1,0:T(8,128)S(1)} %copy-done.2), custom_call_target="tpu_custom_call" | custom-call | flops 4000000000 | bytes 1000000 | tf_op jit(solution)/shard_map/pallas_call | solution.py:55
  5.3 1.1 shard_map.48
  6.4 3.3 %collective-permute-start.3 = (f32[2,520,128]{2,1,0:T(8,128)S(1)}, f32[2,520,128]{2,1,0:T(8,128)S(1)}, u32[]{:S(2)}, u32[]{:S(2)}) collective-permute-start(f32[2,520,128]{2,1,0:T(8,128)S(1)} %get-tuple-element.71), channel_id=1, source_target_pairs={{0,1},{1,0},{2,3},{3,2},{4,5},{5,4},{6,7},{7,6},{8,9},{9,8},{10,11... | collective-permute-start | bytes 1597448 | tf_op jit(solution)/shard_map/ppermute | solution.py:600
  9.7 1.1 shard_map.49
  11.6 1.1 shard_map.55
  13.4 1.1 shard_map.51
  14.7 2.0 %collective-permute-start.4 = (f32[520,128]{1,0:T(8,128)S(1)}, f32[520,128]{1,0:T(8,128)S(1)}, u32[]{:S(2)}, u32[]{:S(2)}) collective-permute-start(f32[520,128]{1,0:T(8,128)S(1)} %get-tuple-element.72.ready), channel_id=1, source_target_pairs={{0,4},{2,6},{4,0},{6,2},{8,12},{10,14},{12,8},{14,10},{1,5},{3,7},... | collective-permute-start | bytes 798728 | tf_op jit(solution)/shard_map/ppermute | solution.py:578
  16.7 0.9 collective-permute-start.8
  17.6 2.3 %collective-permute-start.9 = (f32[520,128]{1,0:T(8,128)S(1)}, f32[520,128]{1,0:T(8,128)S(1)}, u32[]{:S(2)}, u32[]{:S(2)}) collective-permute-start(f32[520,128]{1,0:T(8,128)S(1)} %get-tuple-element.78), channel_id=1, source_target_pairs={{0,12},{2,14},{4,8},{6,10},{8,4},{10,6},{12,0},{14,2},{1,13},{3,15... | collective-permute-start | bytes 798728 | tf_op jit(solution)/shard_map/ppermute | solution.py:578
  20.2 0.9 collective-permute-start.6
  21.4 14.2 %collective-permute-done.2.refs_1_ = f32[520,128]{1,0:T(8,128)S(1)} collective-permute-done((f32[520,128]{1,0:T(8,128)S(1)}, f32[520,128]{1,0:T(8,128)S(1)}, u32[]{:S(2)}, u32[]{:S(2)}) %collective-permute-start.2) | collective-permute-done | bytes 266272 | tf_op jit(solution)/shard_map/ppermute | solution.py:578
  35.6 4.3 %collective-permute-done.4.refs_2_ = f32[520,128]{1,0:T(8,128)S(1)} collective-permute-done((f32[520,128]{1,0:T(8,128)S(1)}, f32[520,128]{1,0:T(8,128)S(1)}, u32[]{:S(2)}, u32[]{:S(2)}) %collective-permute-start.4) | collective-permute-done | bytes 266272 | tf_op jit(solution)/shard_map/ppermute | solution.py:578
  40.0 5.7 %shard_map.53 = (f32[8192,128]{1,0:T(8,128)S(1)}, f32[64,128]{1,0:T(8,128)S(1)}, f32[64,128]{1,0:T(8,128)S(1)}) custom-call(s32[64,128]{1,0:T(8,128)S(1)} %get-tuple-element.59.acc_rows.ready, f32[64,128]{1,0:T(8,128)S(1)} %get-tuple-element.60.flag_rows, f32[8192,128]{1,0:T(8,128)S(1)} %shard_map.47.grouped, f32[520,128]{1,0:T(8,128)S(1)} %get-tuple-element.67.ready.refs_0_), custom_call_target="tpu_custom_call" | custom-call | flops 8000000000 | bytes 1000000 | tf_op jit(solution)/shard_map/pallas_call | solution.py:55
  45.7 1.2 collective-permute-done.10.refs_7_
  46.9 1.0 shard_map.57
  47.9 3.7 %collective-permute-start.11 = (f32[136,128]{1,0:T(8,128)S(1)}, f32[136,128]{1,0:T(8,128)S(1)}, u32[]{:S(2)}, u32[]{:S(2)}) collective-permute-start(f32[136,128]{1,0:T(8,128)S(1)} %get-tuple-element.81), channel_id=1, source_target_pairs={{0,16},{16,0},{32,48},{48,32},{1,17},{17,1},{33,49},{49,33},{2,18}... | collective-permute-start | bytes 208904 | tf_op jit(solution)/shard_map/ppermute | solution.py:619
  51.6 5.1 %collective-permute-start.12 = (f32[136,128]{1,0:T(8,128)S(1)}, f32[136,128]{1,0:T(8,128)S(1)}, u32[]{:S(2)}, u32[]{:S(2)}) collective-permute-start(f32[136,128]{1,0:T(8,128)S(1)} %get-tuple-element.82), channel_id=1, source_target_pairs={{0,32},{16,48},{32,0},{48,16},{1,33},{17,49},{33,1},{49,17},{2,34}... | collective-permute-start | bytes 208904 | tf_op jit(solution)/shard_map/ppermute | solution.py:619
  56.7 2.5 %collective-permute-done.12.r2 = f32[136,128]{1,0:T(8,128)S(1)} collective-permute-done((f32[136,128]{1,0:T(8,128)S(1)}, f32[136,128]{1,0:T(8,128)S(1)}, u32[]{:S(2)}, u32[]{:S(2)}) %collective-permute-start.12) | collective-permute-done | bytes 69664 | tf_op jit(solution)/shard_map/ppermute | solution.py:619
  59.3 3.5 %collective-permute-done.13.r3 = f32[136,128]{1,0:T(8,128)S(1)} collective-permute-done((f32[136,128]{1,0:T(8,128)S(1)}, f32[136,128]{1,0:T(8,128)S(1)}, u32[]{:S(2)}, u32[]{:S(2)}) %collective-permute-start.13) | collective-permute-done | bytes 69664 | tf_op jit(solution)/shard_map/ppermute | solution.py:619
  63.0 3.2 %collective-permute-start.14 = (f32[136,128]{1,0:T(8,128)S(1)}, f32[136,128]{1,0:T(8,128)S(1)}, u32[]{:S(2)}, u32[]{:S(2)}) collective-permute-start(f32[136,128]{1,0:T(8,128)S(1)} %shard_map.58), channel_id=1, source_target_pairs={{0,64},{64,128},{128,192},{1,65},{65,129},{129,193},{2,66},{66,130... | collective-permute-start | bytes 208904 | tf_op jit(solution)/shard_map/ppermute | solution.py:624
  66.2 4.5 %collective-permute-start.15 = (f32[136,128]{1,0:T(8,128)S(1)}, f32[136,128]{1,0:T(8,128)S(1)}, u32[]{:S(2)}, u32[]{:S(2)}) collective-permute-start(f32[136,128]{1,0:T(8,128)S(1)} %shard_map.58), channel_id=1, source_target_pairs={{0,128},{64,192},{1,129},{65,193},{2,130},{66,194},{3,131},{67,195... | collective-permute-start | bytes 208904 | tf_op jit(solution)/shard_map/ppermute | solution.py:624
  70.8 1.3 %collective-permute-start.16 = (f32[136,128]{1,0:T(8,128)S(1)}, f32[136,128]{1,0:T(8,128)S(1)}, u32[]{:S(2)}, u32[]{:S(2)}) collective-permute-start(f32[136,128]{1,0:T(8,128)S(1)} %shard_map.58), channel_id=1, source_target_pairs={{0,192},{1,193},{2,194},{3,195},{4,196},{5,197},{6,198},{7,199},{8... | collective-permute-start | bytes 208904 | tf_op jit(solution)/shard_map/ppermute | solution.py:624
  72.1 1.3 %collective-permute-done.16.p3 = f32[136,128]{1,0:T(8,128)S(1)} collective-permute-done((f32[136,128]{1,0:T(8,128)S(1)}, f32[136,128]{1,0:T(8,128)S(1)}, u32[]{:S(2)}, u32[]{:S(2)}) %collective-permute-start.16) | collective-permute-done | bytes 69664 | tf_op jit(solution)/shard_map/ppermute | solution.py:624
  73.9 3.3 %collective-permute-start.17 = (f32[136,128]{1,0:T(8,128)S(1)}, f32[136,128]{1,0:T(8,128)S(1)}, u32[]{:S(2)}, u32[]{:S(2)}) collective-permute-start(f32[136,128]{1,0:T(8,128)S(1)} %get-tuple-element.85), channel_id=1, source_target_pairs={{0,16},{16,0},{32,48},{48,32},{1,17},{17,1},{33,49},{49,33},{2,18}... | collective-permute-start | bytes 208904 | tf_op jit(solution)/shard_map/ppermute | solution.py:629
  77.2 0.8 collective-permute-start.18
  78.0 2.6 %collective-permute-start.19 = (f32[136,128]{1,0:T(8,128)S(1)}, f32[136,128]{1,0:T(8,128)S(1)}, u32[]{:S(2)}, u32[]{:S(2)}) collective-permute-start(f32[136,128]{1,0:T(8,128)S(1)} %get-tuple-element.87), channel_id=1, source_target_pairs={{0,48},{16,32},{32,16},{48,0},{1,49},{17,33},{33,17},{49,1},{2,50}... | collective-permute-start | bytes 208904 | tf_op jit(solution)/shard_map/ppermute | solution.py:629
  80.6 4.2 %collective-permute-done.18.e2 = f32[136,128]{1,0:T(8,128)S(1)} collective-permute-done((f32[136,128]{1,0:T(8,128)S(1)}, f32[136,128]{1,0:T(8,128)S(1)}, u32[]{:S(2)}, u32[]{:S(2)}) %collective-permute-start.18) | collective-permute-done | bytes 69664 | tf_op jit(solution)/shard_map/ppermute | solution.py:629
  84.9 1.1 shard_map.60
  86.0 0.6 collective-permute-start.20
  86.6 1.6 %collective-permute-start.21 = (f32[520,128]{1,0:T(8,128)S(1)}, f32[520,128]{1,0:T(8,128)S(1)}, u32[]{:S(2)}, u32[]{:S(2)}) collective-permute-start(f32[520,128]{1,0:T(8,128)S(1)} %get-tuple-element.96), channel_id=1, source_target_pairs={{0,12},{2,14},{4,8},{6,10},{8,4},{10,6},{12,0},{14,2},{1,13},{3,15... | collective-permute-start | bytes 798728 | tf_op jit(solution)/shard_map/ppermute | solution.py:578
  88.2 2.0 %collective-permute-start.22 = (f32[520,128]{1,0:T(8,128)S(1)}, f32[520,128]{1,0:T(8,128)S(1)}, u32[]{:S(2)}, u32[]{:S(2)}) collective-permute-start(f32[520,128]{1,0:T(8,128)S(1)} %get-tuple-element.97), channel_id=1, source_target_pairs={{0,8},{2,10},{4,12},{6,14},{8,0},{10,2},{12,4},{14,6},{1,9},{3,11}... | collective-permute-start | bytes 798728 | tf_op jit(solution)/shard_map/ppermute | solution.py:578
  90.2 5.0 %shard_map.61 = (f32[4096,128]{1,0:T(8,128)S(1)}, f32[32,128]{1,0:T(8,128)S(1)}, f32[32,128]{1,0:T(8,128)S(1)}, s32[64,128]{1,0:T(8,128)S(1)}) custom-call(s32[32,128]{1,0:T(8,128)S(1)} %get-tuple-element.58.slot_rows.slots, s32[32,128]{1,0:T(8,128)S(1)} %get-tuple-element.58.slot_rows.slots, s32[32,128]{1,0:T(8,128)S(1)} %bitcast.8, s32[32,128]{1,0:T(8,128)S(1)} %bitcast.4, ...), custom_call_target="tpu_custom_call" | custom-call | flops 10000000000 | bytes 1000000 | tf_op jit(solution)/shard_map/pallas_call | solution.py:55
  95.2 1.3 collective-permute-done.20.refs_0_
  96.5 0.9 collective-permute-done.22.refs_3_
  97.4 0.6 shard_map.62
  98.0 6.0 %collective-permute-start.27 = (f32[4,520,128]{2,1,0:T(8,128)S(1)}, f32[4,520,128]{2,1,0:T(8,128)S(1)}, u32[]{:S(2)}, u32[]{:S(2)}) collective-permute-start(f32[4,520,128]{2,1,0:T(8,128)S(1)} %get-tuple-element.105), channel_id=1, source_target_pairs={{0,1},{1,0},{2,3},{3,2},{4,5},{5,4},{6,7},{7,6},{8,9},{9,8},{10,11... | collective-permute-start | bytes 3194888 | tf_op jit(solution)/shard_map/ppermute | solution.py:661
  103.9 2.2 %collective-permute-start.23 = (f32[520,128]{1,0:T(8,128)S(1)}, f32[520,128]{1,0:T(8,128)S(1)}, u32[]{:S(2)}, u32[]{:S(2)}) collective-permute-start(f32[520,128]{1,0:T(8,128)S(1)} %get-tuple-element.99), channel_id=1, source_target_pairs={{0,6},{2,0},{4,2},{6,4},{8,14},{10,8},{12,10},{14,12},{1,7},{3,1},... | collective-permute-start | bytes 798728 | tf_op jit(solution)/shard_map/ppermute | solution.py:578
  106.1 1.3 %collective-permute-start.25 = (f32[520,128]{1,0:T(8,128)S(1)}, f32[520,128]{1,0:T(8,128)S(1)}, u32[]{:S(2)}, u32[]{:S(2)}) collective-permute-start(f32[520,128]{1,0:T(8,128)S(1)} %get-tuple-element.102), channel_id=1, source_target_pairs={{0,2},{2,4},{4,6},{6,0},{8,10},{10,12},{12,14},{14,8},{1,3},{3,5},... | collective-permute-start | bytes 798728 | tf_op jit(solution)/shard_map/ppermute | solution.py:578
  107.4 1.0 collective-permute-start.26
  108.4 9.0 %collective-permute-done.23.refs_0_ = f32[520,128]{1,0:T(8,128)S(1)} collective-permute-done((f32[520,128]{1,0:T(8,128)S(1)}, f32[520,128]{1,0:T(8,128)S(1)}, u32[]{:S(2)}, u32[]{:S(2)}) %collective-permute-start.23) | collective-permute-done | bytes 266272 | tf_op jit(solution)/shard_map/ppermute | solution.py:578
  117.8 1.0 collective-permute-start.28
  118.8 1.4 %collective-permute-done.26.refs_1_ = f32[520,128]{1,0:T(8,128)S(1)} collective-permute-done((f32[520,128]{1,0:T(8,128)S(1)}, f32[520,128]{1,0:T(8,128)S(1)}, u32[]{:S(2)}, u32[]{:S(2)}) %collective-permute-start.26) | collective-permute-done | bytes 266272 | tf_op jit(solution)/shard_map/ppermute | solution.py:578
  120.6 1.6 %collective-permute-start.29 = (f32[2,520,128]{2,1,0:T(8,128)S(1)}, f32[2,520,128]{2,1,0:T(8,128)S(1)}, u32[]{:S(2)}, u32[]{:S(2)}) collective-permute-start(f32[2,520,128]{2,1,0:T(8,128)S(1)} %get-tuple-element.109), channel_id=1, source_target_pairs={{0,1},{1,0},{2,3},{3,2},{4,5},{5,4},{6,7},{7,6},{8,9},{9,8},{10,11... | collective-permute-start | bytes 1597448 | tf_op jit(solution)/shard_map/ppermute | solution.py:661
  122.2 0.7 shard_map.65
  122.9 0.8 collective-permute-done.29.got2
  123.8 4.5 %shard_map.66 = (f32[16,520,128]{2,1,0:T(8,128)S(1)}, f32[4096,128]{1,0:T(8,128)}) custom-call(s32[64,128]{1,0:T(8,128)S(1)} %get-tuple-element.91.user_rows, f32[4096,128]{1,0:T(8,128)S(1)} %get-tuple-element.92.run, f32[32,128]{1,0:T(8,128)S(1)} %get-tuple-element.93.ready.count, ...), custom_call_target="tpu_custom_call", output_to_operand_aliasing={{0}: (7, {})} | custom-call | flops 1000000 | bytes 1000000 | tf_op jit(solution)/shard_map/pallas_call | solution.py:55
  (40 shorter events, 4.3 us)
Async XLA Ops:
  0.8 1.6 %copy-start.2 = (f32[4096,128]{1,0:T(8,128)S(1)}, f32[4096,128]{1,0:T(8,128)}, u32[]{:S(2)}) copy-start(f32[4096,128]{1,0:T(8,128)} %features.1) | copy-start | bytes 6291460
  6.4 4.8 %collective-permute-start.3 = (f32[2,520,128]{2,1,0:T(8,128)S(1)}, f32[2,520,128]{2,1,0:T(8,128)S(1)}, u32[]{:S(2)}, u32[]{:S(2)}) collective-permute-start(f32[2,520,128]{2,1,0:T(8,128)S(1)} %get-tuple-element.71), channel_id=1, source_target_pairs={{0,1},{1,0},{2,3},{3,2},{4,5},{5,4},{6,7},{7,6},{8,9},{9,8},{10,11... | collective-permute-start | bytes 1597448 | tf_op jit(solution)/shard_map/ppermute | solution.py:600
  10.8 2.3 %collective-permute-start = (f32[2,520,128]{2,1,0:T(8,128)S(1)}, f32[2,520,128]{2,1,0:T(8,128)S(1)}, u32[]{:S(2)}, u32[]{:S(2)}) collective-permute-start(f32[2,520,128]{2,1,0:T(8,128)S(1)} %get-tuple-element.63), channel_id=1, source_target_pairs={{0,1},{1,0},{2,3},{3,2},{4,5},{5,4},{6,7},{7,6},{8,9},{9,8},{10,11... | collective-permute-start | bytes 1597448 | tf_op jit(solution)/shard_map/ppermute | solution.py:600
  12.6 5.0 %collective-permute-start.5 = (f32[2,520,128]{2,1,0:T(8,128)S(1)}, f32[2,520,128]{2,1,0:T(8,128)S(1)}, u32[]{:S(2)}, u32[]{:S(2)}) collective-permute-start(f32[2,520,128]{2,1,0:T(8,128)S(1)} %get-tuple-element.74), channel_id=1, source_target_pairs={{0,1},{1,0},{2,3},{3,2},{4,5},{5,4},{6,7},{7,6},{8,9},{9,8},{10,11... | collective-permute-start | bytes 1597448 | tf_op jit(solution)/shard_map/ppermute | solution.py:600
  14.5 5.7 %collective-permute-start.1 = (f32[2,520,128]{2,1,0:T(8,128)S(1)}, f32[2,520,128]{2,1,0:T(8,128)S(1)}, u32[]{:S(2)}, u32[]{:S(2)}) collective-permute-start(f32[2,520,128]{2,1,0:T(8,128)S(1)} %get-tuple-element.66), channel_id=1, source_target_pairs={{0,1},{1,0},{2,3},{3,2},{4,5},{5,4},{6,7},{7,6},{8,9},{9,8},{10,11... | collective-permute-start | bytes 1597448 | tf_op jit(solution)/shard_map/ppermute | solution.py:600
  14.7 20.9 %collective-permute-start.2 = (f32[520,128]{1,0:T(8,128)S(1)}, f32[520,128]{1,0:T(8,128)S(1)}, u32[]{:S(2)}, u32[]{:S(2)}) collective-permute-start(f32[520,128]{1,0:T(8,128)S(1)} %get-tuple-element.64.ready), channel_id=1, source_target_pairs={{0,2},{2,4},{4,6},{6,0},{8,10},{10,12},{12,14},{14,8},{1,3},{3,5},... | collective-permute-start | bytes 798728 | tf_op jit(solution)/shard_map/ppermute | solution.py:578
  14.7 25.2 %collective-permute-start.4 = (f32[520,128]{1,0:T(8,128)S(1)}, f32[520,128]{1,0:T(8,128)S(1)}, u32[]{:S(2)}, u32[]{:S(2)}) collective-permute-start(f32[520,128]{1,0:T(8,128)S(1)} %get-tuple-element.72.ready), channel_id=1, source_target_pairs={{0,4},{2,6},{4,0},{6,2},{8,12},{10,14},{12,8},{14,10},{1,5},{3,7},... | collective-permute-start | bytes 798728 | tf_op jit(solution)/shard_map/ppermute | solution.py:578
  16.7 29.0 %collective-permute-start.8 = (f32[520,128]{1,0:T(8,128)S(1)}, f32[520,128]{1,0:T(8,128)S(1)}, u32[]{:S(2)}, u32[]{:S(2)}) collective-permute-start(f32[520,128]{1,0:T(8,128)S(1)} %get-tuple-element.77), channel_id=1, source_target_pairs={{0,10},{2,12},{4,14},{6,8},{8,2},{10,4},{12,6},{14,0},{1,11},{3,13... | collective-permute-start | bytes 798728 | tf_op jit(solution)/shard_map/ppermute | solution.py:578
  17.6 28.0 %collective-permute-start.9 = (f32[520,128]{1,0:T(8,128)S(1)}, f32[520,128]{1,0:T(8,128)S(1)}, u32[]{:S(2)}, u32[]{:S(2)}) collective-permute-start(f32[520,128]{1,0:T(8,128)S(1)} %get-tuple-element.78), channel_id=1, source_target_pairs={{0,12},{2,14},{4,8},{6,10},{8,4},{10,6},{12,0},{14,2},{1,13},{3,15... | collective-permute-start | bytes 798728 | tf_op jit(solution)/shard_map/ppermute | solution.py:578
  20.2 25.5 %collective-permute-start.6 = (f32[520,128]{1,0:T(8,128)S(1)}, f32[520,128]{1,0:T(8,128)S(1)}, u32[]{:S(2)}, u32[]{:S(2)}) collective-permute-start(f32[520,128]{1,0:T(8,128)S(1)} %get-tuple-element.75), channel_id=1, source_target_pairs={{0,6},{2,0},{4,2},{6,4},{8,14},{10,8},{12,10},{14,12},{1,7},{3,1},... | collective-permute-start | bytes 798728 | tf_op jit(solution)/shard_map/ppermute | solution.py:578
  35.6 10.0 %collective-permute-start.7 = (f32[520,128]{1,0:T(8,128)S(1)}, f32[520,128]{1,0:T(8,128)S(1)}, u32[]{:S(2)}, u32[]{:S(2)}) collective-permute-start(f32[520,128]{1,0:T(8,128)S(1)} %get-tuple-element.76), channel_id=1, source_target_pairs={{0,8},{2,10},{4,12},{6,14},{8,0},{10,2},{12,4},{14,6},{1,9},{3,11}... | collective-permute-start | bytes 798728 | tf_op jit(solution)/shard_map/ppermute | solution.py:578
  40.0 6.9 %collective-permute-start.10 = (f32[520,128]{1,0:T(8,128)S(1)}, f32[520,128]{1,0:T(8,128)S(1)}, u32[]{:S(2)}, u32[]{:S(2)}) collective-permute-start(f32[520,128]{1,0:T(8,128)S(1)} %get-tuple-element.79), channel_id=1, source_target_pairs={{0,14},{2,8},{4,10},{6,12},{8,6},{10,0},{12,2},{14,4},{1,15},{3,9}... | collective-permute-start | bytes 798728 | tf_op jit(solution)/shard_map/ppermute | solution.py:578
  47.9 42.4 %copy-start = (s32[4096]{0:T(1024)S(1)}, s32[4096]{0:T(1024)}, u32[]{:S(2)}) copy-start(s32[4096]{0:T(1024)} %param.6) | copy-start | bytes 49156
  47.9 42.3 %copy-start.1 = (s32[4096,1]{0,1:T(1,128)S(1)}, s32[4096,1]{0,1:T(1,128)}, u32[]{:S(2)}) copy-start(s32[4096,1]{0,1:T(1,128)} %param.5) | copy-start | bytes 49156
  47.9 8.8 %collective-permute-start.11 = (f32[136,128]{1,0:T(8,128)S(1)}, f32[136,128]{1,0:T(8,128)S(1)}, u32[]{:S(2)}, u32[]{:S(2)}) collective-permute-start(f32[136,128]{1,0:T(8,128)S(1)} %get-tuple-element.81), channel_id=1, source_target_pairs={{0,16},{16,0},{32,48},{48,32},{1,17},{17,1},{33,49},{49,33},{2,18}... | collective-permute-start | bytes 208904 | tf_op jit(solution)/shard_map/ppermute | solution.py:619
  51.6 7.7 %collective-permute-start.12 = (f32[136,128]{1,0:T(8,128)S(1)}, f32[136,128]{1,0:T(8,128)S(1)}, u32[]{:S(2)}, u32[]{:S(2)}) collective-permute-start(f32[136,128]{1,0:T(8,128)S(1)} %get-tuple-element.82), channel_id=1, source_target_pairs={{0,32},{16,48},{32,0},{48,16},{1,33},{17,49},{33,1},{49,17},{2,34}... | collective-permute-start | bytes 208904 | tf_op jit(solution)/shard_map/ppermute | solution.py:619
  56.7 6.0 %collective-permute-start.13 = (f32[136,128]{1,0:T(8,128)S(1)}, f32[136,128]{1,0:T(8,128)S(1)}, u32[]{:S(2)}, u32[]{:S(2)}) collective-permute-start(f32[136,128]{1,0:T(8,128)S(1)} %get-tuple-element.83), channel_id=1, source_target_pairs={{0,48},{16,32},{32,16},{48,0},{1,49},{17,33},{33,17},{49,1},{2,50}... | collective-permute-start | bytes 208904 | tf_op jit(solution)/shard_map/ppermute | solution.py:619
  63.0 9.1 %collective-permute-start.14 = (f32[136,128]{1,0:T(8,128)S(1)}, f32[136,128]{1,0:T(8,128)S(1)}, u32[]{:S(2)}, u32[]{:S(2)}) collective-permute-start(f32[136,128]{1,0:T(8,128)S(1)} %shard_map.58), channel_id=1, source_target_pairs={{0,64},{64,128},{128,192},{1,65},{65,129},{129,193},{2,66},{66,130... | collective-permute-start | bytes 208904 | tf_op jit(solution)/shard_map/ppermute | solution.py:624
  66.2 5.9 %collective-permute-start.15 = (f32[136,128]{1,0:T(8,128)S(1)}, f32[136,128]{1,0:T(8,128)S(1)}, u32[]{:S(2)}, u32[]{:S(2)}) collective-permute-start(f32[136,128]{1,0:T(8,128)S(1)} %shard_map.58), channel_id=1, source_target_pairs={{0,128},{64,192},{1,129},{65,193},{2,130},{66,194},{3,131},{67,195... | collective-permute-start | bytes 208904 | tf_op jit(solution)/shard_map/ppermute | solution.py:624
  70.8 2.7 %collective-permute-start.16 = (f32[136,128]{1,0:T(8,128)S(1)}, f32[136,128]{1,0:T(8,128)S(1)}, u32[]{:S(2)}, u32[]{:S(2)}) collective-permute-start(f32[136,128]{1,0:T(8,128)S(1)} %shard_map.58), channel_id=1, source_target_pairs={{0,192},{1,193},{2,194},{3,195},{4,196},{5,197},{6,198},{7,199},{8... | collective-permute-start | bytes 208904 | tf_op jit(solution)/shard_map/ppermute | solution.py:624
  73.9 6.7 %collective-permute-start.17 = (f32[136,128]{1,0:T(8,128)S(1)}, f32[136,128]{1,0:T(8,128)S(1)}, u32[]{:S(2)}, u32[]{:S(2)}) collective-permute-start(f32[136,128]{1,0:T(8,128)S(1)} %get-tuple-element.85), channel_id=1, source_target_pairs={{0,16},{16,0},{32,48},{48,32},{1,17},{17,1},{33,49},{49,33},{2,18}... | collective-permute-start | bytes 208904 | tf_op jit(solution)/shard_map/ppermute | solution.py:629
  77.2 7.6 %collective-permute-start.18 = (f32[136,128]{1,0:T(8,128)S(1)}, f32[136,128]{1,0:T(8,128)S(1)}, u32[]{:S(2)}, u32[]{:S(2)}) collective-permute-start(f32[136,128]{1,0:T(8,128)S(1)} %get-tuple-element.86), channel_id=1, source_target_pairs={{0,32},{16,48},{32,0},{48,16},{1,33},{17,49},{33,1},{49,17},{2,34}... | collective-permute-start | bytes 208904 | tf_op jit(solution)/shard_map/ppermute | solution.py:629
  78.0 6.9 %collective-permute-start.19 = (f32[136,128]{1,0:T(8,128)S(1)}, f32[136,128]{1,0:T(8,128)S(1)}, u32[]{:S(2)}, u32[]{:S(2)}) collective-permute-start(f32[136,128]{1,0:T(8,128)S(1)} %get-tuple-element.87), channel_id=1, source_target_pairs={{0,48},{16,32},{32,16},{48,0},{1,49},{17,33},{33,17},{49,1},{2,50}... | collective-permute-start | bytes 208904 | tf_op jit(solution)/shard_map/ppermute | solution.py:629
  86.0 10.5 %collective-permute-start.20 = (f32[520,128]{1,0:T(8,128)S(1)}, f32[520,128]{1,0:T(8,128)S(1)}, u32[]{:S(2)}, u32[]{:S(2)}) collective-permute-start(f32[520,128]{1,0:T(8,128)S(1)} %get-tuple-element.95), channel_id=1, source_target_pairs={{0,4},{2,6},{4,0},{6,2},{8,12},{10,14},{12,8},{14,10},{1,5},{3,7},... | collective-permute-start | bytes 798728 | tf_op jit(solution)/shard_map/ppermute | solution.py:578
  86.6 9.9 %collective-permute-start.21 = (f32[520,128]{1,0:T(8,128)S(1)}, f32[520,128]{1,0:T(8,128)S(1)}, u32[]{:S(2)}, u32[]{:S(2)}) collective-permute-start(f32[520,128]{1,0:T(8,128)S(1)} %get-tuple-element.96), channel_id=1, source_target_pairs={{0,12},{2,14},{4,8},{6,10},{8,4},{10,6},{12,0},{14,2},{1,13},{3,15... | collective-permute-start | bytes 798728 | tf_op jit(solution)/shard_map/ppermute | solution.py:578
  88.2 9.2 %collective-permute-start.22 = (f32[520,128]{1,0:T(8,128)S(1)}, f32[520,128]{1,0:T(8,128)S(1)}, u32[]{:S(2)}, u32[]{:S(2)}) collective-permute-start(f32[520,128]{1,0:T(8,128)S(1)} %get-tuple-element.97), channel_id=1, source_target_pairs={{0,8},{2,10},{4,12},{6,14},{8,0},{10,2},{12,4},{14,6},{1,9},{3,11}... | collective-permute-start | bytes 798728 | tf_op jit(solution)/shard_map/ppermute | solution.py:578
  98.0 24.3 %collective-permute-start.27 = (f32[4,520,128]{2,1,0:T(8,128)S(1)}, f32[4,520,128]{2,1,0:T(8,128)S(1)}, u32[]{:S(2)}, u32[]{:S(2)}) collective-permute-start(f32[4,520,128]{2,1,0:T(8,128)S(1)} %get-tuple-element.105), channel_id=1, source_target_pairs={{0,1},{1,0},{2,3},{3,2},{4,5},{5,4},{6,7},{7,6},{8,9},{9,8},{10,11... | collective-permute-start | bytes 3194888 | tf_op jit(solution)/shard_map/ppermute | solution.py:661
  103.9 13.6 %collective-permute-start.23 = (f32[520,128]{1,0:T(8,128)S(1)}, f32[520,128]{1,0:T(8,128)S(1)}, u32[]{:S(2)}, u32[]{:S(2)}) collective-permute-start(f32[520,128]{1,0:T(8,128)S(1)} %get-tuple-element.99), channel_id=1, source_target_pairs={{0,6},{2,0},{4,2},{6,4},{8,14},{10,8},{12,10},{14,12},{1,7},{3,1},... | collective-permute-start | bytes 798728 | tf_op jit(solution)/shard_map/ppermute | solution.py:578
  106.1 11.4 %collective-permute-start.24 = (f32[520,128]{1,0:T(8,128)S(1)}, f32[520,128]{1,0:T(8,128)S(1)}, u32[]{:S(2)}, u32[]{:S(2)}) collective-permute-start(f32[520,128]{1,0:T(8,128)S(1)} %get-tuple-element.100), channel_id=1, source_target_pairs={{0,14},{2,8},{4,10},{6,12},{8,6},{10,0},{12,2},{14,4},{1,15},{3,9}... | collective-permute-start | bytes 798728 | tf_op jit(solution)/shard_map/ppermute | solution.py:578
  106.1 12.8 %collective-permute-start.25 = (f32[520,128]{1,0:T(8,128)S(1)}, f32[520,128]{1,0:T(8,128)S(1)}, u32[]{:S(2)}, u32[]{:S(2)}) collective-permute-start(f32[520,128]{1,0:T(8,128)S(1)} %get-tuple-element.102), channel_id=1, source_target_pairs={{0,2},{2,4},{4,6},{6,0},{8,10},{10,12},{12,14},{14,8},{1,3},{3,5},... | collective-permute-start | bytes 798728 | tf_op jit(solution)/shard_map/ppermute | solution.py:578
  107.4 12.8 %collective-permute-start.26 = (f32[520,128]{1,0:T(8,128)S(1)}, f32[520,128]{1,0:T(8,128)S(1)}, u32[]{:S(2)}, u32[]{:S(2)}) collective-permute-start(f32[520,128]{1,0:T(8,128)S(1)} %get-tuple-element.103), channel_id=1, source_target_pairs={{0,10},{2,12},{4,14},{6,8},{8,2},{10,4},{12,6},{14,0},{1,11},{3,13... | collective-permute-start | bytes 798728 | tf_op jit(solution)/shard_map/ppermute | solution.py:578
  117.8 5.1 %collective-permute-start.28 = (f32[2,520,128]{2,1,0:T(8,128)S(1)}, f32[2,520,128]{2,1,0:T(8,128)S(1)}, u32[]{:S(2)}, u32[]{:S(2)}) collective-permute-start(f32[2,520,128]{2,1,0:T(8,128)S(1)} %get-tuple-element.108), channel_id=1, source_target_pairs={{0,1},{1,0},{2,3},{3,2},{4,5},{5,4},{6,7},{7,6},{8,9},{9,8},{10,11... | collective-permute-start | bytes 1597448 | tf_op jit(solution)/shard_map/ppermute | solution.py:661
  120.6 3.2 %collective-permute-start.29 = (f32[2,520,128]{2,1,0:T(8,128)S(1)}, f32[2,520,128]{2,1,0:T(8,128)S(1)}, u32[]{:S(2)}, u32[]{:S(2)}) collective-permute-start(f32[2,520,128]{2,1,0:T(8,128)S(1)} %get-tuple-element.109), channel_id=1, source_target_pairs={{0,1},{1,0},{2,3},{3,2},{4,5},{5,4},{6,7},{7,6},{8,9},{9,8},{10,11... | collective-permute-start | bytes 1597448 | tf_op jit(solution)/shard_map/ppermute | solution.py:661
